TPU v7x, 128 devices: a whole 4x4x4 slice. The times are simulated.
128 devices in a mesh: dp: 8 (over z_lo, x), blk: 16 (over y, z_hi, core).
Axes of the slice: x: 4, y: 4, z: 4 (z_hi: 2, z_lo: 2; z = z_hi * 2 + z_lo), core: 2. Of those that a mesh axis runs over, the one named last changes fastest.
Arguments:
- inputs: bfloat16 [8, 4096, 1024], P('dp', 'blk'), may hold values from -6 to 6
- upstream: bfloat16 [8, 4096, 1024], P('dp', 'blk'), may hold values from -6 to 6
- gain: float32 [1024], replicated, may hold values from 0.5 to 1.5
- w_query: bfloat16 [1024, 1024], replicated
- w_key: bfloat16 [1024, 256], replicated
- w_value: bfloat16 [1024, 256], replicated, may hold values from -0.1875 to 0.1875
- w_out: bfloat16 [1024, 1024], replicated, may hold values from -0.1875 to 0.1875
- prefix_len: int32 [8], P('dp'), may hold values from 512 to 4032
- bound: int32 [8], P('dp'), may hold values from 0 to 31
Outputs:
- d_inputs: bfloat16 [8, 4096, 1024], P('dp', 'blk')
- d_query: float32 [1024, 1024], P('blk')
- d_key: float32 [1024, 256], P('blk')
- d_value: float32 [1024, 256], P('blk')
- d_out: float32 [1024, 1024], P('blk')
- d_gain: float32 [1024], P('blk')
All inputs are finite; a program needn't handle non-finite values.
Results may differ from a plain program's by a relative error of at most 0.02.
The roundings to bfloat16 on the way count: a program that leaves them out, or rounds other values in their place, can miss the bound.
Values may be sent and summed in bfloat16 or wider, within the bound.
No kernel may reach another device: no remote copies, remote signals or barrier semaphores. Data moves between devices by JAX's collectives and lax.ppermute only.
A program may use at most 128 MiB of HBM per device.

v0:
```python
import math

import jax
import jax.numpy as jnp
from jax import lax
from jax.sharding import PartitionSpec as P

HS = 256
ACT = 64
BLOCK = 128


EPS = 1e-06
NEG = -1e30


def in_one_piece(arrays, axis, dim, along):
    both = jnp.concatenate(arrays, axis=along)
    out, at, finished = (lax.all_gather(both, axis, axis=dim, tiled=True), 0, [])
    for a in arrays:
        finished.append(lax.slice_in_dim(out, at, at + a.shape[along], axis=along))
        at += a.shape[along]
    return tuple(finished)


def sent_together(arrays, axis, dim, along):
    widths = [math.prod(a.shape[along:]) for a in arrays]
    both = jnp.concatenate(
        [a.reshape(*a.shape[:along], w) for a, w in zip(arrays, widths)], axis=along
    )
    out = lax.psum_scatter(both, axis, scatter_dimension=dim, tiled=True)
    blocks = jnp.split(out, [sum(widths[:k]) for k in range(1, len(widths))], axis=along)
    return tuple((b.reshape(*out.shape[:along], *a.shape[along:]) for a, b in zip(arrays, blocks)))


def from_everyone(value, axis):
    copies = jnp.broadcast_to(value, (lax.axis_size(axis), *value.shape))
    return lax.all_to_all(copies, axis, split_axis=0, concat_axis=0, tiled=True)


def taken_together(value, axis):
    everything = from_everyone(value, axis)
    return jnp.sum(everything.astype(jnp.float32), axis=0)


def contract_last(left, right):
    return lax.dot_general(
        left, right, (((1,), (1,)), ((), ())), preferred_element_type=jnp.float32
    )


def contract_first(left, right):
    return lax.dot_general(
        left, right, (((0,), (0,)), ((), ())), preferred_element_type=jnp.float32
    )


def per_device(inputs, upstream, gain, w_query, w_key, w_value, w_out, prefix_len, bound):
    tok = inputs.shape[1]
    cycle_size = lax.axis_size("blk")
    seq = tok * cycle_size
    scaling = HS ** (-0.5)
    heads = w_query.shape[1] // HS
    xf = inputs[0].astype(jnp.float32)
    grad_out = upstream[0]
    inv = lax.rsqrt(jnp.mean(xf * xf, axis=-1, keepdims=True) + EPS)
    normed = xf * inv
    hidden = (normed * gain).astype(jnp.bfloat16)
    query = jnp.dot(hidden, w_query, preferred_element_type=jnp.float32).astype(jnp.bfloat16)
    keys = jnp.dot(hidden, w_key, preferred_element_type=jnp.float32).astype(jnp.bfloat16)
    values = jnp.dot(hidden, w_value, preferred_element_type=jnp.float32).astype(jnp.bfloat16)
    d_attn = contract_last(grad_out, w_out).astype(jnp.bfloat16)
    all_keys, all_values = in_one_piece((keys, values), "blk", 0, 1)
    q_three = query.reshape(tok, heads, HS)
    da_three = d_attn.reshape(tok, heads, HS)
    my_index = lax.axis_index("blk")
    q_pos = my_index * tok + jnp.arange(tok, dtype=jnp.int32)
    plen = prefix_len[0]
    edge = bound[0] * BLOCK
    width = min(512, seq)
    steps_count = seq // width

    def scores_of(key_rows, key_start):
        scores = (
            jnp.einsum("thd,kd->htk", q_three, key_rows, preferred_element_type=jnp.float32)
            * scaling
        )
        k_pos = key_start + jnp.arange(key_rows.shape[0], dtype=jnp.int32)
        key_ok = (k_pos < plen) | (k_pos >= seq - ACT)
        visible = key_ok[None, :] & ((k_pos[None, :] < edge) | (k_pos[None, :] <= q_pos[:, None]))
        return jnp.where(visible[None], scores, NEG)

    def take(array, index):
        return lax.dynamic_slice_in_dim(array, index * width, width, 0)

    def stat_step(index, carry):
        top, total = carry
        scores = scores_of(take(all_keys, index), index * width)
        new_top = jnp.maximum(top, jnp.max(scores, axis=-1))
        total = total * jnp.exp(top - new_top) + jnp.sum(
            jnp.exp(scores - new_top[..., None]), axis=-1
        )
        return (new_top, total)

    start_top = jnp.full((heads, tok), NEG, jnp.float32)
    top, total = lax.fori_loop(
        0, steps_count, stat_step, (start_top, jnp.zeros((heads, tok), jnp.float32))
    )

    def probs_of(scores):
        return jnp.exp(scores - top[..., None]) / total[..., None]

    def attn_step(index, acc):
        probs_b = probs_of(scores_of(take(all_keys, index), index * width)).astype(jnp.bfloat16)
        return acc + jnp.einsum(
            "htk,kd->thd", probs_b, take(all_values, index), preferred_element_type=jnp.float32
        )

    attn_acc = lax.fori_loop(0, steps_count, attn_step, jnp.zeros((tok, heads, HS), jnp.float32))
    attn_three = attn_acc.astype(jnp.bfloat16)
    attn = attn_three.reshape(tok, heads * HS)
    delta = jnp.sum(da_three.astype(jnp.float32) * attn_three.astype(jnp.float32), axis=-1).T

    def grads_of(key_rows, value_rows, key_start):
        probs = probs_of(scores_of(key_rows, key_start))
        probs_b = probs.astype(jnp.bfloat16)
        dprobs = jnp.einsum("thd,kd->htk", da_three, value_rows, preferred_element_type=jnp.float32)
        dscores = (probs * (dprobs - delta[..., None])).astype(jnp.bfloat16)
        return (probs_b, dscores)

    def query_step(index, dq_acc):
        key_rows = take(all_keys, index)
        probs_b, dscores = grads_of(key_rows, take(all_values, index), index * width)
        return dq_acc + jnp.einsum(
            "htk,kd->thd", dscores, key_rows, preferred_element_type=jnp.float32
        )

    zero_dq = jnp.zeros((tok, heads, HS), jnp.float32)
    dq_acc = lax.fori_loop(0, steps_count, query_step, zero_dq)
    key_rows = all_keys
    value_rows = all_values
    probs_b, dscores = grads_of(key_rows, value_rows, jnp.int32(0))
    d_k = jnp.einsum("htk,thd->kd", dscores, q_three, preferred_element_type=jnp.float32) * scaling
    d_v = jnp.einsum("htk,thd->kd", probs_b, da_three, preferred_element_type=jnp.float32)
    mine = lax.psum_scatter(
        jnp.concatenate([d_k, d_v], axis=1), "blk", scatter_dimension=0, tiled=True
    )
    d_query_rows = (dq_acc * scaling).astype(jnp.bfloat16).reshape(tok, heads * HS)
    d_key_rows = mine[:, :HS].astype(jnp.bfloat16)
    d_value_rows = mine[:, HS:].astype(jnp.bfloat16)
    dhidden = (
        contract_last(d_query_rows, w_query)
        + contract_last(d_key_rows, w_key)
        + contract_last(d_value_rows, w_value)
    )
    g_query = contract_first(hidden, d_query_rows)
    g_key = contract_first(hidden, d_key_rows)
    g_value = contract_first(hidden, d_value_rows)
    g_out = contract_first(attn, grad_out)
    g_gain = jnp.sum(dhidden * normed, axis=0)
    scaled = dhidden * gain
    d_in = grad_out.astype(jnp.float32) + inv * (
        scaled - normed * jnp.mean(scaled * normed, axis=-1, keepdims=True)
    )
    shares = tuple(
        (
            part.astype(jnp.float32)
            for part in sent_together(
                (
                    g_query.astype(jnp.bfloat16),
                    g_key.astype(jnp.bfloat16),
                    g_value.astype(jnp.bfloat16),
                    g_out.astype(jnp.bfloat16),
                    g_gain.astype(jnp.bfloat16),
                ),
                "blk",
                0,
                1,
            )
        )
    )
    shares = (
        taken_together(shares[0].astype(jnp.bfloat16), "dp").astype(jnp.float32),
        taken_together(shares[1].astype(jnp.bfloat16), "dp").astype(jnp.float32),
        taken_together(shares[2].astype(jnp.bfloat16), "dp").astype(jnp.float32),
        taken_together(shares[3].astype(jnp.bfloat16), "dp").astype(jnp.float32),
        taken_together(shares[4].astype(jnp.bfloat16), "dp").astype(jnp.float32),
    )
    return (d_in.astype(jnp.bfloat16)[None], shares[0], shares[1], shares[2], shares[3], shares[4])


def solution(mesh):
    placed = (P("dp", "blk", None), P("dp", "blk", None), P(), P(), P(), P(), P(), P("dp"), P("dp"))
    return jax.shard_map(
        per_device,
        mesh=mesh,
        in_specs=placed,
        out_specs=(
            P("dp", "blk", None),
            P("blk", None),
            P("blk", None),
            P("blk", None),
            P("blk", None),
            P("blk"),
        ),
        check_vma=False,
    )
```

profile of v0, /device:TPU:0, one launch (start us, length us, event | category | flops | bytes accessed | tf_op | source)
XLA Modules:
  0.0 479.1 jit_solution(924388052608694182)
XLA Ops:
  15.1 3.3 convolution_convert_fusion.2
  18.4 2.1 copy.158
  21.2 4.0 fusion.82
  25.2 48.9 %all-gather.2.cloned.1.call-done = bf16[4096,512]{0,1:T(8,128)(2,1)} async-done(((bf16[256,512]{0,1:T(8,128)(2,1)}), bf16[4096,512]{0,1:T(8,128)(2,1)}) %all-gather.2.cloned.1.call-update) | async-done | bytes 4194320 | tf_op jit(solution)/shard_map/all_gather | solution.py:19
  74.0 4.7 fusion.124
  78.7 4.1 copy.111
  82.8 46.8 %while.44 = (s32[]{:T(128)}, f32[4,256]{1,0:T(4,128)S(1)}, f32[4,256]{1,0:T(4,128)S(1)}, s32[]{:T(128)}, s32[]{:T(128)}, /*index=5*/bf16[4096,256]{1,0:T(8,128)(...) while((s32[]{:T(128)}, f32[4,256]{1,0:T(4,128)S(1)}, ...), condition=%wide.region_4.5_spmd.clone, body=%wide.region_1.4_spmd.clone.sunk | while | flops 272507136 | bytes 5435590 | solution.py:106
  83.7 2.8 fusion.162
  89.6 2.8 fusion.162
  92.4 2.1 exponential_reduce_fusion.2
  95.4 2.8 fusion.162
  101.3 2.8 fusion.162
  104.1 2.1 exponential_reduce_fusion.2
  107.2 2.8 fusion.162
  113.0 2.8 fusion.162
  115.8 2.1 exponential_reduce_fusion.2
  118.9 2.8 fusion.162
  124.7 2.8 fusion.162
  129.6 34.7 %while.45 = (s32[]{:T(128)}, f32[256,4,256]{0,2,1:T(8,128)}, bf16[4096,256]{0,1:T(8,128)(2,1)}, s32[]{:T(128)}, s32[]{:T(128)}, /*index=5*/bf16[4096,256]{1,0:T(...) while((s32[]{:T(128)}, f32[256,4,256]{0,2,1:T(8,128)}, ...), condition=%wide.region_6.7_spmd.clone, body=%wide.region_5.6_spmd.clone.sunk | while | flops 540413184 | bytes 3426000 | solution.py:119
  130.6 3.0 fusion.168
  134.6 3.4 fusion.168
  139.0 3.4 fusion.168
  143.3 3.4 fusion.168
  147.7 3.4 fusion.168
  152.1 3.4 fusion.168
  156.5 3.4 fusion.168
  160.9 3.4 fusion.168
  164.3 2.3 multiply_reduce_fusion
  166.8 7.3 %fusion.74 = f32[4,256,4096]{1,2,0:T(8,128)S(1)} fusion(f32[4,256]{1,0:T(4,128)S(1)} %get-tuple-element.1204, f32[4,256]{1,0:T(4,128)S(1)} %get-tuple-element.1202, pred[256,4096]{0,1:T(8,128)(4,1)} %fusion.82, bf16[32,4,8,256]{3,2,1,0:T(8,128)(2,1)} %bitcast.225, bf16[4096,512]{0,1:T(8,128)(2,1)} %all-gather.2.cloned.1.call-done), kind=kOutput, calls=%fused_computation.85 | convolution fusion | flops 2164260864 | bytes 20455424 | tf_op jit(solution)/shard_map/thd,kd->htk/dot_general | solution.py:85
  174.1 5.0 %fusion.78 = f32[4096,256]{0,1:T(8,128)} fusion(bf16[256,4,256]{0,2,1:T(8,128)(2,1)S(1)} %bitcast.218, f32[4,256,4096]{1,2,0:T(8,128)S(1)} %fusion.74), kind=kOutput, calls=%fused_computation.91 | convolution fusion | flops 2151677952 | bytes 21495808 | tf_op jit(solution)/shard_map/htk,thd->kd/dot_general | solution.py:144
  181.1 13.2 %fusion.77 = f32[4096,256]{0,1:T(8,128)} fusion(f32[4,256,4096]{1,2,0:T(8,128)} %copy-done.1, f32[4,256]{1,0:T(4,128)S(1)} %copy.115, bf16[32,4,8,256]{3,2,1,0:T(8,128)(2,1)} %bitcast.221, bf16[32,4,8,256]{3,2,1,0:T(8,128)(2,1)} %bitcast.226, bf16[4096,512]{0,1:T(8,128)(2,1)} %all-gather.2.cloned.1.call-done), kind=kOutput, calls=%fused_computation.90 | convolution fusion | flops 4308598784 | bytes 24121344 | tf_op jit(solution)/shard_map/htk,thd->kd/dot_general | solution.py:143
  194.2 7.7 %pad_maximum_fusion = f32[4096,512]{0,1:T(8,128)} fusion(f32[4096,256]{0,1:T(8,128)} %fusion.78, f32[4096,256]{0,1:T(8,128)} %fusion.77), kind=kLoop, calls=%fused_computation.86 | loop fusion | flops 2097152 | bytes 16777216 | tf_op jit(solution)/shard_map/concatenate | solution.py:146
  203.8 64.8 %while.46 = (s32[]{:T(128)}, f32[256,4,256]{0,2,1:T(8,128)}, bf16[4096,256]{1,0:T(8,128)(2,1)}, s32[]{:T(128)}, s32[]{:T(128)}, /*index=5*/bf16[256,4,256]{2,0,1...) while((s32[]{:T(128)}, f32[256,4,256]{0,2,1:T(8,128)}, ...), condition=%wide.region_9.10_spmd.clone, body=%wide.region_8.9_spmd.clone.sunk | while | flops 809897216 | bytes 8410852 | solution.py:139
  204.8 2.8 fusion.174
  207.6 4.3 fusion.176
  212.9 2.8 fusion.174
  215.8 4.7 fusion.176
  221.4 2.8 fusion.174
  224.2 4.4 fusion.176
  229.6 2.8 fusion.174
  232.4 4.2 fusion.176
  237.6 2.8 fusion.174
  240.4 4.2 fusion.176
  245.6 2.8 fusion.174
  248.4 4.2 fusion.176
  253.6 2.8 fusion.174
  256.4 4.2 fusion.176
  261.6 2.8 fusion.174
  264.4 4.2 fusion.176
  270.0 2.2 convert_dynamic-update-slice_fusion.1
  273.9 29.1 %reduce-scatter.5.cloned.1.call-done = f32[256,512]{0,1:T(8,128)} async-done(((f32[4096,512]{0,1:T(8,128)}), f32[256,512]{0,1:T(8,128)}) %reduce-scatter.5.cloned.1.call-update) | async-done | bytes 524304 | tf_op jit(solution)/shard_map/reduce_scatter | solution.py:145
  308.5 2.2 convert_dynamic-update-slice_fusion
  311.3 8.0 %copy.140 = bf16[1024,2561]{1,0:T(8,128)(2,1)} copy(bf16[1024,2561]{0,1:T(8,128)(2,1)} %constant_dynamic-update-slice_fusion) | data formatting | bytes 10489856
  319.3 84.9 %reduce-scatter.7.cloned.1.call-done = bf16[64,2561]{1,0:T(8,128)(2,1)} async-done(((bf16[1024,2561]{1,0:T(8,128)(2,1)}), bf16[64,2561]{1,0:T(8,128)(2,1)}) %reduce-scatter.7.cloned.1.call-update) | async-done | bytes 327824
  405.6 4.3 all-to-all-start.4
  410.7 5.3 %all-to-all-done.4 = bf16[8,1,64]{2,1,0:T(2,128)(2,1)S(1)} async-done(((bf16[8,1,64]{2,1,0:T(2,128)(2,1)}), bf16[8,1,64]{2,1,0:T(2,128)(2,1)S(1)}, u32[]{:S(2)}, u32[]{:S(2)}) %all-to-all-start.4) | async-done | bytes 1056 | tf_op jit(solution)/shard_map/all_to_all | solution.py:38
  416.1 9.7 %all_to_all.26 = bf16[8,64,256]{2,1,0:T(8,128)(2,1)S(1)} all-to-all(bf16[8,64,256]{2,1,0:T(8,128)(2,1)S(1)} %broadcast_in_dim.184), channel_id=1, replica_groups=mesh['dp'=8,'blk'=16] {'dp'}, dimensions={0} | all-to-all | bytes 524288 | tf_op jit(solution)/shard_map/all_to_all | solution.py:38
  426.5 4.0 all-to-all-start.1
  432.2 5.7 %all-to-all-done.1 = bf16[8,64,256]{2,1,0:T(8,128)(2,1)} async-done(((bf16[8,64,256]{2,1,0:T(8,128)(2,1)}), bf16[8,64,256]{2,1,0:T(8,128)(2,1)}, u32[]{:S(2)}, u32[]{:S(2)}) %all-to-all-start.1) | async-done | bytes 262176 | tf_op jit(solution)/shard_map/all_to_all | solution.py:38
  438.9 14.6 %all_to_all.27 = bf16[8,64,1024]{2,1,0:T(8,128)(2,1)} all-to-all(bf16[8,64,1024]{2,1,0:T(8,128)(2,1)S(1)} %broadcast_in_dim.185), channel_id=1, replica_groups=mesh['dp'=8,'blk'=16] {'dp'}, dimensions={0} | all-to-all | bytes 2097152 | tf_op jit(solution)/shard_map/all_to_all | solution.py:38
  454.7 4.2 all-to-all-start
  458.9 2.4 fusion.106
  465.1 5.4 %all-to-all-done = bf16[8,64,1024]{2,1,0:T(8,128)(2,1)} async-done(((bf16[8,64,1024]{2,1,0:T(8,128)(2,1)}), bf16[8,64,1024]{2,1,0:T(8,128)(2,1)}, u32[]{:S(2)}, u32[]{:S(2)}) %all-to-all-start) | async-done | bytes 1048608 | tf_op jit(solution)/shard_map/all_to_all | solution.py:38
  470.4 2.1 convert_reduce_fusion.1
  (193 shorter events, 63.7 us)
Async XLA Ops:
  7.2 5.6 %copy-start = (bf16[1024,1024]{1,0:T(8,128)(2,1)S(1)}, bf16[1024,1024]{1,0:T(8,128)(2,1)}, u32[]{:S(2)}) copy-start(bf16[1024,1024]{1,0:T(8,128)(2,1)} %param.18) | copy-start | bytes 6291460
  7.2 5.6 %copy-start.2 = (bf16[1,256,1024]{2,1,0:T(8,128)(2,1)S(1)}, bf16[1,256,1024]{2,1,0:T(8,128)(2,1)}, u32[]{:S(2)}) copy-start(bf16[1,256,1024]{2,1,0:T(8,128)(2,1)} %param.15) | copy-start | bytes 1572868
  7.2 5.6 %copy-start.11 = (f32[1024]{0:T(1024)S(1)}, f32[1024]{0:T(1024)}, u32[]{:S(2)}) copy-start(f32[1024]{0:T(1024)} %param.17) | copy-start | bytes 12292
  7.2 66.8 %all-gather.2.cloned.1.call-start = ((), (), s32[]{:S(2)}) async-start(), calls=%async_computation.7 | async-start | bytes 4456448 | tf_op jit(solution)/shard_map/all_gather | solution.py:19
  12.7 290.3 %reduce-scatter.5.cloned.1.call-start = ((), (), s32[]{:S(2)}) async-start(), calls=%async_computation.8 | async-start | bytes 8912896 | tf_op jit(solution)/shard_map/reduce_scatter | solution.py:145
  13.6 0.8 copy-start.9
  166.8 7.3 %copy-start.3 = (bf16[256,1024]{0,1:T(8,128)(2,1)S(1)}, bf16[256,1024]{0,1:T(8,128)(2,1)}, u32[]{:S(2)}) copy-start(bf16[256,1024]{0,1:T(8,128)(2,1)} %copy.158) | copy-start | bytes 1572868
  174.1 7.0 %copy-start.1 = (f32[4,256,4096]{1,2,0:T(8,128)}, f32[4,256,4096]{1,2,0:T(8,128)S(1)}, u32[]{:S(2)}) copy-start(f32[4,256,4096]{1,2,0:T(8,128)S(1)} %fusion.74) | copy-start | bytes 50331652
  201.9 202.3 %reduce-scatter.7.cloned.1.call-start = ((), (), s32[]{:S(2)}) async-start(), calls=%async_computation.9 | async-start | bytes 5849088
  273.9 32.7 %copy-start.10 = (bf16[1024,256]{1,0:T(8,128)(2,1)S(1)}, bf16[1024,256]{1,0:T(8,128)(2,1)}, u32[]{:S(2)}) copy-start(bf16[1024,256]{1,0:T(8,128)(2,1)} %param.19) | copy-start | bytes 1572868
  303.0 3.6 copy-start.4
  305.4 1.6 copy-start.8
  307.0 1.6 copy-start.6
  307.0 1.5 copy-start.7
  405.6 10.4 %all-to-all-start.4 = ((bf16[8,1,64]{2,1,0:T(2,128)(2,1)}), bf16[8,1,64]{2,1,0:T(2,128)(2,1)S(1)}, u32[]{:S(2)}, u32[]{:S(2)}) async-start(bf16[8,1,64]{2,1,0:T(2,128)(2,1)} %broadcast_in_dim.187), calls=%async_computation.5 | async-start | bytes 8192 | tf_op jit(solution)/shard_map/all_to_all | solution.py:38
  426.5 11.4 %all-to-all-start.1 = ((bf16[8,64,256]{2,1,0:T(8,128)(2,1)}), bf16[8,64,256]{2,1,0:T(8,128)(2,1)}, u32[]{:S(2)}, u32[]{:S(2)}) async-start(bf16[8,64,256]{2,1,0:T(8,128)(2,1)} %broadcast_in_dim.183), calls=%async_computation.2 | async-start | bytes 524288 | tf_op jit(solution)/shard_map/all_to_all | solution.py:38
  454.7 15.7 %all-to-all-start = ((bf16[8,64,1024]{2,1,0:T(8,128)(2,1)}), bf16[8,64,1024]{2,1,0:T(8,128)(2,1)}, u32[]{:S(2)}, u32[]{:S(2)}) async-start(bf16[8,64,1024]{2,1,0:T(8,128)(2,1)} %broadcast_in_dim.182), calls=%async_computation.1 | async-start | bytes 2097152 | tf_op jit(solution)/shard_map/all_to_all | solution.py:38
  458.9 5.3 %copy-start.5 = (bf16[8,64,1024]{2,1,0:T(8,128)(2,1)S(1)}, bf16[8,64,1024]{2,1,0:T(8,128)(2,1)}, u32[]{:S(2)}) copy-start(bf16[8,64,1024]{2,1,0:T(8,128)(2,1)} %all_to_all.27) | copy-start | bytes 3145732
Sparse Core Ops, SparseCore 0:
  12.8 61.1 all-gather.1
  202.1 100.9 reduce-scatter.4
  319.4 84.7 reduce-scatter.6
where the time goes:
time: 481 us; the launch traced here: 479 us
  waiting for transfers between devices  179 us (37%)
  matrix products  149 us (31%)
  other arithmetic  65.8 us (14%)
  local copies, waits for them, and re-layouts  31.1 us (6%)
  blocking collectives  24.3 us (5%)
  between operations  15.3 us (3%)
  starting transfers between devices  12.7 us (3%)
    unnamed x4, waiting for transfers between devices  85 us
    dot_general x17, matrix products, scores_of(): jnp.einsum('thd,kd->htk', q_three, key_rows, preferred_element_type=jnp.f...  52 us
    all_gather x1, waiting for transfers between devices, in_one_piece(): lax.all_gather(both, axis, axis=dim, tiled=True)  48.9 us
    dot_general x8, matrix products, query_step(): jnp.einsum('htk,kd->thd', dscores, key_rows, preferred_element_type=jnp.f...  34.6 us
    reduce_scatter x1, waiting for transfers between devices, per_device(): lax.psum_scatter(jnp.concatenate([d_k, d_v], axis=1), 'blk', scatter_dime...  29.1 us
    dot_general x8, matrix products, attn_step(): jnp.einsum('htk,kd->thd', probs_b, take(all_values, index), preferred_ele...  26.9 us
    all_to_all x2, blocking collectives, from_everyone(): return lax.all_to_all(copies, axis, split_axis=0, concat_axis=0, tiled=True)  24.3 us
    unnamed x30, local copies, waits for them, and re-layouts  17.3 us
  transfers between devices with their start and end apart: 6, of which 6 were waited for; matrix products, arithmetic and copies ran while one was open for 19% of the time, Pallas kernels for 0%

commit v1 on v0

v1 whole, which is shorter than its diff:
```python
import functools

import jax
import jax.numpy as jnp
from jax import lax
from jax.experimental import pallas as pl
from jax.experimental.pallas import tpu as pltpu
from jax.sharding import PartitionSpec as P

HS = 256
ACT = 64
BLOCK = 128
NEG = -1e30
LOG2E = 1.4426950408889634
VMEM_BYTES = 60 * 1024 * 1024
NT = (((1,), (1,)), ((), ()))


def dot_nt(a, b):
    return lax.dot_general(a, b, NT, preferred_element_type=jnp.float32)


def dot_nn(a, b):
    return jnp.dot(a, b, preferred_element_type=jnp.float32)


def block_state(info, chip, tok, seq):
    my, plen, edge = info[0], info[1], info[2]
    low = chip * (2 * tok)
    high = low + 2 * tok
    first, last = my * tok, my * tok + tok - 1
    seen = ((low < plen) | (high > seq - ACT)) & ((low < edge) | (low <= last))
    full = (high <= plen) & ((high <= edge) | (high - 1 <= first))
    return seen, full


def mask_of(info, chip, tok, seq):
    my, plen, edge, core = info[0], info[1], info[2], info[3]
    rows = lax.broadcasted_iota(jnp.int32, (2 * tok, tok), 0)
    k_pos = chip * (2 * tok) + (rows ^ (core * tok))
    q_pos = my * tok + lax.broadcasted_iota(jnp.int32, (2 * tok, tok), 1)
    key_ok = (k_pos < plen) | (k_pos >= seq - ACT)
    return key_ok & ((k_pos < edge) | (k_pos <= q_pos))


def per_block(info, chips, tok, seq, work, rest):
    def step(chip, carry):
        seen, full = block_state(info, chip, tok, seq)

        @pl.when(full)
        def _():
            work(chip, None)

        @pl.when(seen & jnp.logical_not(full))
        def _():
            work(chip, mask_of(info, chip, tok, seq))

        if rest is not None:

            @pl.when(jnp.logical_not(seen))
            def _():
                rest(chip)

        return carry

    lax.fori_loop(0, chips, step, 0)


def take_in(sources, scratch, sems, tok):
    copies = []
    for n, (own, pair, into) in enumerate(zip(sources[::2], sources[1::2], scratch)):
        copies.append(pltpu.make_async_copy(own, into.at[:, :tok, :], sems.at[2 * n]))
        copies.append(pltpu.make_async_copy(pair, into.at[:, tok:, :], sems.at[2 * n + 1]))
    for c in copies:
        c.start()
    return copies


def head(h):
    return pl.ds(h * HS, HS)


def scaled_scores(keys, q, h, mask):
    s = dot_nt(keys, q[:, head(h)]) * (HS ** (-0.5) * LOG2E)
    return s if mask is None else jnp.where(mask, s, NEG)


def stats_kernel(heads, seq, info, q, k_own, k_pair, lse, keys, top, total, sems):
    tok, chips = q.shape[0], k_own.shape[0]
    copies = take_in((k_own, k_pair), (keys,), sems, tok)
    top[...] = jnp.full(top.shape, NEG, jnp.float32)
    total[...] = jnp.zeros(total.shape, jnp.float32)
    for c in copies:
        c.wait()

    def work(chip, mask):
        for h in range(heads):
            s = scaled_scores(keys[chip], q, h, mask)
            old = top[:, head(h)]
            new = jnp.maximum(old, jnp.max(s, axis=0, keepdims=True))
            top[:, head(h)] = new
            total[:, head(h)] = total[:, head(h)] * jnp.exp2(old - new) + jnp.sum(
                jnp.exp2(s - new), axis=0, keepdims=True
            )

    per_block(info, chips, tok, seq, work, None)
    lse[...] = top[...] + jnp.log(total[...]) * LOG2E


def attend_kernel(
    heads, seq, info, q, da, lse, k_own, k_pair, v_own, v_pair,
    attn_t, delta, dv_own, dv_pair, probs_out,
    keys, values, values_t, da_rows, probs, sems, out_sems,
):
    tok, chips = q.shape[0], k_own.shape[0]
    wide = 2 * tok
    copies = take_in((k_own, k_pair, v_own, v_pair), (keys, values), sems, tok)
    for h in range(heads):
        da_rows[head(h), :] = da[:, head(h)]
    for c in copies:
        c.wait()
    for chip in range(chips):
        values_t[:, pl.ds(chip * wide, wide)] = values[chip].T

    def out_copy(chip):
        rows = pl.ds(pl.multiple_of(chip * wide, wide), wide)
        return pltpu.make_async_copy(probs.at[rows, :], probs_out.at[rows, :], out_sems.at[chip])

    def work(chip, mask):
        rows = pl.ds(pl.multiple_of(chip * wide, wide), wide)
        for h in range(heads):
            s = scaled_scores(keys[chip], q, h, mask)
            probs[rows, head(h)] = jnp.exp2(s - lse[:, head(h)]).astype(jnp.bfloat16)
        dv = dot_nn(probs[rows, :], da_rows[...]).astype(jnp.bfloat16)
        dv_own[chip] = dv[:tok]
        dv_pair[chip] = dv[tok:]
        out_copy(chip).start()

    def rest(chip):
        rows = pl.ds(pl.multiple_of(chip * wide, wide), wide)
        probs[rows, :] = jnp.zeros((wide, heads * HS), jnp.bfloat16)
        dv_own[chip] = jnp.zeros((tok, HS), jnp.bfloat16)
        dv_pair[chip] = jnp.zeros((tok, HS), jnp.bfloat16)
        out_copy(chip).start()

    per_block(info, chips, tok, seq, work, rest)
    for h in range(heads):
        a = dot_nn(values_t[...], probs[:, head(h)]).astype(jnp.bfloat16)
        attn_t[head(h), :] = a
        delta[:, head(h)] = jnp.sum(
            a.astype(jnp.float32) * da_rows[head(h), :].T.astype(jnp.float32), axis=0, keepdims=True
        )
    lax.fori_loop(0, chips, lambda chip, c: (out_copy(chip).wait(), c)[1], 0)


def grads_kernel(
    heads, seq, info, q, da, delta, k_own, k_pair, v_own, v_pair, probs_in,
    dq, dk_own, dk_pair,
    keys, values, keys_t, q_rows, probs, dscores, sems, in_sems,
):
    tok, chips = q.shape[0], k_own.shape[0]
    wide = 2 * tok
    copies = take_in((k_own, k_pair, v_own, v_pair), (keys, values), sems, tok)

    def in_copy(chip):
        rows = pl.ds(pl.multiple_of(chip * wide, wide), wide)
        return pltpu.make_async_copy(probs_in.at[rows, :], probs.at[rows, :], in_sems.at[chip])

    lax.fori_loop(0, chips, lambda chip, c: (in_copy(chip).start(), c)[1], 0)
    for h in range(heads):
        q_rows[head(h), :] = q[:, head(h)]
    for c in copies:
        c.wait()
    for chip in range(chips):
        keys_t[:, pl.ds(chip * wide, wide)] = keys[chip].T

    def step(chip, carry):
        rows = pl.ds(pl.multiple_of(chip * wide, wide), wide)
        in_copy(chip).wait()
        seen, _ = block_state(info, chip, tok, seq)

        @pl.when(seen)
        def _():
            for h in range(heads):
                dp = dot_nt(values[chip], da[:, head(h)])
                p = probs[rows, head(h)].astype(jnp.float32)
                dscores[rows, head(h)] = (p * (dp - delta[:, head(h)])).astype(jnp.bfloat16)
            dk = (dot_nn(dscores[rows, :], q_rows[...]) * HS ** (-0.5)).astype(jnp.bfloat16)
            dk_own[chip] = dk[:tok]
            dk_pair[chip] = dk[tok:]

        @pl.when(jnp.logical_not(seen))
        def _():
            dscores[rows, :] = jnp.zeros((wide, heads * HS), jnp.bfloat16)
            dk_own[chip] = jnp.zeros((tok, HS), jnp.bfloat16)
            dk_pair[chip] = jnp.zeros((tok, HS), jnp.bfloat16)

        return carry

    lax.fori_loop(0, chips, step, 0)
    for h in range(heads):
        d = dot_nn(keys_t[...], dscores[:, head(h)]) * HS ** (-0.5)
        dq[:, head(h)] = d.T.astype(jnp.bfloat16)


SMEM = pl.BlockSpec(memory_space=pltpu.SMEM)
VMEM = pl.BlockSpec(memory_space=pltpu.VMEM)
ANY = pl.BlockSpec(memory_space=pl.ANY)


def params():
    return pltpu.CompilerParams(vmem_limit_bytes=VMEM_BYTES)


def cost(flops, elements):
    return pl.CostEstimate(flops=flops, bytes_accessed=2 * elements, transcendentals=elements)


def run_stats(info, q, k_own, k_pair):
    tok, width = q.shape
    heads, chips = width // HS, k_own.shape[0]
    seq = 2 * tok * chips
    return pl.pallas_call(
        functools.partial(stats_kernel, heads, seq),
        out_shape=jax.ShapeDtypeStruct((1, width), jnp.float32),
        in_specs=[SMEM, VMEM, ANY, ANY],
        out_specs=VMEM,
        scratch_shapes=[
            pltpu.VMEM((chips, 2 * tok, HS), jnp.bfloat16),
            pltpu.VMEM((1, width), jnp.float32),
            pltpu.VMEM((1, width), jnp.float32),
            pltpu.SemaphoreType.DMA((2,)),
        ],
        compiler_params=params(),
        cost_estimate=cost(2 * seq * width * HS, seq * width),
        name="stats",
    )(info, q, k_own, k_pair)


def run_attend(info, q, da, lse, k_own, k_pair, v_own, v_pair):
    tok, width = q.shape
    heads, chips = width // HS, k_own.shape[0]
    seq = 2 * tok * chips
    part = jax.ShapeDtypeStruct((chips, tok, HS), jnp.bfloat16)
    return pl.pallas_call(
        functools.partial(attend_kernel, heads, seq),
        out_shape=(
            jax.ShapeDtypeStruct((width, tok), jnp.bfloat16),
            jax.ShapeDtypeStruct((1, width), jnp.float32),
            part,
            part,
            jax.ShapeDtypeStruct((seq, width), jnp.bfloat16),
        ),
        in_specs=[SMEM, VMEM, VMEM, VMEM, ANY, ANY, ANY, ANY],
        out_specs=(VMEM, VMEM, VMEM, VMEM, ANY),
        scratch_shapes=[
            pltpu.VMEM((chips, 2 * tok, HS), jnp.bfloat16),
            pltpu.VMEM((chips, 2 * tok, HS), jnp.bfloat16),
            pltpu.VMEM((HS, seq), jnp.bfloat16),
            pltpu.VMEM((width, HS), jnp.bfloat16),
            pltpu.VMEM((seq, width), jnp.bfloat16),
            pltpu.SemaphoreType.DMA((4,)),
            pltpu.SemaphoreType.DMA((chips,)),
        ],
        compiler_params=params(),
        cost_estimate=cost(6 * seq * width * HS, seq * width),
        name="attend",
    )(info, q, da, lse, k_own, k_pair, v_own, v_pair)


def run_grads(info, q, da, delta, k_own, k_pair, v_own, v_pair, probs):
    tok, width = q.shape
    heads, chips = width // HS, k_own.shape[0]
    seq = 2 * tok * chips
    part = jax.ShapeDtypeStruct((chips, tok, HS), jnp.bfloat16)
    return pl.pallas_call(
        functools.partial(grads_kernel, heads, seq),
        out_shape=(jax.ShapeDtypeStruct((tok, width), jnp.bfloat16), part, part),
        in_specs=[SMEM, VMEM, VMEM, VMEM, ANY, ANY, ANY, ANY, ANY],
        out_specs=(VMEM, VMEM, VMEM),
        scratch_shapes=[
            pltpu.VMEM((chips, 2 * tok, HS), jnp.bfloat16),
            pltpu.VMEM((chips, 2 * tok, HS), jnp.bfloat16),
            pltpu.VMEM((HS, seq), jnp.bfloat16),
            pltpu.VMEM((width, HS), jnp.bfloat16),
            pltpu.VMEM((seq, width), jnp.bfloat16),
            pltpu.VMEM((seq, width), jnp.bfloat16),
            pltpu.SemaphoreType.DMA((4,)),
            pltpu.SemaphoreType.DMA((chips,)),
        ],
        compiler_params=params(),
        cost_estimate=cost(6 * seq * width * HS, seq * width),
        name="grads",
    )(info, q, da, delta, k_own, k_pair, v_own, v_pair, probs)


EPS = 1e-06


def contract_first(left, right):
    return lax.dot_general(
        left, right, (((0,), (0,)), ((), ())), preferred_element_type=jnp.float32
    )


def same_core(count):
    return [[core + 2 * chip for chip in range(count // 2)] for core in range(2)]


def swap_cores(value):
    count = lax.axis_size("blk")
    return lax.ppermute(value, "blk", [(i, i ^ 1) for i in range(count)])


def exchange_chips(value):
    groups = same_core(lax.axis_size("blk"))
    return lax.all_to_all(value, "blk", 0, 0, tiled=True, axis_index_groups=groups)


def gather_chips(value):
    copies = jnp.broadcast_to(value, (lax.axis_size("blk") // 2, *value.shape))
    return exchange_chips(copies)


def sum_first(parts):
    return jnp.sum(parts.astype(jnp.float32), axis=0)


def reduce_to_owner(own, pair):
    received = swap_cores(pair.astype(jnp.bfloat16))
    chip_sum = own.astype(jnp.float32) + received.astype(jnp.float32)
    return sum_first(exchange_chips(chip_sum.astype(jnp.bfloat16)))


def reduce_weights(grad):
    count, core = lax.axis_size("blk"), lax.axis_index("blk") % 2
    rows = grad.shape[0] // count
    parts = grad.reshape(count // 2, 2, rows, *grad.shape[1:])
    own = lax.dynamic_index_in_dim(parts, core, 1, keepdims=False)
    pair = lax.dynamic_index_in_dim(parts, 1 - core, 1, keepdims=False)
    mine = reduce_to_owner(own, pair).astype(jnp.bfloat16)
    copies = jnp.broadcast_to(mine, (lax.axis_size("dp"), *mine.shape))
    return sum_first(lax.all_to_all(copies, "dp", 0, 0, tiled=True))


def per_device(inputs, upstream, gain, w_query, w_key, w_value, w_out, prefix_len, bound):
    bf16 = jnp.bfloat16
    xf = inputs[0].astype(jnp.float32)
    grad_out = upstream[0]
    my = lax.axis_index("blk")
    count = lax.axis_size("blk")
    inv = lax.rsqrt(jnp.mean(xf * xf, axis=-1, keepdims=True) + EPS)
    normed = xf * inv
    hidden = (normed * gain).astype(bf16)
    keys = dot_nn(hidden, w_key).astype(bf16)
    k_own = gather_chips(keys)
    values = dot_nn(hidden, w_value).astype(bf16)
    v_own = gather_chips(values)
    k_pair = swap_cores(k_own)
    v_pair = swap_cores(v_own)
    query = dot_nn(hidden, w_query).astype(bf16)
    d_attn = dot_nt(grad_out, w_out).astype(bf16)
    info = jnp.stack([my, prefix_len[0], bound[0] * BLOCK, my % 2]).astype(jnp.int32)

    lse = run_stats(info, query, k_own, k_pair)
    attn_t, delta, dv_own, dv_pair, probs = run_attend(
        info, query, d_attn, lse, k_own, k_pair, v_own, v_pair
    )
    d_value_rows = reduce_to_owner(dv_own, dv_pair).astype(bf16)
    g_out = dot_nn(attn_t, grad_out)
    g_value = contract_first(hidden, d_value_rows)

    d_query_rows, dk_own, dk_pair = run_grads(
        info, query, d_attn, delta, k_own, k_pair, v_own, v_pair, probs
    )
    d_key_rows = reduce_to_owner(dk_own, dk_pair).astype(bf16)
    g_query = contract_first(hidden, d_query_rows)
    dhidden = (
        dot_nt(d_query_rows, w_query) + dot_nt(d_key_rows, w_key) + dot_nt(d_value_rows, w_value)
    )
    g_key = contract_first(hidden, d_key_rows)
    g_gain = jnp.sum(dhidden * normed, axis=0)
    scaled = dhidden * gain
    d_in = grad_out.astype(jnp.float32) + inv * (
        scaled - normed * jnp.mean(scaled * normed, axis=-1, keepdims=True)
    )

    rows = g_gain.shape[0] // count
    gain_rows = jnp.pad(g_gain.reshape(count, 1, rows), ((0, 0), (0, 7), (0, HS - rows)))
    late = jnp.concatenate([g_key.reshape(count, rows, HS), gain_rows], axis=1)
    late = reduce_weights(late.reshape(count * (rows + 8), HS))
    early = reduce_weights(jnp.concatenate([g_out, g_value], axis=1))
    d_q = reduce_weights(g_query)
    width = g_out.shape[1]
    return (
        d_in.astype(bf16)[None],
        d_q,
        late[:rows],
        early[:, width:],
        early[:, :width],
        late[rows, :rows],
    )


def solution(mesh):
    placed = (P("dp", "blk", None), P("dp", "blk", None), P(), P(), P(), P(), P(), P("dp"), P("dp"))
    return jax.shard_map(
        per_device,
        mesh=mesh,
        in_specs=placed,
        out_specs=(
            P("dp", "blk", None),
            P("blk", None),
            P("blk", None),
            P("blk", None),
            P("blk", None),
            P("blk"),
        ),
        check_vma=False,
    )
```

time: 481 us -> 282 us (0.59)
  matrix products: 149 us -> 19.6 us
  waiting for transfers between devices: 179 us -> 111 us
  starting transfers between devices: 12.7 us -> 58.6 us
  other arithmetic: 65.8 us -> 28.6 us
  Pallas kernels: 0 us -> 23.3 us
  between operations: 15.3 us -> 2.25 us
  blocking collectives: 24.3 us -> 13.5 us
  local copies, waits for them, and re-layouts: 31.1 us -> 23 us
    dot_general x42 -> x8, matrix products: 143 us -> 17.2 us  [the longest x4 8.84 us: dot_nt(): return lax.dot_general(a, b, NT, preferred_element_type=jnp.float32)]
    all_to_all x3 -> x9, waiting for transfers between devices: 16.3 us -> 111 us  [the longest x6 79.4 us: exchange_chips(): lax.all_to_all(value, 'blk', 0, 0, tiled=True, axis_index_groups=groups)]
    unnamed x4 -> x0, waiting for transfers between devices: 85 us -> none
    all_gather x1 -> x0, waiting for transfers between devices: 48.9 us -> none  [in_one_piece(): lax.all_gather(both, axis, axis=dim, tiled=True)]
    all_to_all x3 -> x9, starting transfers between devices: 12.6 us -> 56.7 us  [the longest x6 34.7 us: exchange_chips(): lax.all_to_all(value, 'blk', 0, 0, tiled=True, axis_index_groups=groups)]
    reduce_scatter x1 -> x0, waiting for transfers between devices: 29.1 us -> none  [per_device(): lax.psum_scatter(jnp.concatenate([d_k, d_v], axis=1), 'blk', scatter_dime...]
    pallas_call x0 -> x3, Pallas kernels: none -> 23.3 us  [the longest x1 9.73 us: run_attend(): pl.pallas_call(functools.partial(attend_kernel, heads, seq), out_shape=(j...]
    reduce_sum x14 -> x9, other arithmetic: 24.5 us -> 8.57 us  [the longest x8 8.08 us: sum_first(): return jnp.sum(parts.astype(jnp.float32), axis=0)]
  transfers between devices with their start and end apart: 6 -> 16, of which waited for: 6 -> 9; matrix products, arithmetic and copies ran while one was open for 19% -> 17% of each run, Pallas kernels for 0% -> 5%
where the time goes in v1:
time: 282 us; the launch traced here: 280 us
  waiting for transfers between devices  111 us (39%)
  starting transfers between devices  58.6 us (21%)
  other arithmetic  28.6 us (10%)
  Pallas kernels  23.3 us (8%)
  local copies, waits for them, and re-layouts  23 us (8%)
  matrix products  19.6 us (7%)
  blocking collectives  13.5 us (5%)
    all_to_all x6, waiting for transfers between devices, exchange_chips(): lax.all_to_all(value, 'blk', 0, 0, tiled=True, axis_index_groups=groups)  79.4 us
    all_to_all x6, starting transfers between devices, exchange_chips(): lax.all_to_all(value, 'blk', 0, 0, tiled=True, axis_index_groups=groups)  34.7 us
    all_to_all x3, waiting for transfers between devices, reduce_weights(): return sum_first(lax.all_to_all(copies, 'dp', 0, 0, tiled=True))  31.7 us
    all_to_all x3, starting transfers between devices, reduce_weights(): return sum_first(lax.all_to_all(copies, 'dp', 0, 0, tiled=True))  22 us
    all_to_all x1, blocking collectives, exchange_chips(): lax.all_to_all(value, 'blk', 0, 0, tiled=True, axis_index_groups=groups)  13.5 us
    convert_element_type x5, other arithmetic, reduce_to_owner(): return sum_first(exchange_chips(chip_sum.astype(jnp.bfloat16)))  12.3 us
    pallas_call x1, Pallas kernels, run_attend(): pl.pallas_call(functools.partial(attend_kernel, heads, seq), out_shape=(j...  9.73 us
    pallas_call x1, Pallas kernels, run_grads(): pl.pallas_call(functools.partial(grads_kernel, heads, seq), out_shape=(ja...  9.26 us
  transfers between devices with their start and end apart: 16, of which 9 were waited for; matrix products, arithmetic and copies ran while one was open for 17% of the time, Pallas kernels for 5%

profile of v1, /device:TPU:0, one launch (start us, length us, event | category | flops | bytes accessed | tf_op | source)
XLA Modules:
  0.0 280.1 jit_solution(9731024183176580198)
XLA Ops:
  0.6 1.4 fusion.15
  2.1 1.6 convolution_convert_fusion.3
  3.7 1.0 broadcast_in_dim.22
  4.7 7.9 %all-to-all-start = ((bf16[8,256,256]{2,1,0:T(8,128)(2,1)}), bf16[8,256,256]{2,1,0:T(8,128)(2,1)}, u32[]{:S(2)}, u32[]{:S(2)}) async-start(bf16[8,256,256]{2,1,0:T(8,128)(2,1)} %broadcast_in_dim.22), calls=%async_computation | async-start | bytes 2097152 | tf_op jit(solution)/shard_map/all_to_all | solution.py:317
  12.6 1.5 convolution_convert_fusion.2
  14.1 14.5 %all-to-all-done.k_own = bf16[8,256,256]{2,1,0:T(8,128)(2,1)} async-done(((bf16[8,256,256]{2,1,0:T(8,128)(2,1)}), bf16[8,256,256]{2,1,0:T(8,128)(2,1)}, u32[]{:S(2)}, u32[]{:S(2)}) %all-to-all-start) | async-done | bytes 1048608 | tf_op jit(solution)/shard_map/all_to_all | solution.py:317
  28.6 1.0 broadcast_in_dim.23
  29.7 4.2 %all-to-all-start.1 = ((bf16[8,256,256]{2,1,0:T(8,128)(2,1)}), bf16[8,256,256]{2,1,0:T(8,128)(2,1)}, u32[]{:S(2)}, u32[]{:S(2)}) async-start(bf16[8,256,256]{2,1,0:T(8,128)(2,1)} %broadcast_in_dim.23), calls=%async_computation.1 | async-start | bytes 2097152 | tf_op jit(solution)/shard_map/all_to_all | solution.py:317
  34.0 15.4 %all-to-all-done.1.v_own = bf16[8,256,256]{2,1,0:T(8,128)(2,1)} async-done(((bf16[8,256,256]{2,1,0:T(8,128)(2,1)}), bf16[8,256,256]{2,1,0:T(8,128)(2,1)}, u32[]{:S(2)}, u32[]{:S(2)}) %all-to-all-start.1) | async-done | bytes 1048608 | tf_op jit(solution)/shard_map/all_to_all | solution.py:317
  50.7 0.6 pad_add_fusion.info
  51.3 3.1 %convolution_convert_fusion.da = bf16[256,1024]{1,0:T(8,128)(2,1)} fusion(bf16[1024,1024]{1,0:T(8,128)(2,1)} %param.15, bf16[1,256,1024]{2,1,0:T(8,128)(2,1)S(1)} %copy-done.11), kind=kOutput, calls=%fused_computation.20 | convolution fusion | flops 537133056 | bytes 3145728 | tf_op jit(solution)/shard_map/dot_general | solution.py:20
  54.5 1.6 convolution_convert_fusion.1.q
  56.0 4.3 %stats.1.lse = f32[1,1024]{1,0:T(1,128)} custom-call(s32[4]{0:T(128)} %pad_add_fusion.info, bf16[256,1024]{1,0:T(8,128)(2,1)} %convolution_convert_fusion.1.q, bf16[8,256,256]{2,1,0:T(8,128)(2,1)} %all-to-all-done.k_own, bf16[8,256,256]{2,1,0:T(8,128)(2,1)} %collective-permute-done.k_pair), custom_call_target="tpu_custom_call" | custom-call | flops 2147483648 | bytes 8388608 | tf_op jit(solution)/shard_map/stats/pallas_call | solution.py:223
  60.3 9.7 %attend.1 = (bf16[1024,256]{1,0:T(8,128)(2,1)}, f32[1,1024]{1,0:T(1,128)}, bf16[8,256,256]{2,1,0:T(8,128)(2,1)}, bf16[8,256,256]{2,1,0:T(8,128)(2,1)}, bf16[4096,1024]{1,0:T(8,128)(2,1)}) custom-call(s32[4]{0:T(128)} %pad_add_fusion.info, bf16[256,1024]{1,0:T(8,128)(2,1)} %convolution_convert_fusion.1.q, bf16[256,1024]{1,0:T(8,128)(2,1)} %convolution_convert_fusion.da, ...), custom_call_target="tpu_custom_call" | custom-call | flops 6442450944 | bytes 8388608 | tf_op jit(solution)/shard_map/attend/pallas_call | solution.py:245
  70.0 0.8 collective-permute-start.3
  70.8 9.3 %grads.1 = (bf16[256,1024]{1,0:T(8,128)(2,1)}, bf16[8,256,256]{2,1,0:T(8,128)(2,1)}, bf16[8,256,256]{2,1,0:T(8,128)(2,1)}) custom-call(s32[4]{0:T(128)} %pad_add_fusion.info, bf16[256,1024]{1,0:T(8,128)(2,1)} %convolution_convert_fusion.1.q, bf16[256,1024]{1,0:T(8,128)(2,1)} %convolution_convert_fusion.da, f32[1,1024]{1,0:T(1,128)} %get-tuple-element.14.delta, ...), custom_call_target="tpu_custom_call" | custom-call | flops 6442450944 | bytes 8388608 | tf_op jit(solution)/shard_map/grads/pallas_call | solution.py:276
  80.2 2.8 add_convert_fusion
  82.9 10.9 %all-to-all-start.3 = ((bf16[8,256,256]{2,1,0:T(8,128)(2,1)}), bf16[8,256,256]{2,1,0:T(8,128)(2,1)}, u32[]{:S(2)}, u32[]{:S(2)}) async-start(bf16[8,256,256]{2,1,0:T(8,128)(2,1)} %add_convert_fusion), calls=%async_computation.3 | async-start | bytes 2097152 | tf_op jit(solution)/shard_map/all_to_all | solution.py:317
  93.9 2.8 add_convert_fusion.1
  96.6 14.6 %all-to-all-done.3 = bf16[8,256,256]{2,1,0:T(8,128)(2,1)} async-done(((bf16[8,256,256]{2,1,0:T(8,128)(2,1)}), bf16[8,256,256]{2,1,0:T(8,128)(2,1)}, u32[]{:S(2)}, u32[]{:S(2)}) %all-to-all-start.3) | async-done | bytes 1048608 | tf_op jit(solution)/shard_map/all_to_all | solution.py:317
  111.3 4.2 %all-to-all-start.2 = ((bf16[8,256,256]{2,1,0:T(8,128)(2,1)}), bf16[8,256,256]{2,1,0:T(8,128)(2,1)}, u32[]{:S(2)}, u32[]{:S(2)}) async-start(bf16[8,256,256]{2,1,0:T(8,128)(2,1)} %add_convert_fusion.1), calls=%async_computation.2 | async-start | bytes 2097152 | tf_op jit(solution)/shard_map/all_to_all | solution.py:317
  115.5 3.7 %fusion.21 = f32[1024,1024]{0,1:T(8,128)} fusion(bf16[1024,256]{1,0:T(8,128)(2,1)} %get-tuple-element.21, bf16[1,256,1024]{2,1,0:T(8,128)(2,1)S(1)} %copy-done.11), kind=kOutput, calls=%fused_computation.42 | convolution fusion | flops 536870912 | bytes 5242880 | tf_op jit(solution)/shard_map/dot_general | solution.py:24
  119.3 1.4 reduce_sum.116
  120.6 2.4 fusion.34
  123.0 1.4 fusion.27
  124.4 6.7 %all-to-all-done.2 = bf16[8,256,256]{2,1,0:T(8,128)(2,1)} async-done(((bf16[8,256,256]{2,1,0:T(8,128)(2,1)}), bf16[8,256,256]{2,1,0:T(8,128)(2,1)}, u32[]{:S(2)}, u32[]{:S(2)}) %all-to-all-start.2) | async-done | bytes 1048608 | tf_op jit(solution)/shard_map/all_to_all | solution.py:317
  131.1 1.4 reduce_sum.115
  132.5 1.5 fusion.33
  134.0 1.9 fusion.2
  135.9 0.5 fusion.14
  136.9 0.7 fusion.19
  137.6 2.1 copy-done.3
  139.7 1.1 fusion.16
  141.3 1.0 copy-done.9
  142.4 0.6 collective-permute-start.5
  143.0 0.6 copy-done.2
  143.6 3.2 %pad_maximum_fusion = f32[1024,1280]{0,1:T(8,128)} fusion(f32[1024,256]{0,1:T(8,128)S(1)} %copy-done.6, f32[1024,1024]{0,1:T(8,128)S(1)} %copy-done.2), kind=kLoop, calls=%fused_computation | loop fusion | flops 1310720 | bytes 10485760 | tf_op jit(solution)/shard_map/concatenate | solution.py:392
  146.8 5.9 %copy.22 = f32[1024,1280]{1,0:T(8,128)} copy(f32[1024,1280]{0,1:T(8,128)} %pad_maximum_fusion) | data formatting | bytes 10485760 | tf_op jit(solution)/shard_map/concatenate | solution.py:392
  152.7 3.0 %fusion.7 = bf16[8,64,1280]{2,1,0:T(8,128)(2,1)} fusion(f32[8,2,64,1280]{3,2,1,0:T(8,128)} %bitcast.71, s32[]{:T(128)S(6)} %select_n.28), kind=kLoop, calls=%fused_computation.19 | loop fusion | bytes 2621444 | tf_op jit(solution)/shard_map/convert_element_type | solution.py:330
  156.2 13.5 %all_to_all.50 = bf16[8,72,256]{2,1,0:T(8,128)(2,1)S(1)} all-to-all(bf16[8,72,256]{2,1,0:T(8,128)(2,1)S(1)} %fusion.17), channel_id=1, replica_groups={{0,2,4,6,8,10,12,14},{1,3,5,7,9,11,13,15},{16,18,20,22,24,26,28,30},{17..., dimensions={0} | all-to-all | bytes 589824 | tf_op jit(solution)/shard_map/all_to_all | solution.py:317
  169.8 0.7 broadcast_in_dim.26
  170.5 13.5 %all-to-all-start.7 = ((bf16[8,72,256]{2,1,0:T(8,128)(2,1)}), bf16[8,72,256]{2,1,0:T(8,128)(2,1)S(1)}, u32[]{:S(2)}, u32[]{:S(2)}) async-start(bf16[8,72,256]{2,1,0:T(8,128)(2,1)} %broadcast_in_dim.26), calls=%async_computation.7 | async-start | bytes 589824 | tf_op jit(solution)/shard_map/all_to_all | solution.py:343
  184.0 3.3 %fusion.1 = bf16[8,64,1024]{2,1,0:T(8,128)(2,1)} fusion(bf16[8,64,1024]{2,1,0:T(8,128)(2,1)} %collective-permute-done.4, f32[8,2,64,1024]{3,2,1,0:T(8,128)} %copy-done.3, s32[]{:T(128)S(6)} %select_n.27), kind=kLoop, calls=%fused_computation.6 | loop fusion | flops 1572864 | bytes 4194308 | tf_op jit(solution)/shard_map/convert_element_type | solution.py:332
  187.3 4.2 %all-to-all-done.7 = bf16[8,72,256]{2,1,0:T(8,128)(2,1)S(1)} async-done(((bf16[8,72,256]{2,1,0:T(8,128)(2,1)}), bf16[8,72,256]{2,1,0:T(8,128)(2,1)S(1)}, u32[]{:S(2)}, u32[]{:S(2)}) %all-to-all-start.7) | async-done | bytes 294944 | tf_op jit(solution)/shard_map/all_to_all | solution.py:343
  191.5 3.6 %all-to-all-start.4 = ((bf16[8,64,1024]{2,1,0:T(8,128)(2,1)}), bf16[8,64,1024]{2,1,0:T(8,128)(2,1)S(1)}, u32[]{:S(2)}, u32[]{:S(2)}) async-start(bf16[8,64,1024]{2,1,0:T(8,128)(2,1)} %fusion.1), calls=%async_computation.4 | async-start | bytes 2097152 | tf_op jit(solution)/shard_map/all_to_all | solution.py:317
  195.1 3.5 %fusion = bf16[8,64,1280]{2,1,0:T(8,128)(2,1)} fusion(bf16[8,64,1280]{2,1,0:T(8,128)(2,1)} %collective-permute-done.6, f32[8,2,64,1280]{3,2,1,0:T(8,128)} %bitcast.72, s32[]{:T(128)S(6)} %select_n.27), kind=kLoop, calls=%fused_computation.2 | loop fusion | flops 1966080 | bytes 5242884 | tf_op jit(solution)/shard_map/convert_element_type | solution.py:332
  198.5 10.7 %all-to-all-done.4 = bf16[8,64,1024]{2,1,0:T(8,128)(2,1)S(1)} async-done(((bf16[8,64,1024]{2,1,0:T(8,128)(2,1)}), bf16[8,64,1024]{2,1,0:T(8,128)(2,1)S(1)}, u32[]{:S(2)}, u32[]{:S(2)}) %all-to-all-start.4) | async-done | bytes 1048608 | tf_op jit(solution)/shard_map/all_to_all | solution.py:317
  209.2 1.0 copy-done.7
  210.2 3.8 %all-to-all-start.8 = ((bf16[8,64,1280]{2,1,0:T(8,128)(2,1)}), bf16[8,64,1280]{2,1,0:T(8,128)(2,1)S(1)}, u32[]{:S(2)}, u32[]{:S(2)}) async-start(bf16[8,64,1280]{2,1,0:T(8,128)(2,1)} %fusion), calls=%async_computation.8 | async-start | bytes 2621440 | tf_op jit(solution)/shard_map/all_to_all | solution.py:317
  214.0 1.4 reduce_sum.118
  215.4 17.5 %all-to-all-done.8 = bf16[8,64,1280]{2,1,0:T(8,128)(2,1)S(1)} async-done(((bf16[8,64,1280]{2,1,0:T(8,128)(2,1)}), bf16[8,64,1280]{2,1,0:T(8,128)(2,1)S(1)}, u32[]{:S(2)}, u32[]{:S(2)}) %all-to-all-start.8) | async-done | bytes 1310752 | tf_op jit(solution)/shard_map/all_to_all | solution.py:317
  232.9 1.1 broadcast_in_dim.25
  234.0 4.3 %all-to-all-start.5 = ((bf16[8,64,1024]{2,1,0:T(8,128)(2,1)}), bf16[8,64,1024]{2,1,0:T(8,128)(2,1)}, u32[]{:S(2)}, u32[]{:S(2)}) async-start(bf16[8,64,1024]{2,1,0:T(8,128)(2,1)} %broadcast_in_dim.25), calls=%async_computation.5 | async-start | bytes 2097152 | tf_op jit(solution)/shard_map/all_to_all | solution.py:343
  238.4 14.7 %all-to-all-done.5 = bf16[8,64,1024]{2,1,0:T(8,128)(2,1)} async-done(((bf16[8,64,1024]{2,1,0:T(8,128)(2,1)}), bf16[8,64,1024]{2,1,0:T(8,128)(2,1)}, u32[]{:S(2)}, u32[]{:S(2)}) %all-to-all-start.5) | async-done | bytes 1048608 | tf_op jit(solution)/shard_map/all_to_all | solution.py:343
  253.1 1.1 broadcast_in_dim.27
  254.2 4.3 %all-to-all-start.9 = ((bf16[8,64,1280]{2,1,0:T(8,128)(2,1)}), bf16[8,64,1280]{2,1,0:T(8,128)(2,1)}, u32[]{:S(2)}, u32[]{:S(2)}) async-start(bf16[8,64,1280]{2,1,0:T(8,128)(2,1)} %broadcast_in_dim.27), calls=%async_computation.9 | async-start | bytes 2621440 | tf_op jit(solution)/shard_map/all_to_all | solution.py:343
  258.5 2.5 fusion.18
  261.1 0.6 slice.16
  261.7 0.5 slice_bitcast_fusion
  262.2 2.1 convert_reduce_fusion.1
  264.3 12.9 %all-to-all-done.9 = bf16[8,64,1280]{2,1,0:T(8,128)(2,1)} async-done(((bf16[8,64,1280]{2,1,0:T(8,128)(2,1)}), bf16[8,64,1280]{2,1,0:T(8,128)(2,1)}, u32[]{:S(2)}, u32[]{:S(2)}) %all-to-all-start.9) | async-done | bytes 1310752 | tf_op jit(solution)/shard_map/all_to_all | solution.py:343
  277.2 1.5 convert_reduce_fusion
  278.7 0.6 slice.17
  279.4 0.7 slice.18
  (47 shorter events, 2.1 us)
Async XLA Ops:
  0.6 53.8 %copy-start = (bf16[1024,1024]{1,0:T(8,128)(2,1)S(1)}, bf16[1024,1024]{1,0:T(8,128)(2,1)}, u32[]{:S(2)}) copy-start(bf16[1024,1024]{1,0:T(8,128)(2,1)} %param.12) | copy-start | bytes 6291460
  2.0 10.6 %copy-start.4 = (bf16[1,256,1024]{2,1,0:T(8,128)(2,1)S(1)}, bf16[1,256,1024]{2,1,0:T(8,128)(2,1)}, u32[]{:S(2)}) copy-start(bf16[1,256,1024]{2,1,0:T(8,128)(2,1)} %param.9) | copy-start | bytes 1572868
  2.0 10.6 %copy-start.13 = (f32[1024]{0:T(1024)S(1)}, f32[1024]{0:T(1024)}, u32[]{:S(2)}) copy-start(f32[1024]{0:T(1024)} %param.11) | copy-start | bytes 12292
  4.7 23.9 %all-to-all-start = ((bf16[8,256,256]{2,1,0:T(8,128)(2,1)}), bf16[8,256,256]{2,1,0:T(8,128)(2,1)}, u32[]{:S(2)}, u32[]{:S(2)}) async-start(bf16[8,256,256]{2,1,0:T(8,128)(2,1)} %broadcast_in_dim.22), calls=%async_computation | async-start | bytes 2097152 | tf_op jit(solution)/shard_map/all_to_all | solution.py:317
  12.6 38.7 %copy-start.11 = (bf16[1,256,1024]{2,1,0:T(8,128)(2,1)S(1)}, bf16[1,256,1024]{2,1,0:T(8,128)(2,1)}, u32[]{:S(2)}) copy-start(bf16[1,256,1024]{2,1,0:T(8,128)(2,1)} %param.10) | copy-start | bytes 1572868
  29.7 19.8 %all-to-all-start.1 = ((bf16[8,256,256]{2,1,0:T(8,128)(2,1)}), bf16[8,256,256]{2,1,0:T(8,128)(2,1)}, u32[]{:S(2)}, u32[]{:S(2)}) async-start(bf16[8,256,256]{2,1,0:T(8,128)(2,1)} %broadcast_in_dim.23), calls=%async_computation.1 | async-start | bytes 2097152 | tf_op jit(solution)/shard_map/all_to_all | solution.py:317
  33.9 22.1 %collective-permute-start = (bf16[8,256,256]{2,1,0:T(8,128)(2,1)}, bf16[8,256,256]{2,1,0:T(8,128)(2,1)}, u32[]{:S(2)}, u32[]{:S(2)}) collective-permute-start(bf16[8,256,256]{2,1,0:T(8,128)(2,1)} %all-to-all-done.k_own), channel_id=1, source_target_pairs={{0,1},{1,0},{2,3},{3,2},{4,5},{5,4},{6,7},{7,6},{8,9},{9,8},{10,11... | collective-permute-start | bytes 3145736 | tf_op jit(solution)/shard_map/ppermute | solution.py:312
  49.4 10.9 %collective-permute-start.1 = (bf16[8,256,256]{2,1,0:T(8,128)(2,1)}, bf16[8,256,256]{2,1,0:T(8,128)(2,1)}, u32[]{:S(2)}, u32[]{:S(2)}) collective-permute-start(bf16[8,256,256]{2,1,0:T(8,128)(2,1)} %all-to-all-done.1.v_own), channel_id=1, source_target_pairs={{0,1},{1,0},{2,3},{3,2},{4,5},{5,4},{6,7},{7,6},{8,9},{9,8},{10,11... | collective-permute-start | bytes 3145736 | tf_op jit(solution)/shard_map/ppermute | solution.py:312
  70.0 10.1 %collective-permute-start.3 = (bf16[8,256,256]{2,1,0:T(8,128)(2,1)}, bf16[8,256,256]{2,1,0:T(8,128)(2,1)}, u32[]{:S(2)}, u32[]{:S(2)}) collective-permute-start(bf16[8,256,256]{2,1,0:T(8,128)(2,1)} %get-tuple-element.20), channel_id=1, source_target_pairs={{0,1},{1,0},{2,3},{3,2},{4,5},{5,4},{6,7},{7,6},{8,9},{9,8},{10,11... | collective-permute-start | bytes 3145736 | tf_op jit(solution)/shard_map/ppermute | solution.py:312
  80.1 13.8 %collective-permute-start.2 = (bf16[8,256,256]{2,1,0:T(8,128)(2,1)}, bf16[8,256,256]{2,1,0:T(8,128)(2,1)}, u32[]{:S(2)}, u32[]{:S(2)}) collective-permute-start(bf16[8,256,256]{2,1,0:T(8,128)(2,1)} %get-tuple-element.18), channel_id=1, source_target_pairs={{0,1},{1,0},{2,3},{3,2},{4,5},{5,4},{6,7},{7,6},{8,9},{9,8},{10,11... | collective-permute-start | bytes 3145736 | tf_op jit(solution)/shard_map/ppermute | solution.py:312
  82.9 28.3 %all-to-all-start.3 = ((bf16[8,256,256]{2,1,0:T(8,128)(2,1)}), bf16[8,256,256]{2,1,0:T(8,128)(2,1)}, u32[]{:S(2)}, u32[]{:S(2)}) async-start(bf16[8,256,256]{2,1,0:T(8,128)(2,1)} %add_convert_fusion), calls=%async_computation.3 | async-start | bytes 2097152 | tf_op jit(solution)/shard_map/all_to_all | solution.py:317
  111.3 19.9 %all-to-all-start.2 = ((bf16[8,256,256]{2,1,0:T(8,128)(2,1)}), bf16[8,256,256]{2,1,0:T(8,128)(2,1)}, u32[]{:S(2)}, u32[]{:S(2)}) async-start(bf16[8,256,256]{2,1,0:T(8,128)(2,1)} %add_convert_fusion.1), calls=%async_computation.2 | async-start | bytes 2097152 | tf_op jit(solution)/shard_map/all_to_all | solution.py:317
  132.5 1.5 copy-start.8
  134.0 1.9 copy-start.5
  135.9 1.0 copy-start.12
  137.6 2.1 copy-start.3
  139.7 3.3 %copy-start.6 = (f32[1024,256]{0,1:T(8,128)S(1)}, f32[1024,256]{0,1:T(8,128)}, u32[]{:S(2)}) copy-start(f32[1024,256]{0,1:T(8,128)} %fusion.27) | copy-start | bytes 3145732
  140.8 43.2 %collective-permute-start.4 = (bf16[8,64,1024]{2,1,0:T(8,128)(2,1)}, bf16[8,64,1024]{2,1,0:T(8,128)(2,1)}, u32[]{:S(2)}, u32[]{:S(2)}) collective-permute-start(bf16[8,64,1024]{2,1,0:T(8,128)(2,1)} %fusion.16), channel_id=1, source_target_pairs={{0,1},{1,0},{2,3},{3,2},{4,5},{5,4},{6,7},{7,6},{8,9},{9,8},{10,11... | collective-permute-start | bytes 3145736 | tf_op jit(solution)/shard_map/ppermute | solution.py:312
  140.9 2.7 copy-start.2
  141.3 1.0 copy-start.9
  142.4 13.8 %collective-permute-start.5 = (bf16[8,72,256]{2,1,0:T(8,128)(2,1)S(1)}, bf16[8,72,256]{2,1,0:T(8,128)(2,1)S(1)}, u32[]{:S(2)}, u32[]{:S(2)}) collective-permute-start(bf16[8,72,256]{2,1,0:T(8,128)(2,1)S(1)} %fusion.24), channel_id=1, source_target_pairs={{0,1},{1,0},{2,3},{3,2},{4,5},{5,4},{6,7},{7,6},{8,9},{9,8},{10,11... | collective-permute-start | bytes 884744 | tf_op jit(solution)/shard_map/ppermute | solution.py:312
  152.7 3.5 %copy-start.10 = (f32[16,72,256]{2,1,0:T(8,128)S(1)}, f32[16,72,256]{2,1,0:T(8,128)}, u32[]{:S(2)}) copy-start(f32[16,72,256]{2,1,0:T(8,128)} %copy-done.9) | copy-start | bytes 3538948
  155.7 39.3 %collective-permute-start.6 = (bf16[8,64,1280]{2,1,0:T(8,128)(2,1)}, bf16[8,64,1280]{2,1,0:T(8,128)(2,1)}, u32[]{:S(2)}, u32[]{:S(2)}) collective-permute-start(bf16[8,64,1280]{2,1,0:T(8,128)(2,1)} %fusion.7), channel_id=1, source_target_pairs={{0,1},{1,0},{2,3},{3,2},{4,5},{5,4},{6,7},{7,6},{8,9},{9,8},{10,11... | collective-permute-start | bytes 3932168 | tf_op jit(solution)/shard_map/ppermute | solution.py:312
  170.5 21.0 %all-to-all-start.7 = ((bf16[8,72,256]{2,1,0:T(8,128)(2,1)}), bf16[8,72,256]{2,1,0:T(8,128)(2,1)S(1)}, u32[]{:S(2)}, u32[]{:S(2)}) async-start(bf16[8,72,256]{2,1,0:T(8,128)(2,1)} %broadcast_in_dim.26), calls=%async_computation.7 | async-start | bytes 589824 | tf_op jit(solution)/shard_map/all_to_all | solution.py:343
  191.5 17.8 %all-to-all-start.4 = ((bf16[8,64,1024]{2,1,0:T(8,128)(2,1)}), bf16[8,64,1024]{2,1,0:T(8,128)(2,1)S(1)}, u32[]{:S(2)}, u32[]{:S(2)}) async-start(bf16[8,64,1024]{2,1,0:T(8,128)(2,1)} %fusion.1), calls=%async_computation.4 | async-start | bytes 2097152 | tf_op jit(solution)/shard_map/all_to_all | solution.py:317
  209.2 1.0 copy-start.7
  210.2 22.7 %all-to-all-start.8 = ((bf16[8,64,1280]{2,1,0:T(8,128)(2,1)}), bf16[8,64,1280]{2,1,0:T(8,128)(2,1)S(1)}, u32[]{:S(2)}, u32[]{:S(2)}) async-start(bf16[8,64,1280]{2,1,0:T(8,128)(2,1)} %fusion), calls=%async_computation.8 | async-start | bytes 2621440 | tf_op jit(solution)/shard_map/all_to_all | solution.py:317
  234.0 19.1 %all-to-all-start.5 = ((bf16[8,64,1024]{2,1,0:T(8,128)(2,1)}), bf16[8,64,1024]{2,1,0:T(8,128)(2,1)}, u32[]{:S(2)}, u32[]{:S(2)}) async-start(bf16[8,64,1024]{2,1,0:T(8,128)(2,1)} %broadcast_in_dim.25), calls=%async_computation.5 | async-start | bytes 2097152 | tf_op jit(solution)/shard_map/all_to_all | solution.py:343
  254.2 23.0 %all-to-all-start.9 = ((bf16[8,64,1280]{2,1,0:T(8,128)(2,1)}), bf16[8,64,1280]{2,1,0:T(8,128)(2,1)}, u32[]{:S(2)}, u32[]{:S(2)}) async-start(bf16[8,64,1280]{2,1,0:T(8,128)(2,1)} %broadcast_in_dim.27), calls=%async_computation.9 | async-start | bytes 2621440 | tf_op jit(solution)/shard_map/all_to_all | solution.py:343
  258.5 21.6 %copy-start.1 = (bf16[1024,1024]{1,0:T(8,128)(2,1)S(1)}, bf16[1024,1024]{1,0:T(8,128)(2,1)}, u32[]{:S(2)}) copy-start(bf16[1024,1024]{1,0:T(8,128)(2,1)} %param.12) | copy-start | bytes 6291460

commit v2 on v1

--- a/solution.py
+++ b/solution.py
@@ -11,6 +11,7 @@
 ACT = 64
 BLOCK = 128
 NEG = -1e30
+EPS = 1e-06
 LOG2E = 1.4426950408889634
 VMEM_BYTES = 60 * 1024 * 1024
 NT = (((1,), (1,)), ((), ()))
@@ -109,7 +110,7 @@
 
 def attend_kernel(
     heads, seq, info, q, da, lse, k_own, k_pair, v_own, v_pair,
-    attn_t, delta, dv_own, dv_pair, probs_out,
+    at_own, at_pair, delta, dv_own, dv_pair, probs_out,
     keys, values, values_t, da_rows, probs, sems, out_sems,
 ):
     tok, chips = q.shape[0], k_own.shape[0]
@@ -146,7 +147,12 @@
     per_block(info, chips, tok, seq, work, rest)
     for h in range(heads):
         a = dot_nn(values_t[...], probs[:, head(h)]).astype(jnp.bfloat16)
-        attn_t[head(h), :] = a
+        per_head = at_own.shape[2] // heads
+        block = HS // per_head
+        for n in range(per_head):
+            put_rows(
+                info, a[n * block : (n + 1) * block].astype(jnp.float32), h * per_head + n, at_own, at_pair
+            )
         delta[:, head(h)] = jnp.sum(
             a.astype(jnp.float32) * da_rows[head(h), :].T.astype(jnp.float32), axis=0, keepdims=True
         )
@@ -237,7 +243,7 @@
     )(info, q, k_own, k_pair)
 
 
-def run_attend(info, q, da, lse, k_own, k_pair, v_own, v_pair):
+def run_attend(info, q, da, lse, k_own, k_pair, v_own, v_pair, filed):
     tok, width = q.shape
     heads, chips = width // HS, k_own.shape[0]
     seq = 2 * tok * chips
@@ -245,14 +251,15 @@
     return pl.pallas_call(
         functools.partial(attend_kernel, heads, seq),
         out_shape=(
-            jax.ShapeDtypeStruct((width, tok), jnp.bfloat16),
+            filed,
+            filed,
             jax.ShapeDtypeStruct((1, width), jnp.float32),
             part,
             part,
             jax.ShapeDtypeStruct((seq, width), jnp.bfloat16),
         ),
         in_specs=[SMEM, VMEM, VMEM, VMEM, ANY, ANY, ANY, ANY],
-        out_specs=(VMEM, VMEM, VMEM, VMEM, ANY),
+        out_specs=(VMEM, VMEM, VMEM, VMEM, VMEM, ANY),
         scratch_shapes=[
             pltpu.VMEM((chips, 2 * tok, HS), jnp.bfloat16),
             pltpu.VMEM((chips, 2 * tok, HS), jnp.bfloat16),
@@ -294,17 +301,118 @@
     )(info, q, da, delta, k_own, k_pair, v_own, v_pair, probs)
 
 
-EPS = 1e-06
-
-
-def contract_first(left, right):
-    return lax.dot_general(
-        left, right, (((0,), (0,)), ((), ())), preferred_element_type=jnp.float32
-    )
-
-
-def same_core(count):
-    return [[core + 2 * chip for chip in range(count // 2)] for core in range(2)]
+def normed_rows(x):
+    xf = x[...].astype(jnp.float32)
+    return xf * lax.rsqrt(jnp.mean(xf * xf, axis=-1, keepdims=True) + EPS)
+
+
+def prepare_kernel(chips, x, gain, w_key, w_value, hidden, k_copies, v_copies):
+    h = (normed_rows(x) * gain[...]).astype(jnp.bfloat16)
+    hidden[...] = h
+    for weight, out in ((w_key, k_copies), (w_value, v_copies)):
+        rows = dot_nn(h, weight[...]).astype(jnp.bfloat16)
+        for chip in range(chips):
+            out[chip] = rows
+
+
+def put_rows(info, rows, chip, own, pair):
+    core, x = info[3], info[4]
+    steps, outer, _, size, _ = own.shape
+
+    def put(same):
+        for n in range(rows.shape[0] // size):
+            place = n % (outer * steps)
+            to = own if (n // (outer * steps)) == same else pair
+            step = (place % steps - x + steps) & (steps - 1)
+            to[step, place // steps, chip] = rows[n * size : (n + 1) * size].astype(to.dtype)
+
+    for same in range(2):
+        pl.when(core == same)(functools.partial(put, same))
+
+
+def project_kernel(info, hidden, grad_out, w_query, w_out, query, d_attn, ht_own, ht_pair):
+    h = hidden[...]
+    query[...] = dot_nn(h, w_query[...]).astype(jnp.bfloat16)
+    d_attn[...] = dot_nt(grad_out[...], w_out[...]).astype(jnp.bfloat16)
+    chips = ht_own.shape[2]
+    block = h.shape[1] // chips
+    for chip in range(chips):
+        part = h[:, chip * block : (chip + 1) * block].astype(jnp.float32).T
+        put_rows(info, part, chip, ht_own, ht_pair)
+
+
+def own_terms_kernel(left, right, received, base, *parts):
+    rows = base.shape[0]
+    for step in range(len(parts) + 1):
+        at = pl.ds(step * rows, rows)
+        total = dot_nn(left[step].reshape(rows, -1), right[...]) + received[at, :].astype(jnp.float32)
+        if step == 0:
+            base[...] = total
+        else:
+            parts[step - 1][...] = total.astype(jnp.bfloat16)
+
+
+def collect_kernel(counts, *refs):
+    out, at = refs[-1], 0
+    for base, *parts in counts:
+        total = refs[base][...]
+        for p in parts:
+            total = total + refs[p][...].astype(jnp.float32)
+        wide = total.shape[1]
+        out[:, pl.ds(at, wide)] = total.astype(jnp.bfloat16)
+        at += wide
+
+
+def add_kernel(a, b, out):
+    out[...] = (a[...].astype(jnp.float32) + b[...].astype(jnp.float32)).astype(out.dtype)
+
+
+def finish_kernel(x, grad_out, gain, dq, dk, dv, w_query, w_key, w_value, d_in):
+    dhidden = (
+        dot_nt(dq[...], w_query[...]) + dot_nt(dk[...], w_key[...]) + dot_nt(dv[...], w_value[...])
+    )
+    xf = x[...].astype(jnp.float32)
+    inv = lax.rsqrt(jnp.mean(xf * xf, axis=-1, keepdims=True) + EPS)
+    normed = xf * inv
+    scaled = dhidden * gain[...]
+    mean = jnp.mean(scaled * normed, axis=-1, keepdims=True)
+    d_in[...] = (grad_out[...].astype(jnp.float32) + inv * (scaled - normed * mean)).astype(d_in.dtype)
+
+
+def call(body, outs, args, flops, smem=0):
+    return pl.pallas_call(
+        body,
+        out_shape=outs,
+        in_specs=[SMEM] * smem + [VMEM] * (len(args) - smem),
+        out_specs=jax.tree.map(lambda _: VMEM, outs),
+        compiler_params=params(),
+        cost_estimate=cost(flops, 1 << 20),
+    )(*args)
+
+
+def shape(*dims, dtype=jnp.bfloat16):
+    return jax.ShapeDtypeStruct(dims, dtype)
+
+
+def run_add(a, b):
+    spec = pl.BlockSpec((2, *a.shape[1:]), lambda i: (i, 0, 0))
+    return pl.pallas_call(
+        add_kernel,
+        grid=(a.shape[0] // 2,),
+        out_shape=jax.ShapeDtypeStruct(a.shape, a.dtype),
+        in_specs=[spec, spec],
+        out_specs=spec,
+        cost_estimate=cost(1 << 30, 1 << 20),
+        name="add",
+    )(a, b)
+
+
+CORES = 2
+X = 4
+
+
+def as_bf16(value):
+    return value.astype(jnp.bfloat16)
 
 
 def swap_cores(value):
@@ -312,94 +420,137 @@
     return lax.ppermute(value, "blk", [(i, i ^ 1) for i in range(count)])
 
 
+def send_along_x(value, step):
+    count = lax.axis_size("dp")
+    return lax.ppermute(
+        value, "dp", [(i, i // X * X + (i + step) % X) for i in range(count)]
+    )
+
+
 def exchange_chips(value):
-    groups = same_core(lax.axis_size("blk"))
+    chips = lax.axis_size("blk") // CORES
+    groups = [[core + CORES * chip for chip in range(chips)] for core in range(CORES)]
     return lax.all_to_all(value, "blk", 0, 0, tiled=True, axis_index_groups=groups)
 
 
-def gather_chips(value):
-    copies = jnp.broadcast_to(value, (lax.axis_size("blk") // 2, *value.shape))
-    return exchange_chips(copies)
+def exchange_plane(value):
+    blk, dp = lax.axis_size("blk"), lax.axis_size("dp")
+    groups = [
+        [(outer * X + x) * blk + chip * CORES + core for outer in range(dp // X) for chip in range(blk // CORES)]
+        for x in range(X)
+        for core in range(CORES)
+    ]
+    return lax.all_to_all(value, ("dp", "blk"), 0, 0, tiled=True, axis_index_groups=groups)
 
 
 def sum_first(parts):
     return jnp.sum(parts.astype(jnp.float32), axis=0)
 
 
-def reduce_to_owner(own, pair):
-    received = swap_cores(pair.astype(jnp.bfloat16))
-    chip_sum = own.astype(jnp.float32) + received.astype(jnp.float32)
-    return sum_first(exchange_chips(chip_sum.astype(jnp.bfloat16)))
-
-
-def reduce_weights(grad):
-    count, core = lax.axis_size("blk"), lax.axis_index("blk") % 2
-    rows = grad.shape[0] // count
-    parts = grad.reshape(count // 2, 2, rows, *grad.shape[1:])
-    own = lax.dynamic_index_in_dim(parts, core, 1, keepdims=False)
-    pair = lax.dynamic_index_in_dim(parts, 1 - core, 1, keepdims=False)
-    mine = reduce_to_owner(own, pair).astype(jnp.bfloat16)
-    copies = jnp.broadcast_to(mine, (lax.axis_size("dp"), *mine.shape))
-    return sum_first(lax.all_to_all(copies, "dp", 0, 0, tiled=True))
+def plane_terms(left_own, left_pair, right):
+    steps, outer, chips, size, tok = left_pair.shape
+    rows, wide = outer * chips * size, right.shape[1]
+    received = swap_cores(as_bf16(dot_nn(left_pair.reshape(steps * rows, tok), right)))
+    base, *parts = call(
+        own_terms_kernel,
+        (shape(rows, wide, dtype=jnp.float32), *[shape(rows, wide)] * (steps - 1)),
+        (left_own, right, received),
+        2 * steps * rows * wide * tok,
+    )
+    arrived = []
+    for step, part in enumerate(parts, 1):
+        arrived.append(send_along_x(part, step))
+    return (base, *arrived)
+
+
+def to_owner(own, pair):
+    received = swap_cores(pair)
+    chip_sum = run_add(own, received)
+    parts = exchange_chips(chip_sum)
+    return as_bf16(sum_first(parts))
 
 
 def per_device(inputs, upstream, gain, w_query, w_key, w_value, w_out, prefix_len, bound):
-    bf16 = jnp.bfloat16
-    xf = inputs[0].astype(jnp.float32)
-    grad_out = upstream[0]
-    my = lax.axis_index("blk")
+    return whole(inputs[0], upstream[0], gain, w_query, w_key, w_value, w_out, prefix_len, bound)
+
+
+def whole(inputs, grad_out, gain, w_query, w_key, w_value, w_out, prefix_len, bound):
+    tok, wide = inputs.shape
+    my, dp = lax.axis_index("blk"), lax.axis_index("dp")
     count = lax.axis_size("blk")
-    inv = lax.rsqrt(jnp.mean(xf * xf, axis=-1, keepdims=True) + EPS)
-    normed = xf * inv
-    hidden = (normed * gain).astype(bf16)
-    keys = dot_nn(hidden, w_key).astype(bf16)
-    k_own = gather_chips(keys)
-    values = dot_nn(hidden, w_value).astype(bf16)
-    v_own = gather_chips(values)
+    chips, outer = count // CORES, lax.axis_size("dp") // X
+    core, x = my % CORES, dp % X
+    info = jnp.stack([my, prefix_len[0], bound[0] * BLOCK, core, x]).astype(jnp.int32)
+    gain_row = gain.reshape(1, wide)
+    filed = shape(X, outer, chips, wide // (count * outer * X), tok)
+    copies = shape(chips, tok, HS)
+    hidden, k_copies, v_copies = call(
+        functools.partial(prepare_kernel, chips),
+        (shape(tok, wide), copies, copies),
+        (inputs, gain_row, w_key, w_value),
+        4 * tok * wide * HS,
+    )
+    k_own = exchange_chips(k_copies)
     k_pair = swap_cores(k_own)
+    v_own = exchange_chips(v_copies)
     v_pair = swap_cores(v_own)
-    query = dot_nn(hidden, w_query).astype(bf16)
-    d_attn = dot_nt(grad_out, w_out).astype(bf16)
-    info = jnp.stack([my, prefix_len[0], bound[0] * BLOCK, my % 2]).astype(jnp.int32)
-
+    query, d_attn, ht_own, ht_pair = call(
+        project_kernel,
+        (shape(tok, w_query.shape[1]), shape(tok, w_out.shape[0]), filed, filed),
+        (info, hidden, grad_out, w_query, w_out),
+        4 * tok * wide * wide,
+        smem=1,
+    )
     lse = run_stats(info, query, k_own, k_pair)
-    attn_t, delta, dv_own, dv_pair, probs = run_attend(
-        info, query, d_attn, lse, k_own, k_pair, v_own, v_pair
-    )
-    d_value_rows = reduce_to_owner(dv_own, dv_pair).astype(bf16)
-    g_out = dot_nn(attn_t, grad_out)
-    g_value = contract_first(hidden, d_value_rows)
-
+    at_own, at_pair, delta, dv_own, dv_pair, probs = run_attend(
+        info, query, d_attn, lse, k_own, k_pair, v_own, v_pair, filed
+    )
+    d_value_rows = to_owner(dv_own, dv_pair)
+    out_terms = plane_terms(at_own, at_pair, grad_out)
     d_query_rows, dk_own, dk_pair = run_grads(
         info, query, d_attn, delta, k_own, k_pair, v_own, v_pair, probs
     )
-    d_key_rows = reduce_to_owner(dk_own, dk_pair).astype(bf16)
-    g_query = contract_first(hidden, d_query_rows)
-    dhidden = (
-        dot_nt(d_query_rows, w_query) + dot_nt(d_key_rows, w_key) + dot_nt(d_value_rows, w_value)
-    )
-    g_key = contract_first(hidden, d_key_rows)
-    g_gain = jnp.sum(dhidden * normed, axis=0)
-    scaled = dhidden * gain
-    d_in = grad_out.astype(jnp.float32) + inv * (
-        scaled - normed * jnp.mean(scaled * normed, axis=-1, keepdims=True)
-    )
-
-    rows = g_gain.shape[0] // count
-    gain_rows = jnp.pad(g_gain.reshape(count, 1, rows), ((0, 0), (0, 7), (0, HS - rows)))
-    late = jnp.concatenate([g_key.reshape(count, rows, HS), gain_rows], axis=1)
-    late = reduce_weights(late.reshape(count * (rows + 8), HS))
-    early = reduce_weights(jnp.concatenate([g_out, g_value], axis=1))
-    d_q = reduce_weights(g_query)
-    width = g_out.shape[1]
-    return (
-        d_in.astype(bf16)[None],
-        d_q,
-        late[:rows],
-        early[:, width:],
-        early[:, :width],
-        late[rows, :rows],
-    )
+    d_key_rows = to_owner(dk_own, dk_pair)
+    query_terms = plane_terms(ht_own, ht_pair, d_query_rows)
+    d_kv_rows = jnp.concatenate([d_key_rows, d_value_rows], axis=1)
+    kv_terms = plane_terms(ht_own, ht_pair, d_kv_rows)
+    sets, at = [], 0
+    for terms in (out_terms, query_terms, kv_terms):
+        sets.append(list(range(at, at + len(terms))))
+        at += len(terms)
+    rows = out_terms[0].shape[0]
+    total_wide = sum(t[0].shape[1] for t in (out_terms, query_terms, kv_terms))
+    mine = call(
+        functools.partial(collect_kernel, sets),
+        shape(rows, total_wide),
+        (*out_terms, *query_terms, *kv_terms),
+        1 << 30,
+    )
+    parts = exchange_plane(mine.reshape(outer * chips, -1, total_wide))
+    summed = as_bf16(sum_first(parts))
+    copies = jnp.broadcast_to(summed, (lax.axis_size("dp"), *summed.shape))
+    shared = lax.all_to_all(copies, "dp", 0, 0, tiled=True)
+    ends = [wide, wide + query.shape[1], wide + query.shape[1] + HS]
+    shared = shared.reshape(-1, total_wide).astype(jnp.float32)
+    d_out, d_query, d_key, d_value = jnp.split(shared, ends, axis=1)
+    d_in = call(
+        finish_kernel,
+        shape(tok, wide),
+        (inputs, grad_out, gain_row, d_query_rows, d_key_rows, d_value_rows, w_query, w_key, w_value),
+        2 * tok * wide * (wide + 2 * HS),
+    )
+
+    rows = d_query.shape[0]
+
+    def my_rows(value):
+        return lax.dynamic_slice_in_dim(value, my * rows, rows, 0).astype(jnp.float32)
+
+    d_gain = (
+        jnp.sum(my_rows(w_query) * d_query, axis=1)
+        + jnp.sum(my_rows(w_key) * d_key, axis=1)
+        + jnp.sum(my_rows(w_value) * d_value, axis=1)
+    ) / my_rows(gain)
+    return (d_in[None], d_query, d_key, d_value, d_out, d_gain)
 
 
 def solution(mesh):

time: 282 us -> 218 us (0.77)
  waiting for transfers between devices: 111 us -> 56.5 us
  Pallas kernels: 23.3 us -> 57.5 us
  blocking collectives: 13.5 us -> 44.2 us
  other arithmetic: 28.6 us -> 5.89 us
  starting transfers between devices: 58.6 us -> 40.7 us
  local copies, waits for them, and re-layouts: 23 us -> 6.05 us
  matrix products: 19.6 us -> 4.08 us
    all_to_all x6 -> x3, waiting for transfers between devices: 79.4 us -> 38.3 us  [exchange_chips(): lax.all_to_all(value, 'blk', 0, 0, tiled=True, axis_index_groups=groups)]
    pallas_call x1 -> x10, Pallas kernels: 9.73 us -> 44 us  [the longest x7 24.3 us: call(): pl.pallas_call(body, out_shape=outs, in_specs=[SMEM] * smem + [VMEM] * (l...]
    all_to_all x3 -> x1, waiting for transfers between devices: 31.7 us -> 3.12 us  [whole(): shared = lax.all_to_all(copies, 'dp', 0, 0, tiled=True)]
    all_to_all x0 -> x1, blocking collectives: none -> 19.4 us  [exchange_plane(): lax.all_to_all(value, ('dp', 'blk'), 0, 0, tiled=True, axis_index_groups=...]
    all_to_all x3 -> x1, starting transfers between devices: 22 us -> 3.43 us  [whole(): shared = lax.all_to_all(copies, 'dp', 0, 0, tiled=True)]
    ppermute x0 -> x9, waiting for transfers between devices: none -> 15 us  [send_along_x(): lax.ppermute(value, 'dp', [(i, i // X * X + (i + step) % X) for i in rang...]
    convert_element_type x5 -> x1, other arithmetic: 12.3 us -> 0.04 us  [whole(): shared = shared.reshape(-1, total_wide).astype(jnp.float32)]
    dot_general x7 -> x0, matrix products: 11.2 us -> none  [the longest x4 8.84 us: dot_nt(): return lax.dot_general(a, b, NT, preferred_element_type=jnp.float32)]
  transfers between devices with their start and end apart: 16 -> 20, of which waited for: 9 -> 9; matrix products, arithmetic and copies ran while one was open for 17% -> 3% of each run, Pallas kernels for 5% -> 18%
where the time goes in v2:
time: 218 us; the launch traced here: 217 us
  Pallas kernels  57.5 us (26%)
  waiting for transfers between devices  56.5 us (26%)
  blocking collectives  44.2 us (20%)
  starting transfers between devices  40.7 us (19%)
  local copies, waits for them, and re-layouts  6.05 us (3%)
  other arithmetic  5.89 us (3%)
  matrix products  4.08 us (2%)
  between operations  2.23 us (1%)
    all_to_all x3, waiting for transfers between devices, exchange_chips(): lax.all_to_all(value, 'blk', 0, 0, tiled=True, axis_index_groups=groups)  38.3 us
    all_to_all x1, blocking collectives, exchange_chips(): lax.all_to_all(value, 'blk', 0, 0, tiled=True, axis_index_groups=groups)  24.8 us
    all_to_all x3, starting transfers between devices, exchange_chips(): lax.all_to_all(value, 'blk', 0, 0, tiled=True, axis_index_groups=groups)  24.6 us
    pallas_call x7, Pallas kernels, call(): pl.pallas_call(body, out_shape=outs, in_specs=[SMEM] * smem + [VMEM] * (l...  24.3 us
    all_to_all x1, blocking collectives, exchange_plane(): lax.all_to_all(value, ('dp', 'blk'), 0, 0, tiled=True, axis_index_groups=...  19.4 us
    ppermute x9, waiting for transfers between devices, send_along_x(): lax.ppermute(value, 'dp', [(i, i // X * X + (i + step) % X) for i in rang...  15 us
    pallas_call x1, Pallas kernels, run_attend(): pl.pallas_call(functools.partial(attend_kernel, heads, seq), out_shape=(f...  12.4 us
    ppermute x9, starting transfers between devices, send_along_x(): lax.ppermute(value, 'dp', [(i, i // X * X + (i + step) % X) for i in rang...  11.1 us
  transfers between devices with their start and end apart: 20, of which 9 were waited for; matrix products, arithmetic and copies ran while one was open for 3% of the time, Pallas kernels for 18%

profile of v2, /device:TPU:0, one launch (start us, length us, event | category | flops | bytes accessed | tf_op | source)
XLA Modules:
  0.0 217.1 jit_solution(9575816383488863077)
XLA Ops:
  0.6 3.4 %shard_map.136 = (bf16[256,1024]{1,0:T(8,128)(2,1)}, bf16[8,256,256]{2,1,0:T(8,128)(2,1)}, bf16[8,256,256]{2,1,0:T(8,128)(2,1)}) custom-call(bf16[256,1024]{1,0:T(8,128)(2,1)} %bitcast.25, f32[1,1024]{1,0:T(1,128)} %bitcast.29, bf16[1024,256]{1,0:T(8,128)(2,1)} %w_key.3, bf16[1024,256]{1,0:T(8,128)(2,1)} %w_value.3), custom_call_target="tpu_custom_call" | custom-call | flops 268435456 | bytes 2097152 | tf_op jit(solution)/shard_map/pallas_call | solution.py:383
  4.0 24.8 %all_to_all.30.k_own = bf16[8,256,256]{2,1,0:T(8,128)(2,1)S(1)} all-to-all(bf16[8,256,256]{2,1,0:T(8,128)(2,1)} %get-tuple-element.37), channel_id=1, replica_groups={{0,2,4,6,8,10,12,14},{1,3,5,7,9,11,13,15},{16,18,20,22,24,26,28,30},{17..., dimensions={0} | all-to-all | bytes 2097152 | tf_op jit(solution)/shard_map/all_to_all | solution.py:433
  28.8 3.6 %all-to-all-start.1 = ((bf16[8,256,256]{2,1,0:T(8,128)(2,1)}), bf16[8,256,256]{2,1,0:T(8,128)(2,1)S(1)}, u32[]{:S(2)}, u32[]{:S(2)}) async-start(bf16[8,256,256]{2,1,0:T(8,128)(2,1)} %get-tuple-element.38), calls=%async_computation.1 | async-start | bytes 2097152 | tf_op jit(solution)/shard_map/all_to_all | solution.py:433
  32.3 0.1 collective-permute-start
  32.4 14.6 %all-to-all-done.1.v_own = bf16[8,256,256]{2,1,0:T(8,128)(2,1)S(1)} async-done(((bf16[8,256,256]{2,1,0:T(8,128)(2,1)}), bf16[8,256,256]{2,1,0:T(8,128)(2,1)S(1)}, u32[]{:S(2)}, u32[]{:S(2)}) %all-to-all-start.1) | async-done | bytes 1048608 | tf_op jit(solution)/shard_map/all_to_all | solution.py:433
  47.0 0.0 collective-permute-start.1
  48.3 0.7 stack.16.info
  49.0 5.7 %shard_map.137 = (bf16[256,1024]{1,0:T(8,128)(2,1)}, bf16[256,1024]{1,0:T(8,128)(2,1)}, bf16[4,2,8,8,256]{4,3,2,1,0:T(8,128)(2,1)}, bf16[4,2,8,8,256]{4,3,2,1,0:T(8,128)(2,1)}) custom-call(s32[5]{0:T(128)} %stack.16.info, bf16[256,1024]{1,0:T(8,128)(2,1)} %get-tuple-element.34.hidden, bf16[256,1024]{1,0:T(8,128)(2,1)} %bitcast.19, ...), custom_call_target="tpu_custom_call" | custom-call | flops 1073741824 | bytes 2097152 | tf_op jit(solution)/shard_map/pallas_call | solution.py:383
  54.7 1.0 copy-done.7
  55.7 4.3 %stats.1.lse = f32[1,1024]{1,0:T(1,128)} custom-call(s32[5]{0:T(128)} %stack.16.info, bf16[256,1024]{1,0:T(8,128)(2,1)} %get-tuple-element.35.q, bf16[8,256,256]{2,1,0:T(8,128)(2,1)} %copy-done.4, bf16[8,256,256]{2,1,0:T(8,128)(2,1)} %copy-done.7), custom_call_target="tpu_custom_call" | custom-call | flops 2147483648 | bytes 8388608 | tf_op jit(solution)/shard_map/stats/pallas_call | solution.py:229
  60.0 0.0 collective-permute-done.1.v_pair
  60.0 12.4 %attend.1 = (bf16[4,2,8,8,256]{4,3,2,1,0:T(8,128)(2,1)}, bf16[4,2,8,8,256]{4,3,2,1,0:T(8,128)(2,1)}, f32[1,1024]{1,0:T(1,128)}, bf16[8,256,256]{2,1,0:T(8,128)(2...) custom-call(s32[5]{0:T(128)} %stack.16.info, bf16[256,1024]{1,0:T(8,128)(2,1)} %get-tuple-element.35.q, ...), custom_call_target="tpu_custom_call" | custom-call | flops 6442450944 | bytes 8388608 | tf_op jit(solution)/shard_map/attend/pallas_call | solution.py:251
  72.4 0.8 collective-permute-start.3
  73.3 9.2 %grads.1 = (bf16[256,1024]{1,0:T(8,128)(2,1)}, bf16[8,256,256]{2,1,0:T(8,128)(2,1)}, bf16[8,256,256]{2,1,0:T(8,128)(2,1)}) custom-call(s32[5]{0:T(128)} %stack.16.info, bf16[256,1024]{1,0:T(8,128)(2,1)} %get-tuple-element.35.q, bf16[256,1024]{1,0:T(8,128)(2,1)} %get-tuple-element.36.da, f32[1,1024]{1,0:T(1,128)} %get-tuple-element.39.delta, ...), custom_call_target="tpu_custom_call" | custom-call | flops 6442450944 | bytes 8388608 | tf_op jit(solution)/shard_map/grads/pallas_call | solution.py:283
  82.5 0.1 collective-permute-start.2
  82.6 0.9 copy-done.9
  83.6 3.6 %add.29 = bf16[8,256,256]{2,1,0:T(8,128)(2,1)} custom-call(bf16[8,256,256]{2,1,0:T(8,128)(2,1)} %get-tuple-element.44.a, bf16[8,256,256]{2,1,0:T(8,128)(2,1)} %copy-done.9), custom_call_target="tpu_custom_call" | custom-call | flops 1073741824 | bytes 2097152 | tf_op jit(solution)/shard_map/add/pallas_call | solution.py:399
  87.2 17.5 %all-to-all-start.3 = ((bf16[8,256,256]{2,1,0:T(8,128)(2,1)}), bf16[8,256,256]{2,1,0:T(8,128)(2,1)S(1)}, u32[]{:S(2)}, u32[]{:S(2)}) async-start(bf16[8,256,256]{2,1,0:T(8,128)(2,1)} %add.29), calls=%async_computation.3 | async-start | bytes 2097152 | tf_op jit(solution)/shard_map/all_to_all | solution.py:433
  104.7 0.0 collective-permute-done.2.b
  104.7 0.9 copy-done.10
  105.6 3.7 %add.28 = bf16[8,256,256]{2,1,0:T(8,128)(2,1)} custom-call(bf16[8,256,256]{2,1,0:T(8,128)(2,1)} %get-tuple-element.42.a, bf16[8,256,256]{2,1,0:T(8,128)(2,1)} %copy-done.10), custom_call_target="tpu_custom_call" | custom-call | flops 1073741824 | bytes 2097152 | tf_op jit(solution)/shard_map/add/pallas_call | solution.py:399
  109.3 12.7 %all-to-all-done.3 = bf16[8,256,256]{2,1,0:T(8,128)(2,1)S(1)} async-done(((bf16[8,256,256]{2,1,0:T(8,128)(2,1)}), bf16[8,256,256]{2,1,0:T(8,128)(2,1)S(1)}, u32[]{:S(2)}, u32[]{:S(2)}) %all-to-all-start.3) | async-done | bytes 1048608 | tf_op jit(solution)/shard_map/all_to_all | solution.py:433
  122.0 3.6 %all-to-all-start.2 = ((bf16[8,256,256]{2,1,0:T(8,128)(2,1)}), bf16[8,256,256]{2,1,0:T(8,128)(2,1)S(1)}, u32[]{:S(2)}, u32[]{:S(2)}) async-start(bf16[8,256,256]{2,1,0:T(8,128)(2,1)} %add.28), calls=%async_computation.2 | async-start | bytes 2097152 | tf_op jit(solution)/shard_map/all_to_all | solution.py:433
  125.6 1.4 convolution_convert_fusion
  127.0 0.0 collective-permute-start.8
  127.0 2.4 %convolution_convert_fusion.1 = bf16[512,1024]{1,0:T(8,128)(2,1)} fusion(bf16[512,256]{1,0:T(8,128)(2,1)} %bitcast.28, bf16[1,256,1024]{2,1,0:T(8,128)(2,1)S(1)} %copy-done), kind=kOutput, calls=%fused_computation.1 | convolution fusion | flops 268959744 | bytes 1835008 | tf_op jit(solution)/shard_map/dot_general | solution.py:25
  129.3 0.5 collective-permute-start.4
  129.9 0.1 reduce_sum.64.dv
  130.0 11.1 %all-to-all-done.2 = bf16[8,256,256]{2,1,0:T(8,128)(2,1)S(1)} async-done(((bf16[8,256,256]{2,1,0:T(8,128)(2,1)}), bf16[8,256,256]{2,1,0:T(8,128)(2,1)S(1)}, u32[]{:S(2)}, u32[]{:S(2)}) %all-to-all-start.2) | async-done | bytes 1048608 | tf_op jit(solution)/shard_map/all_to_all | solution.py:433
  141.1 0.1 reduce_sum.63.dk
  141.2 0.3 convolution_convert_fusion.2
  141.6 0.1 collective-permute-start.12
  141.7 2.8 %shard_map.140 = (f32[128,1024]{1,0:T(8,128)}, bf16[128,1024]{1,0:T(8,128)(2,1)}, bf16[128,1024]{1,0:T(8,128)(2,1)}, bf16[128,1024]{1,0:T(8,128)(2,1)}) custom-call(bf16[4,2,8,8,256]{4,3,2,1,0:T(8,128)(2,1)} %get-tuple-element.52.left, bf16[256,1024]{1,0:T(8,128)(2,1)} %get-tuple-element.41.dq.right, bf16[512,1024]{1,0:T(8,128)(2,1)} %collective-permute-done.8.received), custom_call_target="tpu_custom_call" | custom-call | flops 268435456 | bytes 2097152 | tf_op jit(solution)/shard_map/pallas_call | solution.py:383
  144.4 3.0 %collective-permute-start.10 = (bf16[128,1024]{1,0:T(8,128)(2,1)}, bf16[128,1024]{1,0:T(8,128)(2,1)S(1)}, u32[]{:S(2)}, u32[]{:S(2)}) collective-permute-start(bf16[128,1024]{1,0:T(8,128)(2,1)} %get-tuple-element.56), channel_id=1, source_target_pairs={{0,32},{16,48},{32,0},{48,16},{64,96},{80,112},{96,64},{112,80},{1... | collective-permute-start | bytes 786440 | tf_op jit(solution)/shard_map/ppermute | solution.py:425
  147.4 0.0 collective-permute-start.11
  147.5 2.0 collective-permute-start.9
  149.5 0.0 collective-permute-done.4.received
  149.5 1.0 copy-done.8
  150.5 2.8 %shard_map.139 = (f32[128,1024]{1,0:T(8,128)}, bf16[128,1024]{1,0:T(8,128)(2,1)}, bf16[128,1024]{1,0:T(8,128)(2,1)}, bf16[128,1024]{1,0:T(8,128)(2,1)}) custom-call(bf16[4,2,8,8,256]{4,3,2,1,0:T(8,128)(2,1)} %get-tuple-element.46.left, bf16[256,1024]{1,0:T(8,128)(2,1)} %bitcast.20, bf16[512,1024]{1,0:T(8,128)(2,1)} %copy-done.8), custom_call_target="tpu_custom_call" | custom-call | flops 268435456 | bytes 2097152 | tf_op jit(solution)/shard_map/pallas_call | solution.py:383
  153.2 0.0 collective-permute-start.5
  153.2 2.1 collective-permute-done.10.refs_6_
  155.4 3.0 %collective-permute-start.6 = (bf16[128,1024]{1,0:T(8,128)(2,1)}, bf16[128,1024]{1,0:T(8,128)(2,1)S(1)}, u32[]{:S(2)}, u32[]{:S(2)}) collective-permute-start(bf16[128,1024]{1,0:T(8,128)(2,1)} %get-tuple-element.50), channel_id=1, source_target_pairs={{0,32},{16,48},{32,0},{48,16},{64,96},{80,112},{96,64},{112,80},{1... | collective-permute-start | bytes 786440 | tf_op jit(solution)/shard_map/ppermute | solution.py:425
  158.4 0.8 pad_maximum_fusion.right
  159.2 0.1 copy-done.11
  159.3 2.2 %shard_map.141 = (f32[128,512]{1,0:T(8,128)}, bf16[128,512]{1,0:T(8,128)(2,1)}, bf16[128,512]{1,0:T(8,128)(2,1)}, bf16[128,512]{1,0:T(8,128)(2,1)}) custom-call(bf16[4,2,8,8,256]{4,3,2,1,0:T(8,128)(2,1)} %get-tuple-element.52.left, bf16[256,512]{1,0:T(8,128)(2,1)} %pad_maximum_fusion.right, bf16[512,512]{1,0:T(8,128)(2,1)} %copy-done.11), custom_call_target="tpu_custom_call" | custom-call | flops 134217728 | bytes 2097152 | tf_op jit(solution)/shard_map/pallas_call | solution.py:383
  161.5 1.9 collective-permute-start.13
  163.5 0.5 collective-permute-start.14
  164.0 2.6 %collective-permute-done.5.refs_1_ = bf16[128,1024]{1,0:T(8,128)(2,1)S(1)} collective-permute-done((bf16[128,1024]{1,0:T(8,128)(2,1)}, bf16[128,1024]{1,0:T(8,128)(2,1)S(1)}, u32[]{:S(2)}, u32[]{:S(2)}) %collective-permute-start.5) | collective-permute-done | bytes 262176 | tf_op jit(solution)/shard_map/ppermute | solution.py:425
  166.6 0.5 collective-permute-start.15
  167.2 5.1 %collective-permute-done.6.refs_2_ = bf16[128,1024]{1,0:T(8,128)(2,1)S(1)} collective-permute-done((bf16[128,1024]{1,0:T(8,128)(2,1)}, bf16[128,1024]{1,0:T(8,128)(2,1)S(1)}, u32[]{:S(2)}, u32[]{:S(2)}) %collective-permute-start.6) | collective-permute-done | bytes 262176 | tf_op jit(solution)/shard_map/ppermute | solution.py:425
  172.3 2.6 %collective-permute-done.13.refs_9_ = bf16[128,512]{1,0:T(8,128)(2,1)S(1)} collective-permute-done((bf16[128,512]{1,0:T(8,128)(2,1)}, bf16[128,512]{1,0:T(8,128)(2,1)S(1)}, u32[]{:S(2)}, u32[]{:S(2)}) %collective-permute-start.13) | collective-permute-done | bytes 131104 | tf_op jit(solution)/shard_map/ppermute | solution.py:425
  174.9 2.5 %collective-permute-done.14.refs_10_ = bf16[128,512]{1,0:T(8,128)(2,1)S(1)} collective-permute-done((bf16[128,512]{1,0:T(8,128)(2,1)}, bf16[128,512]{1,0:T(8,128)(2,1)S(1)}, u32[]{:S(2)}, u32[]{:S(2)}) %collective-permute-start.14) | collective-permute-done | bytes 131104 | tf_op jit(solution)/shard_map/ppermute | solution.py:425
  177.5 0.6 copy-done.19
  178.1 0.0 copy-done.20
  178.1 3.0 %shard_map.142 = bf16[128,2560]{1,0:T(8,128)(2,1)} custom-call(f32[128,1024]{1,0:T(8,128)} %get-tuple-element.48.refs_0_, bf16[128,1024]{1,0:T(8,128)(2,1)} %copy-done.15, bf16[128,1024]{1,0:T(8,128)(2,1)} %copy-done.16, bf16[128,1024]{1,0:T(8,128)(2,1)} %copy-done.17, f32[128,1024]{1,0:T(8,128)} %get-tuple-element.54.refs_4_, bf16[128,1024]{1,0:T(8,128)(2,1)} %copy-done.14, ...), custom_call_target="tpu_custom_call" | custom-call | flops 1073741824 | bytes 2097152 | tf_op jit(solution)/shard_map/pallas_call | solution.py:383
  181.1 19.4 %all_to_all.31 = bf16[16,8,2560]{2,1,0:T(8,128)(2,1)S(1)} all-to-all(bf16[16,8,2560]{2,1,0:T(8,128)(2,1)} %bitcast.24), channel_id=1, replica_groups={{0,2,4,6,8,10,12,14,64,66,68,70,72,74,76,78},{1,3,5,7,9,11,13,15,65,67,..., dimensions={0} | all-to-all | bytes 1310720 | tf_op jit(solution)/shard_map/all_to_all | solution.py:443
  200.5 0.1 reduce_sum.65
  200.6 0.7 broadcast_in_dim.7
  201.4 3.4 %all-to-all-start.5 = ((bf16[8,8,2560]{2,1,0:T(8,128)(2,1)}), bf16[8,8,2560]{2,1,0:T(8,128)(2,1)S(1)}, u32[]{:S(2)}, u32[]{:S(2)}) async-start(bf16[8,8,2560]{2,1,0:T(8,128)(2,1)} %broadcast_in_dim.7), calls=%async_computation.5 | async-start | bytes 655360 | tf_op jit(solution)/shard_map/all_to_all | solution.py:532
  204.8 4.4 %shard_map.138 = bf16[256,1024]{1,0:T(8,128)(2,1)} custom-call(bf16[256,1024]{1,0:T(8,128)(2,1)} %bitcast.26, bf16[256,1024]{1,0:T(8,128)(2,1)} %bitcast.21, f32[1,1024]{1,0:T(1,128)} %bitcast.30, bf16[256,1024]{1,0:T(8,128)(2,1)} %get-tuple-element.41.dq.right, bf16[256,256]{1,0:T(8,128)(2,1)} %copy-done.3, bf16[256,256]{1,0:T(8,128)(2,1)} %copy-done.2, ...), custom_call_target="tpu_custom_call" | custom-call | flops 805306368 | bytes 2097152 | tf_op jit(solution)/shard_map/pallas_call | solution.py:383
  209.3 3.1 %all-to-all-done.5 = bf16[8,8,2560]{2,1,0:T(8,128)(2,1)S(1)} async-done(((bf16[8,8,2560]{2,1,0:T(8,128)(2,1)}), bf16[8,8,2560]{2,1,0:T(8,128)(2,1)S(1)}, u32[]{:S(2)}, u32[]{:S(2)}) %all-to-all-start.5) | async-done | bytes 327712 | tf_op jit(solution)/shard_map/all_to_all | solution.py:532
  212.4 1.8 multiply_reduce_fusion
  214.3 1.5 multiply_reduce_fusion.1
  215.8 1.3 dynamic-slice_divide_fusion
  (45 shorter events, 0.1 us)
Async XLA Ops:
  28.8 25.9 %copy-start.4 = (bf16[8,256,256]{2,1,0:T(8,128)(2,1)}, bf16[8,256,256]{2,1,0:T(8,128)(2,1)S(1)}, u32[]{:S(2)}) copy-start(bf16[8,256,256]{2,1,0:T(8,128)(2,1)S(1)} %all_to_all.30.k_own) | copy-start | bytes 3145732
  28.8 18.3 %all-to-all-start.1 = ((bf16[8,256,256]{2,1,0:T(8,128)(2,1)}), bf16[8,256,256]{2,1,0:T(8,128)(2,1)S(1)}, u32[]{:S(2)}, u32[]{:S(2)}) async-start(bf16[8,256,256]{2,1,0:T(8,128)(2,1)} %get-tuple-element.38), calls=%async_computation.1 | async-start | bytes 2097152 | tf_op jit(solution)/shard_map/all_to_all | solution.py:433
  32.3 22.4 %collective-permute-start = (bf16[8,256,256]{2,1,0:T(8,128)(2,1)S(1)}, bf16[8,256,256]{2,1,0:T(8,128)(2,1)S(1)}, u32[]{:S(2)}, u32[]{:S(2)}) collective-permute-start(bf16[8,256,256]{2,1,0:T(8,128)(2,1)S(1)} %all_to_all.30.k_own), channel_id=1, source_target_pairs={{0,1},{1,0},{2,3},{3,2},{4,5},{5,4},{6,7},{7,6},{8,9},{9,8},{10,11... | collective-permute-start | bytes 3145736 | tf_op jit(solution)/shard_map/ppermute | solution.py:420
  47.0 7.7 %copy-start.5 = (bf16[8,256,256]{2,1,0:T(8,128)(2,1)}, bf16[8,256,256]{2,1,0:T(8,128)(2,1)S(1)}, u32[]{:S(2)}) copy-start(bf16[8,256,256]{2,1,0:T(8,128)(2,1)S(1)} %all-to-all-done.1.v_own) | copy-start | bytes 3145732
  47.0 13.0 %collective-permute-start.1 = (bf16[8,256,256]{2,1,0:T(8,128)(2,1)S(1)}, bf16[8,256,256]{2,1,0:T(8,128)(2,1)}, u32[]{:S(2)}, u32[]{:S(2)}) collective-permute-start(bf16[8,256,256]{2,1,0:T(8,128)(2,1)S(1)} %all-to-all-done.1.v_own), channel_id=1, source_target_pairs={{0,1},{1,0},{2,3},{3,2},{4,5},{5,4},{6,7},{7,6},{8,9},{9,8},{10,11... | collective-permute-start | bytes 3145736 | tf_op jit(solution)/shard_map/ppermute | solution.py:420
  54.7 1.0 copy-start.7
  72.4 10.2 %collective-permute-start.3 = (bf16[8,256,256]{2,1,0:T(8,128)(2,1)}, bf16[8,256,256]{2,1,0:T(8,128)(2,1)S(1)}, u32[]{:S(2)}, u32[]{:S(2)}) collective-permute-start(bf16[8,256,256]{2,1,0:T(8,128)(2,1)} %get-tuple-element.45), channel_id=1, source_target_pairs={{0,1},{1,0},{2,3},{3,2},{4,5},{5,4},{6,7},{7,6},{8,9},{9,8},{10,11... | collective-permute-start | bytes 3145736 | tf_op jit(solution)/shard_map/ppermute | solution.py:420
  82.5 22.2 %collective-permute-start.2 = (bf16[8,256,256]{2,1,0:T(8,128)(2,1)}, bf16[8,256,256]{2,1,0:T(8,128)(2,1)S(1)}, u32[]{:S(2)}, u32[]{:S(2)}) collective-permute-start(bf16[8,256,256]{2,1,0:T(8,128)(2,1)} %get-tuple-element.43), channel_id=1, source_target_pairs={{0,1},{1,0},{2,3},{3,2},{4,5},{5,4},{6,7},{7,6},{8,9},{9,8},{10,11... | collective-permute-start | bytes 3145736 | tf_op jit(solution)/shard_map/ppermute | solution.py:420
  82.6 1.0 copy-start.9
  87.2 34.8 %all-to-all-start.3 = ((bf16[8,256,256]{2,1,0:T(8,128)(2,1)}), bf16[8,256,256]{2,1,0:T(8,128)(2,1)S(1)}, u32[]{:S(2)}, u32[]{:S(2)}) async-start(bf16[8,256,256]{2,1,0:T(8,128)(2,1)} %add.29), calls=%async_computation.3 | async-start | bytes 2097152 | tf_op jit(solution)/shard_map/all_to_all | solution.py:433
  104.7 1.0 copy-start.10
  105.6 19.9 %copy-start.1 = (bf16[256,1024]{1,0:T(8,128)(2,1)S(1)}, bf16[256,1024]{1,0:T(8,128)(2,1)}, u32[]{:S(2)}) copy-start(bf16[256,1024]{1,0:T(8,128)(2,1)} %get-tuple-element.41.dq.right) | copy-start | bytes 1572868
  105.6 19.9 %copy-start.6 = (bf16[4,2,8,8,256]{4,3,2,1,0:T(8,128)(2,1)S(1)}, bf16[4,2,8,8,256]{4,3,2,1,0:T(8,128)(2,1)}, u32[]{:S(2)}) copy-start(bf16[4,2,8,8,256]{4,3,2,1,0:T(8,128)(2,1)} %get-tuple-element.53) | copy-start | bytes 786436
  109.3 17.7 %copy-start = (bf16[1,256,1024]{2,1,0:T(8,128)(2,1)S(1)}, bf16[1,256,1024]{2,1,0:T(8,128)(2,1)}, u32[]{:S(2)}) copy-start(bf16[1,256,1024]{2,1,0:T(8,128)(2,1)} %param.10) | copy-start | bytes 1572868
  122.0 19.1 %all-to-all-start.2 = ((bf16[8,256,256]{2,1,0:T(8,128)(2,1)}), bf16[8,256,256]{2,1,0:T(8,128)(2,1)S(1)}, u32[]{:S(2)}, u32[]{:S(2)}) async-start(bf16[8,256,256]{2,1,0:T(8,128)(2,1)} %add.28), calls=%async_computation.2 | async-start | bytes 2097152 | tf_op jit(solution)/shard_map/all_to_all | solution.py:433
  127.0 14.7 %collective-permute-start.8 = (bf16[512,1024]{1,0:T(8,128)(2,1)}, bf16[512,1024]{1,0:T(8,128)(2,1)}, u32[]{:S(2)}, u32[]{:S(2)}) collective-permute-start(bf16[512,1024]{1,0:T(8,128)(2,1)} %convolution_convert_fusion), channel_id=1, source_target_pairs={{0,1},{1,0},{2,3},{3,2},{4,5},{5,4},{6,7},{7,6},{8,9},{9,8},{10,11... | collective-permute-start | bytes 3145736 | tf_op jit(solution)/shard_map/ppermute | solution.py:420
  129.3 20.1 %collective-permute-start.4 = (bf16[512,1024]{1,0:T(8,128)(2,1)}, bf16[512,1024]{1,0:T(8,128)(2,1)S(1)}, u32[]{:S(2)}, u32[]{:S(2)}) collective-permute-start(bf16[512,1024]{1,0:T(8,128)(2,1)} %convolution_convert_fusion.1), channel_id=1, source_target_pairs={{0,1},{1,0},{2,3},{3,2},{4,5},{5,4},{6,7},{7,6},{8,9},{9,8},{10,11... | collective-permute-start | bytes 3145736 | tf_op jit(solution)/shard_map/ppermute | solution.py:420
  130.0 28.4 %copy-start.2 = (bf16[256,256]{1,0:T(8,128)(2,1)}, bf16[256,256]{1,0:T(8,128)(2,1)S(1)}, u32[]{:S(2)}) copy-start(bf16[256,256]{1,0:T(8,128)(2,1)S(1)} %reduce_sum.64.dv) | copy-start | bytes 393220
  141.2 17.2 %copy-start.3 = (bf16[256,256]{1,0:T(8,128)(2,1)}, bf16[256,256]{1,0:T(8,128)(2,1)S(1)}, u32[]{:S(2)}) copy-start(bf16[256,256]{1,0:T(8,128)(2,1)S(1)} %reduce_sum.63.dk) | copy-start | bytes 393220
  141.6 16.8 %collective-permute-start.12 = (bf16[512,512]{1,0:T(8,128)(2,1)S(1)}, bf16[512,512]{1,0:T(8,128)(2,1)S(1)}, u32[]{:S(2)}, u32[]{:S(2)}) collective-permute-start(bf16[512,512]{1,0:T(8,128)(2,1)S(1)} %convolution_convert_fusion.2), channel_id=1, source_target_pairs={{0,1},{1,0},{2,3},{3,2},{4,5},{5,4},{6,7},{7,6},{8,9},{9,8},{10,11... | collective-permute-start | bytes 1572872 | tf_op jit(solution)/shard_map/ppermute | solution.py:420
  144.4 10.9 %collective-permute-start.10 = (bf16[128,1024]{1,0:T(8,128)(2,1)}, bf16[128,1024]{1,0:T(8,128)(2,1)S(1)}, u32[]{:S(2)}, u32[]{:S(2)}) collective-permute-start(bf16[128,1024]{1,0:T(8,128)(2,1)} %get-tuple-element.56), channel_id=1, source_target_pairs={{0,32},{16,48},{32,0},{48,16},{64,96},{80,112},{96,64},{112,80},{1... | collective-permute-start | bytes 786440 | tf_op jit(solution)/shard_map/ppermute | solution.py:425
  147.4 14.1 %collective-permute-start.11 = (bf16[128,1024]{1,0:T(8,128)(2,1)}, bf16[128,1024]{1,0:T(8,128)(2,1)S(1)}, u32[]{:S(2)}, u32[]{:S(2)}) collective-permute-start(bf16[128,1024]{1,0:T(8,128)(2,1)} %get-tuple-element.57), channel_id=1, source_target_pairs={{0,48},{16,0},{32,16},{48,32},{64,112},{80,64},{96,80},{112,96},{1... | collective-permute-start | bytes 786440 | tf_op jit(solution)/shard_map/ppermute | solution.py:425
  147.5 16.0 %collective-permute-start.9 = (bf16[128,1024]{1,0:T(8,128)(2,1)}, bf16[128,1024]{1,0:T(8,128)(2,1)S(1)}, u32[]{:S(2)}, u32[]{:S(2)}) collective-permute-start(bf16[128,1024]{1,0:T(8,128)(2,1)} %get-tuple-element.55), channel_id=1, source_target_pairs={{0,16},{16,32},{32,48},{48,0},{64,80},{80,96},{96,112},{112,64},{1... | collective-permute-start | bytes 786440 | tf_op jit(solution)/shard_map/ppermute | solution.py:425
  149.5 1.0 copy-start.8
  153.2 13.4 %collective-permute-start.5 = (bf16[128,1024]{1,0:T(8,128)(2,1)}, bf16[128,1024]{1,0:T(8,128)(2,1)S(1)}, u32[]{:S(2)}, u32[]{:S(2)}) collective-permute-start(bf16[128,1024]{1,0:T(8,128)(2,1)} %get-tuple-element.49), channel_id=1, source_target_pairs={{0,16},{16,32},{32,48},{48,0},{64,80},{80,96},{96,112},{112,64},{1... | collective-permute-start | bytes 786440 | tf_op jit(solution)/shard_map/ppermute | solution.py:425
  155.4 22.0 %copy-start.12 = (bf16[128,1024]{1,0:T(8,128)(2,1)}, bf16[128,1024]{1,0:T(8,128)(2,1)S(1)}, u32[]{:S(2)}) copy-start(bf16[128,1024]{1,0:T(8,128)(2,1)S(1)} %collective-permute-done.10.refs_6_) | copy-start | bytes 786436
  155.4 16.9 %collective-permute-start.6 = (bf16[128,1024]{1,0:T(8,128)(2,1)}, bf16[128,1024]{1,0:T(8,128)(2,1)S(1)}, u32[]{:S(2)}, u32[]{:S(2)}) collective-permute-start(bf16[128,1024]{1,0:T(8,128)(2,1)} %get-tuple-element.50), channel_id=1, source_target_pairs={{0,32},{16,48},{32,0},{48,16},{64,96},{80,112},{96,64},{112,80},{1... | collective-permute-start | bytes 786440 | tf_op jit(solution)/shard_map/ppermute | solution.py:425
  158.4 0.9 copy-start.11
  158.4 13.9 %collective-permute-start.7 = (bf16[128,1024]{1,0:T(8,128)(2,1)}, bf16[128,1024]{1,0:T(8,128)(2,1)S(1)}, u32[]{:S(2)}, u32[]{:S(2)}) collective-permute-start(bf16[128,1024]{1,0:T(8,128)(2,1)} %get-tuple-element.51), channel_id=1, source_target_pairs={{0,48},{16,0},{32,16},{48,32},{64,112},{80,64},{96,80},{112,96},{1... | collective-permute-start | bytes 786440 | tf_op jit(solution)/shard_map/ppermute | solution.py:425
  161.5 15.9 %copy-start.13 = (bf16[128,1024]{1,0:T(8,128)(2,1)}, bf16[128,1024]{1,0:T(8,128)(2,1)S(1)}, u32[]{:S(2)}) copy-start(bf16[128,1024]{1,0:T(8,128)(2,1)S(1)} %collective-permute-done.11.refs_7_) | copy-start | bytes 786436
  161.5 13.4 %collective-permute-start.13 = (bf16[128,512]{1,0:T(8,128)(2,1)}, bf16[128,512]{1,0:T(8,128)(2,1)S(1)}, u32[]{:S(2)}, u32[]{:S(2)}) collective-permute-start(bf16[128,512]{1,0:T(8,128)(2,1)} %get-tuple-element.59), channel_id=1, source_target_pairs={{0,16},{16,32},{32,48},{48,0},{64,80},{80,96},{96,112},{112,64},{1... | collective-permute-start | bytes 393224 | tf_op jit(solution)/shard_map/ppermute | solution.py:425
  163.5 14.0 %copy-start.14 = (bf16[128,1024]{1,0:T(8,128)(2,1)}, bf16[128,1024]{1,0:T(8,128)(2,1)S(1)}, u32[]{:S(2)}) copy-start(bf16[128,1024]{1,0:T(8,128)(2,1)S(1)} %collective-permute-done.9.refs_5_) | copy-start | bytes 786436
  163.5 13.9 %collective-permute-start.14 = (bf16[128,512]{1,0:T(8,128)(2,1)}, bf16[128,512]{1,0:T(8,128)(2,1)S(1)}, u32[]{:S(2)}, u32[]{:S(2)}) collective-permute-start(bf16[128,512]{1,0:T(8,128)(2,1)} %get-tuple-element.60), channel_id=1, source_target_pairs={{0,32},{16,48},{32,0},{48,16},{64,96},{80,112},{96,64},{112,80},{1... | collective-permute-start | bytes 393224 | tf_op jit(solution)/shard_map/ppermute | solution.py:425
  166.6 10.8 %copy-start.15 = (bf16[128,1024]{1,0:T(8,128)(2,1)}, bf16[128,1024]{1,0:T(8,128)(2,1)S(1)}, u32[]{:S(2)}) copy-start(bf16[128,1024]{1,0:T(8,128)(2,1)S(1)} %collective-permute-done.5.refs_1_) | copy-start | bytes 786436
  166.6 10.8 %collective-permute-start.15 = (bf16[128,512]{1,0:T(8,128)(2,1)}, bf16[128,512]{1,0:T(8,128)(2,1)S(1)}, u32[]{:S(2)}, u32[]{:S(2)}) collective-permute-start(bf16[128,512]{1,0:T(8,128)(2,1)} %get-tuple-element.61), channel_id=1, source_target_pairs={{0,48},{16,0},{32,16},{48,32},{64,112},{80,64},{96,80},{112,96},{1... | collective-permute-start | bytes 393224 | tf_op jit(solution)/shard_map/ppermute | solution.py:425
  172.3 5.2 %copy-start.16 = (bf16[128,1024]{1,0:T(8,128)(2,1)}, bf16[128,1024]{1,0:T(8,128)(2,1)S(1)}, u32[]{:S(2)}) copy-start(bf16[128,1024]{1,0:T(8,128)(2,1)S(1)} %collective-permute-done.6.refs_2_) | copy-start | bytes 786436
  172.3 5.2 %copy-start.17 = (bf16[128,1024]{1,0:T(8,128)(2,1)}, bf16[128,1024]{1,0:T(8,128)(2,1)S(1)}, u32[]{:S(2)}) copy-start(bf16[128,1024]{1,0:T(8,128)(2,1)S(1)} %collective-permute-done.7.refs_3_) | copy-start | bytes 786436
  174.9 2.6 %copy-start.18 = (bf16[128,512]{1,0:T(8,128)(2,1)}, bf16[128,512]{1,0:T(8,128)(2,1)S(1)}, u32[]{:S(2)}) copy-start(bf16[128,512]{1,0:T(8,128)(2,1)S(1)} %collective-permute-done.13.refs_9_) | copy-start | bytes 393220
  177.4 0.7 copy-start.19
  177.4 0.7 copy-start.20
  201.4 11.0 %all-to-all-start.5 = ((bf16[8,8,2560]{2,1,0:T(8,128)(2,1)}), bf16[8,8,2560]{2,1,0:T(8,128)(2,1)S(1)}, u32[]{:S(2)}, u32[]{:S(2)}) async-start(bf16[8,8,2560]{2,1,0:T(8,128)(2,1)} %broadcast_in_dim.7), calls=%async_computation.5 | async-start | bytes 655360 | tf_op jit(solution)/shard_map/all_to_all | solution.py:532

commit v3 on v0

v3 whole, which is shorter than its diff:
```python
import functools

import jax
import jax.numpy as jnp
from jax import lax
from jax.experimental import pallas as pl
from jax.experimental.pallas import tpu as pltpu
from jax.sharding import PartitionSpec as P

HS = 256
ACT = 64
BLOCK = 128
NEG = -1e30
EPS = 1e-06
LOG2E = 1.4426950408889634
VMEM_BYTES = 67043328
NT = (((1,), (1,)), ((), ()))


def dot_nt(a, b):
    return lax.dot_general(a, b, NT, preferred_element_type=jnp.float32)


def dot_nn(a, b):
    return jnp.dot(a, b, preferred_element_type=jnp.float32)


def head(h):
    return pl.ds(h * HS, HS)


def part(half, h, heads):
    return pl.ds((half * heads + h) * HS, HS)


def block_state(info, chip, half, tok, seq):
    rows, plen, edge, core = info[0] ^ half, info[1], info[2], info[3]
    low = (chip * 2 + core) * tok
    high = low + tok
    first, last = rows * tok, rows * tok + tok - 1
    seen = ((low < plen) | (high > seq - ACT)) & ((low < edge) | (low <= last))
    full = (high <= plen) & ((high <= edge) | (high - 1 <= first))
    return seen, full


def mask_of(info, chip, half, tok, seq):
    rows, plen, edge, core = info[0] ^ half, info[1], info[2], info[3]
    k_pos = (chip * 2 + core) * tok + lax.broadcasted_iota(jnp.int32, (tok, tok), 0)
    q_pos = rows * tok + lax.broadcasted_iota(jnp.int32, (tok, tok), 1)
    key_ok = (k_pos < plen) | (k_pos >= seq - ACT)
    return key_ok & ((k_pos < edge) | (k_pos <= q_pos))


def when_seen(info, chip, half, tok, seq, work, rest):
    seen, full = block_state(info, chip, half, tok, seq)

    @pl.when(full)
    def _():
        work(None)

    @pl.when(seen & jnp.logical_not(full))
    def _():
        work(mask_of(info, chip, half, tok, seq))

    if rest is not None:
        pl.when(jnp.logical_not(seen))(rest)


def each_chip(chips, step):
    def body(chip, carry):
        step(chip)
        return carry

    lax.fori_loop(0, chips, body, 0)


def scaled_scores(keys, q, h, mask):
    s = dot_nt(keys, q[0, :, head(h)]) * (HS ** (-0.5) * LOG2E)
    return s if mask is None else jnp.where(mask, s, NEG)


def stats_kernel(heads, seq, info, own, pair, keys, out, top, total):
    chips, tok, _ = keys.shape
    top[...] = jnp.full(top.shape, NEG, jnp.float32)
    total[...] = jnp.zeros(total.shape, jnp.float32)

    def step(chip):
        for half, q in enumerate((own, pair)):

            def work(mask, half=half, q=q):
                for h in range(heads):
                    at = part(half, h, heads)
                    s = scaled_scores(keys[chip], q, h, mask)
                    old = top[:, at]
                    new = jnp.maximum(old, jnp.max(s, axis=0, keepdims=True))
                    top[:, at] = new
                    total[:, at] = total[:, at] * jnp.exp2(old - new) + jnp.sum(
                        jnp.exp2(s - new), axis=0, keepdims=True
                    )

            when_seen(info, chip, half, tok, seq, work, None)

    each_chip(chips, step)
    wide = heads * HS
    for half in range(2):
        out[half, 0:1, :] = top[:, pl.ds(half * wide, wide)]
        out[half, 1:2, :] = total[:, pl.ds(half * wide, wide)]


def attend_kernel(
    heads, seq, info, own, pair, mine, other, keys, values,
    attn, dv, probs_out,
    values_t, da_rows, probs, lse, out_sems,
):
    chips, tok, _ = keys.shape
    wide = heads * HS
    for half, qd in enumerate((own, pair)):
        for h in range(heads):
            da_rows[part(half, h, heads), :] = qd[1, :, head(h)]
        top_a, top_b = mine[half, 0:1, :], other[1 - half, 0:1, :]
        top = jnp.maximum(top_a, top_b)
        total = mine[half, 1:2, :] * jnp.exp2(top_a - top)
        total = total + other[1 - half, 1:2, :] * jnp.exp2(top_b - top)
        lse[:, pl.ds(half * wide, wide)] = top + jnp.log(total) * LOG2E
    for chip in range(chips):
        values_t[:, pl.ds(chip * tok, tok)] = values[chip].T

    def rows_of(chip):
        return pl.ds(pl.multiple_of(chip * tok, tok), tok)

    def out_copy(chip):
        rows = rows_of(chip)
        return pltpu.make_async_copy(probs.at[rows, :], probs_out.at[rows, :], out_sems.at[chip])

    def step(chip):
        rows = rows_of(chip)
        for half, q in enumerate((own, pair)):

            def work(mask, half=half, q=q):
                for h in range(heads):
                    at = part(half, h, heads)
                    s = scaled_scores(keys[chip], q, h, mask)
                    probs[rows, at] = jnp.exp2(s - lse[:, at]).astype(jnp.bfloat16)

            def rest(half=half):
                probs[rows, pl.ds(half * wide, wide)] = jnp.zeros((tok, wide), jnp.bfloat16)

            when_seen(info, chip, half, tok, seq, work, rest)
        dv[chip] = dot_nn(probs[rows, :], da_rows[...]).astype(jnp.bfloat16)
        out_copy(chip).start()

    each_chip(chips, step)
    for half in range(2):
        for h in range(heads):
            attn[half, head(h), :] = dot_nn(values_t[...], probs[:, part(half, h, heads)]).astype(
                jnp.bfloat16
            )
    each_chip(chips, lambda chip: out_copy(chip).wait())


def put_rows(info, rows, chip, own, pair):
    core, x = info[3], info[4]
    steps, outer, _, size, _ = own.shape

    def put(same):
        for n in range(rows.shape[0] // size):
            place = n % (outer * steps)
            to = own if (n // (outer * steps)) == same else pair
            step = (place % steps - x + steps) & (steps - 1)
            to[step, place // steps, chip] = rows[n * size : (n + 1) * size].astype(to.dtype)

    for same in range(2):
        pl.when(core == same)(functools.partial(put, same))


def grads_kernel(
    heads, seq, info, own, pair, mine, other, keys, values, probs_in,
    at_own, at_pair, dk, dq_own, dq_pair,
    keys_t, q_rows, probs, dscores, delta, in_sems,
):
    chips, tok, _ = keys.shape

    def rows_of(chip):
        return pl.ds(pl.multiple_of(chip * tok, tok), tok)

    def in_copy(chip):
        rows = rows_of(chip)
        return pltpu.make_async_copy(probs_in.at[rows, :], probs.at[rows, :], in_sems.at[chip])

    each_chip(chips, lambda chip: in_copy(chip).start())
    per_head = chips // heads
    block = HS // per_head
    for half, qd in enumerate((own, pair)):
        for h in range(heads):
            at = part(half, h, heads)
            q_rows[at, :] = qd[0, :, head(h)]
            both = mine[half, head(h), :].astype(jnp.float32) + other[1 - half, head(h), :].astype(
                jnp.float32
            )
            a = both.astype(jnp.bfloat16).astype(jnp.float32)
            delta[:, at] = jnp.sum(
                a * qd[1, :, head(h)].T.astype(jnp.float32), axis=0, keepdims=True
            )
            if half == 0:
                for n in range(per_head):
                    put_rows(info, a[n * block : (n + 1) * block], h * per_head + n, at_own, at_pair)
    for chip in range(chips):
        keys_t[:, pl.ds(chip * tok, tok)] = keys[chip].T

    def step(chip):
        rows = rows_of(chip)
        in_copy(chip).wait()
        for half, qd in enumerate((own, pair)):
            seen, _ = block_state(info, chip, half, tok, seq)

            @pl.when(seen)
            def _(half=half, qd=qd):
                for h in range(heads):
                    at = part(half, h, heads)
                    dp = dot_nt(values[chip], qd[1, :, head(h)])
                    p = probs[rows, at].astype(jnp.float32)
                    dscores[rows, at] = (p * (dp - delta[:, at])).astype(jnp.bfloat16)

            @pl.when(jnp.logical_not(seen))
            def _(half=half):
                wide = heads * HS
                dscores[rows, pl.ds(half * wide, wide)] = jnp.zeros((tok, wide), jnp.bfloat16)

        dk[chip] = (dot_nn(dscores[rows, :], q_rows[...]) * HS ** (-0.5)).astype(jnp.bfloat16)

    each_chip(chips, step)
    for half, dq in enumerate((dq_own, dq_pair)):
        for h in range(heads):
            d = dot_nn(keys_t[...], dscores[:, part(half, h, heads)]) * HS ** (-0.5)
            dq[:, head(h)] = d.T.astype(jnp.bfloat16)


def prepare_kernel(chips, x, gain, w_key, w_value, hidden, k_copies, v_copies):
    xf = x[...].astype(jnp.float32)
    inv = lax.rsqrt(jnp.mean(xf * xf, axis=-1, keepdims=True) + EPS)
    h = (xf * inv * gain[...]).astype(jnp.bfloat16)
    hidden[...] = h
    for weight, out in ((w_key, k_copies), (w_value, v_copies)):
        rows = dot_nn(h, weight[...]).astype(jnp.bfloat16)
        for chip in range(chips):
            out[chip] = rows


def project_kernel(info, hidden, grad_out, w_query, w_out, both, ht_own, ht_pair):
    h = hidden[...]
    both[0] = dot_nn(h, w_query[...]).astype(jnp.bfloat16)
    both[1] = dot_nt(grad_out[...], w_out[...]).astype(jnp.bfloat16)
    chips = ht_own.shape[2]
    block = h.shape[1] // chips
    for chip in range(chips):
        rows = h[:, chip * block : (chip + 1) * block].astype(jnp.float32).T
        put_rows(info, rows, chip, ht_own, ht_pair)


def step_terms(left, step, right, received):
    rows = left.shape[1] * left.shape[2] * left.shape[3]
    own = dot_nn(left[step].reshape(rows, -1), right)
    return own + received[pl.ds(step * rows, rows), :].astype(jnp.float32)


def own_terms_kernel(left, right, received, base, *parts):
    for step, out in enumerate((base, *parts)):
        out[...] = step_terms(left, step, right[...], received).astype(out.dtype)


def direct_terms(info, left, right, received, out, at):
    wide, steps = right.shape[1], left.shape[0]
    for step in range(steps):
        place = (info[4] + step) & (steps - 1)
        to = pl.ds(pl.multiple_of(at + place * wide, 128), wide)
        out[:, to] = step_terms(left, step, right[...], received).astype(out.dtype)


def direct_kernel(info, left, right, received, out):
    direct_terms(info, left, right, received, out, 0)


def collect_kernel(info, base, one, two, three, query_terms, left, right, received, out):
    total = base[...]
    for arrived in (one, two, three):
        total = total + arrived[...].astype(jnp.float32)
    wide = total.shape[1]
    out[:, pl.ds(0, wide)] = total.astype(out.dtype)
    out[:, pl.ds(wide, query_terms.shape[1])] = query_terms[...]
    direct_terms(info, left, right, received, out, wide + query_terms.shape[1])


def spread_kernel(parts, out):
    total = parts[0].astype(jnp.float32)
    for n in range(1, parts.shape[0]):
        total = total + parts[n].astype(jnp.float32)
    total = total.astype(out.dtype)
    for n in range(out.shape[0]):
        out[n] = total


def weights_kernel(steps, shared, w_query, w_key, w_value, gain, d_query, d_key, d_value, d_out, d_gain):
    size = shared.shape[1]
    wide, heads_wide = d_out.shape[1], d_query.shape[1]
    gains = []
    for place in range(shared.shape[0]):
        outer, x = place // steps, place % steps
        rows = slice(place * size, (place + 1) * size)
        d_out[rows, :] = shared[place, :, pl.ds(0, wide)].astype(jnp.float32)

        def added(at, width):
            total = 0.0
            for source in range(steps):
                total = total + shared[outer * steps + source, :, pl.ds(at, width)].astype(jnp.float32)
            return total

        query = added(wide + x * heads_wide, heads_wide)
        kv = added(wide + steps * heads_wide + x * 2 * HS, 2 * HS)
        d_query[rows, :] = query
        d_key[rows, :] = kv[:, :HS]
        d_value[rows, :] = kv[:, HS:]
        row_sum = (
            jnp.sum(w_query[rows, :].astype(jnp.float32) * query, axis=1, keepdims=True)
            + jnp.sum(w_key[rows, :].astype(jnp.float32) * kv[:, :HS], axis=1, keepdims=True)
            + jnp.sum(w_value[rows, :].astype(jnp.float32) * kv[:, HS:], axis=1, keepdims=True)
        )
        gains.append(jnp.broadcast_to(row_sum, (size, 128)))
    d_gain[...] = jnp.concatenate(gains, axis=0).T[0:1, :] / gain[...]


def finish_kernel(x, grad_out, gain, dq, dkv, w_query, w_key, w_value, d_in):
    dhidden = (
        dot_nt(dq[...], w_query[...])
        + dot_nt(dkv[:, :HS], w_key[...])
        + dot_nt(dkv[:, HS:], w_value[...])
    )
    xf = x[...].astype(jnp.float32)
    inv = lax.rsqrt(jnp.mean(xf * xf, axis=-1, keepdims=True) + EPS)
    normed = xf * inv
    scaled = dhidden * gain[...]
    mean = jnp.mean(scaled * normed, axis=-1, keepdims=True)
    d_in[...] = (grad_out[...].astype(jnp.float32) + inv * (scaled - normed * mean)).astype(d_in.dtype)


SMEM = pl.BlockSpec(memory_space=pltpu.SMEM)
VMEM = pl.BlockSpec(memory_space=pltpu.VMEM)
ANY = pl.BlockSpec(memory_space=pl.ANY)


def shape(*dims, dtype=jnp.bfloat16):
    return jax.ShapeDtypeStruct(dims, dtype)


def call(body, outs, args, flops, smem=0, scratch=(), in_any=(), out_any=()):
    specs = [SMEM if n < smem else ANY if n in in_any else VMEM for n in range(len(args))]
    if isinstance(outs, tuple):
        out_specs = tuple(ANY if n in out_any else VMEM for n in range(len(outs)))
    else:
        out_specs = VMEM
    return pl.pallas_call(
        body,
        out_shape=outs,
        in_specs=specs,
        out_specs=out_specs,
        scratch_shapes=list(scratch),
        compiler_params=pltpu.CompilerParams(vmem_limit_bytes=VMEM_BYTES),
        cost_estimate=pl.CostEstimate(flops=flops, bytes_accessed=1 << 20, transcendentals=0),
    )(*args)


def scratch(*dims, dtype=jnp.bfloat16):
    return pltpu.VMEM(dims, dtype)


def run_stats(info, own, pair, keys):
    _, tok, wide = own.shape
    chips, heads = keys.shape[0], wide // HS
    seq = 2 * tok * chips
    rows = scratch(1, 2 * wide, dtype=jnp.float32)
    return call(
        functools.partial(stats_kernel, heads, seq),
        shape(2, 2, wide, dtype=jnp.float32),
        (info, own, pair, keys),
        2 * seq * wide * HS,
        smem=1,
        scratch=(rows, rows),
    )


def run_attend(info, own, pair, mine, other, keys, values):
    _, tok, wide = own.shape
    chips, heads = keys.shape[0], wide // HS
    seq = 2 * tok * chips
    return call(
        functools.partial(attend_kernel, heads, seq),
        (shape(2, wide, tok), shape(chips, tok, HS), shape(chips * tok, 2 * wide)),
        (info, own, pair, mine, other, keys, values),
        6 * seq * wide * HS,
        smem=1,
        out_any=(2,),
        scratch=(
            scratch(HS, chips * tok),
            scratch(2 * wide, HS),
            scratch(chips * tok, 2 * wide),
            scratch(1, 2 * wide, dtype=jnp.float32),
            pltpu.SemaphoreType.DMA((chips,)),
        ),
    )


def run_grads(info, own, pair, mine, other, keys, values, probs, filed):
    _, tok, wide = own.shape
    chips, heads = keys.shape[0], wide // HS
    seq = 2 * tok * chips
    return call(
        functools.partial(grads_kernel, heads, seq),
        (filed, filed, shape(chips, tok, HS), shape(tok, wide), shape(tok, wide)),
        (info, own, pair, mine, other, keys, values, probs),
        6 * seq * wide * HS,
        smem=1,
        in_any=(7,),
        scratch=(
            scratch(HS, chips * tok),
            scratch(2 * wide, HS),
            scratch(chips * tok, 2 * wide),
            scratch(chips * tok, 2 * wide),
            scratch(1, 2 * wide, dtype=jnp.float32),
            pltpu.SemaphoreType.DMA((chips,)),
        ),
    )


CORES = 2
X = 4


def as_bf16(value):
    return value.astype(jnp.bfloat16)


def swap_cores(value):
    count = lax.axis_size("blk")
    return lax.ppermute(value, "blk", [(i, i ^ 1) for i in range(count)])


def send_along_x(value, step):
    count = lax.axis_size("dp")
    return lax.ppermute(
        value, "dp", [(i, i // X * X + (i + step) % X) for i in range(count)]
    )


def exchange_chips(value):
    chips = lax.axis_size("blk") // CORES
    groups = [[core + CORES * chip for chip in range(chips)] for core in range(CORES)]
    return lax.all_to_all(value, "blk", 0, 0, tiled=True, axis_index_groups=groups)


def exchange_plane(value):
    blk, dp = lax.axis_size("blk"), lax.axis_size("dp")
    groups = [
        [(outer * X + x) * blk + chip * CORES + core for outer in range(dp // X) for chip in range(blk // CORES)]
        for x in range(X)
        for core in range(CORES)
    ]
    return lax.all_to_all(value, ("dp", "blk"), 0, 0, tiled=True, axis_index_groups=groups)


def sum_first(parts):
    return as_bf16(jnp.sum(parts.astype(jnp.float32), axis=0))


def pair_terms(left_pair, right):
    terms = as_bf16(dot_nn(left_pair.reshape(-1, left_pair.shape[-1]), right))
    return swap_cores(terms)


def per_device(inputs, upstream, gain, w_query, w_key, w_value, w_out, prefix_len, bound):
    return whole(inputs[0], upstream[0], gain, w_query, w_key, w_value, w_out, prefix_len, bound)


def whole(inputs, grad_out, gain, w_query, w_key, w_value, w_out, prefix_len, bound):
    tok, wide = inputs.shape
    heads_wide = w_query.shape[1]
    my, dp = lax.axis_index("blk"), lax.axis_index("dp")
    count, share = lax.axis_size("blk"), lax.axis_size("dp")
    chips, outer = count // CORES, share // X
    size = wide // (count * share)
    core, x = my % CORES, dp % X
    info = jnp.stack([my, prefix_len[0], bound[0] * BLOCK, core, x]).astype(jnp.int32)
    gain_row = gain.reshape(1, wide)
    filed = shape(X, outer, chips, size, tok)
    copies = shape(chips, tok, HS)
    hidden, k_copies, v_copies = call(
        functools.partial(prepare_kernel, chips),
        (shape(tok, wide), copies, copies),
        (inputs, gain_row, w_key, w_value),
        4 * tok * wide * HS,
    )
    keys = exchange_chips(k_copies)
    values = exchange_chips(v_copies)
    own, ht_own, ht_pair = call(
        project_kernel,
        (shape(2, tok, heads_wide), filed, filed),
        (info, hidden, grad_out, w_query, w_out),
        4 * tok * wide * wide,
        smem=1,
    )
    pair = swap_cores(own)
    mine = run_stats(info, own, pair, keys)
    other = swap_cores(mine)
    attn, dv, probs = run_attend(info, own, pair, mine, other, keys, values)
    attn_other = swap_cores(attn)
    d_value_rows = sum_first(exchange_chips(dv))
    at_own, at_pair, dk, dq_own, dq_pair = run_grads(
        info, own, pair, attn, attn_other, keys, values, probs, filed
    )
    dq_other = swap_cores(dq_pair)
    d_key_rows = sum_first(exchange_chips(dk))
    d_query_rows = as_bf16(dq_own.astype(jnp.float32) + dq_other.astype(jnp.float32))

    out_received = pair_terms(at_pair, grad_out)
    rows = outer * chips * size
    base, *parts = call(
        own_terms_kernel,
        (shape(rows, wide, dtype=jnp.float32), *[shape(rows, wide)] * (X - 1)),
        (at_own, grad_out, out_received),
        2 * X * rows * wide * tok,
    )
    arrived = []
    for step, terms in enumerate(parts, 1):
        arrived.append(send_along_x(terms, step))
    query_received = pair_terms(ht_pair, d_query_rows)
    query_terms = call(
        direct_kernel,
        shape(rows, X * heads_wide),
        (info, ht_own, d_query_rows, query_received),
        2 * X * rows * heads_wide * tok,
        smem=1,
    )
    d_kv_rows = jnp.concatenate([d_key_rows, d_value_rows], axis=1)
    kv_received = pair_terms(ht_pair, d_kv_rows)
    total = wide + X * (heads_wide + 2 * HS)
    terms = call(
        collect_kernel,
        shape(rows, total),
        (info, base, *arrived, query_terms, ht_own, d_kv_rows, kv_received),
        1 << 30,
        smem=1,
    )
    parts = exchange_plane(terms.reshape(outer * chips, size, total))
    copies = call(spread_kernel, shape(share, size, total), (parts,), 1 << 30)
    shared = lax.all_to_all(copies, "dp", 0, 0, tiled=True)
    d_in = call(
        finish_kernel,
        shape(tok, wide),
        (inputs, grad_out, gain_row, d_query_rows, d_kv_rows, w_query, w_key, w_value),
        2 * tok * wide * (wide + 2 * HS),
    )
    held = wide // count

    def my_rows(value):
        return lax.dynamic_slice_in_dim(value, my * held, held, 0)

    slices = [my_rows(w) for w in (w_query, w_key, w_value)]
    slices.append(my_rows(gain).reshape(1, held))
    f32 = functools.partial(shape, dtype=jnp.float32)
    d_query, d_key, d_value, d_out, d_gain = call(
        functools.partial(weights_kernel, X),
        (f32(held, heads_wide), f32(held, HS), f32(held, HS), f32(held, wide), f32(1, held)),
        (shared, *slices),
        1 << 30,
    )
    return (d_in[None], d_query, d_key, d_value, d_out, d_gain.reshape(held))


def solution(mesh):
    placed = (P("dp", "blk", None), P("dp", "blk", None), P(), P(), P(), P(), P(), P("dp"), P("dp"))
    return jax.shard_map(
        per_device,
        mesh=mesh,
        in_specs=placed,
        out_specs=(
            P("dp", "blk", None),
            P("blk", None),
            P("blk", None),
            P("blk", None),
            P("blk", None),
            P("blk"),
        ),
        check_vma=False,
    )
```

time: 481 us -> 185 us (0.38)
  matrix products: 149 us -> 3.92 us
  waiting for transfers between devices: 179 us -> 45.5 us
  other arithmetic: 65.8 us -> 4.44 us
  Pallas kernels: 0 us -> 55.3 us
  local copies, waits for them, and re-layouts: 31.1 us -> 5.7 us
  starting transfers between devices: 12.7 us -> 35.5 us
  between operations: 15.3 us -> 2.1 us
  blocking collectives: 24.3 us -> 31.2 us
    dot_general x46 -> x3, matrix products: 149 us -> 3.92 us  [dot_nn(): return jnp.dot(a, b, preferred_element_type=jnp.float32)]
    unnamed x4 -> x0, waiting for transfers between devices: 85 us -> none
    pallas_call x0 -> x11, Pallas kernels: none -> 55.3 us  [call(): pl.pallas_call(body, out_shape=outs, in_specs=specs, out_specs=out_specs,...]
    all_gather x1 -> x0, waiting for transfers between devices: 48.9 us -> none  [in_one_piece(): lax.all_gather(both, axis, axis=dim, tiled=True)]
    reduce_scatter x1 -> x0, waiting for transfers between devices: 29.1 us -> none  [per_device(): lax.psum_scatter(jnp.concatenate([d_k, d_v], axis=1), 'blk', scatter_dime...]
    reduce_sum x15 -> x2, other arithmetic: 25.9 us -> 1.52 us  [sum_first(): return as_bf16(jnp.sum(parts.astype(jnp.float32), axis=0))]
    all_to_all x3 -> x5, waiting for transfers between devices: 16.3 us -> 39.3 us  [the longest x4 35.2 us: exchange_chips(): lax.all_to_all(value, 'blk', 0, 0, tiled=True, axis_index_groups=groups)]
    all_to_all x3 -> x5, starting transfers between devices: 12.6 us -> 29.1 us  [the longest x4 24.8 us: exchange_chips(): lax.all_to_all(value, 'blk', 0, 0, tiled=True, axis_index_groups=groups)]
  transfers between devices with their start and end apart: 6 -> 15, of which waited for: 6 -> 8; matrix products, arithmetic and copies ran while one was open for 19% -> 7% of each run, Pallas kernels for 0% -> 17%
where the time goes in v3:
time: 185 us; the launch traced here: 184 us
  Pallas kernels  55.3 us (30%)
  waiting for transfers between devices  45.5 us (25%)
  starting transfers between devices  35.5 us (19%)
  blocking collectives  31.2 us (17%)
  local copies, waits for them, and re-layouts  5.7 us (3%)
  other arithmetic  4.44 us (2%)
  matrix products  3.92 us (2%)
  between operations  2.1 us (1%)
    pallas_call x11, Pallas kernels, call(): pl.pallas_call(body, out_shape=outs, in_specs=specs, out_specs=out_specs,...  55.3 us
    all_to_all x4, waiting for transfers between devices, exchange_chips(): lax.all_to_all(value, 'blk', 0, 0, tiled=True, axis_index_groups=groups)  35.2 us
    all_to_all x1, blocking collectives, exchange_plane(): lax.all_to_all(value, ('dp', 'blk'), 0, 0, tiled=True, axis_index_groups=...  31.2 us
    all_to_all x4, starting transfers between devices, exchange_chips(): lax.all_to_all(value, 'blk', 0, 0, tiled=True, axis_index_groups=groups)  24.8 us
    ppermute x3, waiting for transfers between devices, send_along_x(): lax.ppermute(value, 'dp', [(i, i // X * X + (i + step) % X) for i in rang...  6.23 us
    ppermute x3, starting transfers between devices, send_along_x(): lax.ppermute(value, 'dp', [(i, i // X * X + (i + step) % X) for i in rang...  5.63 us
    all_to_all x1, starting transfers between devices, whole(): shared = lax.all_to_all(copies, 'dp', 0, 0, tiled=True)  4.23 us
    all_to_all x1, waiting for transfers between devices, whole(): shared = lax.all_to_all(copies, 'dp', 0, 0, tiled=True)  4.13 us
  transfers between devices with their start and end apart: 15, of which 8 were waited for; matrix products, arithmetic and copies ran while one was open for 7% of the time, Pallas kernels for 17%

profile of v3, /device:TPU:0, one launch (start us, length us, event | category | flops | bytes accessed | tf_op | source)
XLA Modules:
  0.0 183.6 jit_solution(16450555686800059705)
XLA Ops:
  0.6 3.4 %shard_map.136 = (bf16[256,1024]{1,0:T(8,128)(2,1)}, bf16[8,256,256]{2,1,0:T(8,128)(2,1)}, bf16[8,256,256]{2,1,0:T(8,128)(2,1)}) custom-call(bf16[256,1024]{1,0:T(8,128)(2,1)} %bitcast.23, f32[1,1024]{1,0:T(1,128)} %bitcast.29, bf16[1024,256]{1,0:T(8,128)(2,1)} %w_key.3, bf16[1024,256]{1,0:T(8,128)(2,1)} %w_value.3), custom_call_target="tpu_custom_call" | custom-call | flops 268435456 | bytes 1048576 | tf_op jit(solution)/shard_map/pallas_call | solution.py:360
  4.0 7.9 %all-to-all-start = ((bf16[8,256,256]{2,1,0:T(8,128)(2,1)}), bf16[8,256,256]{2,1,0:T(8,128)(2,1)}, u32[]{:S(2)}, u32[]{:S(2)}) async-start(bf16[8,256,256]{2,1,0:T(8,128)(2,1)} %get-tuple-element.31), calls=%async_computation | async-start | bytes 2097152 | tf_op jit(solution)/shard_map/all_to_all | solution.py:456
  13.2 0.6 stack.16.info
  13.9 5.7 %shard_map.137 = (bf16[2,256,1024]{2,1,0:T(8,128)(2,1)}, bf16[4,2,8,8,256]{4,3,2,1,0:T(8,128)(2,1)}, bf16[4,2,8,8,256]{4,3,2,1,0:T(8,128)(2,1)}) custom-call(s32[5]{0:T(128)} %stack.16.info, bf16[256,1024]{1,0:T(8,128)(2,1)} %get-tuple-element.29.hidden, bf16[256,1024]{1,0:T(8,128)(2,1)} %bitcast.19, bf16[1024,1024]{1,0:T(8,128)(2,1)} %w_query.3, ...), custom_call_target="tpu_custom_call" | custom-call | flops 1073741824 | bytes 1048576 | tf_op jit(solution)/shard_map/pallas_call | solution.py:360
  19.5 0.0 collective-permute-start
  19.5 8.4 %all-to-all-done.keys = bf16[8,256,256]{2,1,0:T(8,128)(2,1)} async-done(((bf16[8,256,256]{2,1,0:T(8,128)(2,1)}), bf16[8,256,256]{2,1,0:T(8,128)(2,1)}, u32[]{:S(2)}, u32[]{:S(2)}) %all-to-all-start) | async-done | bytes 1048608 | tf_op jit(solution)/shard_map/all_to_all | solution.py:456
  28.0 4.2 %all-to-all-start.1 = ((bf16[8,256,256]{2,1,0:T(8,128)(2,1)}), bf16[8,256,256]{2,1,0:T(8,128)(2,1)}, u32[]{:S(2)}, u32[]{:S(2)}) async-start(bf16[8,256,256]{2,1,0:T(8,128)(2,1)} %get-tuple-element.32), calls=%async_computation.1 | async-start | bytes 2097152 | tf_op jit(solution)/shard_map/all_to_all | solution.py:456
  32.2 0.0 collective-permute-done.pair
  32.2 3.8 %shard_map.138.mine = f32[2,2,1024]{2,1,0:T(2,128)} custom-call(s32[5]{0:T(128)} %stack.16.info, bf16[2,256,1024]{2,1,0:T(8,128)(2,1)} %get-tuple-element.30.own, bf16[2,256,1024]{2,1,0:T(8,128)(2,1)} %collective-permute-done.pair, bf16[8,256,256]{2,1,0:T(8,128)(2,1)} %all-to-all-done.keys), custom_call_target="tpu_custom_call" | custom-call | flops 2147483648 | bytes 1048576 | tf_op jit(solution)/shard_map/pallas_call | solution.py:360
  36.1 0.0 collective-permute-start.1
  36.1 11.6 %all-to-all-done.1.values = bf16[8,256,256]{2,1,0:T(8,128)(2,1)} async-done(((bf16[8,256,256]{2,1,0:T(8,128)(2,1)}), bf16[8,256,256]{2,1,0:T(8,128)(2,1)}, u32[]{:S(2)}, u32[]{:S(2)}) %all-to-all-start.1) | async-done | bytes 1048608 | tf_op jit(solution)/shard_map/all_to_all | solution.py:456
  47.7 0.0 collective-permute-done.1.other
  47.7 11.4 %shard_map.139 = (bf16[2,1024,256]{2,1,0:T(8,128)(2,1)}, bf16[8,256,256]{2,1,0:T(8,128)(2,1)}, bf16[2048,2048]{1,0:T(8,128)(2,1)}) custom-call(s32[5]{0:T(128)} %stack.16.info, bf16[2,256,1024]{2,1,0:T(8,128)(2,1)} %get-tuple-element.30.own, bf16[2,256,1024]{2,1,0:T(8,128)(2,1)} %collective-permute-done.pair, f32[2,2,1024]{2,1,0:T(2,128)} %shard_map.138.mine, ...), custom_call_target="tpu_custom_call" | custom-call | flops 6442450944 | bytes 1048576 | tf_op jit(solution)/shard_map/pallas_call | solution.py:360
  59.1 0.1 collective-permute-start.2
  59.2 7.3 %all-to-all-start.3 = ((bf16[8,256,256]{2,1,0:T(8,128)(2,1)}), bf16[8,256,256]{2,1,0:T(8,128)(2,1)}, u32[]{:S(2)}, u32[]{:S(2)}) async-start(bf16[8,256,256]{2,1,0:T(8,128)(2,1)} %get-tuple-element.38), calls=%async_computation.3 | async-start | bytes 2097152 | tf_op jit(solution)/shard_map/all_to_all | solution.py:456
  66.5 0.0 collective-permute-done.2.other
  66.5 12.3 %shard_map.140 = (bf16[4,2,8,8,256]{4,3,2,1,0:T(8,128)(2,1)}, bf16[4,2,8,8,256]{4,3,2,1,0:T(8,128)(2,1)}, bf16[8,256,256]{2,1,0:T(8,128)(2,1)}, bf16[256,1024]{1,0:T(8,128)(2,1)}, bf16[256,1024]{1,0:T(8,128)(2,1)}) custom-call(s32[5]{0:T(128)} %stack.16.info, bf16[2,256,1024]{2,1,0:T(8,128)(2,1)} %get-tuple-element.30.own, ...), custom_call_target="tpu_custom_call" | custom-call | flops 6442450944 | bytes 1048576 | tf_op jit(solution)/shard_map/pallas_call | solution.py:360
  78.8 0.0 copy-start.1
  78.8 0.0 copy-start.5
  78.8 0.1 collective-permute-start.3
  78.9 5.0 %all-to-all-done.3 = bf16[8,256,256]{2,1,0:T(8,128)(2,1)} async-done(((bf16[8,256,256]{2,1,0:T(8,128)(2,1)}), bf16[8,256,256]{2,1,0:T(8,128)(2,1)}, u32[]{:S(2)}, u32[]{:S(2)}) %all-to-all-start.3) | async-done | bytes 1048608 | tf_op jit(solution)/shard_map/all_to_all | solution.py:456
  83.9 5.4 %all-to-all-start.2 = ((bf16[8,256,256]{2,1,0:T(8,128)(2,1)}), bf16[8,256,256]{2,1,0:T(8,128)(2,1)S(1)}, u32[]{:S(2)}, u32[]{:S(2)}) async-start(bf16[8,256,256]{2,1,0:T(8,128)(2,1)} %get-tuple-element.37), calls=%async_computation.2 | async-start | bytes 2097152 | tf_op jit(solution)/shard_map/all_to_all | solution.py:456
  89.3 0.0 copy-done.1
  89.3 1.4 convolution_convert_fusion.1
  90.8 0.1 collective-permute-start.4
  90.9 0.0 collective-permute-done.3
  90.9 0.0 copy-done.5
  90.9 1.2 add_convert_fusion.dq.right
  92.1 0.0 copy-start
  92.2 0.8 copy-done
  92.9 0.0 copy-done.4
  92.9 1.4 convolution_convert_fusion
  94.3 0.4 collective-permute-start.8
  94.8 1.4 reduce_sum.25
  96.1 0.0 copy-start.2
  96.2 10.1 %all-to-all-done.2 = bf16[8,256,256]{2,1,0:T(8,128)(2,1)S(1)} async-done(((bf16[8,256,256]{2,1,0:T(8,128)(2,1)}), bf16[8,256,256]{2,1,0:T(8,128)(2,1)S(1)}, u32[]{:S(2)}, u32[]{:S(2)}) %all-to-all-start.2) | async-done | bytes 1048608 | tf_op jit(solution)/shard_map/all_to_all | solution.py:456
  106.3 0.1 reduce_sum.24
  106.4 0.0 copy-done.2
  106.4 0.0 copy-start.3
  106.4 1.1 convolution_convert_fusion.2
  107.5 0.0 copy-done.3
  107.5 0.0 collective-permute-start.9
  107.5 0.0 collective-permute-done.4.received
  107.5 2.8 %shard_map.142 = (f32[128,1024]{1,0:T(8,128)}, bf16[128,1024]{1,0:T(8,128)(2,1)}, bf16[128,1024]{1,0:T(8,128)(2,1)}, bf16[128,1024]{1,0:T(8,128)(2,1)}) custom-call(bf16[4,2,8,8,256]{4,3,2,1,0:T(8,128)(2,1)} %get-tuple-element.39.left, bf16[256,1024]{1,0:T(8,128)(2,1)} %bitcast.20, bf16[512,1024]{1,0:T(8,128)(2,1)} %collective-permute-done.4.received), custom_call_target="tpu_custom_call" | custom-call | flops 268435456 | bytes 1048576 | tf_op jit(solution)/shard_map/pallas_call | solution.py:360
  110.3 0.1 collective-permute-start.5
  110.4 2.9 %collective-permute-start.6 = (bf16[128,1024]{1,0:T(8,128)(2,1)}, bf16[128,1024]{1,0:T(8,128)(2,1)}, u32[]{:S(2)}, u32[]{:S(2)}) collective-permute-start(bf16[128,1024]{1,0:T(8,128)(2,1)} %get-tuple-element.43), channel_id=1, source_target_pairs={{0,32},{16,48},{32,0},{48,16},{64,96},{80,112},{96,64},{112,80},{1... | collective-permute-start | bytes 786440 | tf_op jit(solution)/shard_map/ppermute | solution.py:448
  113.3 2.6 %collective-permute-start.7 = (bf16[128,1024]{1,0:T(8,128)(2,1)}, bf16[128,1024]{1,0:T(8,128)(2,1)}, u32[]{:S(2)}, u32[]{:S(2)}) collective-permute-start(bf16[128,1024]{1,0:T(8,128)(2,1)} %get-tuple-element.44), channel_id=1, source_target_pairs={{0,48},{16,0},{32,16},{48,32},{64,112},{80,64},{96,80},{112,96},{1... | collective-permute-start | bytes 786440 | tf_op jit(solution)/shard_map/ppermute | solution.py:448
  115.9 1.7 pad_maximum_fusion.dkv.right
  117.6 0.0 collective-permute-done.8.received
  117.6 2.9 %shard_map.143.query_terms = bf16[128,4096]{1,0:T(8,128)(2,1)} custom-call(s32[5]{0:T(128)} %stack.16.info, bf16[4,2,8,8,256]{4,3,2,1,0:T(8,128)(2,1)} %get-tuple-element.45.left, bf16[256,1024]{1,0:T(8,128)(2,1)} %copy-done, bf16[512,1024]{1,0:T(8,128)(2,1)} %collective-permute-done.8.received), custom_call_target="tpu_custom_call" | custom-call | flops 268435456 | bytes 1048576 | tf_op jit(solution)/shard_map/pallas_call | solution.py:360
  120.5 0.1 collective-permute-done.5.one
  120.7 5.5 %collective-permute-done.6.two = bf16[128,1024]{1,0:T(8,128)(2,1)} collective-permute-done((bf16[128,1024]{1,0:T(8,128)(2,1)}, bf16[128,1024]{1,0:T(8,128)(2,1)}, u32[]{:S(2)}, u32[]{:S(2)}) %collective-permute-start.6) | collective-permute-done | bytes 262176 | tf_op jit(solution)/shard_map/ppermute | solution.py:448
  126.2 0.6 collective-permute-done.7.three
  126.8 0.0 collective-permute-done.9.received
  126.8 3.7 %shard_map.144 = bf16[128,7168]{1,0:T(8,128)(2,1)} custom-call(s32[5]{0:T(128)} %stack.16.info, f32[128,1024]{1,0:T(8,128)} %get-tuple-element.41.base, bf16[128,1024]{1,0:T(8,128)(2,1)} %collective-permute-done.5.one, bf16[128,1024]{1,0:T(8,128)(2,1)} %collective-permute-done.6.two, bf16[128,1024]{1,0:T(8,128)(2,1)} %collective-permute-done.7.three, ...), custom_call_target="tpu_custom_call" | custom-call | flops 1073741824 | bytes 1048576 | tf_op jit(solution)/shard_map/pallas_call | solution.py:360
  130.5 31.2 %all_to_all.30.parts = bf16[16,8,7168]{2,1,0:T(8,128)(2,1)} all-to-all(bf16[16,8,7168]{2,1,0:T(8,128)(2,1)} %bitcast.22), channel_id=1, replica_groups={{0,2,4,6,8,10,12,14,64,66,68,70,72,74,76,78},{1,3,5,7,9,11,13,15,65,67,..., dimensions={0} | all-to-all | bytes 3670016 | tf_op jit(solution)/shard_map/all_to_all | solution.py:466
  161.6 2.7 %shard_map.145 = bf16[8,8,7168]{2,1,0:T(8,128)(2,1)} custom-call(bf16[16,8,7168]{2,1,0:T(8,128)(2,1)} %all_to_all.30.parts), custom_call_target="tpu_custom_call" | custom-call | flops 1073741824 | bytes 1048576 | tf_op jit(solution)/shard_map/pallas_call | solution.py:360
  164.3 4.2 %all-to-all-start.5 = ((bf16[8,8,7168]{2,1,0:T(8,128)(2,1)}), bf16[8,8,7168]{2,1,0:T(8,128)(2,1)}, u32[]{:S(2)}, u32[]{:S(2)}) async-start(bf16[8,8,7168]{2,1,0:T(8,128)(2,1)} %shard_map.145), calls=%async_computation.5 | async-start | bytes 1835008 | tf_op jit(solution)/shard_map/all_to_all | solution.py:553
  168.6 1.3 dynamic-slice_bitcast_fusion.gain
  169.9 1.4 constant_dynamic-slice_fusion
  171.3 1.6 constant_dynamic-slice_fusion.2.w_query
  172.8 4.4 %shard_map.141 = bf16[256,1024]{1,0:T(8,128)(2,1)} custom-call(bf16[256,1024]{1,0:T(8,128)(2,1)} %bitcast.24, bf16[256,1024]{1,0:T(8,128)(2,1)} %bitcast.21, f32[1,1024]{1,0:T(1,128)} %bitcast.30, bf16[256,1024]{1,0:T(8,128)(2,1)} %copy-done, bf16[256,512]{1,0:T(8,128)(2,1)} %pad_maximum_fusion.dkv.right, bf16[1024,1024]{1,0:T(8,128)(2,1)} %w_query.3, ...), custom_call_target="tpu_custom_call" | custom-call | flops 805306368 | bytes 1048576 | tf_op jit(solution)/shard_map/pallas_call | solution.py:360
  177.3 4.1 %all-to-all-done.5.shared = bf16[8,8,7168]{2,1,0:T(8,128)(2,1)} async-done(((bf16[8,8,7168]{2,1,0:T(8,128)(2,1)}), bf16[8,8,7168]{2,1,0:T(8,128)(2,1)}, u32[]{:S(2)}, u32[]{:S(2)}) %all-to-all-start.5) | async-done | bytes 917536 | tf_op jit(solution)/shard_map/all_to_all | solution.py:553
  181.4 2.2 %shard_map.146 = (f32[64,1024]{1,0:T(8,128)}, f32[64,256]{1,0:T(8,128)}, f32[64,256]{1,0:T(8,128)}, f32[64,1024]{1,0:T(8,128)}, f32[1,64]{1,0:T(1,128)}) custom-call(bf16[8,8,7168]{2,1,0:T(8,128)(2,1)} %all-to-all-done.5.shared, bf16[64,1024]{1,0:T(8,128)(2,1)} %constant_dynamic-slice_fusion.2.w_query, bf16[64,256]{1,0:T(8,128)(2,1)} %get-tuple-element.53.w_key, ...), custom_call_target="tpu_custom_call" | custom-call | flops 1073741824 | bytes 1048576 | tf_op jit(solution)/shard_map/pallas_call | solution.py:360
  (1 shorter events, 0.0 us)
Async XLA Ops:
  4.0 23.9 %all-to-all-start = ((bf16[8,256,256]{2,1,0:T(8,128)(2,1)}), bf16[8,256,256]{2,1,0:T(8,128)(2,1)}, u32[]{:S(2)}, u32[]{:S(2)}) async-start(bf16[8,256,256]{2,1,0:T(8,128)(2,1)} %get-tuple-element.31), calls=%async_computation | async-start | bytes 2097152 | tf_op jit(solution)/shard_map/all_to_all | solution.py:456
  19.5 12.7 %collective-permute-start = (bf16[2,256,1024]{2,1,0:T(8,128)(2,1)}, bf16[2,256,1024]{2,1,0:T(8,128)(2,1)}, u32[]{:S(2)}, u32[]{:S(2)}) collective-permute-start(bf16[2,256,1024]{2,1,0:T(8,128)(2,1)} %get-tuple-element.30.own), channel_id=1, source_target_pairs={{0,1},{1,0},{2,3},{3,2},{4,5},{5,4},{6,7},{7,6},{8,9},{9,8},{10,11... | collective-permute-start | bytes 3145736 | tf_op jit(solution)/shard_map/ppermute | solution.py:443
  28.0 19.8 %all-to-all-start.1 = ((bf16[8,256,256]{2,1,0:T(8,128)(2,1)}), bf16[8,256,256]{2,1,0:T(8,128)(2,1)}, u32[]{:S(2)}, u32[]{:S(2)}) async-start(bf16[8,256,256]{2,1,0:T(8,128)(2,1)} %get-tuple-element.32), calls=%async_computation.1 | async-start | bytes 2097152 | tf_op jit(solution)/shard_map/all_to_all | solution.py:456
  36.1 11.7 %collective-permute-start.1 = (f32[2,2,1024]{2,1,0:T(2,128)}, f32[2,2,1024]{2,1,0:T(2,128)}, u32[]{:S(2)}, u32[]{:S(2)}) collective-permute-start(f32[2,2,1024]{2,1,0:T(2,128)} %shard_map.138.mine), channel_id=1, source_target_pairs={{0,1},{1,0},{2,3},{3,2},{4,5},{5,4},{6,7},{7,6},{8,9},{9,8},{10,11... | collective-permute-start | bytes 49160 | tf_op jit(solution)/shard_map/ppermute | solution.py:443
  59.1 7.4 %collective-permute-start.2 = (bf16[2,1024,256]{2,1,0:T(8,128)(2,1)}, bf16[2,1024,256]{2,1,0:T(8,128)(2,1)}, u32[]{:S(2)}, u32[]{:S(2)}) collective-permute-start(bf16[2,1024,256]{2,1,0:T(8,128)(2,1)} %get-tuple-element.33.mine), channel_id=1, source_target_pairs={{0,1},{1,0},{2,3},{3,2},{4,5},{5,4},{6,7},{7,6},{8,9},{9,8},{10,11... | collective-permute-start | bytes 3145736 | tf_op jit(solution)/shard_map/ppermute | solution.py:443
  59.2 24.7 %all-to-all-start.3 = ((bf16[8,256,256]{2,1,0:T(8,128)(2,1)}), bf16[8,256,256]{2,1,0:T(8,128)(2,1)}, u32[]{:S(2)}, u32[]{:S(2)}) async-start(bf16[8,256,256]{2,1,0:T(8,128)(2,1)} %get-tuple-element.38), calls=%async_computation.3 | async-start | bytes 2097152 | tf_op jit(solution)/shard_map/all_to_all | solution.py:456
  78.8 10.5 %copy-start.1 = (bf16[1,256,1024]{2,1,0:T(8,128)(2,1)S(1)}, bf16[1,256,1024]{2,1,0:T(8,128)(2,1)}, u32[]{:S(2)}) copy-start(bf16[1,256,1024]{2,1,0:T(8,128)(2,1)} %param.10) | copy-start | bytes 1572868
  78.8 12.1 %copy-start.5 = (bf16[256,1024]{1,0:T(8,128)(2,1)S(1)}, bf16[256,1024]{1,0:T(8,128)(2,1)}, u32[]{:S(2)}) copy-start(bf16[256,1024]{1,0:T(8,128)(2,1)} %get-tuple-element.35) | copy-start | bytes 1572868
  78.8 12.1 %collective-permute-start.3 = (bf16[256,1024]{1,0:T(8,128)(2,1)}, bf16[256,1024]{1,0:T(8,128)(2,1)}, u32[]{:S(2)}, u32[]{:S(2)}) collective-permute-start(bf16[256,1024]{1,0:T(8,128)(2,1)} %get-tuple-element.36), channel_id=1, source_target_pairs={{0,1},{1,0},{2,3},{3,2},{4,5},{5,4},{6,7},{7,6},{8,9},{9,8},{10,11... | collective-permute-start | bytes 1572872 | tf_op jit(solution)/shard_map/ppermute | solution.py:443
  83.9 22.3 %all-to-all-start.2 = ((bf16[8,256,256]{2,1,0:T(8,128)(2,1)}), bf16[8,256,256]{2,1,0:T(8,128)(2,1)S(1)}, u32[]{:S(2)}, u32[]{:S(2)}) async-start(bf16[8,256,256]{2,1,0:T(8,128)(2,1)} %get-tuple-element.37), calls=%async_computation.2 | async-start | bytes 2097152 | tf_op jit(solution)/shard_map/all_to_all | solution.py:456
  89.3 3.6 %copy-start.4 = (bf16[4,2,8,8,256]{4,3,2,1,0:T(8,128)(2,1)S(1)}, bf16[4,2,8,8,256]{4,3,2,1,0:T(8,128)(2,1)}, u32[]{:S(2)}) copy-start(bf16[4,2,8,8,256]{4,3,2,1,0:T(8,128)(2,1)} %get-tuple-element.46) | copy-start | bytes 786436
  90.8 16.8 %collective-permute-start.4 = (bf16[512,1024]{1,0:T(8,128)(2,1)S(1)}, bf16[512,1024]{1,0:T(8,128)(2,1)}, u32[]{:S(2)}, u32[]{:S(2)}) collective-permute-start(bf16[512,1024]{1,0:T(8,128)(2,1)S(1)} %convolution_convert_fusion.1), channel_id=1, source_target_pairs={{0,1},{1,0},{2,3},{3,2},{4,5},{5,4},{6,7},{7,6},{8,9},{9,8},{10,11... | collective-permute-start | bytes 3145736 | tf_op jit(solution)/shard_map/ppermute | solution.py:443
  92.1 0.8 copy-start
  94.3 23.3 %collective-permute-start.8 = (bf16[512,1024]{1,0:T(8,128)(2,1)}, bf16[512,1024]{1,0:T(8,128)(2,1)}, u32[]{:S(2)}, u32[]{:S(2)}) collective-permute-start(bf16[512,1024]{1,0:T(8,128)(2,1)} %convolution_convert_fusion), channel_id=1, source_target_pairs={{0,1},{1,0},{2,3},{3,2},{4,5},{5,4},{6,7},{7,6},{8,9},{9,8},{10,11... | collective-permute-start | bytes 3145736 | tf_op jit(solution)/shard_map/ppermute | solution.py:443
  96.1 10.3 %copy-start.2 = (bf16[256,256]{1,0:T(8,128)(2,1)}, bf16[256,256]{1,0:T(8,128)(2,1)S(1)}, u32[]{:S(2)}) copy-start(bf16[256,256]{1,0:T(8,128)(2,1)S(1)} %reduce_sum.25) | copy-start | bytes 393220
  106.4 1.1 copy-start.3
  107.5 19.2 %collective-permute-start.9 = (bf16[512,512]{1,0:T(8,128)(2,1)}, bf16[512,512]{1,0:T(8,128)(2,1)}, u32[]{:S(2)}, u32[]{:S(2)}) collective-permute-start(bf16[512,512]{1,0:T(8,128)(2,1)} %convolution_convert_fusion.2), channel_id=1, source_target_pairs={{0,1},{1,0},{2,3},{3,2},{4,5},{5,4},{6,7},{7,6},{8,9},{9,8},{10,11... | collective-permute-start | bytes 1572872 | tf_op jit(solution)/shard_map/ppermute | solution.py:443
  110.3 10.4 %collective-permute-start.5 = (bf16[128,1024]{1,0:T(8,128)(2,1)}, bf16[128,1024]{1,0:T(8,128)(2,1)}, u32[]{:S(2)}, u32[]{:S(2)}) collective-permute-start(bf16[128,1024]{1,0:T(8,128)(2,1)} %get-tuple-element.42), channel_id=1, source_target_pairs={{0,16},{16,32},{32,48},{48,0},{64,80},{80,96},{96,112},{112,64},{1... | collective-permute-start | bytes 786440 | tf_op jit(solution)/shard_map/ppermute | solution.py:448
  110.4 15.8 %collective-permute-start.6 = (bf16[128,1024]{1,0:T(8,128)(2,1)}, bf16[128,1024]{1,0:T(8,128)(2,1)}, u32[]{:S(2)}, u32[]{:S(2)}) collective-permute-start(bf16[128,1024]{1,0:T(8,128)(2,1)} %get-tuple-element.43), channel_id=1, source_target_pairs={{0,32},{16,48},{32,0},{48,16},{64,96},{80,112},{96,64},{112,80},{1... | collective-permute-start | bytes 786440 | tf_op jit(solution)/shard_map/ppermute | solution.py:448
  113.3 13.5 %collective-permute-start.7 = (bf16[128,1024]{1,0:T(8,128)(2,1)}, bf16[128,1024]{1,0:T(8,128)(2,1)}, u32[]{:S(2)}, u32[]{:S(2)}) collective-permute-start(bf16[128,1024]{1,0:T(8,128)(2,1)} %get-tuple-element.44), channel_id=1, source_target_pairs={{0,48},{16,0},{32,16},{48,32},{64,112},{80,64},{96,80},{112,96},{1... | collective-permute-start | bytes 786440 | tf_op jit(solution)/shard_map/ppermute | solution.py:448
  164.3 17.1 %all-to-all-start.5 = ((bf16[8,8,7168]{2,1,0:T(8,128)(2,1)}), bf16[8,8,7168]{2,1,0:T(8,128)(2,1)}, u32[]{:S(2)}, u32[]{:S(2)}) async-start(bf16[8,8,7168]{2,1,0:T(8,128)(2,1)} %shard_map.145), calls=%async_computation.5 | async-start | bytes 1835008 | tf_op jit(solution)/shard_map/all_to_all | solution.py:553

commit v4 on v3

--- a/solution.py
+++ b/solution.py
@@ -107,12 +107,18 @@
         out[half, 1:2, :] = total[:, pl.ds(half * wide, wide)]
 
 
-def attend_kernel(
-    heads, seq, info, own, pair, mine, other, keys, values,
-    attn, dv, probs_out,
-    values_t, da_rows, probs, lse, out_sems,
-):
+def take_values(blocks, values, sems):
+    copies = [pltpu.make_async_copy(b, values.at[n], sems.at[n]) for n, b in enumerate(blocks)]
+    for c in copies:
+        c.start()
+    return copies
+
+
+def attend_kernel(heads, seq, info, own, pair, mine, other, keys, *refs):
     chips, tok, _ = keys.shape
+    blocks = refs[:chips]
+    attn, dv, probs_out, values, values_t, da_rows, probs, lse, out_sems, in_sems = refs[chips:]
+    copies = take_values(blocks, values, in_sems)
     wide = heads * HS
     for half, qd in enumerate((own, pair)):
         for h in range(heads):
@@ -122,8 +128,10 @@
         total = mine[half, 1:2, :] * jnp.exp2(top_a - top)
         total = total + other[1 - half, 1:2, :] * jnp.exp2(top_b - top)
         lse[:, pl.ds(half * wide, wide)] = top + jnp.log(total) * LOG2E
+    for c in copies:
+        c.wait()
     for chip in range(chips):
-        values_t[:, pl.ds(chip * tok, tok)] = values[chip].T
+        values_t[:, pl.ds(chip * tok, tok)] = values[chip ^ (info[0] // 2)].T
 
     def rows_of(chip):
         return pl.ds(pl.multiple_of(chip * tok, tok), tok)
@@ -173,12 +181,12 @@
         pl.when(core == same)(functools.partial(put, same))
 
 
-def grads_kernel(
-    heads, seq, info, own, pair, mine, other, keys, values, probs_in,
-    at_own, at_pair, dk, dq_own, dq_pair,
-    keys_t, q_rows, probs, dscores, delta, in_sems,
-):
+def grads_kernel(heads, seq, info, own, pair, mine, other, keys, *refs):
     chips, tok, _ = keys.shape
+    blocks, probs_in = refs[:chips], refs[chips]
+    at_own, at_pair, dk, dq_own, dq_pair = refs[chips + 1 : chips + 6]
+    values, keys_t, q_rows, probs, dscores, delta, in_sems, v_sems = refs[chips + 6 :]
+    copies = take_values(blocks, values, v_sems)
 
     def rows_of(chip):
         return pl.ds(pl.multiple_of(chip * tok, tok), tok)
@@ -206,6 +214,8 @@
                     put_rows(info, a[n * block : (n + 1) * block], h * per_head + n, at_own, at_pair)
     for chip in range(chips):
         keys_t[:, pl.ds(chip * tok, tok)] = keys[chip].T
+    for c in copies:
+        c.wait()
 
     def step(chip):
         rows = rows_of(chip)
@@ -217,7 +227,7 @@
             def _(half=half, qd=qd):
                 for h in range(heads):
                     at = part(half, h, heads)
-                    dp = dot_nt(values[chip], qd[1, :, head(h)])
+                    dp = dot_nt(values[chip ^ (info[0] // 2)], qd[1, :, head(h)])
                     p = probs[rows, at].astype(jnp.float32)
                     dscores[rows, at] = (p * (dp - delta[:, at])).astype(jnp.bfloat16)
 
@@ -235,15 +245,15 @@
             dq[:, head(h)] = d.T.astype(jnp.bfloat16)
 
 
-def prepare_kernel(chips, x, gain, w_key, w_value, hidden, k_copies, v_copies):
+def prepare_kernel(chips, x, gain, w_key, w_value, hidden, k_copies, values):
     xf = x[...].astype(jnp.float32)
     inv = lax.rsqrt(jnp.mean(xf * xf, axis=-1, keepdims=True) + EPS)
     h = (xf * inv * gain[...]).astype(jnp.bfloat16)
     hidden[...] = h
-    for weight, out in ((w_key, k_copies), (w_value, v_copies)):
-        rows = dot_nn(h, weight[...]).astype(jnp.bfloat16)
-        for chip in range(chips):
-            out[chip] = rows
+    rows = dot_nn(h, w_key[...]).astype(jnp.bfloat16)
+    for chip in range(chips):
+        k_copies[chip] = rows
+    values[...] = dot_nn(h, w_value[...]).astype(jnp.bfloat16)
 
 
 def project_kernel(info, hidden, grad_out, w_query, w_out, both, ht_own, ht_pair):
@@ -280,23 +290,33 @@
     direct_terms(info, left, right, received, out, 0)
 
 
-def collect_kernel(info, base, one, two, three, query_terms, left, right, received, out):
+def collect_kernel(info, base, one, two, three, left, right, received, out):
     total = base[...]
     for arrived in (one, two, three):
         total = total + arrived[...].astype(jnp.float32)
     wide = total.shape[1]
     out[:, pl.ds(0, wide)] = total.astype(out.dtype)
-    out[:, pl.ds(wide, query_terms.shape[1])] = query_terms[...]
-    direct_terms(info, left, right, received, out, wide + query_terms.shape[1])
-
-
-def spread_kernel(parts, out):
+    direct_terms(info, left, right, received, out, wide)
+
+
+def added_parts(parts):
     total = parts[0].astype(jnp.float32)
     for n in range(1, parts.shape[0]):
         total = total + parts[n].astype(jnp.float32)
-    total = total.astype(out.dtype)
+    return total.astype(jnp.bfloat16)
+
+
+def total_kernel(parts, out):
+    out[...] = added_parts(parts)
+
+
+def spread_kernel(first, parts, query, out):
+    total = added_parts(parts)
+    last = first + query.shape[1]
     for n in range(out.shape[0]):
-        out[n] = total
+        out[n, :, pl.ds(0, first)] = total[:, :first]
+        out[n, :, pl.ds(first, query.shape[1])] = query[...]
+        out[n, :, pl.ds(last, total.shape[1] - first)] = total[:, first:]
 
 
 def weights_kernel(steps, shared, w_query, w_key, w_value, gain, d_query, d_key, d_value, d_out, d_gain):
@@ -394,15 +414,18 @@
     return call(
         functools.partial(attend_kernel, heads, seq),
         (shape(2, wide, tok), shape(chips, tok, HS), shape(chips * tok, 2 * wide)),
-        (info, own, pair, mine, other, keys, values),
+        (info, own, pair, mine, other, keys, *values),
         6 * seq * wide * HS,
         smem=1,
+        in_any=range(6, 6 + chips),
         out_any=(2,),
         scratch=(
+            scratch(chips, tok, HS),
             scratch(HS, chips * tok),
             scratch(2 * wide, HS),
             scratch(chips * tok, 2 * wide),
             scratch(1, 2 * wide, dtype=jnp.float32),
+            pltpu.SemaphoreType.DMA((chips,)),
             pltpu.SemaphoreType.DMA((chips,)),
         ),
     )
@@ -415,16 +438,18 @@
     return call(
         functools.partial(grads_kernel, heads, seq),
         (filed, filed, shape(chips, tok, HS), shape(tok, wide), shape(tok, wide)),
-        (info, own, pair, mine, other, keys, values, probs),
+        (info, own, pair, mine, other, keys, *values, probs),
         6 * seq * wide * HS,
         smem=1,
-        in_any=(7,),
+        in_any=range(6, 7 + chips),
         scratch=(
+            scratch(chips, tok, HS),
             scratch(HS, chips * tok),
             scratch(2 * wide, HS),
             scratch(chips * tok, 2 * wide),
             scratch(chips * tok, 2 * wide),
             scratch(1, 2 * wide, dtype=jnp.float32),
+            pltpu.SemaphoreType.DMA((chips,)),
             pltpu.SemaphoreType.DMA((chips,)),
         ),
     )
@@ -463,6 +488,7 @@
         for x in range(X)
         for core in range(CORES)
     ]
+    value = value.reshape(dp // X * (blk // CORES), -1, value.shape[1])
     return lax.all_to_all(value, ("dp", "blk"), 0, 0, tiled=True, axis_index_groups=groups)
 
 
@@ -491,14 +517,17 @@
     gain_row = gain.reshape(1, wide)
     filed = shape(X, outer, chips, size, tok)
     copies = shape(chips, tok, HS)
-    hidden, k_copies, v_copies = call(
+    hidden, k_copies, my_values = call(
         functools.partial(prepare_kernel, chips),
-        (shape(tok, wide), copies, copies),
+        (shape(tok, wide), copies, shape(tok, HS)),
         (inputs, gain_row, w_key, w_value),
         4 * tok * wide * HS,
     )
     keys = exchange_chips(k_copies)
-    values = exchange_chips(v_copies)
+    values = [my_values]
+    for other in range(1, chips):
+        steps = [(i, i ^ (other * CORES)) for i in range(count)]
+        values.append(lax.ppermute(my_values, "blk", steps))
     own, ht_own, ht_pair = call(
         project_kernel,
         (shape(2, tok, heads_wide), filed, filed),
@@ -543,13 +572,20 @@
     total = wide + X * (heads_wide + 2 * HS)
     terms = call(
         collect_kernel,
-        shape(rows, total),
-        (info, base, *arrived, query_terms, ht_own, d_kv_rows, kv_received),
+        shape(rows, wide + 2 * HS * X),
+        (info, base, *arrived, ht_own, d_kv_rows, kv_received),
         1 << 30,
         smem=1,
     )
-    parts = exchange_plane(terms.reshape(outer * chips, size, total))
-    copies = call(spread_kernel, shape(share, size, total), (parts,), 1 << 30)
+    query_parts = exchange_plane(query_terms)
+    query_total = call(total_kernel, shape(size, X * heads_wide), (query_parts,), 1 << 30)
+    parts = exchange_plane(terms)
+    copies = call(
+        functools.partial(spread_kernel, wide),
+        shape(share, size, total),
+        (parts, query_total),
+        1 << 30,
+    )
     shared = lax.all_to_all(copies, "dp", 0, 0, tiled=True)
     d_in = call(
         finish_kernel,

time: 185 us -> 212 us (1.15)
  blocking collectives: 31.2 us -> 0 us
  waiting for transfers between devices: 45.5 us -> 75.1 us
  starting transfers between devices: 35.5 us -> 65 us
    all_to_all x1 -> x0, blocking collectives: 31.2 us -> none  [exchange_plane(): lax.all_to_all(value, ('dp', 'blk'), 0, 0, tiled=True, axis_index_groups=...]
    ppermute x0 -> x7, waiting for transfers between devices: none -> 19.3 us  [whole(): values.append(lax.ppermute(my_values, 'blk', steps))]
    all_to_all x0 -> x2, starting transfers between devices: none -> 14.8 us  [exchange_plane(): lax.all_to_all(value, ('dp', 'blk'), 0, 0, tiled=True, axis_index_groups=...]
    ppermute x0 -> x7, starting transfers between devices: none -> 14.2 us  [whole(): values.append(lax.ppermute(my_values, 'blk', steps))]
    all_to_all x0 -> x2, waiting for transfers between devices: none -> 11.9 us  [exchange_plane(): lax.all_to_all(value, ('dp', 'blk'), 0, 0, tiled=True, axis_index_groups=...]
    all_to_all x4 -> x3, waiting for transfers between devices: 35.2 us -> 26.4 us  [exchange_chips(): lax.all_to_all(value, 'blk', 0, 0, tiled=True, axis_index_groups=groups)]
    ppermute x3, waiting for transfers between devices: 6.23 us -> 10.4 us  [send_along_x(): lax.ppermute(value, 'dp', [(i, i // X * X + (i + step) % X) for i in rang...]
    ppermute x7, waiting for transfers between devices: 0.02 us -> 3.12 us  [swap_cores(): return lax.ppermute(value, 'blk', [(i, i ^ 1) for i in range(count)])]
  transfers between devices with their start and end apart: 15 -> 23, of which waited for: 8 -> 10; matrix products, arithmetic and copies ran while one was open for 7% -> 5% of each run, Pallas kernels for 17% -> 9%
where the time goes in v4:
time: 212 us; the launch traced here: 211 us
  waiting for transfers between devices  75.1 us (35%)
  starting transfers between devices  65 us (31%)
  Pallas kernels  56.7 us (27%)
  local copies, waits for them, and re-layouts  5.78 us (3%)
  other arithmetic  3.45 us (2%)
  matrix products  3.02 us (1%)
  between operations  2.18 us (1%)
    pallas_call x12, Pallas kernels, call(): pl.pallas_call(body, out_shape=outs, in_specs=specs, out_specs=out_specs,...  56.7 us
    all_to_all x3, waiting for transfers between devices, exchange_chips(): lax.all_to_all(value, 'blk', 0, 0, tiled=True, axis_index_groups=groups)  26.4 us
    all_to_all x3, starting transfers between devices, exchange_chips(): lax.all_to_all(value, 'blk', 0, 0, tiled=True, axis_index_groups=groups)  26.2 us
    ppermute x7, waiting for transfers between devices, whole(): values.append(lax.ppermute(my_values, 'blk', steps))  19.3 us
    all_to_all x2, starting transfers between devices, exchange_plane(): lax.all_to_all(value, ('dp', 'blk'), 0, 0, tiled=True, axis_index_groups=...  14.8 us
    ppermute x7, starting transfers between devices, whole(): values.append(lax.ppermute(my_values, 'blk', steps))  14.2 us
    all_to_all x2, waiting for transfers between devices, exchange_plane(): lax.all_to_all(value, ('dp', 'blk'), 0, 0, tiled=True, axis_index_groups=...  11.9 us
    ppermute x3, waiting for transfers between devices, send_along_x(): lax.ppermute(value, 'dp', [(i, i // X * X + (i + step) % X) for i in rang...  10.4 us
  transfers between devices with their start and end apart: 23, of which 10 were waited for; matrix products, arithmetic and copies ran while one was open for 5% of the time, Pallas kernels for 9%

profile of v4, /device:TPU:0, one launch (start us, length us, event | category | flops | bytes accessed | tf_op | source)
XLA Modules:
  0.0 211.2 jit_solution(4468584369485937025)
XLA Ops:
  1.9 3.0 %shard_map.136 = (bf16[256,1024]{1,0:T(8,128)(2,1)}, bf16[8,256,256]{2,1,0:T(8,128)(2,1)}, bf16[256,256]{1,0:T(8,128)(2,1)}) custom-call(bf16[256,1024]{1,0:T(8,128)(2,1)} %bitcast.24, f32[1,1024]{1,0:T(1,128)} %bitcast.31, bf16[1024,256]{1,0:T(8,128)(2,1)} %w_key.3, bf16[1024,256]{1,0:T(8,128)(2,1)} %w_value.3), custom_call_target="tpu_custom_call" | custom-call | flops 268435456 | bytes 1048576 | tf_op jit(solution)/shard_map/pallas_call | solution.py:380
  4.9 0.6 stack.16.info
  5.5 5.7 %shard_map.137 = (bf16[2,256,1024]{2,1,0:T(8,128)(2,1)}, bf16[4,2,8,8,256]{4,3,2,1,0:T(8,128)(2,1)}, bf16[4,2,8,8,256]{4,3,2,1,0:T(8,128)(2,1)}) custom-call(s32[5]{0:T(128)} %stack.16.info, bf16[256,1024]{1,0:T(8,128)(2,1)} %get-tuple-element.29.hidden, bf16[256,1024]{1,0:T(8,128)(2,1)} %bitcast.20, bf16[1024,1024]{1,0:T(8,128)(2,1)} %w_query.3, ...), custom_call_target="tpu_custom_call" | custom-call | flops 1073741824 | bytes 1048576 | tf_op jit(solution)/shard_map/pallas_call | solution.py:380
  11.2 7.9 %all-to-all-start = ((bf16[8,256,256]{2,1,0:T(8,128)(2,1)}), bf16[8,256,256]{2,1,0:T(8,128)(2,1)}, u32[]{:S(2)}, u32[]{:S(2)}) async-start(bf16[8,256,256]{2,1,0:T(8,128)(2,1)} %get-tuple-element.31), calls=%async_computation | async-start | bytes 2097152 | tf_op jit(solution)/shard_map/all_to_all | solution.py:481
  19.1 5.6 %collective-permute-start.8 = (bf16[256,256]{1,0:T(8,128)(2,1)}, bf16[256,256]{1,0:T(8,128)(2,1)}, u32[]{:S(2)}, u32[]{:S(2)}) collective-permute-start(bf16[256,256]{1,0:T(8,128)(2,1)} %get-tuple-element.32.refs_0_), channel_id=1, source_target_pairs={{0,14},{1,15},{2,12},{3,13},{4,10},{5,11},{6,8},{7,9},{8,6},{9,7},... | collective-permute-start | bytes 393224 | tf_op jit(solution)/shard_map/ppermute | solution.py:530
  24.8 0.6 collective-permute-start.7
  25.3 1.8 collective-permute-start.6
  27.1 1.2 collective-permute-start.5
  28.3 17.9 %collective-permute-done.8.refs_7_ = bf16[256,256]{1,0:T(8,128)(2,1)} collective-permute-done((bf16[256,256]{1,0:T(8,128)(2,1)}, bf16[256,256]{1,0:T(8,128)(2,1)}, u32[]{:S(2)}, u32[]{:S(2)}) %collective-permute-start.8) | collective-permute-done | bytes 131104 | tf_op jit(solution)/shard_map/ppermute | solution.py:530
  46.3 1.4 collective-permute-start.4
  47.7 0.0 collective-permute-done.7.refs_6_
  47.7 0.6 collective-permute-start.3
  48.3 3.0 %collective-permute-start.2 = (bf16[256,256]{1,0:T(8,128)(2,1)}, bf16[256,256]{1,0:T(8,128)(2,1)}, u32[]{:S(2)}, u32[]{:S(2)}) collective-permute-start(bf16[256,256]{1,0:T(8,128)(2,1)} %get-tuple-element.32.refs_0_), channel_id=1, source_target_pairs={{0,2},{1,3},{2,0},{3,1},{4,6},{5,7},{6,4},{7,5},{8,10},{9,11},{10,... | collective-permute-start | bytes 393224 | tf_op jit(solution)/shard_map/ppermute | solution.py:530
  51.3 0.0 all-to-all-done.keys
  51.3 3.8 %shard_map.138.mine = f32[2,2,1024]{2,1,0:T(2,128)} custom-call(s32[5]{0:T(128)} %stack.16.info, bf16[2,256,1024]{2,1,0:T(8,128)(2,1)} %get-tuple-element.30.own, bf16[2,256,1024]{2,1,0:T(8,128)(2,1)} %collective-permute-done.pair, bf16[8,256,256]{2,1,0:T(8,128)(2,1)} %all-to-all-done.keys), custom_call_target="tpu_custom_call" | custom-call | flops 2147483648 | bytes 1048576 | tf_op jit(solution)/shard_map/pallas_call | solution.py:380
  55.1 0.0 collective-permute-done.4.refs_3_
  55.1 0.0 collective-permute-done.3.refs_2_
  55.1 1.4 collective-permute-done.2.refs_1_
  56.5 0.1 collective-permute-done.1.other
  56.6 12.4 %shard_map.139 = (bf16[2,1024,256]{2,1,0:T(8,128)(2,1)}, bf16[8,256,256]{2,1,0:T(8,128)(2,1)}, bf16[2048,2048]{1,0:T(8,128)(2,1)}) custom-call(s32[5]{0:T(128)} %stack.16.info, bf16[2,256,1024]{2,1,0:T(8,128)(2,1)} %get-tuple-element.30.own, bf16[2,256,1024]{2,1,0:T(8,128)(2,1)} %collective-permute-done.pair, f32[2,2,1024]{2,1,0:T(2,128)} %shard_map.138.mine, ...), custom_call_target="tpu_custom_call" | custom-call | flops 6442450944 | bytes 1048576 | tf_op jit(solution)/shard_map/pallas_call | solution.py:380
  69.0 0.1 collective-permute-start.9
  69.1 3.0 %collective-permute-done.9.other = bf16[2,1024,256]{2,1,0:T(8,128)(2,1)} collective-permute-done((bf16[2,1024,256]{2,1,0:T(8,128)(2,1)}, bf16[2,1024,256]{2,1,0:T(8,128)(2,1)}, u32[]{:S(2)}, u32[]{:S(2)}) %collective-permute-start.9) | collective-permute-done | bytes 1048608 | tf_op jit(solution)/shard_map/ppermute | solution.py:468
  72.1 12.4 %shard_map.140 = (bf16[4,2,8,8,256]{4,3,2,1,0:T(8,128)(2,1)}, bf16[4,2,8,8,256]{4,3,2,1,0:T(8,128)(2,1)}, bf16[8,256,256]{2,1,0:T(8,128)(2,1)}, bf16[256,1024]{1,0:T(8,128)(2,1)}, bf16[256,1024]{1,0:T(8,128)(2,1)}) custom-call(s32[5]{0:T(128)} %stack.16.info, bf16[2,256,1024]{2,1,0:T(8,128)(2,1)} %get-tuple-element.30.own, ...), custom_call_target="tpu_custom_call" | custom-call | flops 6442450944 | bytes 1048576 | tf_op jit(solution)/shard_map/pallas_call | solution.py:380
  84.5 0.0 copy-start.8
  84.5 0.0 copy-start.6
  84.5 0.1 collective-permute-start.10
  84.6 14.1 %all-to-all-start.2 = ((bf16[8,256,256]{2,1,0:T(8,128)(2,1)}), bf16[8,256,256]{2,1,0:T(8,128)(2,1)S(1)}, u32[]{:S(2)}, u32[]{:S(2)}) async-start(bf16[8,256,256]{2,1,0:T(8,128)(2,1)} %get-tuple-element.38), calls=%async_computation.2 | async-start | bytes 2097152 | tf_op jit(solution)/shard_map/all_to_all | solution.py:481
  98.7 0.0 collective-permute-done.10
  98.7 0.2 add_convert_fusion.dq.right
  98.9 0.0 copy-start.1
  98.9 0.8 copy-done
  99.7 0.4 convolution_convert_fusion
  100.1 0.2 collective-permute-start.16
  100.3 15.3 %all-to-all-done.2 = bf16[8,256,256]{2,1,0:T(8,128)(2,1)S(1)} async-done(((bf16[8,256,256]{2,1,0:T(8,128)(2,1)}), bf16[8,256,256]{2,1,0:T(8,128)(2,1)S(1)}, u32[]{:S(2)}, u32[]{:S(2)}) %all-to-all-start.2) | async-done | bytes 1048608 | tf_op jit(solution)/shard_map/all_to_all | solution.py:481
  115.6 4.2 %all-to-all-start.1 = ((bf16[8,256,256]{2,1,0:T(8,128)(2,1)}), bf16[8,256,256]{2,1,0:T(8,128)(2,1)}, u32[]{:S(2)}, u32[]{:S(2)}) async-start(bf16[8,256,256]{2,1,0:T(8,128)(2,1)} %get-tuple-element.37), calls=%async_computation.1 | async-start | bytes 2097152 | tf_op jit(solution)/shard_map/all_to_all | solution.py:481
  119.9 1.5 convolution_convert_fusion.1
  121.4 2.9 %shard_map.144 = bf16[128,4096]{1,0:T(8,128)(2,1)} custom-call(s32[5]{0:T(128)} %stack.16.info, bf16[4,2,8,8,256]{4,3,2,1,0:T(8,128)(2,1)} %get-tuple-element.45.left, bf16[256,1024]{1,0:T(8,128)(2,1)} %copy-done, bf16[512,1024]{1,0:T(8,128)(2,1)} %collective-permute-done.16.received), custom_call_target="tpu_custom_call" | custom-call | flops 268435456 | bytes 1048576 | tf_op jit(solution)/shard_map/pallas_call | solution.py:380
  124.3 11.1 %all-to-all-done.1 = bf16[8,256,256]{2,1,0:T(8,128)(2,1)} async-done(((bf16[8,256,256]{2,1,0:T(8,128)(2,1)}), bf16[8,256,256]{2,1,0:T(8,128)(2,1)}, u32[]{:S(2)}, u32[]{:S(2)}) %all-to-all-start.1) | async-done | bytes 1048608 | tf_op jit(solution)/shard_map/all_to_all | solution.py:481
  135.4 7.6 %all-to-all-start.4 = ((bf16[16,8,4096]{2,1,0:T(8,128)(2,1)}), bf16[16,8,4096]{2,1,0:T(8,128)(2,1)}, u32[]{:S(2)}, u32[]{:S(2)}) async-start(bf16[16,8,4096]{2,1,0:T(8,128)(2,1)} %bitcast.23), calls=%async_computation.4 | async-start | bytes 2097152 | tf_op jit(solution)/shard_map/all_to_all | solution.py:492
  143.0 0.1 reduce_sum.25
  143.1 1.4 reduce_sum.24
  144.6 1.1 convolution_convert_fusion.2
  145.7 0.0 collective-permute-start.15
  145.7 2.8 %shard_map.142 = (f32[128,1024]{1,0:T(8,128)}, bf16[128,1024]{1,0:T(8,128)(2,1)}, bf16[128,1024]{1,0:T(8,128)(2,1)}, bf16[128,1024]{1,0:T(8,128)(2,1)}) custom-call(bf16[4,2,8,8,256]{4,3,2,1,0:T(8,128)(2,1)} %get-tuple-element.39.left, bf16[256,1024]{1,0:T(8,128)(2,1)} %bitcast.21, bf16[512,1024]{1,0:T(8,128)(2,1)} %collective-permute-done.11.received), custom_call_target="tpu_custom_call" | custom-call | flops 268435456 | bytes 1048576 | tf_op jit(solution)/shard_map/pallas_call | solution.py:380
  148.5 0.0 collective-permute-start.12
  148.5 1.7 collective-permute-start.13
  150.2 2.6 %collective-permute-start.14 = (bf16[128,1024]{1,0:T(8,128)(2,1)}, bf16[128,1024]{1,0:T(8,128)(2,1)}, u32[]{:S(2)}, u32[]{:S(2)}) collective-permute-start(bf16[128,1024]{1,0:T(8,128)(2,1)} %get-tuple-element.44), channel_id=1, source_target_pairs={{0,48},{16,0},{32,16},{48,32},{64,112},{80,64},{96,80},{112,96},{1... | collective-permute-start | bytes 786440 | tf_op jit(solution)/shard_map/ppermute | solution.py:473
  152.9 1.7 pad_maximum_fusion.dkv.right
  154.5 9.8 %collective-permute-done.12.one = bf16[128,1024]{1,0:T(8,128)(2,1)} collective-permute-done((bf16[128,1024]{1,0:T(8,128)(2,1)}, bf16[128,1024]{1,0:T(8,128)(2,1)}, u32[]{:S(2)}, u32[]{:S(2)}) %collective-permute-start.12) | collective-permute-done | bytes 262176 | tf_op jit(solution)/shard_map/ppermute | solution.py:473
  164.4 0.0 collective-permute-done.13.two
  164.4 0.6 collective-permute-done.14.three
  165.0 0.0 collective-permute-done.15.received
  165.0 3.0 %shard_map.143 = bf16[128,3072]{1,0:T(8,128)(2,1)} custom-call(s32[5]{0:T(128)} %stack.16.info, f32[128,1024]{1,0:T(8,128)} %get-tuple-element.41.base, bf16[128,1024]{1,0:T(8,128)(2,1)} %collective-permute-done.12.one, bf16[128,1024]{1,0:T(8,128)(2,1)} %collective-permute-done.13.two, bf16[128,1024]{1,0:T(8,128)(2,1)} %collective-permute-done.14.three, ...), custom_call_target="tpu_custom_call" | custom-call | flops 1073741824 | bytes 1048576 | tf_op jit(solution)/shard_map/pallas_call | solution.py:380
  168.0 7.2 %all-to-all-start.3 = ((bf16[16,8,3072]{2,1,0:T(8,128)(2,1)}), bf16[16,8,3072]{2,1,0:T(8,128)(2,1)}, u32[]{:S(2)}, u32[]{:S(2)}) async-start(bf16[16,8,3072]{2,1,0:T(8,128)(2,1)} %bitcast.28), calls=%async_computation.3 | async-start | bytes 1572864 | tf_op jit(solution)/shard_map/all_to_all | solution.py:492
  175.2 2.0 shard_map.145.query
  177.2 11.9 %all-to-all-done.3.parts = bf16[16,8,3072]{2,1,0:T(8,128)(2,1)} async-done(((bf16[16,8,3072]{2,1,0:T(8,128)(2,1)}), bf16[16,8,3072]{2,1,0:T(8,128)(2,1)}, u32[]{:S(2)}, u32[]{:S(2)}) %all-to-all-start.3) | async-done | bytes 786464 | tf_op jit(solution)/shard_map/all_to_all | solution.py:492
  189.1 2.2 %shard_map.146 = bf16[8,8,7168]{2,1,0:T(8,128)(2,1)} custom-call(bf16[16,8,3072]{2,1,0:T(8,128)(2,1)} %all-to-all-done.3.parts, bf16[8,4096]{1,0:T(8,128)(2,1)} %shard_map.145.query), custom_call_target="tpu_custom_call" | custom-call | flops 1073741824 | bytes 1048576 | tf_op jit(solution)/shard_map/pallas_call | solution.py:380
  191.3 5.2 %all-to-all-start.5 = ((bf16[8,8,7168]{2,1,0:T(8,128)(2,1)}), bf16[8,8,7168]{2,1,0:T(8,128)(2,1)}, u32[]{:S(2)}, u32[]{:S(2)}) async-start(bf16[8,8,7168]{2,1,0:T(8,128)(2,1)} %shard_map.146), calls=%async_computation.5 | async-start | bytes 1835008 | tf_op jit(solution)/shard_map/all_to_all | solution.py:589
  196.4 1.3 dynamic-slice_bitcast_fusion.gain
  197.8 1.4 constant_dynamic-slice_fusion
  199.2 1.6 constant_dynamic-slice_fusion.2.w_query
  200.8 4.4 %shard_map.141 = bf16[256,1024]{1,0:T(8,128)(2,1)} custom-call(bf16[256,1024]{1,0:T(8,128)(2,1)} %bitcast.25, bf16[256,1024]{1,0:T(8,128)(2,1)} %bitcast.22, f32[1,1024]{1,0:T(1,128)} %bitcast.32, bf16[256,1024]{1,0:T(8,128)(2,1)} %copy-done, bf16[256,512]{1,0:T(8,128)(2,1)} %pad_maximum_fusion.dkv.right, bf16[1024,1024]{1,0:T(8,128)(2,1)} %w_query.3, ...), custom_call_target="tpu_custom_call" | custom-call | flops 805306368 | bytes 1048576 | tf_op jit(solution)/shard_map/pallas_call | solution.py:380
  205.2 3.8 %all-to-all-done.5.shared = bf16[8,8,7168]{2,1,0:T(8,128)(2,1)} async-done(((bf16[8,8,7168]{2,1,0:T(8,128)(2,1)}), bf16[8,8,7168]{2,1,0:T(8,128)(2,1)}, u32[]{:S(2)}, u32[]{:S(2)}) %all-to-all-start.5) | async-done | bytes 917536 | tf_op jit(solution)/shard_map/all_to_all | solution.py:589
  209.0 2.2 %shard_map.147 = (f32[64,1024]{1,0:T(8,128)}, f32[64,256]{1,0:T(8,128)}, f32[64,256]{1,0:T(8,128)}, f32[64,1024]{1,0:T(8,128)}, f32[1,64]{1,0:T(1,128)}) custom-call(bf16[8,8,7168]{2,1,0:T(8,128)(2,1)} %all-to-all-done.5.shared, bf16[64,1024]{1,0:T(8,128)(2,1)} %constant_dynamic-slice_fusion.2.w_query, bf16[64,256]{1,0:T(8,128)(2,1)} %get-tuple-element.53.w_key, ...), custom_call_target="tpu_custom_call" | custom-call | flops 1073741824 | bytes 1048576 | tf_op jit(solution)/shard_map/pallas_call | solution.py:380
  (25 shorter events, 0.1 us)
Async XLA Ops:
  11.2 37.1 %collective-permute-start = (bf16[2,256,1024]{2,1,0:T(8,128)(2,1)}, bf16[2,256,1024]{2,1,0:T(8,128)(2,1)}, u32[]{:S(2)}, u32[]{:S(2)}) collective-permute-start(bf16[2,256,1024]{2,1,0:T(8,128)(2,1)} %get-tuple-element.30.own), channel_id=1, source_target_pairs={{0,1},{1,0},{2,3},{3,2},{4,5},{5,4},{6,7},{7,6},{8,9},{9,8},{10,11... | collective-permute-start | bytes 3145736 | tf_op jit(solution)/shard_map/ppermute | solution.py:468
  11.2 40.0 %all-to-all-start = ((bf16[8,256,256]{2,1,0:T(8,128)(2,1)}), bf16[8,256,256]{2,1,0:T(8,128)(2,1)}, u32[]{:S(2)}, u32[]{:S(2)}) async-start(bf16[8,256,256]{2,1,0:T(8,128)(2,1)} %get-tuple-element.31), calls=%async_computation | async-start | bytes 2097152 | tf_op jit(solution)/shard_map/all_to_all | solution.py:481
  19.1 27.1 %collective-permute-start.8 = (bf16[256,256]{1,0:T(8,128)(2,1)}, bf16[256,256]{1,0:T(8,128)(2,1)}, u32[]{:S(2)}, u32[]{:S(2)}) collective-permute-start(bf16[256,256]{1,0:T(8,128)(2,1)} %get-tuple-element.32.refs_0_), channel_id=1, source_target_pairs={{0,14},{1,15},{2,12},{3,13},{4,10},{5,11},{6,8},{7,9},{8,6},{9,7},... | collective-permute-start | bytes 393224 | tf_op jit(solution)/shard_map/ppermute | solution.py:530
  24.8 22.9 %collective-permute-start.7 = (bf16[256,256]{1,0:T(8,128)(2,1)}, bf16[256,256]{1,0:T(8,128)(2,1)}, u32[]{:S(2)}, u32[]{:S(2)}) collective-permute-start(bf16[256,256]{1,0:T(8,128)(2,1)} %get-tuple-element.32.refs_0_), channel_id=1, source_target_pairs={{0,12},{1,13},{2,14},{3,15},{4,8},{5,9},{6,10},{7,11},{8,4},{9,5},... | collective-permute-start | bytes 393224 | tf_op jit(solution)/shard_map/ppermute | solution.py:530
  25.3 29.8 %collective-permute-start.6 = (bf16[256,256]{1,0:T(8,128)(2,1)}, bf16[256,256]{1,0:T(8,128)(2,1)}, u32[]{:S(2)}, u32[]{:S(2)}) collective-permute-start(bf16[256,256]{1,0:T(8,128)(2,1)} %get-tuple-element.32.refs_0_), channel_id=1, source_target_pairs={{0,10},{1,11},{2,8},{3,9},{4,14},{5,15},{6,12},{7,13},{8,2},{9,3},... | collective-permute-start | bytes 393224 | tf_op jit(solution)/shard_map/ppermute | solution.py:530
  27.1 28.0 %collective-permute-start.5 = (bf16[256,256]{1,0:T(8,128)(2,1)}, bf16[256,256]{1,0:T(8,128)(2,1)}, u32[]{:S(2)}, u32[]{:S(2)}) collective-permute-start(bf16[256,256]{1,0:T(8,128)(2,1)} %get-tuple-element.32.refs_0_), channel_id=1, source_target_pairs={{0,8},{1,9},{2,10},{3,11},{4,12},{5,13},{6,14},{7,15},{8,0},{9,1},... | collective-permute-start | bytes 393224 | tf_op jit(solution)/shard_map/ppermute | solution.py:530
  46.3 8.9 %collective-permute-start.4 = (bf16[256,256]{1,0:T(8,128)(2,1)}, bf16[256,256]{1,0:T(8,128)(2,1)}, u32[]{:S(2)}, u32[]{:S(2)}) collective-permute-start(bf16[256,256]{1,0:T(8,128)(2,1)} %get-tuple-element.32.refs_0_), channel_id=1, source_target_pairs={{0,6},{1,7},{2,4},{3,5},{4,2},{5,3},{6,0},{7,1},{8,14},{9,15},{10,... | collective-permute-start | bytes 393224 | tf_op jit(solution)/shard_map/ppermute | solution.py:530
  47.7 7.5 %collective-permute-start.3 = (bf16[256,256]{1,0:T(8,128)(2,1)}, bf16[256,256]{1,0:T(8,128)(2,1)}, u32[]{:S(2)}, u32[]{:S(2)}) collective-permute-start(bf16[256,256]{1,0:T(8,128)(2,1)} %get-tuple-element.32.refs_0_), channel_id=1, source_target_pairs={{0,4},{1,5},{2,6},{3,7},{4,0},{5,1},{6,2},{7,3},{8,12},{9,13},{10,... | collective-permute-start | bytes 393224 | tf_op jit(solution)/shard_map/ppermute | solution.py:530
  48.3 8.2 %collective-permute-start.2 = (bf16[256,256]{1,0:T(8,128)(2,1)}, bf16[256,256]{1,0:T(8,128)(2,1)}, u32[]{:S(2)}, u32[]{:S(2)}) collective-permute-start(bf16[256,256]{1,0:T(8,128)(2,1)} %get-tuple-element.32.refs_0_), channel_id=1, source_target_pairs={{0,2},{1,3},{2,0},{3,1},{4,6},{5,7},{6,4},{7,5},{8,10},{9,11},{10,... | collective-permute-start | bytes 393224 | tf_op jit(solution)/shard_map/ppermute | solution.py:530
  55.1 1.5 collective-permute-start.1
  69.0 3.1 %collective-permute-start.9 = (bf16[2,1024,256]{2,1,0:T(8,128)(2,1)}, bf16[2,1024,256]{2,1,0:T(8,128)(2,1)}, u32[]{:S(2)}, u32[]{:S(2)}) collective-permute-start(bf16[2,1024,256]{2,1,0:T(8,128)(2,1)} %get-tuple-element.33.mine), channel_id=1, source_target_pairs={{0,1},{1,0},{2,3},{3,2},{4,5},{5,4},{6,7},{7,6},{8,9},{9,8},{10,11... | collective-permute-start | bytes 3145736 | tf_op jit(solution)/shard_map/ppermute | solution.py:468
  84.5 14.2 %copy-start.8 = (bf16[256,1024]{1,0:T(8,128)(2,1)S(1)}, bf16[256,1024]{1,0:T(8,128)(2,1)}, u32[]{:S(2)}) copy-start(bf16[256,1024]{1,0:T(8,128)(2,1)} %get-tuple-element.35) | copy-start | bytes 1572868
  84.5 15.2 %copy-start.6 = (bf16[4,2,8,8,256]{4,3,2,1,0:T(8,128)(2,1)S(1)}, bf16[4,2,8,8,256]{4,3,2,1,0:T(8,128)(2,1)}, u32[]{:S(2)}) copy-start(bf16[4,2,8,8,256]{4,3,2,1,0:T(8,128)(2,1)} %get-tuple-element.46) | copy-start | bytes 786436
  84.5 14.2 %collective-permute-start.10 = (bf16[256,1024]{1,0:T(8,128)(2,1)}, bf16[256,1024]{1,0:T(8,128)(2,1)S(1)}, u32[]{:S(2)}, u32[]{:S(2)}) collective-permute-start(bf16[256,1024]{1,0:T(8,128)(2,1)} %get-tuple-element.36), channel_id=1, source_target_pairs={{0,1},{1,0},{2,3},{3,2},{4,5},{5,4},{6,7},{7,6},{8,9},{9,8},{10,11... | collective-permute-start | bytes 1572872 | tf_op jit(solution)/shard_map/ppermute | solution.py:468
  84.6 31.0 %all-to-all-start.2 = ((bf16[8,256,256]{2,1,0:T(8,128)(2,1)}), bf16[8,256,256]{2,1,0:T(8,128)(2,1)S(1)}, u32[]{:S(2)}, u32[]{:S(2)}) async-start(bf16[8,256,256]{2,1,0:T(8,128)(2,1)} %get-tuple-element.38), calls=%async_computation.2 | async-start | bytes 2097152 | tf_op jit(solution)/shard_map/all_to_all | solution.py:481
  98.9 0.8 copy-start
  98.9 21.0 %copy-start.1 = (bf16[1,256,1024]{2,1,0:T(8,128)(2,1)S(1)}, bf16[1,256,1024]{2,1,0:T(8,128)(2,1)}, u32[]{:S(2)}) copy-start(bf16[1,256,1024]{2,1,0:T(8,128)(2,1)} %param.10) | copy-start | bytes 1572868
  98.9 21.0 %copy-start.9 = (bf16[4,2,8,8,256]{4,3,2,1,0:T(8,128)(2,1)S(1)}, bf16[4,2,8,8,256]{4,3,2,1,0:T(8,128)(2,1)}, u32[]{:S(2)}) copy-start(bf16[4,2,8,8,256]{4,3,2,1,0:T(8,128)(2,1)} %get-tuple-element.40) | copy-start | bytes 786436
  100.1 21.2 %collective-permute-start.16 = (bf16[512,1024]{1,0:T(8,128)(2,1)S(1)}, bf16[512,1024]{1,0:T(8,128)(2,1)}, u32[]{:S(2)}, u32[]{:S(2)}) collective-permute-start(bf16[512,1024]{1,0:T(8,128)(2,1)S(1)} %convolution_convert_fusion), channel_id=1, source_target_pairs={{0,1},{1,0},{2,3},{3,2},{4,5},{5,4},{6,7},{7,6},{8,9},{9,8},{10,11... | collective-permute-start | bytes 3145736 | tf_op jit(solution)/shard_map/ppermute | solution.py:468
  115.6 5.7 %copy-start.2 = (bf16[8,256,256]{2,1,0:T(8,128)(2,1)}, bf16[8,256,256]{2,1,0:T(8,128)(2,1)S(1)}, u32[]{:S(2)}) copy-start(bf16[8,256,256]{2,1,0:T(8,128)(2,1)S(1)} %all-to-all-done.2) | copy-start | bytes 3145732
  115.6 19.7 %all-to-all-start.1 = ((bf16[8,256,256]{2,1,0:T(8,128)(2,1)}), bf16[8,256,256]{2,1,0:T(8,128)(2,1)}, u32[]{:S(2)}, u32[]{:S(2)}) async-start(bf16[8,256,256]{2,1,0:T(8,128)(2,1)} %get-tuple-element.37), calls=%async_computation.1 | async-start | bytes 2097152 | tf_op jit(solution)/shard_map/all_to_all | solution.py:481
  121.4 24.4 %collective-permute-start.11 = (bf16[512,1024]{1,0:T(8,128)(2,1)}, bf16[512,1024]{1,0:T(8,128)(2,1)}, u32[]{:S(2)}, u32[]{:S(2)}) collective-permute-start(bf16[512,1024]{1,0:T(8,128)(2,1)} %convolution_convert_fusion.1), channel_id=1, source_target_pairs={{0,1},{1,0},{2,3},{3,2},{4,5},{5,4},{6,7},{7,6},{8,9},{9,8},{10,11... | collective-permute-start | bytes 3145736 | tf_op jit(solution)/shard_map/ppermute | solution.py:468
  124.3 18.7 %copy-start.3 = (bf16[8,256,256]{2,1,0:T(8,128)(2,1)S(1)}, bf16[8,256,256]{2,1,0:T(8,128)(2,1)}, u32[]{:S(2)}) copy-start(bf16[8,256,256]{2,1,0:T(8,128)(2,1)} %copy-done.2) | copy-start | bytes 3145732
  135.4 9.2 %copy-start.7 = (bf16[4,2,8,8,256]{4,3,2,1,0:T(8,128)(2,1)S(1)}, bf16[4,2,8,8,256]{4,3,2,1,0:T(8,128)(2,1)}, u32[]{:S(2)}) copy-start(bf16[4,2,8,8,256]{4,3,2,1,0:T(8,128)(2,1)} %get-tuple-element.46) | copy-start | bytes 786436
  135.4 32.6 %all-to-all-start.4 = ((bf16[16,8,4096]{2,1,0:T(8,128)(2,1)}), bf16[16,8,4096]{2,1,0:T(8,128)(2,1)}, u32[]{:S(2)}, u32[]{:S(2)}) async-start(bf16[16,8,4096]{2,1,0:T(8,128)(2,1)} %bitcast.23), calls=%async_computation.4 | async-start | bytes 2097152 | tf_op jit(solution)/shard_map/all_to_all | solution.py:492
  143.1 1.4 copy-start.4
  144.6 1.1 copy-start.5
  145.7 19.2 %collective-permute-start.15 = (bf16[512,512]{1,0:T(8,128)(2,1)}, bf16[512,512]{1,0:T(8,128)(2,1)}, u32[]{:S(2)}, u32[]{:S(2)}) collective-permute-start(bf16[512,512]{1,0:T(8,128)(2,1)} %convolution_convert_fusion.2), channel_id=1, source_target_pairs={{0,1},{1,0},{2,3},{3,2},{4,5},{5,4},{6,7},{7,6},{8,9},{9,8},{10,11... | collective-permute-start | bytes 1572872 | tf_op jit(solution)/shard_map/ppermute | solution.py:468
  148.5 15.9 %collective-permute-start.12 = (bf16[128,1024]{1,0:T(8,128)(2,1)}, bf16[128,1024]{1,0:T(8,128)(2,1)}, u32[]{:S(2)}, u32[]{:S(2)}) collective-permute-start(bf16[128,1024]{1,0:T(8,128)(2,1)} %get-tuple-element.42), channel_id=1, source_target_pairs={{0,16},{16,32},{32,48},{48,0},{64,80},{80,96},{96,112},{112,64},{1... | collective-permute-start | bytes 786440 | tf_op jit(solution)/shard_map/ppermute | solution.py:473
  148.5 15.9 %collective-permute-start.13 = (bf16[128,1024]{1,0:T(8,128)(2,1)}, bf16[128,1024]{1,0:T(8,128)(2,1)}, u32[]{:S(2)}, u32[]{:S(2)}) collective-permute-start(bf16[128,1024]{1,0:T(8,128)(2,1)} %get-tuple-element.43), channel_id=1, source_target_pairs={{0,32},{16,48},{32,0},{48,16},{64,96},{80,112},{96,64},{112,80},{1... | collective-permute-start | bytes 786440 | tf_op jit(solution)/shard_map/ppermute | solution.py:473
  150.2 14.8 %collective-permute-start.14 = (bf16[128,1024]{1,0:T(8,128)(2,1)}, bf16[128,1024]{1,0:T(8,128)(2,1)}, u32[]{:S(2)}, u32[]{:S(2)}) collective-permute-start(bf16[128,1024]{1,0:T(8,128)(2,1)} %get-tuple-element.44), channel_id=1, source_target_pairs={{0,48},{16,0},{32,16},{48,32},{64,112},{80,64},{96,80},{112,96},{1... | collective-permute-start | bytes 786440 | tf_op jit(solution)/shard_map/ppermute | solution.py:473
  168.0 21.1 %all-to-all-start.3 = ((bf16[16,8,3072]{2,1,0:T(8,128)(2,1)}), bf16[16,8,3072]{2,1,0:T(8,128)(2,1)}, u32[]{:S(2)}, u32[]{:S(2)}) async-start(bf16[16,8,3072]{2,1,0:T(8,128)(2,1)} %bitcast.28), calls=%async_computation.3 | async-start | bytes 1572864 | tf_op jit(solution)/shard_map/all_to_all | solution.py:492
  191.3 17.7 %all-to-all-start.5 = ((bf16[8,8,7168]{2,1,0:T(8,128)(2,1)}), bf16[8,8,7168]{2,1,0:T(8,128)(2,1)}, u32[]{:S(2)}, u32[]{:S(2)}) async-start(bf16[8,8,7168]{2,1,0:T(8,128)(2,1)} %shard_map.146), calls=%async_computation.5 | async-start | bytes 1835008 | tf_op jit(solution)/shard_map/all_to_all | solution.py:589

commit v5 on v3

--- a/solution.py
+++ b/solution.py
@@ -166,6 +166,8 @@
         for n in range(rows.shape[0] // size):
             place = n % (outer * steps)
             to = own if (n // (outer * steps)) == same else pair
+            if to is None:
+                continue
             step = (place % steps - x + steps) & (steps - 1)
             to[step, place // steps, chip] = rows[n * size : (n + 1) * size].astype(to.dtype)
 
@@ -175,7 +177,7 @@
 
 def grads_kernel(
     heads, seq, info, own, pair, mine, other, keys, values, probs_in,
-    at_own, at_pair, dk, dq_own, dq_pair,
+    at_own, at_pair, dk, dq,
     keys_t, q_rows, probs, dscores, delta, in_sems,
 ):
     chips, tok, _ = keys.shape
@@ -201,9 +203,8 @@
             delta[:, at] = jnp.sum(
                 a * qd[1, :, head(h)].T.astype(jnp.float32), axis=0, keepdims=True
             )
-            if half == 0:
-                for n in range(per_head):
-                    put_rows(info, a[n * block : (n + 1) * block], h * per_head + n, at_own, at_pair)
+            for n in range(per_head):
+                put_rows(info, a[n * block : (n + 1) * block], h * per_head + n, (at_own, at_pair)[half], None)
     for chip in range(chips):
         keys_t[:, pl.ds(chip * tok, tok)] = keys[chip].T
 
@@ -229,10 +230,10 @@
         dk[chip] = (dot_nn(dscores[rows, :], q_rows[...]) * HS ** (-0.5)).astype(jnp.bfloat16)
 
     each_chip(chips, step)
-    for half, dq in enumerate((dq_own, dq_pair)):
+    for half in range(2):
         for h in range(heads):
             d = dot_nn(keys_t[...], dscores[:, part(half, h, heads)]) * HS ** (-0.5)
-            dq[:, head(h)] = d.T.astype(jnp.bfloat16)
+            dq[half, :, head(h)] = d.T.astype(jnp.bfloat16)
 
 
 def prepare_kernel(chips, x, gain, w_key, w_value, hidden, k_copies, v_copies):
@@ -250,6 +251,7 @@
     h = hidden[...]
     both[0] = dot_nn(h, w_query[...]).astype(jnp.bfloat16)
     both[1] = dot_nt(grad_out[...], w_out[...]).astype(jnp.bfloat16)
+    both[2] = grad_out[...]
     chips = ht_own.shape[2]
     block = h.shape[1] // chips
     for chip in range(chips):
@@ -257,37 +259,53 @@
         put_rows(info, rows, chip, ht_own, ht_pair)
 
 
-def step_terms(left, step, right, received):
-    rows = left.shape[1] * left.shape[2] * left.shape[3]
-    own = dot_nn(left[step].reshape(rows, -1), right)
-    return own + received[pl.ds(step * rows, rows), :].astype(jnp.float32)
-
-
-def own_terms_kernel(left, right, received, base, *parts):
-    for step, out in enumerate((base, *parts)):
-        out[...] = step_terms(left, step, right[...], received).astype(out.dtype)
-
-
-def direct_terms(info, left, right, received, out, at):
-    wide, steps = right.shape[1], left.shape[0]
+def step_terms(lefts, rights, step):
+    total = 0.0
+    for left, right in zip(lefts, rights):
+        rows = left.shape[1] * left.shape[2] * left.shape[3]
+        total = total + dot_nn(left[step].reshape(rows, -1), right)
+    return total
+
+
+def direct_terms(info, lefts, rights, out, at):
+    wide, steps = rights[0].shape[1], lefts[0].shape[0]
     for step in range(steps):
         place = (info[4] + step) & (steps - 1)
         to = pl.ds(pl.multiple_of(at + place * wide, 128), wide)
-        out[:, to] = step_terms(left, step, right[...], received).astype(out.dtype)
-
-
-def direct_kernel(info, left, right, received, out):
-    direct_terms(info, left, right, received, out, 0)
-
-
-def collect_kernel(info, base, one, two, three, query_terms, left, right, received, out):
+        out[:, to] = step_terms(lefts, rights, step).astype(out.dtype)
+
+
+def terms_kernel(
+    info, at_own, at_pair, own, pair, ht_own, ht_pair, dq_mine, dq_other,
+    dq, query_terms, base, *parts,
+):
+    for step, out in enumerate((base, *parts)):
+        out[...] = step_terms((at_own, at_pair), (own[2], pair[2]), step).astype(out.dtype)
+    rights = [
+        (dq_mine[half].astype(jnp.float32) + dq_other[1 - half].astype(jnp.float32)).astype(dq.dtype)
+        for half in range(2)
+    ]
+    dq[...] = rights[0]
+    direct_terms(info, (ht_own, ht_pair), rights, query_terms, 0)
+
+
+def rows_kernel(dk_parts, dv_parts, out):
+    for at, parts in ((0, dk_parts), (HS, dv_parts)):
+        total = parts[0].astype(jnp.float32)
+        for n in range(1, parts.shape[0]):
+            total = total + parts[n].astype(jnp.float32)
+        out[:, pl.ds(at, HS)] = total.astype(out.dtype)
+
+
+def collect_kernel(info, base, one, two, three, query_terms, ht_own, ht_pair, dkv, dkv_pair, out):
     total = base[...]
     for arrived in (one, two, three):
         total = total + arrived[...].astype(jnp.float32)
     wide = total.shape[1]
     out[:, pl.ds(0, wide)] = total.astype(out.dtype)
     out[:, pl.ds(wide, query_terms.shape[1])] = query_terms[...]
-    direct_terms(info, left, right, received, out, wide + query_terms.shape[1])
+    rights = (dkv[...], dkv_pair[...])
+    direct_terms(info, (ht_own, ht_pair), rights, out, wide + query_terms.shape[1])
 
 
 def spread_kernel(parts, out):
@@ -373,7 +391,7 @@
 
 
 def run_stats(info, own, pair, keys):
-    _, tok, wide = own.shape
+    tok, wide = own.shape[1:]
     chips, heads = keys.shape[0], wide // HS
     seq = 2 * tok * chips
     rows = scratch(1, 2 * wide, dtype=jnp.float32)
@@ -388,7 +406,7 @@
 
 
 def run_attend(info, own, pair, mine, other, keys, values):
-    _, tok, wide = own.shape
+    tok, wide = own.shape[1:]
     chips, heads = keys.shape[0], wide // HS
     seq = 2 * tok * chips
     return call(
@@ -409,12 +427,12 @@
 
 
 def run_grads(info, own, pair, mine, other, keys, values, probs, filed):
-    _, tok, wide = own.shape
+    tok, wide = own.shape[1:]
     chips, heads = keys.shape[0], wide // HS
     seq = 2 * tok * chips
     return call(
         functools.partial(grads_kernel, heads, seq),
-        (filed, filed, shape(chips, tok, HS), shape(tok, wide), shape(tok, wide)),
+        (filed, filed, shape(chips, tok, HS), shape(2, tok, wide)),
         (info, own, pair, mine, other, keys, values, probs),
         6 * seq * wide * HS,
         smem=1,
@@ -434,10 +452,6 @@
 X = 4
 
 
-def as_bf16(value):
-    return value.astype(jnp.bfloat16)
-
-
 def swap_cores(value):
     count = lax.axis_size("blk")
     return lax.ppermute(value, "blk", [(i, i ^ 1) for i in range(count)])
@@ -464,15 +478,6 @@
         for core in range(CORES)
     ]
     return lax.all_to_all(value, ("dp", "blk"), 0, 0, tiled=True, axis_index_groups=groups)
-
-
-def sum_first(parts):
-    return as_bf16(jnp.sum(parts.astype(jnp.float32), axis=0))
-
-
-def pair_terms(left_pair, right):
-    terms = as_bf16(dot_nn(left_pair.reshape(-1, left_pair.shape[-1]), right))
-    return swap_cores(terms)
 
 
 def per_device(inputs, upstream, gain, w_query, w_key, w_value, w_out, prefix_len, bound):
@@ -501,50 +506,46 @@
     values = exchange_chips(v_copies)
     own, ht_own, ht_pair = call(
         project_kernel,
-        (shape(2, tok, heads_wide), filed, filed),
+        (shape(3, tok, heads_wide), filed, filed),
         (info, hidden, grad_out, w_query, w_out),
         4 * tok * wide * wide,
         smem=1,
     )
     pair = swap_cores(own)
+    ht_pair = swap_cores(ht_pair)
     mine = run_stats(info, own, pair, keys)
     other = swap_cores(mine)
     attn, dv, probs = run_attend(info, own, pair, mine, other, keys, values)
     attn_other = swap_cores(attn)
-    d_value_rows = sum_first(exchange_chips(dv))
-    at_own, at_pair, dk, dq_own, dq_pair = run_grads(
+    dv_parts = exchange_chips(dv)
+    at_own, at_pair, dk, dq_mine = run_grads(
         info, own, pair, attn, attn_other, keys, values, probs, filed
     )
-    dq_other = swap_cores(dq_pair)
-    d_key_rows = sum_first(exchange_chips(dk))
-    d_query_rows = as_bf16(dq_own.astype(jnp.float32) + dq_other.astype(jnp.float32))
-
-    out_received = pair_terms(at_pair, grad_out)
+    dq_other = swap_cores(dq_mine)
+    dk_parts = exchange_chips(dk)
     rows = outer * chips * size
-    base, *parts = call(
-        own_terms_kernel,
-        (shape(rows, wide, dtype=jnp.float32), *[shape(rows, wide)] * (X - 1)),
-        (at_own, grad_out, out_received),
-        2 * X * rows * wide * tok,
+    d_query_rows, query_terms, base, *parts = call(
+        terms_kernel,
+        (
+            shape(tok, heads_wide),
+            shape(rows, X * heads_wide),
+            shape(rows, wide, dtype=jnp.float32),
+            *[shape(rows, wide)] * (X - 1),
+        ),
+        (info, at_own, at_pair, own, pair, ht_own, ht_pair, dq_mine, dq_other),
+        8 * X * rows * wide * tok,
+        smem=1,
     )
     arrived = []
     for step, terms in enumerate(parts, 1):
         arrived.append(send_along_x(terms, step))
-    query_received = pair_terms(ht_pair, d_query_rows)
-    query_terms = call(
-        direct_kernel,
-        shape(rows, X * heads_wide),
-        (info, ht_own, d_query_rows, query_received),
-        2 * X * rows * heads_wide * tok,
-        smem=1,
-    )
-    d_kv_rows = jnp.concatenate([d_key_rows, d_value_rows], axis=1)
-    kv_received = pair_terms(ht_pair, d_kv_rows)
+    d_kv_rows = call(rows_kernel, shape(tok, 2 * HS), (dk_parts, dv_parts), 1 << 30)
+    d_kv_pair = swap_cores(d_kv_rows)
     total = wide + X * (heads_wide + 2 * HS)
     terms = call(
         collect_kernel,
         shape(rows, total),
-        (info, base, *arrived, query_terms, ht_own, d_kv_rows, kv_received),
+        (info, base, *arrived, query_terms, ht_own, ht_pair, d_kv_rows, d_kv_pair),
         1 << 30,
         smem=1,
     )

time: 185 us -> 190 us (1.027)
  waiting for transfers between devices: 45.5 us -> 55.9 us
  other arithmetic: 4.44 us -> 0 us
  matrix products: 3.92 us -> 0 us
  Pallas kernels: 55.3 us -> 59.2 us
    all_to_all x4, waiting for transfers between devices: 35.2 us -> 41 us  [exchange_chips(): lax.all_to_all(value, 'blk', 0, 0, tiled=True, axis_index_groups=groups)]
    ppermute x3, waiting for transfers between devices: 6.23 us -> 10.8 us  [send_along_x(): lax.ppermute(value, 'dp', [(i, i // X * X + (i + step) % X) for i in rang...]
    dot_general x3 -> x0, matrix products: 3.92 us -> none  [dot_nn(): return jnp.dot(a, b, preferred_element_type=jnp.float32)]
    pallas_call x11, Pallas kernels: 55.3 us -> 59.2 us  [call(): pl.pallas_call(body, out_shape=outs, in_specs=specs, out_specs=out_specs,...]
  transfers between devices with their start and end apart: 15 -> 14, of which waited for: 8 -> 8; matrix products, arithmetic and copies ran while one was open for 7% -> 3% of each run, Pallas kernels for 17% -> 19%
where the time goes in v5:
time: 190 us; the launch traced here: 189 us
  Pallas kernels  59.2 us (31%)
  waiting for transfers between devices  55.9 us (29%)
  starting transfers between devices  35.7 us (19%)
  blocking collectives  31.1 us (16%)
  local copies, waits for them, and re-layouts  4.97 us (3%)
  between operations  2.03 us (1%)
    pallas_call x11, Pallas kernels, call(): pl.pallas_call(body, out_shape=outs, in_specs=specs, out_specs=out_specs,...  59.2 us
    all_to_all x4, waiting for transfers between devices, exchange_chips(): lax.all_to_all(value, 'blk', 0, 0, tiled=True, axis_index_groups=groups)  41 us
    all_to_all x1, blocking collectives, exchange_plane(): lax.all_to_all(value, ('dp', 'blk'), 0, 0, tiled=True, axis_index_groups=...  31.1 us
    all_to_all x4, starting transfers between devices, exchange_chips(): lax.all_to_all(value, 'blk', 0, 0, tiled=True, axis_index_groups=groups)  25.5 us
    ppermute x3, waiting for transfers between devices, send_along_x(): lax.ppermute(value, 'dp', [(i, i // X * X + (i + step) % X) for i in rang...  10.8 us
    ppermute x3, starting transfers between devices, send_along_x(): lax.ppermute(value, 'dp', [(i, i // X * X + (i + step) % X) for i in rang...  5.62 us
    all_to_all x1, starting transfers between devices, whole(): shared = lax.all_to_all(copies, 'dp', 0, 0, tiled=True)  4.24 us
    all_to_all x1, waiting for transfers between devices, whole(): shared = lax.all_to_all(copies, 'dp', 0, 0, tiled=True)  4.12 us
  transfers between devices with their start and end apart: 14, of which 8 were waited for; matrix products, arithmetic and copies ran while one was open for 3% of the time, Pallas kernels for 19%

profile of v5, /device:TPU:0, one launch (start us, length us, event | category | flops | bytes accessed | tf_op | source)
XLA Modules:
  0.0 189.0 jit_solution(11041645959267797974)
XLA Ops:
  0.6 3.4 %shard_map.136 = (bf16[256,1024]{1,0:T(8,128)(2,1)}, bf16[8,256,256]{2,1,0:T(8,128)(2,1)}, bf16[8,256,256]{2,1,0:T(8,128)(2,1)}) custom-call(bf16[256,1024]{1,0:T(8,128)(2,1)} %bitcast.12, f32[1,1024]{1,0:T(1,128)} %bitcast.17, bf16[1024,256]{1,0:T(8,128)(2,1)} %w_key.3, bf16[1024,256]{1,0:T(8,128)(2,1)} %w_value.3), custom_call_target="tpu_custom_call" | custom-call | flops 268435456 | bytes 1048576 | tf_op jit(solution)/shard_map/pallas_call | solution.py:378
  4.0 7.9 %all-to-all-start = ((bf16[8,256,256]{2,1,0:T(8,128)(2,1)}), bf16[8,256,256]{2,1,0:T(8,128)(2,1)}, u32[]{:S(2)}, u32[]{:S(2)}) async-start(bf16[8,256,256]{2,1,0:T(8,128)(2,1)} %get-tuple-element.32), calls=%async_computation | async-start | bytes 2097152 | tf_op jit(solution)/shard_map/all_to_all | solution.py:470
  13.2 0.7 stack.16.info
  13.9 5.9 %shard_map.137 = (bf16[3,256,1024]{2,1,0:T(8,128)(2,1)}, bf16[4,2,8,8,256]{4,3,2,1,0:T(8,128)(2,1)}, bf16[4,2,8,8,256]{4,3,2,1,0:T(8,128)(2,1)}) custom-call(s32[5]{0:T(128)} %stack.16.info, bf16[256,1024]{1,0:T(8,128)(2,1)} %get-tuple-element.30.hidden, bf16[256,1024]{1,0:T(8,128)(2,1)} %bitcast.14, bf16[1024,1024]{1,0:T(8,128)(2,1)} %w_query.3, ...), custom_call_target="tpu_custom_call" | custom-call | flops 1073741824 | bytes 1048576 | tf_op jit(solution)/shard_map/pallas_call | solution.py:378
  19.8 0.0 collective-permute-start
  19.8 8.2 %all-to-all-done.keys = bf16[8,256,256]{2,1,0:T(8,128)(2,1)} async-done(((bf16[8,256,256]{2,1,0:T(8,128)(2,1)}), bf16[8,256,256]{2,1,0:T(8,128)(2,1)}, u32[]{:S(2)}, u32[]{:S(2)}) %all-to-all-start) | async-done | bytes 1048608 | tf_op jit(solution)/shard_map/all_to_all | solution.py:470
  28.0 4.2 %all-to-all-start.1 = ((bf16[8,256,256]{2,1,0:T(8,128)(2,1)}), bf16[8,256,256]{2,1,0:T(8,128)(2,1)}, u32[]{:S(2)}, u32[]{:S(2)}) async-start(bf16[8,256,256]{2,1,0:T(8,128)(2,1)} %get-tuple-element.33), calls=%async_computation.1 | async-start | bytes 2097152 | tf_op jit(solution)/shard_map/all_to_all | solution.py:470
  32.2 0.0 collective-permute-done.pair
  32.2 4.2 %shard_map.138.mine = f32[2,2,1024]{2,1,0:T(2,128)} custom-call(s32[5]{0:T(128)} %stack.16.info, bf16[3,256,1024]{2,1,0:T(8,128)(2,1)} %get-tuple-element.31.own, bf16[3,256,1024]{2,1,0:T(8,128)(2,1)} %collective-permute-done.pair, bf16[8,256,256]{2,1,0:T(8,128)(2,1)} %all-to-all-done.keys), custom_call_target="tpu_custom_call" | custom-call | flops 2147483648 | bytes 1048576 | tf_op jit(solution)/shard_map/pallas_call | solution.py:378
  36.4 0.0 collective-permute-start.1
  36.4 11.3 %all-to-all-done.1.values = bf16[8,256,256]{2,1,0:T(8,128)(2,1)} async-done(((bf16[8,256,256]{2,1,0:T(8,128)(2,1)}), bf16[8,256,256]{2,1,0:T(8,128)(2,1)}, u32[]{:S(2)}, u32[]{:S(2)}) %all-to-all-start.1) | async-done | bytes 1048608 | tf_op jit(solution)/shard_map/all_to_all | solution.py:470
  47.7 0.0 collective-permute-done.1.other
  47.7 11.7 %shard_map.139 = (bf16[2,1024,256]{2,1,0:T(8,128)(2,1)}, bf16[8,256,256]{2,1,0:T(8,128)(2,1)}, bf16[2048,2048]{1,0:T(8,128)(2,1)}) custom-call(s32[5]{0:T(128)} %stack.16.info, bf16[3,256,1024]{2,1,0:T(8,128)(2,1)} %get-tuple-element.31.own, bf16[3,256,1024]{2,1,0:T(8,128)(2,1)} %collective-permute-done.pair, f32[2,2,1024]{2,1,0:T(2,128)} %shard_map.138.mine, ...), custom_call_target="tpu_custom_call" | custom-call | flops 6442450944 | bytes 1048576 | tf_op jit(solution)/shard_map/pallas_call | solution.py:378
  59.4 0.1 collective-permute-start.2
  59.5 7.3 %all-to-all-start.3 = ((bf16[8,256,256]{2,1,0:T(8,128)(2,1)}), bf16[8,256,256]{2,1,0:T(8,128)(2,1)}, u32[]{:S(2)}, u32[]{:S(2)}) async-start(bf16[8,256,256]{2,1,0:T(8,128)(2,1)} %get-tuple-element.43), calls=%async_computation.3 | async-start | bytes 2097152 | tf_op jit(solution)/shard_map/all_to_all | solution.py:470
  66.8 0.0 collective-permute-done.2.other
  66.8 13.1 %shard_map.140 = (bf16[4,2,8,8,256]{4,3,2,1,0:T(8,128)(2,1)}, bf16[4,2,8,8,256]{4,3,2,1,0:T(8,128)(2,1)}, bf16[8,256,256]{2,1,0:T(8,128)(2,1)}, bf16[2,256,1024]{2,1,0:T(8,128)(2,1)}) custom-call(s32[5]{0:T(128)} %stack.16.info, bf16[3,256,1024]{2,1,0:T(8,128)(2,1)} %get-tuple-element.31.own, bf16[3,256,1024]{2,1,0:T(8,128)(2,1)} %collective-permute-done.pair, ...), custom_call_target="tpu_custom_call" | custom-call | flops 6442450944 | bytes 1048576 | tf_op jit(solution)/shard_map/pallas_call | solution.py:378
  79.9 0.1 collective-permute-start.4
  80.0 4.2 %all-to-all-done.3.dv_parts = bf16[8,256,256]{2,1,0:T(8,128)(2,1)} async-done(((bf16[8,256,256]{2,1,0:T(8,128)(2,1)}), bf16[8,256,256]{2,1,0:T(8,128)(2,1)}, u32[]{:S(2)}, u32[]{:S(2)}) %all-to-all-start.3) | async-done | bytes 1048608 | tf_op jit(solution)/shard_map/all_to_all | solution.py:470
  84.2 6.0 %all-to-all-start.2 = ((bf16[8,256,256]{2,1,0:T(8,128)(2,1)}), bf16[8,256,256]{2,1,0:T(8,128)(2,1)}, u32[]{:S(2)}, u32[]{:S(2)}) async-start(bf16[8,256,256]{2,1,0:T(8,128)(2,1)} %get-tuple-element.42), calls=%async_computation.2 | async-start | bytes 2097152 | tf_op jit(solution)/shard_map/all_to_all | solution.py:470
  90.2 0.2 collective-permute-start.3
  90.4 17.2 %all-to-all-done.2.dk_parts = bf16[8,256,256]{2,1,0:T(8,128)(2,1)} async-done(((bf16[8,256,256]{2,1,0:T(8,128)(2,1)}), bf16[8,256,256]{2,1,0:T(8,128)(2,1)}, u32[]{:S(2)}, u32[]{:S(2)}) %all-to-all-start.2) | async-done | bytes 1048608 | tf_op jit(solution)/shard_map/all_to_all | solution.py:470
  107.6 2.5 %shard_map.142.dkv = bf16[256,512]{1,0:T(8,128)(2,1)} custom-call(bf16[8,256,256]{2,1,0:T(8,128)(2,1)} %all-to-all-done.2.dk_parts, bf16[8,256,256]{2,1,0:T(8,128)(2,1)} %all-to-all-done.3.dv_parts), custom_call_target="tpu_custom_call" | custom-call | flops 1073741824 | bytes 1048576 | tf_op jit(solution)/shard_map/pallas_call | solution.py:378
  110.2 0.0 collective-permute-start.8
  110.2 0.0 collective-permute-done.3.ht_pair
  110.2 0.0 collective-permute-done.4.dq_other
  110.2 5.4 %shard_map.141 = (bf16[256,1024]{1,0:T(8,128)(2,1)}, bf16[128,4096]{1,0:T(8,128)(2,1)}, f32[128,1024]{1,0:T(8,128)}, bf16[128,1024]{1,0:T(8,128)(2,1)}, bf16[128...) custom-call(s32[5]{0:T(128)} %stack.16.info, bf16[4,2,8,8,256]{4,3,2,1,0:T(8,128)(2,1)} %get-tuple-element.36.at_own, ...), custom_call_target="tpu_custom_call" | custom-call | flops 1073741824 | bytes 1048576 | tf_op jit(solution)/shard_map/pallas_call | solution.py:378
  115.5 0.0 collective-permute-start.5
  115.5 3.1 %collective-permute-start.6 = (bf16[128,1024]{1,0:T(8,128)(2,1)}, bf16[128,1024]{1,0:T(8,128)(2,1)}, u32[]{:S(2)}, u32[]{:S(2)}) collective-permute-start(bf16[128,1024]{1,0:T(8,128)(2,1)} %get-tuple-element.46), channel_id=1, source_target_pairs={{0,32},{16,48},{32,0},{48,16},{64,96},{80,112},{96,64},{112,80},{1... | collective-permute-start | bytes 786440 | tf_op jit(solution)/shard_map/ppermute | solution.py:462
  118.6 2.5 %collective-permute-start.7 = (bf16[128,1024]{1,0:T(8,128)(2,1)}, bf16[128,1024]{1,0:T(8,128)(2,1)}, u32[]{:S(2)}, u32[]{:S(2)}) collective-permute-start(bf16[128,1024]{1,0:T(8,128)(2,1)} %get-tuple-element.47), channel_id=1, source_target_pairs={{0,48},{16,0},{32,16},{48,32},{64,112},{80,64},{96,80},{112,96},{1... | collective-permute-start | bytes 786440 | tf_op jit(solution)/shard_map/ppermute | solution.py:462
  121.2 0.0 collective-permute-done.8.dkv_pair
  121.2 4.8 %collective-permute-done.5.one = bf16[128,1024]{1,0:T(8,128)(2,1)} collective-permute-done((bf16[128,1024]{1,0:T(8,128)(2,1)}, bf16[128,1024]{1,0:T(8,128)(2,1)}, u32[]{:S(2)}, u32[]{:S(2)}) %collective-permute-start.5) | collective-permute-done | bytes 262176 | tf_op jit(solution)/shard_map/ppermute | solution.py:462
  125.9 5.5 %collective-permute-done.6.two = bf16[128,1024]{1,0:T(8,128)(2,1)} collective-permute-done((bf16[128,1024]{1,0:T(8,128)(2,1)}, bf16[128,1024]{1,0:T(8,128)(2,1)}, u32[]{:S(2)}, u32[]{:S(2)}) %collective-permute-start.6) | collective-permute-done | bytes 262176 | tf_op jit(solution)/shard_map/ppermute | solution.py:462
  131.4 0.6 collective-permute-done.7.three
  132.0 3.8 %shard_map.144 = bf16[128,7168]{1,0:T(8,128)(2,1)} custom-call(s32[5]{0:T(128)} %stack.16.info, f32[128,1024]{1,0:T(8,128)} %get-tuple-element.44.base, bf16[128,1024]{1,0:T(8,128)(2,1)} %collective-permute-done.5.one, bf16[128,1024]{1,0:T(8,128)(2,1)} %collective-permute-done.6.two, bf16[128,1024]{1,0:T(8,128)(2,1)} %collective-permute-done.7.three, ...), custom_call_target="tpu_custom_call" | custom-call | flops 1073741824 | bytes 1048576 | tf_op jit(solution)/shard_map/pallas_call | solution.py:378
  135.8 31.1 %all_to_all.30.parts = bf16[16,8,7168]{2,1,0:T(8,128)(2,1)} all-to-all(bf16[16,8,7168]{2,1,0:T(8,128)(2,1)} %bitcast.11), channel_id=1, replica_groups={{0,2,4,6,8,10,12,14,64,66,68,70,72,74,76,78},{1,3,5,7,9,11,13,15,65,67,..., dimensions={0} | all-to-all | bytes 3670016 | tf_op jit(solution)/shard_map/all_to_all | solution.py:480
  166.9 2.7 %shard_map.145 = bf16[8,8,7168]{2,1,0:T(8,128)(2,1)} custom-call(bf16[16,8,7168]{2,1,0:T(8,128)(2,1)} %all_to_all.30.parts), custom_call_target="tpu_custom_call" | custom-call | flops 1073741824 | bytes 1048576 | tf_op jit(solution)/shard_map/pallas_call | solution.py:378
  169.6 4.2 %all-to-all-start.5 = ((bf16[8,8,7168]{2,1,0:T(8,128)(2,1)}), bf16[8,8,7168]{2,1,0:T(8,128)(2,1)}, u32[]{:S(2)}, u32[]{:S(2)}) async-start(bf16[8,8,7168]{2,1,0:T(8,128)(2,1)} %shard_map.145), calls=%async_computation.5 | async-start | bytes 1835008 | tf_op jit(solution)/shard_map/all_to_all | solution.py:554
  173.9 1.3 dynamic-slice_bitcast_fusion.gain
  175.2 1.4 constant_dynamic-slice_fusion
  176.6 1.6 constant_dynamic-slice_fusion.2.w_query
  178.2 4.4 %shard_map.143 = bf16[256,1024]{1,0:T(8,128)(2,1)} custom-call(bf16[256,1024]{1,0:T(8,128)(2,1)} %bitcast.13, bf16[256,1024]{1,0:T(8,128)(2,1)} %bitcast.15, f32[1,1024]{1,0:T(1,128)} %bitcast.18, bf16[256,1024]{1,0:T(8,128)(2,1)} %get-tuple-element.41.dq, bf16[256,512]{1,0:T(8,128)(2,1)} %shard_map.142.dkv, bf16[1024,1024]{1,0:T(8,128)(2,1)} %w_query.3, ...), custom_call_target="tpu_custom_call" | custom-call | flops 805306368 | bytes 1048576 | tf_op jit(solution)/shard_map/pallas_call | solution.py:378
  182.6 4.1 %all-to-all-done.5.shared = bf16[8,8,7168]{2,1,0:T(8,128)(2,1)} async-done(((bf16[8,8,7168]{2,1,0:T(8,128)(2,1)}), bf16[8,8,7168]{2,1,0:T(8,128)(2,1)}, u32[]{:S(2)}, u32[]{:S(2)}) %all-to-all-start.5) | async-done | bytes 917536 | tf_op jit(solution)/shard_map/all_to_all | solution.py:554
  186.7 2.2 %shard_map.146 = (f32[64,1024]{1,0:T(8,128)}, f32[64,256]{1,0:T(8,128)}, f32[64,256]{1,0:T(8,128)}, f32[64,1024]{1,0:T(8,128)}, f32[1,64]{1,0:T(1,128)}) custom-call(bf16[8,8,7168]{2,1,0:T(8,128)(2,1)} %all-to-all-done.5.shared, bf16[64,1024]{1,0:T(8,128)(2,1)} %constant_dynamic-slice_fusion.2.w_query, bf16[64,256]{1,0:T(8,128)(2,1)} %get-tuple-element.55.w_key, ...), custom_call_target="tpu_custom_call" | custom-call | flops 1073741824 | bytes 1048576 | tf_op jit(solution)/shard_map/pallas_call | solution.py:378
Async XLA Ops:
  4.0 23.9 %all-to-all-start = ((bf16[8,256,256]{2,1,0:T(8,128)(2,1)}), bf16[8,256,256]{2,1,0:T(8,128)(2,1)}, u32[]{:S(2)}, u32[]{:S(2)}) async-start(bf16[8,256,256]{2,1,0:T(8,128)(2,1)} %get-tuple-element.32), calls=%async_computation | async-start | bytes 2097152 | tf_op jit(solution)/shard_map/all_to_all | solution.py:470
  19.8 12.5 %collective-permute-start = (bf16[3,256,1024]{2,1,0:T(8,128)(2,1)}, bf16[3,256,1024]{2,1,0:T(8,128)(2,1)}, u32[]{:S(2)}, u32[]{:S(2)}) collective-permute-start(bf16[3,256,1024]{2,1,0:T(8,128)(2,1)} %get-tuple-element.31.own), channel_id=1, source_target_pairs={{0,1},{1,0},{2,3},{3,2},{4,5},{5,4},{6,7},{7,6},{8,9},{9,8},{10,11... | collective-permute-start | bytes 4718600 | tf_op jit(solution)/shard_map/ppermute | solution.py:457
  28.0 19.8 %all-to-all-start.1 = ((bf16[8,256,256]{2,1,0:T(8,128)(2,1)}), bf16[8,256,256]{2,1,0:T(8,128)(2,1)}, u32[]{:S(2)}, u32[]{:S(2)}) async-start(bf16[8,256,256]{2,1,0:T(8,128)(2,1)} %get-tuple-element.33), calls=%async_computation.1 | async-start | bytes 2097152 | tf_op jit(solution)/shard_map/all_to_all | solution.py:470
  36.4 11.3 %collective-permute-start.1 = (f32[2,2,1024]{2,1,0:T(2,128)}, f32[2,2,1024]{2,1,0:T(2,128)}, u32[]{:S(2)}, u32[]{:S(2)}) collective-permute-start(f32[2,2,1024]{2,1,0:T(2,128)} %shard_map.138.mine), channel_id=1, source_target_pairs={{0,1},{1,0},{2,3},{3,2},{4,5},{5,4},{6,7},{7,6},{8,9},{9,8},{10,11... | collective-permute-start | bytes 49160 | tf_op jit(solution)/shard_map/ppermute | solution.py:457
  59.4 7.4 %collective-permute-start.2 = (bf16[2,1024,256]{2,1,0:T(8,128)(2,1)}, bf16[2,1024,256]{2,1,0:T(8,128)(2,1)}, u32[]{:S(2)}, u32[]{:S(2)}) collective-permute-start(bf16[2,1024,256]{2,1,0:T(8,128)(2,1)} %get-tuple-element.34.mine), channel_id=1, source_target_pairs={{0,1},{1,0},{2,3},{3,2},{4,5},{5,4},{6,7},{7,6},{8,9},{9,8},{10,11... | collective-permute-start | bytes 3145736 | tf_op jit(solution)/shard_map/ppermute | solution.py:457
  59.5 24.7 %all-to-all-start.3 = ((bf16[8,256,256]{2,1,0:T(8,128)(2,1)}), bf16[8,256,256]{2,1,0:T(8,128)(2,1)}, u32[]{:S(2)}, u32[]{:S(2)}) async-start(bf16[8,256,256]{2,1,0:T(8,128)(2,1)} %get-tuple-element.43), calls=%async_computation.3 | async-start | bytes 2097152 | tf_op jit(solution)/shard_map/all_to_all | solution.py:470
  79.9 30.3 %collective-permute-start.4 = (bf16[2,256,1024]{2,1,0:T(8,128)(2,1)}, bf16[2,256,1024]{2,1,0:T(8,128)(2,1)}, u32[]{:S(2)}, u32[]{:S(2)}) collective-permute-start(bf16[2,256,1024]{2,1,0:T(8,128)(2,1)} %get-tuple-element.40.dq_mine), channel_id=1, source_target_pairs={{0,1},{1,0},{2,3},{3,2},{4,5},{5,4},{6,7},{7,6},{8,9},{9,8},{10,11... | collective-permute-start | bytes 3145736 | tf_op jit(solution)/shard_map/ppermute | solution.py:457
  84.2 23.4 %all-to-all-start.2 = ((bf16[8,256,256]{2,1,0:T(8,128)(2,1)}), bf16[8,256,256]{2,1,0:T(8,128)(2,1)}, u32[]{:S(2)}, u32[]{:S(2)}) async-start(bf16[8,256,256]{2,1,0:T(8,128)(2,1)} %get-tuple-element.42), calls=%async_computation.2 | async-start | bytes 2097152 | tf_op jit(solution)/shard_map/all_to_all | solution.py:470
  90.2 19.9 %collective-permute-start.3 = (bf16[4,2,8,8,256]{4,3,2,1,0:T(8,128)(2,1)}, bf16[4,2,8,8,256]{4,3,2,1,0:T(8,128)(2,1)}, u32[]{:S(2)}, u32[]{:S(2)}) collective-permute-start(bf16[4,2,8,8,256]{4,3,2,1,0:T(8,128)(2,1)} %get-tuple-element.39), channel_id=1, source_target_pairs={{0,1},{1,0},{2,3},{3,2},{4,5},{5,4},{6,7},{7,6},{8,9},{9,8},{10,11... | collective-permute-start | bytes 786440 | tf_op jit(solution)/shard_map/ppermute | solution.py:457
  110.2 11.0 %collective-permute-start.8 = (bf16[256,512]{1,0:T(8,128)(2,1)}, bf16[256,512]{1,0:T(8,128)(2,1)}, u32[]{:S(2)}, u32[]{:S(2)}) collective-permute-start(bf16[256,512]{1,0:T(8,128)(2,1)} %shard_map.142.dkv), channel_id=1, source_target_pairs={{0,1},{1,0},{2,3},{3,2},{4,5},{5,4},{6,7},{7,6},{8,9},{9,8},{10,11... | collective-permute-start | bytes 786440 | tf_op jit(solution)/shard_map/ppermute | solution.py:457
  115.5 10.4 %collective-permute-start.5 = (bf16[128,1024]{1,0:T(8,128)(2,1)}, bf16[128,1024]{1,0:T(8,128)(2,1)}, u32[]{:S(2)}, u32[]{:S(2)}) collective-permute-start(bf16[128,1024]{1,0:T(8,128)(2,1)} %get-tuple-element.45), channel_id=1, source_target_pairs={{0,16},{16,32},{32,48},{48,0},{64,80},{80,96},{96,112},{112,64},{1... | collective-permute-start | bytes 786440 | tf_op jit(solution)/shard_map/ppermute | solution.py:462
  115.5 15.9 %collective-permute-start.6 = (bf16[128,1024]{1,0:T(8,128)(2,1)}, bf16[128,1024]{1,0:T(8,128)(2,1)}, u32[]{:S(2)}, u32[]{:S(2)}) collective-permute-start(bf16[128,1024]{1,0:T(8,128)(2,1)} %get-tuple-element.46), channel_id=1, source_target_pairs={{0,32},{16,48},{32,0},{48,16},{64,96},{80,112},{96,64},{112,80},{1... | collective-permute-start | bytes 786440 | tf_op jit(solution)/shard_map/ppermute | solution.py:462
  118.6 13.4 %collective-permute-start.7 = (bf16[128,1024]{1,0:T(8,128)(2,1)}, bf16[128,1024]{1,0:T(8,128)(2,1)}, u32[]{:S(2)}, u32[]{:S(2)}) collective-permute-start(bf16[128,1024]{1,0:T(8,128)(2,1)} %get-tuple-element.47), channel_id=1, source_target_pairs={{0,48},{16,0},{32,16},{48,32},{64,112},{80,64},{96,80},{112,96},{1... | collective-permute-start | bytes 786440 | tf_op jit(solution)/shard_map/ppermute | solution.py:462
  169.6 17.1 %all-to-all-start.5 = ((bf16[8,8,7168]{2,1,0:T(8,128)(2,1)}), bf16[8,8,7168]{2,1,0:T(8,128)(2,1)}, u32[]{:S(2)}, u32[]{:S(2)}) async-start(bf16[8,8,7168]{2,1,0:T(8,128)(2,1)} %shard_map.145), calls=%async_computation.5 | async-start | bytes 1835008 | tf_op jit(solution)/shard_map/all_to_all | solution.py:554

commit v6 on v5

--- a/solution.py
+++ b/solution.py
@@ -276,17 +276,18 @@
 
 
 def terms_kernel(
-    info, at_own, at_pair, own, pair, ht_own, ht_pair, dq_mine, dq_other,
-    dq, query_terms, base, *parts,
+    info, at_own, at_pair, own, pair, ht_own, ht_pair, dq_mine, dq_other, dq, base, *parts
 ):
-    for step, out in enumerate((base, *parts)):
-        out[...] = step_terms((at_own, at_pair), (own[2], pair[2]), step).astype(out.dtype)
     rights = [
         (dq_mine[half].astype(jnp.float32) + dq_other[1 - half].astype(jnp.float32)).astype(dq.dtype)
         for half in range(2)
     ]
     dq[...] = rights[0]
-    direct_terms(info, (ht_own, ht_pair), rights, query_terms, 0)
+    for step, out in enumerate((base, *parts)):
+        g_out = step_terms((at_own, at_pair), (own[2], pair[2]), step)
+        out[:, pl.ds(0, g_out.shape[1])] = g_out.astype(out.dtype)
+        g_query = step_terms((ht_own, ht_pair), rights, step)
+        out[:, pl.ds(g_out.shape[1], g_query.shape[1])] = g_query.astype(out.dtype)
 
 
 def rows_kernel(dk_parts, dv_parts, out):
@@ -297,24 +298,34 @@
         out[:, pl.ds(at, HS)] = total.astype(out.dtype)
 
 
-def collect_kernel(info, base, one, two, three, query_terms, ht_own, ht_pair, dkv, dkv_pair, out):
+def kv_kernel(info, ht_own, ht_pair, dkv, dkv_pair, out):
+    direct_terms(info, (ht_own, ht_pair), (dkv[...], dkv_pair[...]), out, 0)
+
+
+def collect_kernel(base, one, two, three, out):
     total = base[...]
     for arrived in (one, two, three):
         total = total + arrived[...].astype(jnp.float32)
-    wide = total.shape[1]
-    out[:, pl.ds(0, wide)] = total.astype(out.dtype)
-    out[:, pl.ds(wide, query_terms.shape[1])] = query_terms[...]
-    rights = (dkv[...], dkv_pair[...])
-    direct_terms(info, (ht_own, ht_pair), rights, out, wide + query_terms.shape[1])
-
-
-def spread_kernel(parts, out):
+    out[...] = total.astype(out.dtype)
+
+
+def added_parts(parts):
     total = parts[0].astype(jnp.float32)
     for n in range(1, parts.shape[0]):
         total = total + parts[n].astype(jnp.float32)
-    total = total.astype(out.dtype)
+    return total.astype(jnp.bfloat16)
+
+
+def total_kernel(parts, out):
+    out[...] = added_parts(parts)
+
+
+def spread_kernel(parts, kv, out):
+    total = added_parts(parts)
+    wide = total.shape[1]
     for n in range(out.shape[0]):
-        out[n] = total
+        out[n, :, pl.ds(0, wide)] = total
+        out[n, :, pl.ds(wide, kv.shape[1])] = kv[...]
 
 
 def weights_kernel(steps, shared, w_query, w_key, w_value, gain, d_query, d_key, d_value, d_out, d_gain):
@@ -325,15 +336,11 @@
         outer, x = place // steps, place % steps
         rows = slice(place * size, (place + 1) * size)
         d_out[rows, :] = shared[place, :, pl.ds(0, wide)].astype(jnp.float32)
-
-        def added(at, width):
-            total = 0.0
-            for source in range(steps):
-                total = total + shared[outer * steps + source, :, pl.ds(at, width)].astype(jnp.float32)
-            return total
-
-        query = added(wide + x * heads_wide, heads_wide)
-        kv = added(wide + steps * heads_wide + x * 2 * HS, 2 * HS)
+        query = shared[place, :, pl.ds(wide, heads_wide)].astype(jnp.float32)
+        kv = 0.0
+        for source in range(steps):
+            at = pl.ds(wide + heads_wide + x * 2 * HS, 2 * HS)
+            kv = kv + shared[outer * steps + source, :, at].astype(jnp.float32)
         d_query[rows, :] = query
         d_key[rows, :] = kv[:, :HS]
         d_value[rows, :] = kv[:, HS:]
@@ -477,6 +484,7 @@
         for x in range(X)
         for core in range(CORES)
     ]
+    value = value.reshape(dp // X * (blk // CORES), -1, value.shape[1])
     return lax.all_to_all(value, ("dp", "blk"), 0, 0, tiled=True, axis_index_groups=groups)
 
 
@@ -524,13 +532,12 @@
     dq_other = swap_cores(dq_mine)
     dk_parts = exchange_chips(dk)
     rows = outer * chips * size
-    d_query_rows, query_terms, base, *parts = call(
+    d_query_rows, base, *parts = call(
         terms_kernel,
         (
             shape(tok, heads_wide),
-            shape(rows, X * heads_wide),
-            shape(rows, wide, dtype=jnp.float32),
-            *[shape(rows, wide)] * (X - 1),
+            shape(rows, wide + heads_wide, dtype=jnp.float32),
+            *[shape(rows, wide + heads_wide)] * (X - 1),
         ),
         (info, at_own, at_pair, own, pair, ht_own, ht_pair, dq_mine, dq_other),
         8 * X * rows * wide * tok,
@@ -541,16 +548,19 @@
         arrived.append(send_along_x(terms, step))
     d_kv_rows = call(rows_kernel, shape(tok, 2 * HS), (dk_parts, dv_parts), 1 << 30)
     d_kv_pair = swap_cores(d_kv_rows)
-    total = wide + X * (heads_wide + 2 * HS)
-    terms = call(
-        collect_kernel,
-        shape(rows, total),
-        (info, base, *arrived, query_terms, ht_own, ht_pair, d_kv_rows, d_kv_pair),
+    kv_terms = call(
+        kv_kernel,
+        shape(rows, X * 2 * HS),
+        (info, ht_own, ht_pair, d_kv_rows, d_kv_pair),
         1 << 30,
         smem=1,
     )
-    parts = exchange_plane(terms.reshape(outer * chips, size, total))
-    copies = call(spread_kernel, shape(share, size, total), (parts,), 1 << 30)
+    kv_parts = exchange_plane(kv_terms)
+    terms = call(collect_kernel, shape(rows, wide + heads_wide), (base, *arrived), 1 << 30)
+    parts = exchange_plane(terms)
+    kv_total = call(total_kernel, shape(size, X * 2 * HS), (kv_parts,), 1 << 30)
+    total = wide + heads_wide + X * 2 * HS
+    copies = call(spread_kernel, shape(share, size, total), (parts, kv_total), 1 << 30)
     shared = lax.all_to_all(copies, "dp", 0, 0, tiled=True)
     d_in = call(
         finish_kernel,

time: 190 us -> 179 us (0.942)
  blocking collectives: 31.1 us -> 0 us
  starting transfers between devices: 35.7 us -> 47.2 us
  waiting for transfers between devices: 55.9 us -> 63.1 us
    all_to_all x1 -> x0, blocking collectives: 31.1 us -> none  [exchange_plane(): lax.all_to_all(value, ('dp', 'blk'), 0, 0, tiled=True, axis_index_groups=...]
    all_to_all x0 -> x2, starting transfers between devices: none -> 11.2 us  [exchange_plane(): lax.all_to_all(value, ('dp', 'blk'), 0, 0, tiled=True, axis_index_groups=...]
    all_to_all x0 -> x2, waiting for transfers between devices: none -> 9.29 us  [exchange_plane(): lax.all_to_all(value, ('dp', 'blk'), 0, 0, tiled=True, axis_index_groups=...]
    ppermute x3, waiting for transfers between devices: 10.8 us -> 15 us  [send_along_x(): lax.ppermute(value, 'dp', [(i, i // X * X + (i + step) % X) for i in rang...]
    all_to_all x1, waiting for transfers between devices: 4.12 us -> 0.01 us  [whole(): shared = lax.all_to_all(copies, 'dp', 0, 0, tiled=True)]
    all_to_all x4, waiting for transfers between devices: 41 us -> 38.8 us  [exchange_chips(): lax.all_to_all(value, 'blk', 0, 0, tiled=True, axis_index_groups=groups)]
    pallas_call x11 -> x13, Pallas kernels: 59.2 us -> 61 us  [call(): pl.pallas_call(body, out_shape=outs, in_specs=specs, out_specs=out_specs,...]
  transfers between devices with their start and end apart: 14 -> 16, of which waited for: 8 -> 8; matrix products, arithmetic and copies ran while one was open for 3% -> 3% of each run, Pallas kernels for 19% -> 24%
where the time goes in v6:
time: 179 us; the launch traced here: 178 us
  waiting for transfers between devices  63.1 us (35%)
  Pallas kernels  61 us (34%)
  starting transfers between devices  47.2 us (26%)
  local copies, waits for them, and re-layouts  4.89 us (3%)
  between operations  2.04 us (1%)
    pallas_call x13, Pallas kernels, call(): pl.pallas_call(body, out_shape=outs, in_specs=specs, out_specs=out_specs,...  61 us
    all_to_all x4, waiting for transfers between devices, exchange_chips(): lax.all_to_all(value, 'blk', 0, 0, tiled=True, axis_index_groups=groups)  38.8 us
    all_to_all x4, starting transfers between devices, exchange_chips(): lax.all_to_all(value, 'blk', 0, 0, tiled=True, axis_index_groups=groups)  25.4 us
    ppermute x3, waiting for transfers between devices, send_along_x(): lax.ppermute(value, 'dp', [(i, i // X * X + (i + step) % X) for i in rang...  15 us
    all_to_all x2, starting transfers between devices, exchange_plane(): lax.all_to_all(value, ('dp', 'blk'), 0, 0, tiled=True, axis_index_groups=...  11.2 us
    all_to_all x2, waiting for transfers between devices, exchange_plane(): lax.all_to_all(value, ('dp', 'blk'), 0, 0, tiled=True, axis_index_groups=...  9.29 us
    ppermute x3, starting transfers between devices, send_along_x(): lax.ppermute(value, 'dp', [(i, i // X * X + (i + step) % X) for i in rang...  5.91 us
    all_to_all x1, starting transfers between devices, whole(): shared = lax.all_to_all(copies, 'dp', 0, 0, tiled=True)  4.14 us
  transfers between devices with their start and end apart: 16, of which 8 were waited for; matrix products, arithmetic and copies ran while one was open for 3% of the time, Pallas kernels for 24%

profile of v6, /device:TPU:0, one launch (start us, length us, event | category | flops | bytes accessed | tf_op | source)
XLA Modules:
  0.0 178.2 jit_solution(14762544800169340025)
XLA Ops:
  0.6 3.4 %shard_map.136 = (bf16[256,1024]{1,0:T(8,128)(2,1)}, bf16[8,256,256]{2,1,0:T(8,128)(2,1)}, bf16[8,256,256]{2,1,0:T(8,128)(2,1)}) custom-call(bf16[256,1024]{1,0:T(8,128)(2,1)} %bitcast.12, f32[1,1024]{1,0:T(1,128)} %bitcast.19, bf16[1024,256]{1,0:T(8,128)(2,1)} %w_key.3, bf16[1024,256]{1,0:T(8,128)(2,1)} %w_value.3), custom_call_target="tpu_custom_call" | custom-call | flops 268435456 | bytes 1048576 | tf_op jit(solution)/shard_map/pallas_call | solution.py:385
  4.0 7.9 %all-to-all-start = ((bf16[8,256,256]{2,1,0:T(8,128)(2,1)}), bf16[8,256,256]{2,1,0:T(8,128)(2,1)}, u32[]{:S(2)}, u32[]{:S(2)}) async-start(bf16[8,256,256]{2,1,0:T(8,128)(2,1)} %get-tuple-element.31), calls=%async_computation | async-start | bytes 2097152 | tf_op jit(solution)/shard_map/all_to_all | solution.py:477
  13.2 0.6 stack.16.info
  13.8 5.9 %shard_map.137 = (bf16[3,256,1024]{2,1,0:T(8,128)(2,1)}, bf16[4,2,8,8,256]{4,3,2,1,0:T(8,128)(2,1)}, bf16[4,2,8,8,256]{4,3,2,1,0:T(8,128)(2,1)}) custom-call(s32[5]{0:T(128)} %stack.16.info, bf16[256,1024]{1,0:T(8,128)(2,1)} %get-tuple-element.29.hidden, bf16[256,1024]{1,0:T(8,128)(2,1)} %bitcast.14, bf16[1024,1024]{1,0:T(8,128)(2,1)} %w_query.3, ...), custom_call_target="tpu_custom_call" | custom-call | flops 1073741824 | bytes 1048576 | tf_op jit(solution)/shard_map/pallas_call | solution.py:385
  19.7 0.0 collective-permute-start
  19.7 8.3 %all-to-all-done.keys = bf16[8,256,256]{2,1,0:T(8,128)(2,1)} async-done(((bf16[8,256,256]{2,1,0:T(8,128)(2,1)}), bf16[8,256,256]{2,1,0:T(8,128)(2,1)}, u32[]{:S(2)}, u32[]{:S(2)}) %all-to-all-start) | async-done | bytes 1048608 | tf_op jit(solution)/shard_map/all_to_all | solution.py:477
  28.0 4.2 %all-to-all-start.1 = ((bf16[8,256,256]{2,1,0:T(8,128)(2,1)}), bf16[8,256,256]{2,1,0:T(8,128)(2,1)}, u32[]{:S(2)}, u32[]{:S(2)}) async-start(bf16[8,256,256]{2,1,0:T(8,128)(2,1)} %get-tuple-element.32), calls=%async_computation.1 | async-start | bytes 2097152 | tf_op jit(solution)/shard_map/all_to_all | solution.py:477
  32.2 0.0 collective-permute-done.pair
  32.2 4.2 %shard_map.138.mine = f32[2,2,1024]{2,1,0:T(2,128)} custom-call(s32[5]{0:T(128)} %stack.16.info, bf16[3,256,1024]{2,1,0:T(8,128)(2,1)} %get-tuple-element.30.own, bf16[3,256,1024]{2,1,0:T(8,128)(2,1)} %collective-permute-done.pair, bf16[8,256,256]{2,1,0:T(8,128)(2,1)} %all-to-all-done.keys), custom_call_target="tpu_custom_call" | custom-call | flops 2147483648 | bytes 1048576 | tf_op jit(solution)/shard_map/pallas_call | solution.py:385
  36.4 0.0 collective-permute-start.1
  36.4 11.3 %all-to-all-done.1.values = bf16[8,256,256]{2,1,0:T(8,128)(2,1)} async-done(((bf16[8,256,256]{2,1,0:T(8,128)(2,1)}), bf16[8,256,256]{2,1,0:T(8,128)(2,1)}, u32[]{:S(2)}, u32[]{:S(2)}) %all-to-all-start.1) | async-done | bytes 1048608 | tf_op jit(solution)/shard_map/all_to_all | solution.py:477
  47.7 0.0 collective-permute-done.1.other
  47.7 11.7 %shard_map.139 = (bf16[2,1024,256]{2,1,0:T(8,128)(2,1)}, bf16[8,256,256]{2,1,0:T(8,128)(2,1)}, bf16[2048,2048]{1,0:T(8,128)(2,1)}) custom-call(s32[5]{0:T(128)} %stack.16.info, bf16[3,256,1024]{2,1,0:T(8,128)(2,1)} %get-tuple-element.30.own, bf16[3,256,1024]{2,1,0:T(8,128)(2,1)} %collective-permute-done.pair, f32[2,2,1024]{2,1,0:T(2,128)} %shard_map.138.mine, ...), custom_call_target="tpu_custom_call" | custom-call | flops 6442450944 | bytes 1048576 | tf_op jit(solution)/shard_map/pallas_call | solution.py:385
  59.4 0.1 collective-permute-start.2
  59.5 7.3 %all-to-all-start.3 = ((bf16[8,256,256]{2,1,0:T(8,128)(2,1)}), bf16[8,256,256]{2,1,0:T(8,128)(2,1)}, u32[]{:S(2)}, u32[]{:S(2)}) async-start(bf16[8,256,256]{2,1,0:T(8,128)(2,1)} %get-tuple-element.42), calls=%async_computation.3 | async-start | bytes 2097152 | tf_op jit(solution)/shard_map/all_to_all | solution.py:477
  66.8 0.0 collective-permute-done.2.other
  66.8 13.1 %shard_map.140 = (bf16[4,2,8,8,256]{4,3,2,1,0:T(8,128)(2,1)}, bf16[4,2,8,8,256]{4,3,2,1,0:T(8,128)(2,1)}, bf16[8,256,256]{2,1,0:T(8,128)(2,1)}, bf16[2,256,1024]{2,1,0:T(8,128)(2,1)}) custom-call(s32[5]{0:T(128)} %stack.16.info, bf16[3,256,1024]{2,1,0:T(8,128)(2,1)} %get-tuple-element.30.own, bf16[3,256,1024]{2,1,0:T(8,128)(2,1)} %collective-permute-done.pair, ...), custom_call_target="tpu_custom_call" | custom-call | flops 6442450944 | bytes 1048576 | tf_op jit(solution)/shard_map/pallas_call | solution.py:385
  79.9 4.3 %all-to-all-done.3.dv_parts = bf16[8,256,256]{2,1,0:T(8,128)(2,1)} async-done(((bf16[8,256,256]{2,1,0:T(8,128)(2,1)}), bf16[8,256,256]{2,1,0:T(8,128)(2,1)}, u32[]{:S(2)}, u32[]{:S(2)}) %all-to-all-start.3) | async-done | bytes 1048608 | tf_op jit(solution)/shard_map/all_to_all | solution.py:477
  84.2 5.9 %all-to-all-start.2 = ((bf16[8,256,256]{2,1,0:T(8,128)(2,1)}), bf16[8,256,256]{2,1,0:T(8,128)(2,1)}, u32[]{:S(2)}, u32[]{:S(2)}) async-start(bf16[8,256,256]{2,1,0:T(8,128)(2,1)} %get-tuple-element.41), calls=%async_computation.2 | async-start | bytes 2097152 | tf_op jit(solution)/shard_map/all_to_all | solution.py:477
  90.1 0.0 collective-permute-start.4
  90.1 0.5 collective-permute-start.3
  90.6 14.9 %all-to-all-done.2.dk_parts = bf16[8,256,256]{2,1,0:T(8,128)(2,1)} async-done(((bf16[8,256,256]{2,1,0:T(8,128)(2,1)}), bf16[8,256,256]{2,1,0:T(8,128)(2,1)}, u32[]{:S(2)}, u32[]{:S(2)}) %all-to-all-start.2) | async-done | bytes 1048608 | tf_op jit(solution)/shard_map/all_to_all | solution.py:477
  105.5 2.5 %shard_map.142.dkv = bf16[256,512]{1,0:T(8,128)(2,1)} custom-call(bf16[8,256,256]{2,1,0:T(8,128)(2,1)} %all-to-all-done.2.dk_parts, bf16[8,256,256]{2,1,0:T(8,128)(2,1)} %all-to-all-done.3.dv_parts), custom_call_target="tpu_custom_call" | custom-call | flops 1073741824 | bytes 1048576 | tf_op jit(solution)/shard_map/pallas_call | solution.py:385
  108.0 0.0 collective-permute-start.8
  108.0 0.0 collective-permute-done.3.ht_pair
  108.0 0.0 collective-permute-done.4.dq_other
  108.0 5.0 %shard_map.141 = (bf16[256,1024]{1,0:T(8,128)(2,1)}, f32[128,2048]{1,0:T(8,128)}, bf16[128,2048]{1,0:T(8,128)(2,1)}, bf16[128,2048]{1,0:T(8,128)(2,1)}, bf16[128,2048]{1,0:T(8,128)(2,1)}) custom-call(s32[5]{0:T(128)} %stack.16.info, bf16[4,2,8,8,256]{4,3,2,1,0:T(8,128)(2,1)} %get-tuple-element.35.at_own, ...), custom_call_target="tpu_custom_call" | custom-call | flops 1073741824 | bytes 1048576 | tf_op jit(solution)/shard_map/pallas_call | solution.py:385
  113.1 1.5 collective-permute-start.5
  114.6 1.7 collective-permute-start.6
  116.4 2.6 %collective-permute-start.7 = (bf16[128,2048]{1,0:T(8,128)(2,1)}, bf16[128,2048]{1,0:T(8,128)(2,1)}, u32[]{:S(2)}, u32[]{:S(2)}) collective-permute-start(bf16[128,2048]{1,0:T(8,128)(2,1)} %get-tuple-element.46), channel_id=1, source_target_pairs={{0,48},{16,0},{32,16},{48,32},{64,112},{80,64},{96,80},{112,96},{1... | collective-permute-start | bytes 1572872 | tf_op jit(solution)/shard_map/ppermute | solution.py:469
  119.0 0.0 collective-permute-done.8.dkv_pair
  119.0 2.5 %shard_map.145 = bf16[128,2048]{1,0:T(8,128)(2,1)} custom-call(s32[5]{0:T(128)} %stack.16.info, bf16[4,2,8,8,256]{4,3,2,1,0:T(8,128)(2,1)} %get-tuple-element.37.ht_own, bf16[4,2,8,8,256]{4,3,2,1,0:T(8,128)(2,1)} %collective-permute-done.3.ht_pair, bf16[256,512]{1,0:T(8,128)(2,1)} %shard_map.142.dkv, bf16[256,512]{1,0:T(8,128)(2,1)} %collective-permute-done.8.dkv_pair), custom_call_target="tpu_custom_call" | custom-call | flops 1073741824 | bytes 1048576 | tf_op jit(solution)/shard_map/pallas_call | solution.py:385
  121.5 4.3 %all-to-all-start.5 = ((bf16[16,8,2048]{2,1,0:T(8,128)(2,1)}), bf16[16,8,2048]{2,1,0:T(8,128)(2,1)}, u32[]{:S(2)}, u32[]{:S(2)}) async-start(bf16[16,8,2048]{2,1,0:T(8,128)(2,1)} %bitcast.17), calls=%async_computation.5 | async-start | bytes 1048576 | tf_op jit(solution)/shard_map/all_to_all | solution.py:488
  125.8 3.1 %collective-permute-done.5.one = bf16[128,2048]{1,0:T(8,128)(2,1)} collective-permute-done((bf16[128,2048]{1,0:T(8,128)(2,1)}, bf16[128,2048]{1,0:T(8,128)(2,1)}, u32[]{:S(2)}, u32[]{:S(2)}) %collective-permute-start.5) | collective-permute-done | bytes 524320 | tf_op jit(solution)/shard_map/ppermute | solution.py:469
  129.0 11.6 %collective-permute-done.6.two = bf16[128,2048]{1,0:T(8,128)(2,1)} collective-permute-done((bf16[128,2048]{1,0:T(8,128)(2,1)}, bf16[128,2048]{1,0:T(8,128)(2,1)}, u32[]{:S(2)}, u32[]{:S(2)}) %collective-permute-start.6) | collective-permute-done | bytes 524320 | tf_op jit(solution)/shard_map/ppermute | solution.py:469
  140.5 0.3 collective-permute-done.7.three
  140.8 2.7 %shard_map.144 = bf16[128,2048]{1,0:T(8,128)(2,1)} custom-call(f32[128,2048]{1,0:T(8,128)} %get-tuple-element.43.base, bf16[128,2048]{1,0:T(8,128)(2,1)} %collective-permute-done.5.one, bf16[128,2048]{1,0:T(8,128)(2,1)} %collective-permute-done.6.two, bf16[128,2048]{1,0:T(8,128)(2,1)} %collective-permute-done.7.three), custom_call_target="tpu_custom_call" | custom-call | flops 1073741824 | bytes 1048576 | tf_op jit(solution)/shard_map/pallas_call | solution.py:385
  143.5 0.0 all-to-all-done.5.parts
  143.5 6.8 %all-to-all-start.4 = ((bf16[16,8,2048]{2,1,0:T(8,128)(2,1)}), bf16[16,8,2048]{2,1,0:T(8,128)(2,1)}, u32[]{:S(2)}, u32[]{:S(2)}) async-start(bf16[16,8,2048]{2,1,0:T(8,128)(2,1)} %bitcast.18), calls=%async_computation.4 | async-start | bytes 1048576 | tf_op jit(solution)/shard_map/all_to_all | solution.py:488
  150.4 1.7 shard_map.146.kv
  152.1 9.3 %all-to-all-done.4.parts = bf16[16,8,2048]{2,1,0:T(8,128)(2,1)} async-done(((bf16[16,8,2048]{2,1,0:T(8,128)(2,1)}), bf16[16,8,2048]{2,1,0:T(8,128)(2,1)}, u32[]{:S(2)}, u32[]{:S(2)}) %all-to-all-start.4) | async-done | bytes 524320 | tf_op jit(solution)/shard_map/all_to_all | solution.py:488
  161.4 1.9 %shard_map.147 = bf16[8,8,4096]{2,1,0:T(8,128)(2,1)} custom-call(bf16[16,8,2048]{2,1,0:T(8,128)(2,1)} %all-to-all-done.4.parts, bf16[8,2048]{1,0:T(8,128)(2,1)} %shard_map.146.kv), custom_call_target="tpu_custom_call" | custom-call | flops 1073741824 | bytes 1048576 | tf_op jit(solution)/shard_map/pallas_call | solution.py:385
  163.3 4.1 %all-to-all-start.6 = ((bf16[8,8,4096]{2,1,0:T(8,128)(2,1)}), bf16[8,8,4096]{2,1,0:T(8,128)(2,1)}, u32[]{:S(2)}, u32[]{:S(2)}) async-start(bf16[8,8,4096]{2,1,0:T(8,128)(2,1)} %shard_map.147), calls=%async_computation.6 | async-start | bytes 1048576 | tf_op jit(solution)/shard_map/all_to_all | solution.py:564
  167.5 1.3 dynamic-slice_bitcast_fusion.gain
  168.8 1.4 constant_dynamic-slice_fusion
  170.2 1.6 constant_dynamic-slice_fusion.2.w_query
  171.7 4.4 %shard_map.143 = bf16[256,1024]{1,0:T(8,128)(2,1)} custom-call(bf16[256,1024]{1,0:T(8,128)(2,1)} %bitcast.13, bf16[256,1024]{1,0:T(8,128)(2,1)} %bitcast.15, f32[1,1024]{1,0:T(1,128)} %bitcast.20, bf16[256,1024]{1,0:T(8,128)(2,1)} %get-tuple-element.40.dq, bf16[256,512]{1,0:T(8,128)(2,1)} %shard_map.142.dkv, bf16[1024,1024]{1,0:T(8,128)(2,1)} %w_query.3, ...), custom_call_target="tpu_custom_call" | custom-call | flops 805306368 | bytes 1048576 | tf_op jit(solution)/shard_map/pallas_call | solution.py:385
  176.2 0.0 all-to-all-done.6.shared
  176.2 2.0 %shard_map.148 = (f32[64,1024]{1,0:T(8,128)}, f32[64,256]{1,0:T(8,128)}, f32[64,256]{1,0:T(8,128)}, f32[64,1024]{1,0:T(8,128)}, f32[1,64]{1,0:T(1,128)}) custom-call(bf16[8,8,4096]{2,1,0:T(8,128)(2,1)} %all-to-all-done.6.shared, bf16[64,1024]{1,0:T(8,128)(2,1)} %constant_dynamic-slice_fusion.2.w_query, bf16[64,256]{1,0:T(8,128)(2,1)} %get-tuple-element.53.w_key, ...), custom_call_target="tpu_custom_call" | custom-call | flops 1073741824 | bytes 1048576 | tf_op jit(solution)/shard_map/pallas_call | solution.py:385
Async XLA Ops:
  4.0 23.9 %all-to-all-start = ((bf16[8,256,256]{2,1,0:T(8,128)(2,1)}), bf16[8,256,256]{2,1,0:T(8,128)(2,1)}, u32[]{:S(2)}, u32[]{:S(2)}) async-start(bf16[8,256,256]{2,1,0:T(8,128)(2,1)} %get-tuple-element.31), calls=%async_computation | async-start | bytes 2097152 | tf_op jit(solution)/shard_map/all_to_all | solution.py:477
  19.7 12.5 %collective-permute-start = (bf16[3,256,1024]{2,1,0:T(8,128)(2,1)}, bf16[3,256,1024]{2,1,0:T(8,128)(2,1)}, u32[]{:S(2)}, u32[]{:S(2)}) collective-permute-start(bf16[3,256,1024]{2,1,0:T(8,128)(2,1)} %get-tuple-element.30.own), channel_id=1, source_target_pairs={{0,1},{1,0},{2,3},{3,2},{4,5},{5,4},{6,7},{7,6},{8,9},{9,8},{10,11... | collective-permute-start | bytes 4718600 | tf_op jit(solution)/shard_map/ppermute | solution.py:464
  28.0 19.8 %all-to-all-start.1 = ((bf16[8,256,256]{2,1,0:T(8,128)(2,1)}), bf16[8,256,256]{2,1,0:T(8,128)(2,1)}, u32[]{:S(2)}, u32[]{:S(2)}) async-start(bf16[8,256,256]{2,1,0:T(8,128)(2,1)} %get-tuple-element.32), calls=%async_computation.1 | async-start | bytes 2097152 | tf_op jit(solution)/shard_map/all_to_all | solution.py:477
  36.4 11.3 %collective-permute-start.1 = (f32[2,2,1024]{2,1,0:T(2,128)}, f32[2,2,1024]{2,1,0:T(2,128)}, u32[]{:S(2)}, u32[]{:S(2)}) collective-permute-start(f32[2,2,1024]{2,1,0:T(2,128)} %shard_map.138.mine), channel_id=1, source_target_pairs={{0,1},{1,0},{2,3},{3,2},{4,5},{5,4},{6,7},{7,6},{8,9},{9,8},{10,11... | collective-permute-start | bytes 49160 | tf_op jit(solution)/shard_map/ppermute | solution.py:464
  59.4 7.4 %collective-permute-start.2 = (bf16[2,1024,256]{2,1,0:T(8,128)(2,1)}, bf16[2,1024,256]{2,1,0:T(8,128)(2,1)}, u32[]{:S(2)}, u32[]{:S(2)}) collective-permute-start(bf16[2,1024,256]{2,1,0:T(8,128)(2,1)} %get-tuple-element.33.mine), channel_id=1, source_target_pairs={{0,1},{1,0},{2,3},{3,2},{4,5},{5,4},{6,7},{7,6},{8,9},{9,8},{10,11... | collective-permute-start | bytes 3145736 | tf_op jit(solution)/shard_map/ppermute | solution.py:464
  59.5 24.7 %all-to-all-start.3 = ((bf16[8,256,256]{2,1,0:T(8,128)(2,1)}), bf16[8,256,256]{2,1,0:T(8,128)(2,1)}, u32[]{:S(2)}, u32[]{:S(2)}) async-start(bf16[8,256,256]{2,1,0:T(8,128)(2,1)} %get-tuple-element.42), calls=%async_computation.3 | async-start | bytes 2097152 | tf_op jit(solution)/shard_map/all_to_all | solution.py:477
  84.2 21.3 %all-to-all-start.2 = ((bf16[8,256,256]{2,1,0:T(8,128)(2,1)}), bf16[8,256,256]{2,1,0:T(8,128)(2,1)}, u32[]{:S(2)}, u32[]{:S(2)}) async-start(bf16[8,256,256]{2,1,0:T(8,128)(2,1)} %get-tuple-element.41), calls=%async_computation.2 | async-start | bytes 2097152 | tf_op jit(solution)/shard_map/all_to_all | solution.py:477
  90.1 17.9 %collective-permute-start.4 = (bf16[2,256,1024]{2,1,0:T(8,128)(2,1)}, bf16[2,256,1024]{2,1,0:T(8,128)(2,1)}, u32[]{:S(2)}, u32[]{:S(2)}) collective-permute-start(bf16[2,256,1024]{2,1,0:T(8,128)(2,1)} %get-tuple-element.39.dq_mine), channel_id=1, source_target_pairs={{0,1},{1,0},{2,3},{3,2},{4,5},{5,4},{6,7},{7,6},{8,9},{9,8},{10,11... | collective-permute-start | bytes 3145736 | tf_op jit(solution)/shard_map/ppermute | solution.py:464
  90.1 17.9 %collective-permute-start.3 = (bf16[4,2,8,8,256]{4,3,2,1,0:T(8,128)(2,1)}, bf16[4,2,8,8,256]{4,3,2,1,0:T(8,128)(2,1)}, u32[]{:S(2)}, u32[]{:S(2)}) collective-permute-start(bf16[4,2,8,8,256]{4,3,2,1,0:T(8,128)(2,1)} %get-tuple-element.38), channel_id=1, source_target_pairs={{0,1},{1,0},{2,3},{3,2},{4,5},{5,4},{6,7},{7,6},{8,9},{9,8},{10,11... | collective-permute-start | bytes 786440 | tf_op jit(solution)/shard_map/ppermute | solution.py:464
  108.0 11.0 %collective-permute-start.8 = (bf16[256,512]{1,0:T(8,128)(2,1)}, bf16[256,512]{1,0:T(8,128)(2,1)}, u32[]{:S(2)}, u32[]{:S(2)}) collective-permute-start(bf16[256,512]{1,0:T(8,128)(2,1)} %shard_map.142.dkv), channel_id=1, source_target_pairs={{0,1},{1,0},{2,3},{3,2},{4,5},{5,4},{6,7},{7,6},{8,9},{9,8},{10,11... | collective-permute-start | bytes 786440 | tf_op jit(solution)/shard_map/ppermute | solution.py:464
  113.1 15.9 %collective-permute-start.5 = (bf16[128,2048]{1,0:T(8,128)(2,1)}, bf16[128,2048]{1,0:T(8,128)(2,1)}, u32[]{:S(2)}, u32[]{:S(2)}) collective-permute-start(bf16[128,2048]{1,0:T(8,128)(2,1)} %get-tuple-element.44), channel_id=1, source_target_pairs={{0,16},{16,32},{32,48},{48,0},{64,80},{80,96},{96,112},{112,64},{1... | collective-permute-start | bytes 1572872 | tf_op jit(solution)/shard_map/ppermute | solution.py:469
  114.6 25.9 %collective-permute-start.6 = (bf16[128,2048]{1,0:T(8,128)(2,1)}, bf16[128,2048]{1,0:T(8,128)(2,1)}, u32[]{:S(2)}, u32[]{:S(2)}) collective-permute-start(bf16[128,2048]{1,0:T(8,128)(2,1)} %get-tuple-element.45), channel_id=1, source_target_pairs={{0,32},{16,48},{32,0},{48,16},{64,96},{80,112},{96,64},{112,80},{1... | collective-permute-start | bytes 1572872 | tf_op jit(solution)/shard_map/ppermute | solution.py:469
  116.4 24.4 %collective-permute-start.7 = (bf16[128,2048]{1,0:T(8,128)(2,1)}, bf16[128,2048]{1,0:T(8,128)(2,1)}, u32[]{:S(2)}, u32[]{:S(2)}) collective-permute-start(bf16[128,2048]{1,0:T(8,128)(2,1)} %get-tuple-element.46), channel_id=1, source_target_pairs={{0,48},{16,0},{32,16},{48,32},{64,112},{80,64},{96,80},{112,96},{1... | collective-permute-start | bytes 1572872 | tf_op jit(solution)/shard_map/ppermute | solution.py:469
  121.5 22.0 %all-to-all-start.5 = ((bf16[16,8,2048]{2,1,0:T(8,128)(2,1)}), bf16[16,8,2048]{2,1,0:T(8,128)(2,1)}, u32[]{:S(2)}, u32[]{:S(2)}) async-start(bf16[16,8,2048]{2,1,0:T(8,128)(2,1)} %bitcast.17), calls=%async_computation.5 | async-start | bytes 1048576 | tf_op jit(solution)/shard_map/all_to_all | solution.py:488
  143.5 17.9 %all-to-all-start.4 = ((bf16[16,8,2048]{2,1,0:T(8,128)(2,1)}), bf16[16,8,2048]{2,1,0:T(8,128)(2,1)}, u32[]{:S(2)}, u32[]{:S(2)}) async-start(bf16[16,8,2048]{2,1,0:T(8,128)(2,1)} %bitcast.18), calls=%async_computation.4 | async-start | bytes 1048576 | tf_op jit(solution)/shard_map/all_to_all | solution.py:488
  163.3 12.9 %all-to-all-start.6 = ((bf16[8,8,4096]{2,1,0:T(8,128)(2,1)}), bf16[8,8,4096]{2,1,0:T(8,128)(2,1)}, u32[]{:S(2)}, u32[]{:S(2)}) async-start(bf16[8,8,4096]{2,1,0:T(8,128)(2,1)} %shard_map.147), calls=%async_computation.6 | async-start | bytes 1048576 | tf_op jit(solution)/shard_map/all_to_all | solution.py:564

commit v7 on v6

--- a/solution.py
+++ b/solution.py
@@ -108,9 +108,9 @@
 
 
 def attend_kernel(
-    heads, seq, info, own, pair, mine, other, keys, values,
-    attn, dv, probs_out,
-    values_t, da_rows, probs, lse, out_sems,
+    heads, seq, info, own, pair, mine, other, keys, values_in,
+    attn, dv_out, probs_out,
+    values, values_t, da_rows, dv, probs, lse, value_sem, dv_sems, out_sems,
 ):
     chips, tok, _ = keys.shape
     wide = heads * HS
@@ -122,8 +122,11 @@
         total = mine[half, 1:2, :] * jnp.exp2(top_a - top)
         total = total + other[1 - half, 1:2, :] * jnp.exp2(top_b - top)
         lse[:, pl.ds(half * wide, wide)] = top + jnp.log(total) * LOG2E
-    for chip in range(chips):
-        values_t[:, pl.ds(chip * tok, tok)] = values[chip].T
+    value_copy = pltpu.make_async_copy(values_in, values, value_sem)
+    value_copy.start()
+
+    def dv_copy(chip):
+        return pltpu.make_async_copy(dv.at[chip], dv_out.at[chip], dv_sems.at[chip])
 
     def rows_of(chip):
         return pl.ds(pl.multiple_of(chip * tok, tok), tok)
@@ -148,13 +151,18 @@
             when_seen(info, chip, half, tok, seq, work, rest)
         dv[chip] = dot_nn(probs[rows, :], da_rows[...]).astype(jnp.bfloat16)
         out_copy(chip).start()
+        dv_copy(chip).start()
 
     each_chip(chips, step)
+    value_copy.wait()
+    for chip in range(chips):
+        values_t[:, pl.ds(chip * tok, tok)] = values[chip].T
     for half in range(2):
         for h in range(heads):
             attn[half, head(h), :] = dot_nn(values_t[...], probs[:, part(half, h, heads)]).astype(
                 jnp.bfloat16
             )
+    each_chip(chips, lambda chip: dv_copy(chip).wait())
     each_chip(chips, lambda chip: out_copy(chip).wait())
 
 
@@ -176,11 +184,16 @@
 
 
 def grads_kernel(
-    heads, seq, info, own, pair, mine, other, keys, values, probs_in,
-    at_own, at_pair, dk, dq,
-    keys_t, q_rows, probs, dscores, delta, in_sems,
+    heads, seq, info, own, pair, mine, other, keys_in, values, probs_in,
+    at_own, at_pair, dk_out, dq,
+    keys, keys_t, q_rows, dk, probs, dscores, delta, key_sem, dk_sems, in_sems,
 ):
-    chips, tok, _ = keys.shape
+    chips, tok, _ = values.shape
+    key_copy = pltpu.make_async_copy(keys_in, keys, key_sem)
+    key_copy.start()
+
+    def dk_copy(chip):
+        return pltpu.make_async_copy(dk.at[chip], dk_out.at[chip], dk_sems.at[chip])
 
     def rows_of(chip):
         return pl.ds(pl.multiple_of(chip * tok, tok), tok)
@@ -205,8 +218,6 @@
             )
             for n in range(per_head):
                 put_rows(info, a[n * block : (n + 1) * block], h * per_head + n, (at_own, at_pair)[half], None)
-    for chip in range(chips):
-        keys_t[:, pl.ds(chip * tok, tok)] = keys[chip].T
 
     def step(chip):
         rows = rows_of(chip)
@@ -228,30 +239,36 @@
                 dscores[rows, pl.ds(half * wide, wide)] = jnp.zeros((tok, wide), jnp.bfloat16)
 
         dk[chip] = (dot_nn(dscores[rows, :], q_rows[...]) * HS ** (-0.5)).astype(jnp.bfloat16)
+        dk_copy(chip).start()
 
     each_chip(chips, step)
+    key_copy.wait()
+    for chip in range(chips):
+        keys_t[:, pl.ds(chip * tok, tok)] = keys[chip].T
     for half in range(2):
         for h in range(heads):
             d = dot_nn(keys_t[...], dscores[:, part(half, h, heads)]) * HS ** (-0.5)
             dq[half, :, head(h)] = d.T.astype(jnp.bfloat16)
-
-
-def prepare_kernel(chips, x, gain, w_key, w_value, hidden, k_copies, v_copies):
+    each_chip(chips, lambda chip: dk_copy(chip).wait())
+
+
+def prepare_kernel(chips, x, gain, w_key, hidden, k_copies):
     xf = x[...].astype(jnp.float32)
     inv = lax.rsqrt(jnp.mean(xf * xf, axis=-1, keepdims=True) + EPS)
     h = (xf * inv * gain[...]).astype(jnp.bfloat16)
     hidden[...] = h
-    for weight, out in ((w_key, k_copies), (w_value, v_copies)):
-        rows = dot_nn(h, weight[...]).astype(jnp.bfloat16)
-        for chip in range(chips):
-            out[chip] = rows
-
-
-def project_kernel(info, hidden, grad_out, w_query, w_out, both, ht_own, ht_pair):
+    rows = dot_nn(h, w_key[...]).astype(jnp.bfloat16)
+    for chip in range(chips):
+        k_copies[chip] = rows
+
+
+def project_kernel(info, hidden, grad_out, w_query, w_out, w_value, both, v_copies, ht_own, ht_pair):
     h = hidden[...]
+    values = dot_nn(h, w_value[...]).astype(jnp.bfloat16)
+    for chip in range(v_copies.shape[0]):
+        v_copies[chip] = values
     both[0] = dot_nn(h, w_query[...]).astype(jnp.bfloat16)
     both[1] = dot_nt(grad_out[...], w_out[...]).astype(jnp.bfloat16)
-    both[2] = grad_out[...]
     chips = ht_own.shape[2]
     block = h.shape[1] // chips
     for chip in range(chips):
@@ -276,7 +293,7 @@
 
 
 def terms_kernel(
-    info, at_own, at_pair, own, pair, ht_own, ht_pair, dq_mine, dq_other, dq, base, *parts
+    info, at_own, at_pair, go_own, go_pair, ht_own, ht_pair, dq_mine, dq_other, dq, base, *parts
 ):
     rights = [
         (dq_mine[half].astype(jnp.float32) + dq_other[1 - half].astype(jnp.float32)).astype(dq.dtype)
@@ -284,18 +301,15 @@
     ]
     dq[...] = rights[0]
     for step, out in enumerate((base, *parts)):
-        g_out = step_terms((at_own, at_pair), (own[2], pair[2]), step)
+        g_out = step_terms((at_own, at_pair), (go_own[...], go_pair[...]), step)
         out[:, pl.ds(0, g_out.shape[1])] = g_out.astype(out.dtype)
         g_query = step_terms((ht_own, ht_pair), rights, step)
         out[:, pl.ds(g_out.shape[1], g_query.shape[1])] = g_query.astype(out.dtype)
 
 
-def rows_kernel(dk_parts, dv_parts, out):
-    for at, parts in ((0, dk_parts), (HS, dv_parts)):
-        total = parts[0].astype(jnp.float32)
-        for n in range(1, parts.shape[0]):
-            total = total + parts[n].astype(jnp.float32)
-        out[:, pl.ds(at, HS)] = total.astype(out.dtype)
+def rows_kernel(dk_parts, dv_rows, out):
+    out[:, pl.ds(0, HS)] = added_parts(dk_parts)
+    out[:, pl.ds(HS, HS)] = dv_rows[...]
 
 
 def kv_kernel(info, ht_own, ht_pair, dkv, dkv_pair, out):
@@ -422,12 +436,17 @@
         (info, own, pair, mine, other, keys, values),
         6 * seq * wide * HS,
         smem=1,
-        out_any=(2,),
+        in_any=(6,),
+        out_any=(1, 2),
         scratch=(
+            scratch(chips, tok, HS),
             scratch(HS, chips * tok),
             scratch(2 * wide, HS),
+            scratch(chips, tok, HS),
             scratch(chips * tok, 2 * wide),
             scratch(1, 2 * wide, dtype=jnp.float32),
+            pltpu.SemaphoreType.DMA,
+            pltpu.SemaphoreType.DMA((chips,)),
             pltpu.SemaphoreType.DMA((chips,)),
         ),
     )
@@ -443,13 +462,18 @@
         (info, own, pair, mine, other, keys, values, probs),
         6 * seq * wide * HS,
         smem=1,
-        in_any=(7,),
+        in_any=(5, 7),
+        out_any=(2,),
         scratch=(
+            scratch(chips, tok, HS),
             scratch(HS, chips * tok),
             scratch(2 * wide, HS),
+            scratch(chips, tok, HS),
             scratch(chips * tok, 2 * wide),
             scratch(chips * tok, 2 * wide),
             scratch(1, 2 * wide, dtype=jnp.float32),
+            pltpu.SemaphoreType.DMA,
+            pltpu.SemaphoreType.DMA((chips,)),
             pltpu.SemaphoreType.DMA((chips,)),
         ),
     )
@@ -504,22 +528,23 @@
     gain_row = gain.reshape(1, wide)
     filed = shape(X, outer, chips, size, tok)
     copies = shape(chips, tok, HS)
-    hidden, k_copies, v_copies = call(
+    hidden, k_copies = call(
         functools.partial(prepare_kernel, chips),
-        (shape(tok, wide), copies, copies),
-        (inputs, gain_row, w_key, w_value),
+        (shape(tok, wide), copies),
+        (inputs, gain_row, w_key),
         4 * tok * wide * HS,
     )
     keys = exchange_chips(k_copies)
-    values = exchange_chips(v_copies)
-    own, ht_own, ht_pair = call(
+    own, v_copies, ht_own, ht_pair = call(
         project_kernel,
-        (shape(3, tok, heads_wide), filed, filed),
-        (info, hidden, grad_out, w_query, w_out),
+        (shape(2, tok, heads_wide), copies, filed, filed),
+        (info, hidden, grad_out, w_query, w_out, w_value),
         4 * tok * wide * wide,
         smem=1,
     )
+    values = exchange_chips(v_copies)
     pair = swap_cores(own)
+    grad_pair = swap_cores(grad_out)
     ht_pair = swap_cores(ht_pair)
     mine = run_stats(info, own, pair, keys)
     other = swap_cores(mine)
@@ -539,14 +564,15 @@
             shape(rows, wide + heads_wide, dtype=jnp.float32),
             *[shape(rows, wide + heads_wide)] * (X - 1),
         ),
-        (info, at_own, at_pair, own, pair, ht_own, ht_pair, dq_mine, dq_other),
+        (info, at_own, at_pair, grad_out, grad_pair, ht_own, ht_pair, dq_mine, dq_other),
         8 * X * rows * wide * tok,
         smem=1,
     )
     arrived = []
     for step, terms in enumerate(parts, 1):
         arrived.append(send_along_x(terms, step))
-    d_kv_rows = call(rows_kernel, shape(tok, 2 * HS), (dk_parts, dv_parts), 1 << 30)
+    d_value_rows = call(total_kernel, shape(tok, HS), (dv_parts,), 1 << 30)
+    d_kv_rows = call(rows_kernel, shape(tok, 2 * HS), (dk_parts, d_value_rows), 1 << 30)
     d_kv_pair = swap_cores(d_kv_rows)
     kv_terms = call(
         kv_kernel,

time: 179 us -> 178 us (level)
  waiting for transfers between devices: 63.1 us -> 61.1 us
    all_to_all x4, waiting for transfers between devices: 38.8 us -> 36.8 us  [exchange_chips(): lax.all_to_all(value, 'blk', 0, 0, tiled=True, axis_index_groups=groups)]
    dynamic_slice x2 -> x3, local copies, waits for them, and re-layouts: 2.96 us -> 4.28 us  [my_rows(): return lax.dynamic_slice_in_dim(value, my * held, held, 0)]
    pallas_call x13 -> x14, Pallas kernels: 61 us -> 59.9 us  [call(): pl.pallas_call(body, out_shape=outs, in_specs=specs, out_specs=out_specs,...]
  transfers between devices with their start and end apart: 16 -> 17, of which waited for: 8 -> 8; matrix products, arithmetic and copies ran while one was open for 3% -> 4% of each run, Pallas kernels for 24% -> 24%
where the time goes in v7:
time: 178 us; the launch traced here: 176 us
  waiting for transfers between devices  61.1 us (34%)
  Pallas kernels  59.9 us (34%)
  starting transfers between devices  47.1 us (26%)
  local copies, waits for them, and re-layouts  6.26 us (4%)
  between operations  2.05 us (1%)
    pallas_call x14, Pallas kernels, call(): pl.pallas_call(body, out_shape=outs, in_specs=specs, out_specs=out_specs,...  59.9 us
    all_to_all x4, waiting for transfers between devices, exchange_chips(): lax.all_to_all(value, 'blk', 0, 0, tiled=True, axis_index_groups=groups)  36.8 us
    all_to_all x4, starting transfers between devices, exchange_chips(): lax.all_to_all(value, 'blk', 0, 0, tiled=True, axis_index_groups=groups)  25.1 us
    ppermute x3, waiting for transfers between devices, send_along_x(): lax.ppermute(value, 'dp', [(i, i // X * X + (i + step) % X) for i in rang...  15 us
    all_to_all x2, starting transfers between devices, exchange_plane(): lax.all_to_all(value, ('dp', 'blk'), 0, 0, tiled=True, axis_index_groups=...  11.2 us
    all_to_all x2, waiting for transfers between devices, exchange_plane(): lax.all_to_all(value, ('dp', 'blk'), 0, 0, tiled=True, axis_index_groups=...  9.28 us
    ppermute x3, starting transfers between devices, send_along_x(): lax.ppermute(value, 'dp', [(i, i // X * X + (i + step) % X) for i in rang...  5.92 us
    dynamic_slice x3, local copies, waits for them, and re-layouts, my_rows(): return lax.dynamic_slice_in_dim(value, my * held, held, 0)  4.28 us
  transfers between devices with their start and end apart: 17, of which 8 were waited for; matrix products, arithmetic and copies ran while one was open for 4% of the time, Pallas kernels for 24%

profile of v7, /device:TPU:0, one launch (start us, length us, event | category | flops | bytes accessed | tf_op | source)
XLA Modules:
  0.0 176.4 jit_solution(17681832664992068900)
XLA Ops:
  0.6 2.6 %shard_map.136 = (bf16[256,1024]{1,0:T(8,128)(2,1)}, bf16[8,256,256]{2,1,0:T(8,128)(2,1)}) custom-call(bf16[256,1024]{1,0:T(8,128)(2,1)} %bitcast.12, f32[1,1024]{1,0:T(1,128)} %bitcast.17, bf16[1024,256]{1,0:T(8,128)(2,1)} %w_key.3), custom_call_target="tpu_custom_call" | custom-call | flops 268435456 | bytes 1048576 | tf_op jit(solution)/shard_map/pallas_call | solution.py:399
  3.2 7.9 %all-to-all-start = ((bf16[8,256,256]{2,1,0:T(8,128)(2,1)}), bf16[8,256,256]{2,1,0:T(8,128)(2,1)}, u32[]{:S(2)}, u32[]{:S(2)}) async-start(bf16[8,256,256]{2,1,0:T(8,128)(2,1)} %get-tuple-element.31), calls=%async_computation | async-start | bytes 2097152 | tf_op jit(solution)/shard_map/all_to_all | solution.py:501
  12.4 0.7 stack.16.info
  13.1 6.2 %shard_map.137 = (bf16[2,256,1024]{2,1,0:T(8,128)(2,1)}, bf16[8,256,256]{2,1,0:T(8,128)(2,1)}, bf16[4,2,8,8,256]{4,3,2,1,0:T(8,128)(2,1)}, bf16[4,2,8,8,256]{4,3,2,1,0:T(8,128)(2,1)}) custom-call(s32[5]{0:T(128)} %stack.16.info, bf16[256,1024]{1,0:T(8,128)(2,1)} %get-tuple-element.29.hidden, bf16[256,1024]{1,0:T(8,128)(2,1)} %bitcast.1.grad_out.go_own, ...), custom_call_target="tpu_custom_call" | custom-call | flops 1073741824 | bytes 1048576 | tf_op jit(solution)/shard_map/pallas_call | solution.py:399
  19.3 0.0 collective-permute-start
  19.3 7.8 %all-to-all-done.keys.keys_in = bf16[8,256,256]{2,1,0:T(8,128)(2,1)} async-done(((bf16[8,256,256]{2,1,0:T(8,128)(2,1)}), bf16[8,256,256]{2,1,0:T(8,128)(2,1)}, u32[]{:S(2)}, u32[]{:S(2)}) %all-to-all-start) | async-done | bytes 1048608 | tf_op jit(solution)/shard_map/all_to_all | solution.py:501
  27.1 4.2 %all-to-all-start.1 = ((bf16[8,256,256]{2,1,0:T(8,128)(2,1)}), bf16[8,256,256]{2,1,0:T(8,128)(2,1)}, u32[]{:S(2)}, u32[]{:S(2)}) async-start(bf16[8,256,256]{2,1,0:T(8,128)(2,1)} %get-tuple-element.32), calls=%async_computation.1 | async-start | bytes 2097152 | tf_op jit(solution)/shard_map/all_to_all | solution.py:501
  31.4 0.0 collective-permute-done.pair
  31.4 3.8 %shard_map.138.mine = f32[2,2,1024]{2,1,0:T(2,128)} custom-call(s32[5]{0:T(128)} %stack.16.info, bf16[2,256,1024]{2,1,0:T(8,128)(2,1)} %get-tuple-element.30.own, bf16[2,256,1024]{2,1,0:T(8,128)(2,1)} %collective-permute-done.pair, bf16[8,256,256]{2,1,0:T(8,128)(2,1)} %all-to-all-done.keys.keys_in), custom_call_target="tpu_custom_call" | custom-call | flops 2147483648 | bytes 1048576 | tf_op jit(solution)/shard_map/pallas_call | solution.py:399
  35.3 0.0 collective-permute-start.1
  35.3 11.7 %all-to-all-done.1.values_in.values = bf16[8,256,256]{2,1,0:T(8,128)(2,1)} async-done(((bf16[8,256,256]{2,1,0:T(8,128)(2,1)}), bf16[8,256,256]{2,1,0:T(8,128)(2,1)}, u32[]{:S(2)}, u32[]{:S(2)}) %all-to-all-start.1) | async-done | bytes 1048608 | tf_op jit(solution)/shard_map/all_to_all | solution.py:501
  46.9 0.0 collective-permute-done.1.other
  46.9 10.6 %shard_map.139 = (bf16[2,1024,256]{2,1,0:T(8,128)(2,1)}, bf16[8,256,256]{2,1,0:T(8,128)(2,1)}, bf16[2048,2048]{1,0:T(8,128)(2,1)}) custom-call(s32[5]{0:T(128)} %stack.16.info, bf16[2,256,1024]{2,1,0:T(8,128)(2,1)} %get-tuple-element.30.own, bf16[2,256,1024]{2,1,0:T(8,128)(2,1)} %collective-permute-done.pair, f32[2,2,1024]{2,1,0:T(2,128)} %shard_map.138.mine, ...), custom_call_target="tpu_custom_call" | custom-call | flops 6442450944 | bytes 1048576 | tf_op jit(solution)/shard_map/pallas_call | solution.py:399
  57.5 0.1 collective-permute-start.2
  57.6 7.3 %all-to-all-start.3 = ((bf16[8,256,256]{2,1,0:T(8,128)(2,1)}), bf16[8,256,256]{2,1,0:T(8,128)(2,1)}, u32[]{:S(2)}, u32[]{:S(2)}) async-start(bf16[8,256,256]{2,1,0:T(8,128)(2,1)} %get-tuple-element.42), calls=%async_computation.3 | async-start | bytes 2097152 | tf_op jit(solution)/shard_map/all_to_all | solution.py:501
  64.9 0.0 collective-permute-done.2.other
  65.0 12.8 %shard_map.140 = (bf16[4,2,8,8,256]{4,3,2,1,0:T(8,128)(2,1)}, bf16[4,2,8,8,256]{4,3,2,1,0:T(8,128)(2,1)}, bf16[8,256,256]{2,1,0:T(8,128)(2,1)}, bf16[2,256,1024]{2,1,0:T(8,128)(2,1)}) custom-call(s32[5]{0:T(128)} %stack.16.info, bf16[2,256,1024]{2,1,0:T(8,128)(2,1)} %get-tuple-element.30.own, bf16[2,256,1024]{2,1,0:T(8,128)(2,1)} %collective-permute-done.pair, ...), custom_call_target="tpu_custom_call" | custom-call | flops 6442450944 | bytes 1048576 | tf_op jit(solution)/shard_map/pallas_call | solution.py:399
  77.8 4.6 %all-to-all-done.3.parts = bf16[8,256,256]{2,1,0:T(8,128)(2,1)} async-done(((bf16[8,256,256]{2,1,0:T(8,128)(2,1)}), bf16[8,256,256]{2,1,0:T(8,128)(2,1)}, u32[]{:S(2)}, u32[]{:S(2)}) %all-to-all-start.3) | async-done | bytes 1048608 | tf_op jit(solution)/shard_map/all_to_all | solution.py:501
  82.3 5.7 %all-to-all-start.2 = ((bf16[8,256,256]{2,1,0:T(8,128)(2,1)}), bf16[8,256,256]{2,1,0:T(8,128)(2,1)}, u32[]{:S(2)}, u32[]{:S(2)}) async-start(bf16[8,256,256]{2,1,0:T(8,128)(2,1)} %get-tuple-element.41), calls=%async_computation.2 | async-start | bytes 2097152 | tf_op jit(solution)/shard_map/all_to_all | solution.py:501
  88.0 0.0 collective-permute-start.5
  88.0 0.5 collective-permute-start.3
  88.5 0.1 collective-permute-start.4
  88.6 2.0 %shard_map.142.dv_rows = bf16[256,256]{1,0:T(8,128)(2,1)} custom-call(bf16[8,256,256]{2,1,0:T(8,128)(2,1)} %all-to-all-done.3.parts), custom_call_target="tpu_custom_call" | custom-call | flops 1073741824 | bytes 1048576 | tf_op jit(solution)/shard_map/pallas_call | solution.py:399
  90.6 12.8 %all-to-all-done.2.dk_parts = bf16[8,256,256]{2,1,0:T(8,128)(2,1)} async-done(((bf16[8,256,256]{2,1,0:T(8,128)(2,1)}), bf16[8,256,256]{2,1,0:T(8,128)(2,1)}, u32[]{:S(2)}, u32[]{:S(2)}) %all-to-all-start.2) | async-done | bytes 1048608 | tf_op jit(solution)/shard_map/all_to_all | solution.py:501
  103.4 2.1 %shard_map.143.dkv = bf16[256,512]{1,0:T(8,128)(2,1)} custom-call(bf16[8,256,256]{2,1,0:T(8,128)(2,1)} %all-to-all-done.2.dk_parts, bf16[256,256]{1,0:T(8,128)(2,1)} %shard_map.142.dv_rows), custom_call_target="tpu_custom_call" | custom-call | flops 1073741824 | bytes 1048576 | tf_op jit(solution)/shard_map/pallas_call | solution.py:399
  105.5 0.0 collective-permute-start.9
  105.5 0.0 collective-permute-done.4.ht_pair
  105.5 0.0 collective-permute-done.3.go_pair
  105.5 0.0 collective-permute-done.5.dq_other
  105.5 4.4 %shard_map.141 = (bf16[256,1024]{1,0:T(8,128)(2,1)}, f32[128,2048]{1,0:T(8,128)}, bf16[128,2048]{1,0:T(8,128)(2,1)}, bf16[128,2048]{1,0:T(8,128)(2,1)}, bf16[128,2048]{1,0:T(8,128)(2,1)}) custom-call(s32[5]{0:T(128)} %stack.16.info, bf16[4,2,8,8,256]{4,3,2,1,0:T(8,128)(2,1)} %get-tuple-element.35.at_own, ...), custom_call_target="tpu_custom_call" | custom-call | flops 1073741824 | bytes 1048576 | tf_op jit(solution)/shard_map/pallas_call | solution.py:399
  109.9 1.6 collective-permute-start.6
  111.5 1.7 collective-permute-start.7
  113.2 2.6 %collective-permute-start.8 = (bf16[128,2048]{1,0:T(8,128)(2,1)}, bf16[128,2048]{1,0:T(8,128)(2,1)}, u32[]{:S(2)}, u32[]{:S(2)}) collective-permute-start(bf16[128,2048]{1,0:T(8,128)(2,1)} %get-tuple-element.46), channel_id=1, source_target_pairs={{0,48},{16,0},{32,16},{48,32},{64,112},{80,64},{96,80},{112,96},{1... | collective-permute-start | bytes 1572872 | tf_op jit(solution)/shard_map/ppermute | solution.py:493
  115.8 0.0 collective-permute-done.9.dkv_pair
  115.8 2.5 %shard_map.146 = bf16[128,2048]{1,0:T(8,128)(2,1)} custom-call(s32[5]{0:T(128)} %stack.16.info, bf16[4,2,8,8,256]{4,3,2,1,0:T(8,128)(2,1)} %get-tuple-element.37.ht_own, bf16[4,2,8,8,256]{4,3,2,1,0:T(8,128)(2,1)} %collective-permute-done.4.ht_pair, bf16[256,512]{1,0:T(8,128)(2,1)} %shard_map.143.dkv, bf16[256,512]{1,0:T(8,128)(2,1)} %collective-permute-done.9.dkv_pair), custom_call_target="tpu_custom_call" | custom-call | flops 1073741824 | bytes 1048576 | tf_op jit(solution)/shard_map/pallas_call | solution.py:399
  118.3 4.3 %all-to-all-start.5 = ((bf16[16,8,2048]{2,1,0:T(8,128)(2,1)}), bf16[16,8,2048]{2,1,0:T(8,128)(2,1)}, u32[]{:S(2)}, u32[]{:S(2)}) async-start(bf16[16,8,2048]{2,1,0:T(8,128)(2,1)} %bitcast.16), calls=%async_computation.5 | async-start | bytes 1048576 | tf_op jit(solution)/shard_map/all_to_all | solution.py:512
  122.7 3.1 %collective-permute-done.6.one = bf16[128,2048]{1,0:T(8,128)(2,1)} collective-permute-done((bf16[128,2048]{1,0:T(8,128)(2,1)}, bf16[128,2048]{1,0:T(8,128)(2,1)}, u32[]{:S(2)}, u32[]{:S(2)}) %collective-permute-start.6) | collective-permute-done | bytes 524320 | tf_op jit(solution)/shard_map/ppermute | solution.py:493
  125.8 11.6 %collective-permute-done.7.two = bf16[128,2048]{1,0:T(8,128)(2,1)} collective-permute-done((bf16[128,2048]{1,0:T(8,128)(2,1)}, bf16[128,2048]{1,0:T(8,128)(2,1)}, u32[]{:S(2)}, u32[]{:S(2)}) %collective-permute-start.7) | collective-permute-done | bytes 524320 | tf_op jit(solution)/shard_map/ppermute | solution.py:493
  137.3 0.3 collective-permute-done.8.three
  137.6 2.7 %shard_map.145 = bf16[128,2048]{1,0:T(8,128)(2,1)} custom-call(f32[128,2048]{1,0:T(8,128)} %get-tuple-element.43.base, bf16[128,2048]{1,0:T(8,128)(2,1)} %collective-permute-done.6.one, bf16[128,2048]{1,0:T(8,128)(2,1)} %collective-permute-done.7.two, bf16[128,2048]{1,0:T(8,128)(2,1)} %collective-permute-done.8.three), custom_call_target="tpu_custom_call" | custom-call | flops 1073741824 | bytes 1048576 | tf_op jit(solution)/shard_map/pallas_call | solution.py:399
  140.3 0.0 all-to-all-done.5.parts
  140.3 6.9 %all-to-all-start.4 = ((bf16[16,8,2048]{2,1,0:T(8,128)(2,1)}), bf16[16,8,2048]{2,1,0:T(8,128)(2,1)}, u32[]{:S(2)}, u32[]{:S(2)}) async-start(bf16[16,8,2048]{2,1,0:T(8,128)(2,1)} %bitcast.15), calls=%async_computation.4 | async-start | bytes 1048576 | tf_op jit(solution)/shard_map/all_to_all | solution.py:512
  147.2 1.7 shard_map.147.kv
  149.0 9.3 %all-to-all-done.4.parts = bf16[16,8,2048]{2,1,0:T(8,128)(2,1)} async-done(((bf16[16,8,2048]{2,1,0:T(8,128)(2,1)}), bf16[16,8,2048]{2,1,0:T(8,128)(2,1)}, u32[]{:S(2)}, u32[]{:S(2)}) %all-to-all-start.4) | async-done | bytes 524320 | tf_op jit(solution)/shard_map/all_to_all | solution.py:512
  158.2 1.9 %shard_map.148 = bf16[8,8,4096]{2,1,0:T(8,128)(2,1)} custom-call(bf16[16,8,2048]{2,1,0:T(8,128)(2,1)} %all-to-all-done.4.parts, bf16[8,2048]{1,0:T(8,128)(2,1)} %shard_map.147.kv), custom_call_target="tpu_custom_call" | custom-call | flops 1073741824 | bytes 1048576 | tf_op jit(solution)/shard_map/pallas_call | solution.py:399
  160.2 4.1 %all-to-all-start.6 = ((bf16[8,8,4096]{2,1,0:T(8,128)(2,1)}), bf16[8,8,4096]{2,1,0:T(8,128)(2,1)}, u32[]{:S(2)}, u32[]{:S(2)}) async-start(bf16[8,8,4096]{2,1,0:T(8,128)(2,1)} %shard_map.148), calls=%async_computation.6 | async-start | bytes 1048576 | tf_op jit(solution)/shard_map/all_to_all | solution.py:590
  164.3 1.3 dynamic-slice_bitcast_fusion.gain
  165.6 1.4 constant_dynamic-slice_fusion.1.w_key
  167.0 1.4 constant_dynamic-slice_fusion.w_value
  168.4 1.6 constant_dynamic-slice_fusion.2.w_query
  169.9 4.4 %shard_map.144 = bf16[256,1024]{1,0:T(8,128)(2,1)} custom-call(bf16[256,1024]{1,0:T(8,128)(2,1)} %bitcast.13, bf16[256,1024]{1,0:T(8,128)(2,1)} %bitcast.1.grad_out.go_own, f32[1,1024]{1,0:T(1,128)} %bitcast.18, bf16[256,1024]{1,0:T(8,128)(2,1)} %get-tuple-element.40.dq, bf16[256,512]{1,0:T(8,128)(2,1)} %shard_map.143.dkv, bf16[1024,1024]{1,0:T(8,128)(2,1)} %w_query.3, ...), custom_call_target="tpu_custom_call" | custom-call | flops 805306368 | bytes 1048576 | tf_op jit(solution)/shard_map/pallas_call | solution.py:399
  174.4 0.0 all-to-all-done.6.shared
  174.4 2.0 %shard_map.149 = (f32[64,1024]{1,0:T(8,128)}, f32[64,256]{1,0:T(8,128)}, f32[64,256]{1,0:T(8,128)}, f32[64,1024]{1,0:T(8,128)}, f32[1,64]{1,0:T(1,128)}) custom-call(bf16[8,8,4096]{2,1,0:T(8,128)(2,1)} %all-to-all-done.6.shared, bf16[64,1024]{1,0:T(8,128)(2,1)} %constant_dynamic-slice_fusion.2.w_query, bf16[64,256]{1,0:T(8,128)(2,1)} %constant_dynamic-slice_fusion.1.w_key, ...), custom_call_target="tpu_custom_call" | custom-call | flops 1073741824 | bytes 1048576 | tf_op jit(solution)/shard_map/pallas_call | solution.py:399
Async XLA Ops:
  3.2 23.9 %all-to-all-start = ((bf16[8,256,256]{2,1,0:T(8,128)(2,1)}), bf16[8,256,256]{2,1,0:T(8,128)(2,1)}, u32[]{:S(2)}, u32[]{:S(2)}) async-start(bf16[8,256,256]{2,1,0:T(8,128)(2,1)} %get-tuple-element.31), calls=%async_computation | async-start | bytes 2097152 | tf_op jit(solution)/shard_map/all_to_all | solution.py:501
  19.3 12.1 %collective-permute-start = (bf16[2,256,1024]{2,1,0:T(8,128)(2,1)}, bf16[2,256,1024]{2,1,0:T(8,128)(2,1)}, u32[]{:S(2)}, u32[]{:S(2)}) collective-permute-start(bf16[2,256,1024]{2,1,0:T(8,128)(2,1)} %get-tuple-element.30.own), channel_id=1, source_target_pairs={{0,1},{1,0},{2,3},{3,2},{4,5},{5,4},{6,7},{7,6},{8,9},{9,8},{10,11... | collective-permute-start | bytes 3145736 | tf_op jit(solution)/shard_map/ppermute | solution.py:488
  27.1 19.8 %all-to-all-start.1 = ((bf16[8,256,256]{2,1,0:T(8,128)(2,1)}), bf16[8,256,256]{2,1,0:T(8,128)(2,1)}, u32[]{:S(2)}, u32[]{:S(2)}) async-start(bf16[8,256,256]{2,1,0:T(8,128)(2,1)} %get-tuple-element.32), calls=%async_computation.1 | async-start | bytes 2097152 | tf_op jit(solution)/shard_map/all_to_all | solution.py:501
  35.3 11.7 %collective-permute-start.1 = (f32[2,2,1024]{2,1,0:T(2,128)}, f32[2,2,1024]{2,1,0:T(2,128)}, u32[]{:S(2)}, u32[]{:S(2)}) collective-permute-start(f32[2,2,1024]{2,1,0:T(2,128)} %shard_map.138.mine), channel_id=1, source_target_pairs={{0,1},{1,0},{2,3},{3,2},{4,5},{5,4},{6,7},{7,6},{8,9},{9,8},{10,11... | collective-permute-start | bytes 49160 | tf_op jit(solution)/shard_map/ppermute | solution.py:488
  57.5 7.4 %collective-permute-start.2 = (bf16[2,1024,256]{2,1,0:T(8,128)(2,1)}, bf16[2,1024,256]{2,1,0:T(8,128)(2,1)}, u32[]{:S(2)}, u32[]{:S(2)}) collective-permute-start(bf16[2,1024,256]{2,1,0:T(8,128)(2,1)} %get-tuple-element.33.mine), channel_id=1, source_target_pairs={{0,1},{1,0},{2,3},{3,2},{4,5},{5,4},{6,7},{7,6},{8,9},{9,8},{10,11... | collective-permute-start | bytes 3145736 | tf_op jit(solution)/shard_map/ppermute | solution.py:488
  57.6 24.7 %all-to-all-start.3 = ((bf16[8,256,256]{2,1,0:T(8,128)(2,1)}), bf16[8,256,256]{2,1,0:T(8,128)(2,1)}, u32[]{:S(2)}, u32[]{:S(2)}) async-start(bf16[8,256,256]{2,1,0:T(8,128)(2,1)} %get-tuple-element.42), calls=%async_computation.3 | async-start | bytes 2097152 | tf_op jit(solution)/shard_map/all_to_all | solution.py:501
  82.3 21.1 %all-to-all-start.2 = ((bf16[8,256,256]{2,1,0:T(8,128)(2,1)}), bf16[8,256,256]{2,1,0:T(8,128)(2,1)}, u32[]{:S(2)}, u32[]{:S(2)}) async-start(bf16[8,256,256]{2,1,0:T(8,128)(2,1)} %get-tuple-element.41), calls=%async_computation.2 | async-start | bytes 2097152 | tf_op jit(solution)/shard_map/all_to_all | solution.py:501
  88.0 17.5 %collective-permute-start.5 = (bf16[2,256,1024]{2,1,0:T(8,128)(2,1)}, bf16[2,256,1024]{2,1,0:T(8,128)(2,1)}, u32[]{:S(2)}, u32[]{:S(2)}) collective-permute-start(bf16[2,256,1024]{2,1,0:T(8,128)(2,1)} %get-tuple-element.39.dq_mine), channel_id=1, source_target_pairs={{0,1},{1,0},{2,3},{3,2},{4,5},{5,4},{6,7},{7,6},{8,9},{9,8},{10,11... | collective-permute-start | bytes 3145736 | tf_op jit(solution)/shard_map/ppermute | solution.py:488
  88.0 17.5 %collective-permute-start.3 = (bf16[256,1024]{1,0:T(8,128)(2,1)}, bf16[256,1024]{1,0:T(8,128)(2,1)}, u32[]{:S(2)}, u32[]{:S(2)}) collective-permute-start(bf16[256,1024]{1,0:T(8,128)(2,1)} %bitcast.1.grad_out.go_own), channel_id=1, source_target_pairs={{0,1},{1,0},{2,3},{3,2},{4,5},{5,4},{6,7},{7,6},{8,9},{9,8},{10,11... | collective-permute-start | bytes 1572872 | tf_op jit(solution)/shard_map/ppermute | solution.py:488
  88.5 17.0 %collective-permute-start.4 = (bf16[4,2,8,8,256]{4,3,2,1,0:T(8,128)(2,1)}, bf16[4,2,8,8,256]{4,3,2,1,0:T(8,128)(2,1)}, u32[]{:S(2)}, u32[]{:S(2)}) collective-permute-start(bf16[4,2,8,8,256]{4,3,2,1,0:T(8,128)(2,1)} %get-tuple-element.38), channel_id=1, source_target_pairs={{0,1},{1,0},{2,3},{3,2},{4,5},{5,4},{6,7},{7,6},{8,9},{9,8},{10,11... | collective-permute-start | bytes 786440 | tf_op jit(solution)/shard_map/ppermute | solution.py:488
  105.5 10.4 %collective-permute-start.9 = (bf16[256,512]{1,0:T(8,128)(2,1)}, bf16[256,512]{1,0:T(8,128)(2,1)}, u32[]{:S(2)}, u32[]{:S(2)}) collective-permute-start(bf16[256,512]{1,0:T(8,128)(2,1)} %shard_map.143.dkv), channel_id=1, source_target_pairs={{0,1},{1,0},{2,3},{3,2},{4,5},{5,4},{6,7},{7,6},{8,9},{9,8},{10,11... | collective-permute-start | bytes 786440 | tf_op jit(solution)/shard_map/ppermute | solution.py:488
  109.9 15.9 %collective-permute-start.6 = (bf16[128,2048]{1,0:T(8,128)(2,1)}, bf16[128,2048]{1,0:T(8,128)(2,1)}, u32[]{:S(2)}, u32[]{:S(2)}) collective-permute-start(bf16[128,2048]{1,0:T(8,128)(2,1)} %get-tuple-element.44), channel_id=1, source_target_pairs={{0,16},{16,32},{32,48},{48,0},{64,80},{80,96},{96,112},{112,64},{1... | collective-permute-start | bytes 1572872 | tf_op jit(solution)/shard_map/ppermute | solution.py:493
  111.5 25.9 %collective-permute-start.7 = (bf16[128,2048]{1,0:T(8,128)(2,1)}, bf16[128,2048]{1,0:T(8,128)(2,1)}, u32[]{:S(2)}, u32[]{:S(2)}) collective-permute-start(bf16[128,2048]{1,0:T(8,128)(2,1)} %get-tuple-element.45), channel_id=1, source_target_pairs={{0,32},{16,48},{32,0},{48,16},{64,96},{80,112},{96,64},{112,80},{1... | collective-permute-start | bytes 1572872 | tf_op jit(solution)/shard_map/ppermute | solution.py:493
  113.2 24.4 %collective-permute-start.8 = (bf16[128,2048]{1,0:T(8,128)(2,1)}, bf16[128,2048]{1,0:T(8,128)(2,1)}, u32[]{:S(2)}, u32[]{:S(2)}) collective-permute-start(bf16[128,2048]{1,0:T(8,128)(2,1)} %get-tuple-element.46), channel_id=1, source_target_pairs={{0,48},{16,0},{32,16},{48,32},{64,112},{80,64},{96,80},{112,96},{1... | collective-permute-start | bytes 1572872 | tf_op jit(solution)/shard_map/ppermute | solution.py:493
  118.3 22.0 %all-to-all-start.5 = ((bf16[16,8,2048]{2,1,0:T(8,128)(2,1)}), bf16[16,8,2048]{2,1,0:T(8,128)(2,1)}, u32[]{:S(2)}, u32[]{:S(2)}) async-start(bf16[16,8,2048]{2,1,0:T(8,128)(2,1)} %bitcast.16), calls=%async_computation.5 | async-start | bytes 1048576 | tf_op jit(solution)/shard_map/all_to_all | solution.py:512
  140.3 17.9 %all-to-all-start.4 = ((bf16[16,8,2048]{2,1,0:T(8,128)(2,1)}), bf16[16,8,2048]{2,1,0:T(8,128)(2,1)}, u32[]{:S(2)}, u32[]{:S(2)}) async-start(bf16[16,8,2048]{2,1,0:T(8,128)(2,1)} %bitcast.15), calls=%async_computation.4 | async-start | bytes 1048576 | tf_op jit(solution)/shard_map/all_to_all | solution.py:512
  160.2 14.2 %all-to-all-start.6 = ((bf16[8,8,4096]{2,1,0:T(8,128)(2,1)}), bf16[8,8,4096]{2,1,0:T(8,128)(2,1)}, u32[]{:S(2)}, u32[]{:S(2)}) async-start(bf16[8,8,4096]{2,1,0:T(8,128)(2,1)} %shard_map.148), calls=%async_computation.6 | async-start | bytes 1048576 | tf_op jit(solution)/shard_map/all_to_all | solution.py:590

commit v8 on v7

--- a/solution.py
+++ b/solution.py
@@ -185,7 +185,7 @@
 
 def grads_kernel(
     heads, seq, info, own, pair, mine, other, keys_in, values, probs_in,
-    at_own, at_pair, dk_out, dq,
+    dk_out, dq,
     keys, keys_t, q_rows, dk, probs, dscores, delta, key_sem, dk_sems, in_sems,
 ):
     chips, tok, _ = values.shape
@@ -203,8 +203,6 @@
         return pltpu.make_async_copy(probs_in.at[rows, :], probs.at[rows, :], in_sems.at[chip])
 
     each_chip(chips, lambda chip: in_copy(chip).start())
-    per_head = chips // heads
-    block = HS // per_head
     for half, qd in enumerate((own, pair)):
         for h in range(heads):
             at = part(half, h, heads)
@@ -216,8 +214,6 @@
             delta[:, at] = jnp.sum(
                 a * qd[1, :, head(h)].T.astype(jnp.float32), axis=0, keepdims=True
             )
-            for n in range(per_head):
-                put_rows(info, a[n * block : (n + 1) * block], h * per_head + n, (at_own, at_pair)[half], None)
 
     def step(chip):
         rows = rows_of(chip)
@@ -293,15 +289,24 @@
 
 
 def terms_kernel(
-    info, at_own, at_pair, go_own, go_pair, ht_own, ht_pair, dq_mine, dq_other, dq, base, *parts
+    info, attn, attn_other, go_own, go_pair, ht_own, ht_pair, dq_mine, dq_other, dq, *refs
 ):
+    outs, filed = refs[:-2], refs[-2:]
+    block = attn.shape[1] // ht_own.shape[2]
+    for half in range(2):
+        for chip in range(ht_own.shape[2]):
+            rows = pl.ds(chip * block, block)
+            both = attn[half, rows, :].astype(jnp.float32) + attn_other[1 - half, rows, :].astype(
+                jnp.float32
+            )
+            put_rows(info, both, chip, filed[half], None)
     rights = [
         (dq_mine[half].astype(jnp.float32) + dq_other[1 - half].astype(jnp.float32)).astype(dq.dtype)
         for half in range(2)
     ]
     dq[...] = rights[0]
-    for step, out in enumerate((base, *parts)):
-        g_out = step_terms((at_own, at_pair), (go_own[...], go_pair[...]), step)
+    for step, out in enumerate(outs):
+        g_out = step_terms(filed, (go_own[...], go_pair[...]), step)
         out[:, pl.ds(0, g_out.shape[1])] = g_out.astype(out.dtype)
         g_query = step_terms((ht_own, ht_pair), rights, step)
         out[:, pl.ds(g_out.shape[1], g_query.shape[1])] = g_query.astype(out.dtype)
@@ -342,8 +347,22 @@
         out[n, :, pl.ds(wide, kv.shape[1])] = kv[...]
 
 
-def weights_kernel(steps, shared, w_query, w_key, w_value, gain, d_query, d_key, d_value, d_out, d_gain):
+def weights_kernel(
+    steps, info, shared, gain, wq_in, wk_in, wv_in,
+    d_query, d_key, d_value, d_out, d_gain,
+    w_query, w_key, w_value, sems,
+):
     size = shared.shape[1]
+    held = d_out.shape[0]
+    mine = pl.ds(pl.multiple_of(info[0] * held, held), held)
+    copies = [
+        pltpu.make_async_copy(w.at[mine, :], into, sems.at[n])
+        for n, (w, into) in enumerate(((wq_in, w_query), (wk_in, w_key), (wv_in, w_value)))
+    ]
+    for c in copies:
+        c.start()
+    for c in copies:
+        c.wait()
     wide, heads_wide = d_out.shape[1], d_query.shape[1]
     gains = []
     for place in range(shared.shape[0]):
@@ -364,7 +383,7 @@
             + jnp.sum(w_value[rows, :].astype(jnp.float32) * kv[:, HS:], axis=1, keepdims=True)
         )
         gains.append(jnp.broadcast_to(row_sum, (size, 128)))
-    d_gain[...] = jnp.concatenate(gains, axis=0).T[0:1, :] / gain[...]
+    d_gain[...] = jnp.concatenate(gains, axis=0).T[0:1, :] / gain[pl.ds(info[0], 1), :]
 
 
 def finish_kernel(x, grad_out, gain, dq, dkv, w_query, w_key, w_value, d_in):
@@ -452,18 +471,18 @@
     )
 
 
-def run_grads(info, own, pair, mine, other, keys, values, probs, filed):
+def run_grads(info, own, pair, mine, other, keys, values, probs):
     tok, wide = own.shape[1:]
     chips, heads = keys.shape[0], wide // HS
     seq = 2 * tok * chips
     return call(
         functools.partial(grads_kernel, heads, seq),
-        (filed, filed, shape(chips, tok, HS), shape(2, tok, wide)),
+        (shape(chips, tok, HS), shape(2, tok, wide)),
         (info, own, pair, mine, other, keys, values, probs),
         6 * seq * wide * HS,
         smem=1,
         in_any=(5, 7),
-        out_any=(2,),
+        out_any=(0,),
         scratch=(
             scratch(chips, tok, HS),
             scratch(HS, chips * tok),
@@ -551,9 +570,7 @@
     attn, dv, probs = run_attend(info, own, pair, mine, other, keys, values)
     attn_other = swap_cores(attn)
     dv_parts = exchange_chips(dv)
-    at_own, at_pair, dk, dq_mine = run_grads(
-        info, own, pair, attn, attn_other, keys, values, probs, filed
-    )
+    dk, dq_mine = run_grads(info, own, pair, attn, attn_other, keys, values, probs)
     dq_other = swap_cores(dq_mine)
     dk_parts = exchange_chips(dk)
     rows = outer * chips * size
@@ -564,9 +581,10 @@
             shape(rows, wide + heads_wide, dtype=jnp.float32),
             *[shape(rows, wide + heads_wide)] * (X - 1),
         ),
-        (info, at_own, at_pair, grad_out, grad_pair, ht_own, ht_pair, dq_mine, dq_other),
+        (info, attn, attn_other, grad_out, grad_pair, ht_own, ht_pair, dq_mine, dq_other),
         8 * X * rows * wide * tok,
         smem=1,
+        scratch=[scratch(*filed.shape)] * 2,
     )
     arrived = []
     for step, terms in enumerate(parts, 1):
@@ -595,18 +613,20 @@
         2 * tok * wide * (wide + 2 * HS),
     )
     held = wide // count
-
-    def my_rows(value):
-        return lax.dynamic_slice_in_dim(value, my * held, held, 0)
-
-    slices = [my_rows(w) for w in (w_query, w_key, w_value)]
-    slices.append(my_rows(gain).reshape(1, held))
     f32 = functools.partial(shape, dtype=jnp.float32)
     d_query, d_key, d_value, d_out, d_gain = call(
         functools.partial(weights_kernel, X),
         (f32(held, heads_wide), f32(held, HS), f32(held, HS), f32(held, wide), f32(1, held)),
-        (shared, *slices),
+        (info, shared, gain.reshape(count, held), w_query, w_key, w_value),
         1 << 30,
+        smem=1,
+        in_any=(3, 4, 5),
+        scratch=(
+            scratch(held, heads_wide),
+            scratch(held, HS),
+            scratch(held, HS),
+            pltpu.SemaphoreType.DMA((3,)),
+        ),
     )
     return (d_in[None], d_query, d_key, d_value, d_out, d_gain.reshape(held))
 

time: 178 us -> 178 us (level)
  local copies, waits for them, and re-layouts: 6.26 us -> 2.02 us
  waiting for transfers between devices: 61.1 us -> 64.2 us
    dynamic_slice x3 -> x0, local copies, waits for them, and re-layouts: 4.28 us -> none  [my_rows(): return lax.dynamic_slice_in_dim(value, my * held, held, 0)]
    all_to_all x1, waiting for transfers between devices: 0.01 us -> 2.91 us  [whole(): shared = lax.all_to_all(copies, 'dp', 0, 0, tiled=True)]
  transfers between devices with their start and end apart: 17 -> 17, of which waited for: 8 -> 9; matrix products, arithmetic and copies ran while one was open for 4% -> 1% of each run, Pallas kernels for 24% -> 24%
where the time goes in v8:
time: 178 us; the launch traced here: 177 us
  waiting for transfers between devices  64.2 us (36%)
  Pallas kernels  61.4 us (34%)
  starting transfers between devices  46.8 us (26%)
  between operations  2.2 us (1%)
  local copies, waits for them, and re-layouts  2.02 us (1%)
    pallas_call x14, Pallas kernels, call(): pl.pallas_call(body, out_shape=outs, in_specs=specs, out_specs=out_specs,...  61.4 us
    all_to_all x4, waiting for transfers between devices, exchange_chips(): lax.all_to_all(value, 'blk', 0, 0, tiled=True, axis_index_groups=groups)  37.1 us
    all_to_all x4, starting transfers between devices, exchange_chips(): lax.all_to_all(value, 'blk', 0, 0, tiled=True, axis_index_groups=groups)  24.8 us
    ppermute x3, waiting for transfers between devices, send_along_x(): lax.ppermute(value, 'dp', [(i, i // X * X + (i + step) % X) for i in rang...  15 us
    all_to_all x2, starting transfers between devices, exchange_plane(): lax.all_to_all(value, ('dp', 'blk'), 0, 0, tiled=True, axis_index_groups=...  11.2 us
    all_to_all x2, waiting for transfers between devices, exchange_plane(): lax.all_to_all(value, ('dp', 'blk'), 0, 0, tiled=True, axis_index_groups=...  9.27 us
    ppermute x3, starting transfers between devices, send_along_x(): lax.ppermute(value, 'dp', [(i, i // X * X + (i + step) % X) for i in rang...  5.93 us
    all_to_all x1, starting transfers between devices, whole(): shared = lax.all_to_all(copies, 'dp', 0, 0, tiled=True)  4.14 us
  transfers between devices with their start and end apart: 17, of which 9 were waited for; matrix products, arithmetic and copies ran while one was open for 1% of the time, Pallas kernels for 24%

profile of v8, /device:TPU:0, one launch (start us, length us, event | category | flops | bytes accessed | tf_op | source)
XLA Modules:
  0.0 176.7 jit_solution(11927015316516648874)
XLA Ops:
  0.6 2.6 %shard_map.136 = (bf16[256,1024]{1,0:T(8,128)(2,1)}, bf16[8,256,256]{2,1,0:T(8,128)(2,1)}) custom-call(bf16[256,1024]{1,0:T(8,128)(2,1)} %bitcast.10, f32[1,1024]{1,0:T(1,128)} %bitcast.15, bf16[1024,256]{1,0:T(8,128)(2,1)} %wk_in.1), custom_call_target="tpu_custom_call" | custom-call | flops 268435456 | bytes 1048576 | tf_op jit(solution)/shard_map/pallas_call | solution.py:418
  3.3 7.9 %all-to-all-start = ((bf16[8,256,256]{2,1,0:T(8,128)(2,1)}), bf16[8,256,256]{2,1,0:T(8,128)(2,1)}, u32[]{:S(2)}, u32[]{:S(2)}) async-start(bf16[8,256,256]{2,1,0:T(8,128)(2,1)} %get-tuple-element.29), calls=%async_computation | async-start | bytes 2097152 | tf_op jit(solution)/shard_map/all_to_all | solution.py:520
  12.5 0.7 stack.16.info
  13.1 6.2 %shard_map.137 = (bf16[2,256,1024]{2,1,0:T(8,128)(2,1)}, bf16[8,256,256]{2,1,0:T(8,128)(2,1)}, bf16[4,2,8,8,256]{4,3,2,1,0:T(8,128)(2,1)}, bf16[4,2,8,8,256]{4,3,2,1,0:T(8,128)(2,1)}) custom-call(s32[5]{0:T(128)} %stack.16.info, bf16[256,1024]{1,0:T(8,128)(2,1)} %get-tuple-element.27.hidden, bf16[256,1024]{1,0:T(8,128)(2,1)} %bitcast.1.grad_out.go_own, ...), custom_call_target="tpu_custom_call" | custom-call | flops 1073741824 | bytes 1048576 | tf_op jit(solution)/shard_map/pallas_call | solution.py:418
  19.4 0.0 collective-permute-start
  19.4 7.8 %all-to-all-done.keys.keys_in = bf16[8,256,256]{2,1,0:T(8,128)(2,1)} async-done(((bf16[8,256,256]{2,1,0:T(8,128)(2,1)}), bf16[8,256,256]{2,1,0:T(8,128)(2,1)}, u32[]{:S(2)}, u32[]{:S(2)}) %all-to-all-start) | async-done | bytes 1048608 | tf_op jit(solution)/shard_map/all_to_all | solution.py:520
  27.2 4.2 %all-to-all-start.1 = ((bf16[8,256,256]{2,1,0:T(8,128)(2,1)}), bf16[8,256,256]{2,1,0:T(8,128)(2,1)}, u32[]{:S(2)}, u32[]{:S(2)}) async-start(bf16[8,256,256]{2,1,0:T(8,128)(2,1)} %get-tuple-element.30), calls=%async_computation.1 | async-start | bytes 2097152 | tf_op jit(solution)/shard_map/all_to_all | solution.py:520
  31.4 0.0 collective-permute-done.pair
  31.4 3.8 %shard_map.138.mine = f32[2,2,1024]{2,1,0:T(2,128)} custom-call(s32[5]{0:T(128)} %stack.16.info, bf16[2,256,1024]{2,1,0:T(8,128)(2,1)} %get-tuple-element.28.own, bf16[2,256,1024]{2,1,0:T(8,128)(2,1)} %collective-permute-done.pair, bf16[8,256,256]{2,1,0:T(8,128)(2,1)} %all-to-all-done.keys.keys_in), custom_call_target="tpu_custom_call" | custom-call | flops 2147483648 | bytes 1048576 | tf_op jit(solution)/shard_map/pallas_call | solution.py:418
  35.3 0.0 collective-permute-start.1
  35.3 11.7 %all-to-all-done.1.values_in.values = bf16[8,256,256]{2,1,0:T(8,128)(2,1)} async-done(((bf16[8,256,256]{2,1,0:T(8,128)(2,1)}), bf16[8,256,256]{2,1,0:T(8,128)(2,1)}, u32[]{:S(2)}, u32[]{:S(2)}) %all-to-all-start.1) | async-done | bytes 1048608 | tf_op jit(solution)/shard_map/all_to_all | solution.py:520
  46.9 0.0 collective-permute-done.1.other
  46.9 10.7 %shard_map.139 = (bf16[2,1024,256]{2,1,0:T(8,128)(2,1)}, bf16[8,256,256]{2,1,0:T(8,128)(2,1)}, bf16[2048,2048]{1,0:T(8,128)(2,1)}) custom-call(s32[5]{0:T(128)} %stack.16.info, bf16[2,256,1024]{2,1,0:T(8,128)(2,1)} %get-tuple-element.28.own, bf16[2,256,1024]{2,1,0:T(8,128)(2,1)} %collective-permute-done.pair, f32[2,2,1024]{2,1,0:T(2,128)} %shard_map.138.mine, ...), custom_call_target="tpu_custom_call" | custom-call | flops 6442450944 | bytes 1048576 | tf_op jit(solution)/shard_map/pallas_call | solution.py:418
  57.6 0.1 collective-permute-start.2
  57.7 7.3 %all-to-all-start.3 = ((bf16[8,256,256]{2,1,0:T(8,128)(2,1)}), bf16[8,256,256]{2,1,0:T(8,128)(2,1)}, u32[]{:S(2)}, u32[]{:S(2)}) async-start(bf16[8,256,256]{2,1,0:T(8,128)(2,1)} %get-tuple-element.38), calls=%async_computation.3 | async-start | bytes 2097152 | tf_op jit(solution)/shard_map/all_to_all | solution.py:520
  65.0 0.0 collective-permute-done.2.other.attn_other
  65.0 12.5 %shard_map.140 = (bf16[8,256,256]{2,1,0:T(8,128)(2,1)}, bf16[2,256,1024]{2,1,0:T(8,128)(2,1)}) custom-call(s32[5]{0:T(128)} %stack.16.info, bf16[2,256,1024]{2,1,0:T(8,128)(2,1)} %get-tuple-element.28.own, bf16[2,256,1024]{2,1,0:T(8,128)(2,1)} %collective-permute-done.pair, bf16[2,1024,256]{2,1,0:T(8,128)(2,1)} %get-tuple-element.31.mine.attn, ...), custom_call_target="tpu_custom_call" | custom-call | flops 6442450944 | bytes 1048576 | tf_op jit(solution)/shard_map/pallas_call | solution.py:418
  77.6 4.8 %all-to-all-done.3.parts = bf16[8,256,256]{2,1,0:T(8,128)(2,1)} async-done(((bf16[8,256,256]{2,1,0:T(8,128)(2,1)}), bf16[8,256,256]{2,1,0:T(8,128)(2,1)}, u32[]{:S(2)}, u32[]{:S(2)}) %all-to-all-start.3) | async-done | bytes 1048608 | tf_op jit(solution)/shard_map/all_to_all | solution.py:520
  82.4 5.4 %all-to-all-start.2 = ((bf16[8,256,256]{2,1,0:T(8,128)(2,1)}), bf16[8,256,256]{2,1,0:T(8,128)(2,1)}, u32[]{:S(2)}, u32[]{:S(2)}) async-start(bf16[8,256,256]{2,1,0:T(8,128)(2,1)} %get-tuple-element.37), calls=%async_computation.2 | async-start | bytes 2097152 | tf_op jit(solution)/shard_map/all_to_all | solution.py:520
  87.8 0.0 collective-permute-start.5
  87.8 0.5 collective-permute-start.3
  88.3 0.1 collective-permute-start.4
  88.4 2.0 %shard_map.142.dv_rows = bf16[256,256]{1,0:T(8,128)(2,1)} custom-call(bf16[8,256,256]{2,1,0:T(8,128)(2,1)} %all-to-all-done.3.parts), custom_call_target="tpu_custom_call" | custom-call | flops 1073741824 | bytes 1048576 | tf_op jit(solution)/shard_map/pallas_call | solution.py:418
  90.4 12.8 %all-to-all-done.2.dk_parts = bf16[8,256,256]{2,1,0:T(8,128)(2,1)} async-done(((bf16[8,256,256]{2,1,0:T(8,128)(2,1)}), bf16[8,256,256]{2,1,0:T(8,128)(2,1)}, u32[]{:S(2)}, u32[]{:S(2)}) %all-to-all-start.2) | async-done | bytes 1048608 | tf_op jit(solution)/shard_map/all_to_all | solution.py:520
  103.2 2.1 %shard_map.143.dkv = bf16[256,512]{1,0:T(8,128)(2,1)} custom-call(bf16[8,256,256]{2,1,0:T(8,128)(2,1)} %all-to-all-done.2.dk_parts, bf16[256,256]{1,0:T(8,128)(2,1)} %shard_map.142.dv_rows), custom_call_target="tpu_custom_call" | custom-call | flops 1073741824 | bytes 1048576 | tf_op jit(solution)/shard_map/pallas_call | solution.py:418
  105.3 0.0 collective-permute-start.9
  105.3 0.0 collective-permute-done.4.ht_pair
  105.3 0.0 collective-permute-done.3.go_pair
  105.3 0.0 collective-permute-done.5.dq_other
  105.3 5.3 %shard_map.141 = (bf16[256,1024]{1,0:T(8,128)(2,1)}, f32[128,2048]{1,0:T(8,128)}, bf16[128,2048]{1,0:T(8,128)(2,1)}, bf16[128,2048]{1,0:T(8,128)(2,1)}, bf16[128,2048]{1,0:T(8,128)(2,1)}) custom-call(s32[5]{0:T(128)} %stack.16.info, bf16[2,1024,256]{2,1,0:T(8,128)(2,1)} %get-tuple-element.31.mine.attn, ...), custom_call_target="tpu_custom_call" | custom-call | flops 1073741824 | bytes 1048576 | tf_op jit(solution)/shard_map/pallas_call | solution.py:418
  110.6 1.4 collective-permute-start.6
  112.0 1.9 %collective-permute-start.7 = (bf16[128,2048]{1,0:T(8,128)(2,1)}, bf16[128,2048]{1,0:T(8,128)(2,1)}, u32[]{:S(2)}, u32[]{:S(2)}) collective-permute-start(bf16[128,2048]{1,0:T(8,128)(2,1)} %get-tuple-element.41), channel_id=1, source_target_pairs={{0,32},{16,48},{32,0},{48,16},{64,96},{80,112},{96,64},{112,80},{1... | collective-permute-start | bytes 1572872 | tf_op jit(solution)/shard_map/ppermute | solution.py:512
  113.9 2.6 %collective-permute-start.8 = (bf16[128,2048]{1,0:T(8,128)(2,1)}, bf16[128,2048]{1,0:T(8,128)(2,1)}, u32[]{:S(2)}, u32[]{:S(2)}) collective-permute-start(bf16[128,2048]{1,0:T(8,128)(2,1)} %get-tuple-element.42), channel_id=1, source_target_pairs={{0,48},{16,0},{32,16},{48,32},{64,112},{80,64},{96,80},{112,96},{1... | collective-permute-start | bytes 1572872 | tf_op jit(solution)/shard_map/ppermute | solution.py:512
  116.5 0.0 collective-permute-done.9.dkv_pair
  116.5 2.5 %shard_map.146 = bf16[128,2048]{1,0:T(8,128)(2,1)} custom-call(s32[5]{0:T(128)} %stack.16.info, bf16[4,2,8,8,256]{4,3,2,1,0:T(8,128)(2,1)} %get-tuple-element.32.ht_own, bf16[4,2,8,8,256]{4,3,2,1,0:T(8,128)(2,1)} %collective-permute-done.4.ht_pair, bf16[256,512]{1,0:T(8,128)(2,1)} %shard_map.143.dkv, bf16[256,512]{1,0:T(8,128)(2,1)} %collective-permute-done.9.dkv_pair), custom_call_target="tpu_custom_call" | custom-call | flops 1073741824 | bytes 1048576 | tf_op jit(solution)/shard_map/pallas_call | solution.py:418
  119.0 4.3 %all-to-all-start.5 = ((bf16[16,8,2048]{2,1,0:T(8,128)(2,1)}), bf16[16,8,2048]{2,1,0:T(8,128)(2,1)}, u32[]{:S(2)}, u32[]{:S(2)}) async-start(bf16[16,8,2048]{2,1,0:T(8,128)(2,1)} %bitcast.13), calls=%async_computation.5 | async-start | bytes 1048576 | tf_op jit(solution)/shard_map/all_to_all | solution.py:531
  123.3 3.1 %collective-permute-done.6.one = bf16[128,2048]{1,0:T(8,128)(2,1)} collective-permute-done((bf16[128,2048]{1,0:T(8,128)(2,1)}, bf16[128,2048]{1,0:T(8,128)(2,1)}, u32[]{:S(2)}, u32[]{:S(2)}) %collective-permute-start.6) | collective-permute-done | bytes 524320 | tf_op jit(solution)/shard_map/ppermute | solution.py:512
  126.4 11.6 %collective-permute-done.7.two = bf16[128,2048]{1,0:T(8,128)(2,1)} collective-permute-done((bf16[128,2048]{1,0:T(8,128)(2,1)}, bf16[128,2048]{1,0:T(8,128)(2,1)}, u32[]{:S(2)}, u32[]{:S(2)}) %collective-permute-start.7) | collective-permute-done | bytes 524320 | tf_op jit(solution)/shard_map/ppermute | solution.py:512
  138.0 0.3 collective-permute-done.8.three
  138.3 2.7 %shard_map.145 = bf16[128,2048]{1,0:T(8,128)(2,1)} custom-call(f32[128,2048]{1,0:T(8,128)} %get-tuple-element.39.base, bf16[128,2048]{1,0:T(8,128)(2,1)} %collective-permute-done.6.one, bf16[128,2048]{1,0:T(8,128)(2,1)} %collective-permute-done.7.two, bf16[128,2048]{1,0:T(8,128)(2,1)} %collective-permute-done.8.three), custom_call_target="tpu_custom_call" | custom-call | flops 1073741824 | bytes 1048576 | tf_op jit(solution)/shard_map/pallas_call | solution.py:418
  141.0 0.0 all-to-all-done.5.parts
  141.0 6.9 %all-to-all-start.4 = ((bf16[16,8,2048]{2,1,0:T(8,128)(2,1)}), bf16[16,8,2048]{2,1,0:T(8,128)(2,1)}, u32[]{:S(2)}, u32[]{:S(2)}) async-start(bf16[16,8,2048]{2,1,0:T(8,128)(2,1)} %bitcast.14), calls=%async_computation.4 | async-start | bytes 1048576 | tf_op jit(solution)/shard_map/all_to_all | solution.py:531
  147.9 1.7 shard_map.147.kv
  149.6 9.3 %all-to-all-done.4.parts = bf16[16,8,2048]{2,1,0:T(8,128)(2,1)} async-done(((bf16[16,8,2048]{2,1,0:T(8,128)(2,1)}), bf16[16,8,2048]{2,1,0:T(8,128)(2,1)}, u32[]{:S(2)}, u32[]{:S(2)}) %all-to-all-start.4) | async-done | bytes 524320 | tf_op jit(solution)/shard_map/all_to_all | solution.py:531
  158.9 1.9 %shard_map.148 = bf16[8,8,4096]{2,1,0:T(8,128)(2,1)} custom-call(bf16[16,8,2048]{2,1,0:T(8,128)(2,1)} %all-to-all-done.4.parts, bf16[8,2048]{1,0:T(8,128)(2,1)} %shard_map.147.kv), custom_call_target="tpu_custom_call" | custom-call | flops 1073741824 | bytes 1048576 | tf_op jit(solution)/shard_map/pallas_call | solution.py:418
  160.8 4.1 %all-to-all-start.6 = ((bf16[8,8,4096]{2,1,0:T(8,128)(2,1)}), bf16[8,8,4096]{2,1,0:T(8,128)(2,1)}, u32[]{:S(2)}, u32[]{:S(2)}) async-start(bf16[8,8,4096]{2,1,0:T(8,128)(2,1)} %shard_map.148), calls=%async_computation.6 | async-start | bytes 1048576 | tf_op jit(solution)/shard_map/all_to_all | solution.py:608
  165.0 1.3 reshape.33.gain
  166.3 4.4 %shard_map.144 = bf16[256,1024]{1,0:T(8,128)(2,1)} custom-call(bf16[256,1024]{1,0:T(8,128)(2,1)} %bitcast.11, bf16[256,1024]{1,0:T(8,128)(2,1)} %bitcast.1.grad_out.go_own, f32[1,1024]{1,0:T(1,128)} %bitcast.16, bf16[256,1024]{1,0:T(8,128)(2,1)} %get-tuple-element.36.dq, bf16[256,512]{1,0:T(8,128)(2,1)} %shard_map.143.dkv, bf16[1024,1024]{1,0:T(8,128)(2,1)} %wq_in.1, ...), custom_call_target="tpu_custom_call" | custom-call | flops 805306368 | bytes 1048576 | tf_op jit(solution)/shard_map/pallas_call | solution.py:418
  170.7 2.9 %all-to-all-done.6.shared = bf16[8,8,4096]{2,1,0:T(8,128)(2,1)} async-done(((bf16[8,8,4096]{2,1,0:T(8,128)(2,1)}), bf16[8,8,4096]{2,1,0:T(8,128)(2,1)}, u32[]{:S(2)}, u32[]{:S(2)}) %all-to-all-start.6) | async-done | bytes 524320 | tf_op jit(solution)/shard_map/all_to_all | solution.py:608
  173.7 2.9 %shard_map.149 = (f32[64,1024]{1,0:T(8,128)}, f32[64,256]{1,0:T(8,128)}, f32[64,256]{1,0:T(8,128)}, f32[64,1024]{1,0:T(8,128)}, f32[1,64]{1,0:T(1,128)}) custom-call(s32[5]{0:T(128)} %stack.16.info, bf16[8,8,4096]{2,1,0:T(8,128)(2,1)} %all-to-all-done.6.shared, f32[16,64]{1,0:T(8,128)} %reshape.33.gain, bf16[1024,1024]{1,0:T(8,128)(2,1)} %wq_in.1, ...), custom_call_target="tpu_custom_call" | custom-call | flops 1073741824 | bytes 1048576 | tf_op jit(solution)/shard_map/pallas_call | solution.py:418
Async XLA Ops:
  3.3 23.9 %all-to-all-start = ((bf16[8,256,256]{2,1,0:T(8,128)(2,1)}), bf16[8,256,256]{2,1,0:T(8,128)(2,1)}, u32[]{:S(2)}, u32[]{:S(2)}) async-start(bf16[8,256,256]{2,1,0:T(8,128)(2,1)} %get-tuple-element.29), calls=%async_computation | async-start | bytes 2097152 | tf_op jit(solution)/shard_map/all_to_all | solution.py:520
  19.4 12.1 %collective-permute-start = (bf16[2,256,1024]{2,1,0:T(8,128)(2,1)}, bf16[2,256,1024]{2,1,0:T(8,128)(2,1)}, u32[]{:S(2)}, u32[]{:S(2)}) collective-permute-start(bf16[2,256,1024]{2,1,0:T(8,128)(2,1)} %get-tuple-element.28.own), channel_id=1, source_target_pairs={{0,1},{1,0},{2,3},{3,2},{4,5},{5,4},{6,7},{7,6},{8,9},{9,8},{10,11... | collective-permute-start | bytes 3145736 | tf_op jit(solution)/shard_map/ppermute | solution.py:507
  27.2 19.8 %all-to-all-start.1 = ((bf16[8,256,256]{2,1,0:T(8,128)(2,1)}), bf16[8,256,256]{2,1,0:T(8,128)(2,1)}, u32[]{:S(2)}, u32[]{:S(2)}) async-start(bf16[8,256,256]{2,1,0:T(8,128)(2,1)} %get-tuple-element.30), calls=%async_computation.1 | async-start | bytes 2097152 | tf_op jit(solution)/shard_map/all_to_all | solution.py:520
  35.3 11.7 %collective-permute-start.1 = (f32[2,2,1024]{2,1,0:T(2,128)}, f32[2,2,1024]{2,1,0:T(2,128)}, u32[]{:S(2)}, u32[]{:S(2)}) collective-permute-start(f32[2,2,1024]{2,1,0:T(2,128)} %shard_map.138.mine), channel_id=1, source_target_pairs={{0,1},{1,0},{2,3},{3,2},{4,5},{5,4},{6,7},{7,6},{8,9},{9,8},{10,11... | collective-permute-start | bytes 49160 | tf_op jit(solution)/shard_map/ppermute | solution.py:507
  57.6 7.4 %collective-permute-start.2 = (bf16[2,1024,256]{2,1,0:T(8,128)(2,1)}, bf16[2,1024,256]{2,1,0:T(8,128)(2,1)}, u32[]{:S(2)}, u32[]{:S(2)}) collective-permute-start(bf16[2,1024,256]{2,1,0:T(8,128)(2,1)} %get-tuple-element.31.mine.attn), channel_id=1, source_target_pairs={{0,1},{1,0},{2,3},{3,2},{4,5},{5,4},{6,7},{7,6},{8,9},{9,8},{10,11... | collective-permute-start | bytes 3145736 | tf_op jit(solution)/shard_map/ppermute | solution.py:507
  57.7 24.7 %all-to-all-start.3 = ((bf16[8,256,256]{2,1,0:T(8,128)(2,1)}), bf16[8,256,256]{2,1,0:T(8,128)(2,1)}, u32[]{:S(2)}, u32[]{:S(2)}) async-start(bf16[8,256,256]{2,1,0:T(8,128)(2,1)} %get-tuple-element.38), calls=%async_computation.3 | async-start | bytes 2097152 | tf_op jit(solution)/shard_map/all_to_all | solution.py:520
  82.4 20.8 %all-to-all-start.2 = ((bf16[8,256,256]{2,1,0:T(8,128)(2,1)}), bf16[8,256,256]{2,1,0:T(8,128)(2,1)}, u32[]{:S(2)}, u32[]{:S(2)}) async-start(bf16[8,256,256]{2,1,0:T(8,128)(2,1)} %get-tuple-element.37), calls=%async_computation.2 | async-start | bytes 2097152 | tf_op jit(solution)/shard_map/all_to_all | solution.py:520
  87.8 17.5 %collective-permute-start.5 = (bf16[2,256,1024]{2,1,0:T(8,128)(2,1)}, bf16[2,256,1024]{2,1,0:T(8,128)(2,1)}, u32[]{:S(2)}, u32[]{:S(2)}) collective-permute-start(bf16[2,256,1024]{2,1,0:T(8,128)(2,1)} %get-tuple-element.35.dq_mine), channel_id=1, source_target_pairs={{0,1},{1,0},{2,3},{3,2},{4,5},{5,4},{6,7},{7,6},{8,9},{9,8},{10,11... | collective-permute-start | bytes 3145736 | tf_op jit(solution)/shard_map/ppermute | solution.py:507
  87.8 17.5 %collective-permute-start.3 = (bf16[256,1024]{1,0:T(8,128)(2,1)}, bf16[256,1024]{1,0:T(8,128)(2,1)}, u32[]{:S(2)}, u32[]{:S(2)}) collective-permute-start(bf16[256,1024]{1,0:T(8,128)(2,1)} %bitcast.1.grad_out.go_own), channel_id=1, source_target_pairs={{0,1},{1,0},{2,3},{3,2},{4,5},{5,4},{6,7},{7,6},{8,9},{9,8},{10,11... | collective-permute-start | bytes 1572872 | tf_op jit(solution)/shard_map/ppermute | solution.py:507
  88.3 17.0 %collective-permute-start.4 = (bf16[4,2,8,8,256]{4,3,2,1,0:T(8,128)(2,1)}, bf16[4,2,8,8,256]{4,3,2,1,0:T(8,128)(2,1)}, u32[]{:S(2)}, u32[]{:S(2)}) collective-permute-start(bf16[4,2,8,8,256]{4,3,2,1,0:T(8,128)(2,1)} %get-tuple-element.33), channel_id=1, source_target_pairs={{0,1},{1,0},{2,3},{3,2},{4,5},{5,4},{6,7},{7,6},{8,9},{9,8},{10,11... | collective-permute-start | bytes 786440 | tf_op jit(solution)/shard_map/ppermute | solution.py:507
  105.3 11.2 %collective-permute-start.9 = (bf16[256,512]{1,0:T(8,128)(2,1)}, bf16[256,512]{1,0:T(8,128)(2,1)}, u32[]{:S(2)}, u32[]{:S(2)}) collective-permute-start(bf16[256,512]{1,0:T(8,128)(2,1)} %shard_map.143.dkv), channel_id=1, source_target_pairs={{0,1},{1,0},{2,3},{3,2},{4,5},{5,4},{6,7},{7,6},{8,9},{9,8},{10,11... | collective-permute-start | bytes 786440 | tf_op jit(solution)/shard_map/ppermute | solution.py:507
  110.6 15.8 %collective-permute-start.6 = (bf16[128,2048]{1,0:T(8,128)(2,1)}, bf16[128,2048]{1,0:T(8,128)(2,1)}, u32[]{:S(2)}, u32[]{:S(2)}) collective-permute-start(bf16[128,2048]{1,0:T(8,128)(2,1)} %get-tuple-element.40), channel_id=1, source_target_pairs={{0,16},{16,32},{32,48},{48,0},{64,80},{80,96},{96,112},{112,64},{1... | collective-permute-start | bytes 1572872 | tf_op jit(solution)/shard_map/ppermute | solution.py:512
  112.0 26.0 %collective-permute-start.7 = (bf16[128,2048]{1,0:T(8,128)(2,1)}, bf16[128,2048]{1,0:T(8,128)(2,1)}, u32[]{:S(2)}, u32[]{:S(2)}) collective-permute-start(bf16[128,2048]{1,0:T(8,128)(2,1)} %get-tuple-element.41), channel_id=1, source_target_pairs={{0,32},{16,48},{32,0},{48,16},{64,96},{80,112},{96,64},{112,80},{1... | collective-permute-start | bytes 1572872 | tf_op jit(solution)/shard_map/ppermute | solution.py:512
  113.9 24.4 %collective-permute-start.8 = (bf16[128,2048]{1,0:T(8,128)(2,1)}, bf16[128,2048]{1,0:T(8,128)(2,1)}, u32[]{:S(2)}, u32[]{:S(2)}) collective-permute-start(bf16[128,2048]{1,0:T(8,128)(2,1)} %get-tuple-element.42), channel_id=1, source_target_pairs={{0,48},{16,0},{32,16},{48,32},{64,112},{80,64},{96,80},{112,96},{1... | collective-permute-start | bytes 1572872 | tf_op jit(solution)/shard_map/ppermute | solution.py:512
  119.0 22.0 %all-to-all-start.5 = ((bf16[16,8,2048]{2,1,0:T(8,128)(2,1)}), bf16[16,8,2048]{2,1,0:T(8,128)(2,1)}, u32[]{:S(2)}, u32[]{:S(2)}) async-start(bf16[16,8,2048]{2,1,0:T(8,128)(2,1)} %bitcast.13), calls=%async_computation.5 | async-start | bytes 1048576 | tf_op jit(solution)/shard_map/all_to_all | solution.py:531
  141.0 17.9 %all-to-all-start.4 = ((bf16[16,8,2048]{2,1,0:T(8,128)(2,1)}), bf16[16,8,2048]{2,1,0:T(8,128)(2,1)}, u32[]{:S(2)}, u32[]{:S(2)}) async-start(bf16[16,8,2048]{2,1,0:T(8,128)(2,1)} %bitcast.14), calls=%async_computation.4 | async-start | bytes 1048576 | tf_op jit(solution)/shard_map/all_to_all | solution.py:531
  160.8 12.8 %all-to-all-start.6 = ((bf16[8,8,4096]{2,1,0:T(8,128)(2,1)}), bf16[8,8,4096]{2,1,0:T(8,128)(2,1)}, u32[]{:S(2)}, u32[]{:S(2)}) async-start(bf16[8,8,4096]{2,1,0:T(8,128)(2,1)} %shard_map.148), calls=%async_computation.6 | async-start | bytes 1048576 | tf_op jit(solution)/shard_map/all_to_all | solution.py:608

commit v9 on v8

--- a/solution.py
+++ b/solution.py
@@ -339,6 +339,18 @@
     out[...] = added_parts(parts)
 
 
+def split_kernel(info, parts, *outs):
+    steps = len(outs)
+    for step, out in enumerate(outs):
+        wide = out.shape[1]
+        place = (info[4] + step) & (steps - 1)
+        at = pl.ds(pl.multiple_of(place * wide, 128), wide)
+        total = parts[0, :, at].astype(jnp.float32)
+        for n in range(1, parts.shape[0]):
+            total = total + parts[n, :, at].astype(jnp.float32)
+        out[...] = total.astype(out.dtype)
+
+
 def spread_kernel(parts, kv, out):
     total = added_parts(parts)
     wide = total.shape[1]
@@ -348,7 +360,7 @@
 
 
 def weights_kernel(
-    steps, info, shared, gain, wq_in, wk_in, wv_in,
+    info, shared, gain, wq_in, wk_in, wv_in,
     d_query, d_key, d_value, d_out, d_gain,
     w_query, w_key, w_value, sems,
 ):
@@ -366,14 +378,10 @@
     wide, heads_wide = d_out.shape[1], d_query.shape[1]
     gains = []
     for place in range(shared.shape[0]):
-        outer, x = place // steps, place % steps
         rows = slice(place * size, (place + 1) * size)
         d_out[rows, :] = shared[place, :, pl.ds(0, wide)].astype(jnp.float32)
         query = shared[place, :, pl.ds(wide, heads_wide)].astype(jnp.float32)
-        kv = 0.0
-        for source in range(steps):
-            at = pl.ds(wide + heads_wide + x * 2 * HS, 2 * HS)
-            kv = kv + shared[outer * steps + source, :, at].astype(jnp.float32)
+        kv = shared[place, :, pl.ds(wide + heads_wide, 2 * HS)].astype(jnp.float32)
         d_query[rows, :] = query
         d_key[rows, :] = kv[:, :HS]
         d_value[rows, :] = kv[:, HS:]
@@ -602,8 +610,18 @@
     kv_parts = exchange_plane(kv_terms)
     terms = call(collect_kernel, shape(rows, wide + heads_wide), (base, *arrived), 1 << 30)
     parts = exchange_plane(terms)
-    kv_total = call(total_kernel, shape(size, X * 2 * HS), (kv_parts,), 1 << 30)
-    total = wide + heads_wide + X * 2 * HS
+    kv_base, *kv_pieces = call(
+        split_kernel,
+        (shape(size, 2 * HS, dtype=jnp.float32), *[shape(size, 2 * HS)] * (X - 1)),
+        (info, kv_parts),
+        1 << 30,
+        smem=1,
+    )
+    kv_arrived = []
+    for step, piece in enumerate(kv_pieces, 1):
+        kv_arrived.append(send_along_x(piece, step))
+    kv_total = call(collect_kernel, shape(size, 2 * HS), (kv_base, *kv_arrived), 1 << 20)
+    total = wide + heads_wide + 2 * HS
     copies = call(spread_kernel, shape(share, size, total), (parts, kv_total), 1 << 30)
     shared = lax.all_to_all(copies, "dp", 0, 0, tiled=True)
     d_in = call(
@@ -615,7 +633,7 @@
     held = wide // count
     f32 = functools.partial(shape, dtype=jnp.float32)
     d_query, d_key, d_value, d_out, d_gain = call(
-        functools.partial(weights_kernel, X),
+        weights_kernel,
         (f32(held, heads_wide), f32(held, HS), f32(held, HS), f32(held, wide), f32(1, held)),
         (info, shared, gain.reshape(count, held), w_query, w_key, w_value),
         1 << 30,

time: 178 us -> 176 us (0.989)
  waiting for transfers between devices: 64.2 us -> 58 us
  starting transfers between devices: 46.8 us -> 50.6 us
    all_to_all x2, waiting for transfers between devices: 9.27 us -> 0.15 us  [exchange_plane(): lax.all_to_all(value, ('dp', 'blk'), 0, 0, tiled=True, axis_index_groups=...]
    ppermute x3 -> x6, waiting for transfers between devices: 15 us -> 18.9 us  [send_along_x(): lax.ppermute(value, 'dp', [(i, i // X * X + (i + step) % X) for i in rang...]
    ppermute x3 -> x6, starting transfers between devices: 5.93 us -> 9.73 us  [send_along_x(): lax.ppermute(value, 'dp', [(i, i // X * X + (i + step) % X) for i in rang...]
    pallas_call x14 -> x15, Pallas kernels: 61.4 us -> 62.6 us  [call(): pl.pallas_call(body, out_shape=outs, in_specs=specs, out_specs=out_specs,...]
  transfers between devices with their start and end apart: 17 -> 20, of which waited for: 9 -> 12; matrix products, arithmetic and copies ran while one was open for 1% -> 1% of each run, Pallas kernels for 24% -> 25%
where the time goes in v9:
time: 176 us; the launch traced here: 175 us
  Pallas kernels  62.6 us (36%)
  waiting for transfers between devices  58 us (33%)
  starting transfers between devices  50.6 us (29%)
  between operations  2.21 us (1%)
  local copies, waits for them, and re-layouts  2.01 us (1%)
    pallas_call x15, Pallas kernels, call(): pl.pallas_call(body, out_shape=outs, in_specs=specs, out_specs=out_specs,...  62.6 us
    all_to_all x4, waiting for transfers between devices, exchange_chips(): lax.all_to_all(value, 'blk', 0, 0, tiled=True, axis_index_groups=groups)  37.1 us
    all_to_all x4, starting transfers between devices, exchange_chips(): lax.all_to_all(value, 'blk', 0, 0, tiled=True, axis_index_groups=groups)  24.9 us
    ppermute x6, waiting for transfers between devices, send_along_x(): lax.ppermute(value, 'dp', [(i, i // X * X + (i + step) % X) for i in rang...  18.9 us
    all_to_all x2, starting transfers between devices, exchange_plane(): lax.all_to_all(value, ('dp', 'blk'), 0, 0, tiled=True, axis_index_groups=...  11.2 us
    ppermute x6, starting transfers between devices, send_along_x(): lax.ppermute(value, 'dp', [(i, i // X * X + (i + step) % X) for i in rang...  9.73 us
    all_to_all x1, starting transfers between devices, whole(): shared = lax.all_to_all(copies, 'dp', 0, 0, tiled=True)  4.08 us
  transfers between devices with their start and end apart: 20, of which 12 were waited for; matrix products, arithmetic and copies ran while one was open for 1% of the time, Pallas kernels for 25%

profile of v9, /device:TPU:0, one launch (start us, length us, event | category | flops | bytes accessed | tf_op | source)
XLA Modules:
  0.0 175.4 jit_solution(308619640794318598)
XLA Ops:
  0.6 2.6 %shard_map.136 = (bf16[256,1024]{1,0:T(8,128)(2,1)}, bf16[8,256,256]{2,1,0:T(8,128)(2,1)}) custom-call(bf16[256,1024]{1,0:T(8,128)(2,1)} %bitcast.10, f32[1,1024]{1,0:T(1,128)} %bitcast.15, bf16[1024,256]{1,0:T(8,128)(2,1)} %wk_in.1), custom_call_target="tpu_custom_call" | custom-call | flops 268435456 | bytes 1048576 | tf_op jit(solution)/shard_map/pallas_call | solution.py:426
  3.2 7.9 %all-to-all-start = ((bf16[8,256,256]{2,1,0:T(8,128)(2,1)}), bf16[8,256,256]{2,1,0:T(8,128)(2,1)}, u32[]{:S(2)}, u32[]{:S(2)}) async-start(bf16[8,256,256]{2,1,0:T(8,128)(2,1)} %get-tuple-element.33), calls=%async_computation | async-start | bytes 2097152 | tf_op jit(solution)/shard_map/all_to_all | solution.py:528
  12.4 0.7 stack.16.info
  13.1 6.2 %shard_map.137 = (bf16[2,256,1024]{2,1,0:T(8,128)(2,1)}, bf16[8,256,256]{2,1,0:T(8,128)(2,1)}, bf16[4,2,8,8,256]{4,3,2,1,0:T(8,128)(2,1)}, bf16[4,2,8,8,256]{4,3,2,1,0:T(8,128)(2,1)}) custom-call(s32[5]{0:T(128)} %stack.16.info, bf16[256,1024]{1,0:T(8,128)(2,1)} %get-tuple-element.31.hidden, bf16[256,1024]{1,0:T(8,128)(2,1)} %bitcast.1.grad_out.go_own, ...), custom_call_target="tpu_custom_call" | custom-call | flops 1073741824 | bytes 1048576 | tf_op jit(solution)/shard_map/pallas_call | solution.py:426
  19.3 0.0 collective-permute-start
  19.3 7.8 %all-to-all-done.keys.keys_in = bf16[8,256,256]{2,1,0:T(8,128)(2,1)} async-done(((bf16[8,256,256]{2,1,0:T(8,128)(2,1)}), bf16[8,256,256]{2,1,0:T(8,128)(2,1)}, u32[]{:S(2)}, u32[]{:S(2)}) %all-to-all-start) | async-done | bytes 1048608 | tf_op jit(solution)/shard_map/all_to_all | solution.py:528
  27.2 4.2 %all-to-all-start.1 = ((bf16[8,256,256]{2,1,0:T(8,128)(2,1)}), bf16[8,256,256]{2,1,0:T(8,128)(2,1)}, u32[]{:S(2)}, u32[]{:S(2)}) async-start(bf16[8,256,256]{2,1,0:T(8,128)(2,1)} %get-tuple-element.34), calls=%async_computation.1 | async-start | bytes 2097152 | tf_op jit(solution)/shard_map/all_to_all | solution.py:528
  31.4 0.0 collective-permute-done.pair
  31.4 3.8 %shard_map.138.mine = f32[2,2,1024]{2,1,0:T(2,128)} custom-call(s32[5]{0:T(128)} %stack.16.info, bf16[2,256,1024]{2,1,0:T(8,128)(2,1)} %get-tuple-element.32.own, bf16[2,256,1024]{2,1,0:T(8,128)(2,1)} %collective-permute-done.pair, bf16[8,256,256]{2,1,0:T(8,128)(2,1)} %all-to-all-done.keys.keys_in), custom_call_target="tpu_custom_call" | custom-call | flops 2147483648 | bytes 1048576 | tf_op jit(solution)/shard_map/pallas_call | solution.py:426
  35.3 0.0 collective-permute-start.1
  35.3 11.7 %all-to-all-done.1.values_in.values = bf16[8,256,256]{2,1,0:T(8,128)(2,1)} async-done(((bf16[8,256,256]{2,1,0:T(8,128)(2,1)}), bf16[8,256,256]{2,1,0:T(8,128)(2,1)}, u32[]{:S(2)}, u32[]{:S(2)}) %all-to-all-start.1) | async-done | bytes 1048608 | tf_op jit(solution)/shard_map/all_to_all | solution.py:528
  46.9 0.0 collective-permute-done.1.other
  46.9 10.7 %shard_map.139 = (bf16[2,1024,256]{2,1,0:T(8,128)(2,1)}, bf16[8,256,256]{2,1,0:T(8,128)(2,1)}, bf16[2048,2048]{1,0:T(8,128)(2,1)}) custom-call(s32[5]{0:T(128)} %stack.16.info, bf16[2,256,1024]{2,1,0:T(8,128)(2,1)} %get-tuple-element.32.own, bf16[2,256,1024]{2,1,0:T(8,128)(2,1)} %collective-permute-done.pair, f32[2,2,1024]{2,1,0:T(2,128)} %shard_map.138.mine, ...), custom_call_target="tpu_custom_call" | custom-call | flops 6442450944 | bytes 1048576 | tf_op jit(solution)/shard_map/pallas_call | solution.py:426
  57.6 0.1 collective-permute-start.2
  57.7 7.3 %all-to-all-start.3 = ((bf16[8,256,256]{2,1,0:T(8,128)(2,1)}), bf16[8,256,256]{2,1,0:T(8,128)(2,1)}, u32[]{:S(2)}, u32[]{:S(2)}) async-start(bf16[8,256,256]{2,1,0:T(8,128)(2,1)} %get-tuple-element.42), calls=%async_computation.3 | async-start | bytes 2097152 | tf_op jit(solution)/shard_map/all_to_all | solution.py:528
  65.0 0.0 collective-permute-done.2.other.attn_other
  65.0 12.6 %shard_map.140 = (bf16[8,256,256]{2,1,0:T(8,128)(2,1)}, bf16[2,256,1024]{2,1,0:T(8,128)(2,1)}) custom-call(s32[5]{0:T(128)} %stack.16.info, bf16[2,256,1024]{2,1,0:T(8,128)(2,1)} %get-tuple-element.32.own, bf16[2,256,1024]{2,1,0:T(8,128)(2,1)} %collective-permute-done.pair, bf16[2,1024,256]{2,1,0:T(8,128)(2,1)} %get-tuple-element.35.mine.attn, ...), custom_call_target="tpu_custom_call" | custom-call | flops 6442450944 | bytes 1048576 | tf_op jit(solution)/shard_map/pallas_call | solution.py:426
  77.6 4.8 %all-to-all-done.3.parts = bf16[8,256,256]{2,1,0:T(8,128)(2,1)} async-done(((bf16[8,256,256]{2,1,0:T(8,128)(2,1)}), bf16[8,256,256]{2,1,0:T(8,128)(2,1)}, u32[]{:S(2)}, u32[]{:S(2)}) %all-to-all-start.3) | async-done | bytes 1048608 | tf_op jit(solution)/shard_map/all_to_all | solution.py:528
  82.4 5.4 %all-to-all-start.2 = ((bf16[8,256,256]{2,1,0:T(8,128)(2,1)}), bf16[8,256,256]{2,1,0:T(8,128)(2,1)}, u32[]{:S(2)}, u32[]{:S(2)}) async-start(bf16[8,256,256]{2,1,0:T(8,128)(2,1)} %get-tuple-element.41), calls=%async_computation.2 | async-start | bytes 2097152 | tf_op jit(solution)/shard_map/all_to_all | solution.py:528
  87.8 0.0 collective-permute-start.5
  87.8 0.5 collective-permute-start.3
  88.3 0.1 collective-permute-start.4
  88.4 2.0 %shard_map.142.dv_rows = bf16[256,256]{1,0:T(8,128)(2,1)} custom-call(bf16[8,256,256]{2,1,0:T(8,128)(2,1)} %all-to-all-done.3.parts), custom_call_target="tpu_custom_call" | custom-call | flops 1073741824 | bytes 1048576 | tf_op jit(solution)/shard_map/pallas_call | solution.py:426
  90.4 12.8 %all-to-all-done.2.dk_parts = bf16[8,256,256]{2,1,0:T(8,128)(2,1)} async-done(((bf16[8,256,256]{2,1,0:T(8,128)(2,1)}), bf16[8,256,256]{2,1,0:T(8,128)(2,1)}, u32[]{:S(2)}, u32[]{:S(2)}) %all-to-all-start.2) | async-done | bytes 1048608 | tf_op jit(solution)/shard_map/all_to_all | solution.py:528
  103.2 2.1 %shard_map.143.dkv = bf16[256,512]{1,0:T(8,128)(2,1)} custom-call(bf16[8,256,256]{2,1,0:T(8,128)(2,1)} %all-to-all-done.2.dk_parts, bf16[256,256]{1,0:T(8,128)(2,1)} %shard_map.142.dv_rows), custom_call_target="tpu_custom_call" | custom-call | flops 1073741824 | bytes 1048576 | tf_op jit(solution)/shard_map/pallas_call | solution.py:426
  105.3 0.0 collective-permute-start.9
  105.3 0.0 collective-permute-done.4.ht_pair
  105.3 0.0 collective-permute-done.3.go_pair
  105.3 0.0 collective-permute-done.5.dq_other
  105.3 5.3 %shard_map.141 = (bf16[256,1024]{1,0:T(8,128)(2,1)}, f32[128,2048]{1,0:T(8,128)}, bf16[128,2048]{1,0:T(8,128)(2,1)}, bf16[128,2048]{1,0:T(8,128)(2,1)}, bf16[128,2048]{1,0:T(8,128)(2,1)}) custom-call(s32[5]{0:T(128)} %stack.16.info, bf16[2,1024,256]{2,1,0:T(8,128)(2,1)} %get-tuple-element.35.mine.attn, ...), custom_call_target="tpu_custom_call" | custom-call | flops 1073741824 | bytes 1048576 | tf_op jit(solution)/shard_map/pallas_call | solution.py:426
  110.6 1.4 collective-permute-start.6
  112.0 1.9 %collective-permute-start.7 = (bf16[128,2048]{1,0:T(8,128)(2,1)}, bf16[128,2048]{1,0:T(8,128)(2,1)}, u32[]{:S(2)}, u32[]{:S(2)}) collective-permute-start(bf16[128,2048]{1,0:T(8,128)(2,1)} %get-tuple-element.45), channel_id=1, source_target_pairs={{0,32},{16,48},{32,0},{48,16},{64,96},{80,112},{96,64},{112,80},{1... | collective-permute-start | bytes 1572872 | tf_op jit(solution)/shard_map/ppermute | solution.py:520
  113.9 2.6 %collective-permute-start.8 = (bf16[128,2048]{1,0:T(8,128)(2,1)}, bf16[128,2048]{1,0:T(8,128)(2,1)}, u32[]{:S(2)}, u32[]{:S(2)}) collective-permute-start(bf16[128,2048]{1,0:T(8,128)(2,1)} %get-tuple-element.46), channel_id=1, source_target_pairs={{0,48},{16,0},{32,16},{48,32},{64,112},{80,64},{96,80},{112,96},{1... | collective-permute-start | bytes 1572872 | tf_op jit(solution)/shard_map/ppermute | solution.py:520
  116.5 0.0 collective-permute-done.9.dkv_pair
  116.5 2.5 %shard_map.146 = bf16[128,2048]{1,0:T(8,128)(2,1)} custom-call(s32[5]{0:T(128)} %stack.16.info, bf16[4,2,8,8,256]{4,3,2,1,0:T(8,128)(2,1)} %get-tuple-element.36.ht_own, bf16[4,2,8,8,256]{4,3,2,1,0:T(8,128)(2,1)} %collective-permute-done.4.ht_pair, bf16[256,512]{1,0:T(8,128)(2,1)} %shard_map.143.dkv, bf16[256,512]{1,0:T(8,128)(2,1)} %collective-permute-done.9.dkv_pair), custom_call_target="tpu_custom_call" | custom-call | flops 1073741824 | bytes 1048576 | tf_op jit(solution)/shard_map/pallas_call | solution.py:426
  119.0 4.3 %all-to-all-start.5 = ((bf16[16,8,2048]{2,1,0:T(8,128)(2,1)}), bf16[16,8,2048]{2,1,0:T(8,128)(2,1)}, u32[]{:S(2)}, u32[]{:S(2)}) async-start(bf16[16,8,2048]{2,1,0:T(8,128)(2,1)} %bitcast.14), calls=%async_computation.5 | async-start | bytes 1048576 | tf_op jit(solution)/shard_map/all_to_all | solution.py:539
  123.3 3.1 %collective-permute-done.6.one = bf16[128,2048]{1,0:T(8,128)(2,1)} collective-permute-done((bf16[128,2048]{1,0:T(8,128)(2,1)}, bf16[128,2048]{1,0:T(8,128)(2,1)}, u32[]{:S(2)}, u32[]{:S(2)}) %collective-permute-start.6) | collective-permute-done | bytes 524320 | tf_op jit(solution)/shard_map/ppermute | solution.py:520
  126.4 11.6 %collective-permute-done.7.two = bf16[128,2048]{1,0:T(8,128)(2,1)} collective-permute-done((bf16[128,2048]{1,0:T(8,128)(2,1)}, bf16[128,2048]{1,0:T(8,128)(2,1)}, u32[]{:S(2)}, u32[]{:S(2)}) %collective-permute-start.7) | collective-permute-done | bytes 524320 | tf_op jit(solution)/shard_map/ppermute | solution.py:520
  138.0 0.3 collective-permute-done.8.three
  138.3 2.7 %shard_map.145 = bf16[128,2048]{1,0:T(8,128)(2,1)} custom-call(f32[128,2048]{1,0:T(8,128)} %get-tuple-element.43.base, bf16[128,2048]{1,0:T(8,128)(2,1)} %collective-permute-done.6.one, bf16[128,2048]{1,0:T(8,128)(2,1)} %collective-permute-done.7.two, bf16[128,2048]{1,0:T(8,128)(2,1)} %collective-permute-done.8.three), custom_call_target="tpu_custom_call" | custom-call | flops 1073741824 | bytes 1048576 | tf_op jit(solution)/shard_map/pallas_call | solution.py:426
  141.0 0.0 all-to-all-done.5.parts
  141.0 6.9 %all-to-all-start.4 = ((bf16[16,8,2048]{2,1,0:T(8,128)(2,1)}), bf16[16,8,2048]{2,1,0:T(8,128)(2,1)}, u32[]{:S(2)}, u32[]{:S(2)}) async-start(bf16[16,8,2048]{2,1,0:T(8,128)(2,1)} %bitcast.13), calls=%async_computation.4 | async-start | bytes 1048576 | tf_op jit(solution)/shard_map/all_to_all | solution.py:539
  147.8 1.7 shard_map.147
  149.6 0.2 collective-permute-start.10
  149.8 3.6 %collective-permute-start.11 = (bf16[8,512]{1,0:T(8,128)(2,1)}, bf16[8,512]{1,0:T(8,128)(2,1)}, u32[]{:S(2)}, u32[]{:S(2)}) collective-permute-start(bf16[8,512]{1,0:T(8,128)(2,1)} %get-tuple-element.49), channel_id=1, source_target_pairs={{0,32},{16,48},{32,0},{48,16},{64,96},{80,112},{96,64},{112,80},{1... | collective-permute-start | bytes 24584 | tf_op jit(solution)/shard_map/ppermute | solution.py:520
  153.4 0.0 collective-permute-start.12
  153.4 1.4 collective-permute-done.10.one
  154.8 0.7 collective-permute-done.11.two
  155.4 1.9 %collective-permute-done.12.three = bf16[8,512]{1,0:T(8,128)(2,1)} collective-permute-done((bf16[8,512]{1,0:T(8,128)(2,1)}, bf16[8,512]{1,0:T(8,128)(2,1)}, u32[]{:S(2)}, u32[]{:S(2)}) %collective-permute-start.12) | collective-permute-done | bytes 8224 | tf_op jit(solution)/shard_map/ppermute | solution.py:520
  157.3 1.4 shard_map.148.kv
  158.7 0.1 all-to-all-done.4.parts
  158.8 1.8 %shard_map.149 = bf16[8,8,2560]{2,1,0:T(8,128)(2,1)} custom-call(bf16[16,8,2048]{2,1,0:T(8,128)(2,1)} %all-to-all-done.4.parts, bf16[8,512]{1,0:T(8,128)(2,1)} %shard_map.148.kv), custom_call_target="tpu_custom_call" | custom-call | flops 1073741824 | bytes 1048576 | tf_op jit(solution)/shard_map/pallas_call | solution.py:426
  160.7 4.1 %all-to-all-start.6 = ((bf16[8,8,2560]{2,1,0:T(8,128)(2,1)}), bf16[8,8,2560]{2,1,0:T(8,128)(2,1)}, u32[]{:S(2)}, u32[]{:S(2)}) async-start(bf16[8,8,2560]{2,1,0:T(8,128)(2,1)} %shard_map.149), calls=%async_computation.6 | async-start | bytes 655360 | tf_op jit(solution)/shard_map/all_to_all | solution.py:626
  164.8 1.3 reshape.33.gain
  166.1 4.4 %shard_map.144 = bf16[256,1024]{1,0:T(8,128)(2,1)} custom-call(bf16[256,1024]{1,0:T(8,128)(2,1)} %bitcast.11, bf16[256,1024]{1,0:T(8,128)(2,1)} %bitcast.1.grad_out.go_own, f32[1,1024]{1,0:T(1,128)} %bitcast.16, bf16[256,1024]{1,0:T(8,128)(2,1)} %get-tuple-element.40.dq, bf16[256,512]{1,0:T(8,128)(2,1)} %shard_map.143.dkv, bf16[1024,1024]{1,0:T(8,128)(2,1)} %wq_in.1, ...), custom_call_target="tpu_custom_call" | custom-call | flops 805306368 | bytes 1048576 | tf_op jit(solution)/shard_map/pallas_call | solution.py:426
  170.6 1.9 %all-to-all-done.6.shared = bf16[8,8,2560]{2,1,0:T(8,128)(2,1)} async-done(((bf16[8,8,2560]{2,1,0:T(8,128)(2,1)}), bf16[8,8,2560]{2,1,0:T(8,128)(2,1)}, u32[]{:S(2)}, u32[]{:S(2)}) %all-to-all-start.6) | async-done | bytes 327712 | tf_op jit(solution)/shard_map/all_to_all | solution.py:626
  172.4 2.8 %shard_map.150 = (f32[64,1024]{1,0:T(8,128)}, f32[64,256]{1,0:T(8,128)}, f32[64,256]{1,0:T(8,128)}, f32[64,1024]{1,0:T(8,128)}, f32[1,64]{1,0:T(1,128)}) custom-call(s32[5]{0:T(128)} %stack.16.info, bf16[8,8,2560]{2,1,0:T(8,128)(2,1)} %all-to-all-done.6.shared, f32[16,64]{1,0:T(8,128)} %reshape.33.gain, bf16[1024,1024]{1,0:T(8,128)(2,1)} %wq_in.1, ...), custom_call_target="tpu_custom_call" | custom-call | flops 1073741824 | bytes 1048576 | tf_op jit(solution)/shard_map/pallas_call | solution.py:426
Async XLA Ops:
  3.2 23.9 %all-to-all-start = ((bf16[8,256,256]{2,1,0:T(8,128)(2,1)}), bf16[8,256,256]{2,1,0:T(8,128)(2,1)}, u32[]{:S(2)}, u32[]{:S(2)}) async-start(bf16[8,256,256]{2,1,0:T(8,128)(2,1)} %get-tuple-element.33), calls=%async_computation | async-start | bytes 2097152 | tf_op jit(solution)/shard_map/all_to_all | solution.py:528
  19.3 12.1 %collective-permute-start = (bf16[2,256,1024]{2,1,0:T(8,128)(2,1)}, bf16[2,256,1024]{2,1,0:T(8,128)(2,1)}, u32[]{:S(2)}, u32[]{:S(2)}) collective-permute-start(bf16[2,256,1024]{2,1,0:T(8,128)(2,1)} %get-tuple-element.32.own), channel_id=1, source_target_pairs={{0,1},{1,0},{2,3},{3,2},{4,5},{5,4},{6,7},{7,6},{8,9},{9,8},{10,11... | collective-permute-start | bytes 3145736 | tf_op jit(solution)/shard_map/ppermute | solution.py:515
  27.2 19.8 %all-to-all-start.1 = ((bf16[8,256,256]{2,1,0:T(8,128)(2,1)}), bf16[8,256,256]{2,1,0:T(8,128)(2,1)}, u32[]{:S(2)}, u32[]{:S(2)}) async-start(bf16[8,256,256]{2,1,0:T(8,128)(2,1)} %get-tuple-element.34), calls=%async_computation.1 | async-start | bytes 2097152 | tf_op jit(solution)/shard_map/all_to_all | solution.py:528
  35.3 11.7 %collective-permute-start.1 = (f32[2,2,1024]{2,1,0:T(2,128)}, f32[2,2,1024]{2,1,0:T(2,128)}, u32[]{:S(2)}, u32[]{:S(2)}) collective-permute-start(f32[2,2,1024]{2,1,0:T(2,128)} %shard_map.138.mine), channel_id=1, source_target_pairs={{0,1},{1,0},{2,3},{3,2},{4,5},{5,4},{6,7},{7,6},{8,9},{9,8},{10,11... | collective-permute-start | bytes 49160 | tf_op jit(solution)/shard_map/ppermute | solution.py:515
  57.6 7.4 %collective-permute-start.2 = (bf16[2,1024,256]{2,1,0:T(8,128)(2,1)}, bf16[2,1024,256]{2,1,0:T(8,128)(2,1)}, u32[]{:S(2)}, u32[]{:S(2)}) collective-permute-start(bf16[2,1024,256]{2,1,0:T(8,128)(2,1)} %get-tuple-element.35.mine.attn), channel_id=1, source_target_pairs={{0,1},{1,0},{2,3},{3,2},{4,5},{5,4},{6,7},{7,6},{8,9},{9,8},{10,11... | collective-permute-start | bytes 3145736 | tf_op jit(solution)/shard_map/ppermute | solution.py:515
  57.7 24.7 %all-to-all-start.3 = ((bf16[8,256,256]{2,1,0:T(8,128)(2,1)}), bf16[8,256,256]{2,1,0:T(8,128)(2,1)}, u32[]{:S(2)}, u32[]{:S(2)}) async-start(bf16[8,256,256]{2,1,0:T(8,128)(2,1)} %get-tuple-element.42), calls=%async_computation.3 | async-start | bytes 2097152 | tf_op jit(solution)/shard_map/all_to_all | solution.py:528
  82.4 20.8 %all-to-all-start.2 = ((bf16[8,256,256]{2,1,0:T(8,128)(2,1)}), bf16[8,256,256]{2,1,0:T(8,128)(2,1)}, u32[]{:S(2)}, u32[]{:S(2)}) async-start(bf16[8,256,256]{2,1,0:T(8,128)(2,1)} %get-tuple-element.41), calls=%async_computation.2 | async-start | bytes 2097152 | tf_op jit(solution)/shard_map/all_to_all | solution.py:528
  87.8 17.5 %collective-permute-start.5 = (bf16[2,256,1024]{2,1,0:T(8,128)(2,1)}, bf16[2,256,1024]{2,1,0:T(8,128)(2,1)}, u32[]{:S(2)}, u32[]{:S(2)}) collective-permute-start(bf16[2,256,1024]{2,1,0:T(8,128)(2,1)} %get-tuple-element.39.dq_mine), channel_id=1, source_target_pairs={{0,1},{1,0},{2,3},{3,2},{4,5},{5,4},{6,7},{7,6},{8,9},{9,8},{10,11... | collective-permute-start | bytes 3145736 | tf_op jit(solution)/shard_map/ppermute | solution.py:515
  87.8 17.5 %collective-permute-start.3 = (bf16[256,1024]{1,0:T(8,128)(2,1)}, bf16[256,1024]{1,0:T(8,128)(2,1)}, u32[]{:S(2)}, u32[]{:S(2)}) collective-permute-start(bf16[256,1024]{1,0:T(8,128)(2,1)} %bitcast.1.grad_out.go_own), channel_id=1, source_target_pairs={{0,1},{1,0},{2,3},{3,2},{4,5},{5,4},{6,7},{7,6},{8,9},{9,8},{10,11... | collective-permute-start | bytes 1572872 | tf_op jit(solution)/shard_map/ppermute | solution.py:515
  88.3 17.0 %collective-permute-start.4 = (bf16[4,2,8,8,256]{4,3,2,1,0:T(8,128)(2,1)}, bf16[4,2,8,8,256]{4,3,2,1,0:T(8,128)(2,1)}, u32[]{:S(2)}, u32[]{:S(2)}) collective-permute-start(bf16[4,2,8,8,256]{4,3,2,1,0:T(8,128)(2,1)} %get-tuple-element.37), channel_id=1, source_target_pairs={{0,1},{1,0},{2,3},{3,2},{4,5},{5,4},{6,7},{7,6},{8,9},{9,8},{10,11... | collective-permute-start | bytes 786440 | tf_op jit(solution)/shard_map/ppermute | solution.py:515
  105.3 11.2 %collective-permute-start.9 = (bf16[256,512]{1,0:T(8,128)(2,1)}, bf16[256,512]{1,0:T(8,128)(2,1)}, u32[]{:S(2)}, u32[]{:S(2)}) collective-permute-start(bf16[256,512]{1,0:T(8,128)(2,1)} %shard_map.143.dkv), channel_id=1, source_target_pairs={{0,1},{1,0},{2,3},{3,2},{4,5},{5,4},{6,7},{7,6},{8,9},{9,8},{10,11... | collective-permute-start | bytes 786440 | tf_op jit(solution)/shard_map/ppermute | solution.py:515
  110.6 15.8 %collective-permute-start.6 = (bf16[128,2048]{1,0:T(8,128)(2,1)}, bf16[128,2048]{1,0:T(8,128)(2,1)}, u32[]{:S(2)}, u32[]{:S(2)}) collective-permute-start(bf16[128,2048]{1,0:T(8,128)(2,1)} %get-tuple-element.44), channel_id=1, source_target_pairs={{0,16},{16,32},{32,48},{48,0},{64,80},{80,96},{96,112},{112,64},{1... | collective-permute-start | bytes 1572872 | tf_op jit(solution)/shard_map/ppermute | solution.py:520
  112.0 26.0 %collective-permute-start.7 = (bf16[128,2048]{1,0:T(8,128)(2,1)}, bf16[128,2048]{1,0:T(8,128)(2,1)}, u32[]{:S(2)}, u32[]{:S(2)}) collective-permute-start(bf16[128,2048]{1,0:T(8,128)(2,1)} %get-tuple-element.45), channel_id=1, source_target_pairs={{0,32},{16,48},{32,0},{48,16},{64,96},{80,112},{96,64},{112,80},{1... | collective-permute-start | bytes 1572872 | tf_op jit(solution)/shard_map/ppermute | solution.py:520
  113.9 24.4 %collective-permute-start.8 = (bf16[128,2048]{1,0:T(8,128)(2,1)}, bf16[128,2048]{1,0:T(8,128)(2,1)}, u32[]{:S(2)}, u32[]{:S(2)}) collective-permute-start(bf16[128,2048]{1,0:T(8,128)(2,1)} %get-tuple-element.46), channel_id=1, source_target_pairs={{0,48},{16,0},{32,16},{48,32},{64,112},{80,64},{96,80},{112,96},{1... | collective-permute-start | bytes 1572872 | tf_op jit(solution)/shard_map/ppermute | solution.py:520
  119.0 22.0 %all-to-all-start.5 = ((bf16[16,8,2048]{2,1,0:T(8,128)(2,1)}), bf16[16,8,2048]{2,1,0:T(8,128)(2,1)}, u32[]{:S(2)}, u32[]{:S(2)}) async-start(bf16[16,8,2048]{2,1,0:T(8,128)(2,1)} %bitcast.14), calls=%async_computation.5 | async-start | bytes 1048576 | tf_op jit(solution)/shard_map/all_to_all | solution.py:539
  141.0 17.9 %all-to-all-start.4 = ((bf16[16,8,2048]{2,1,0:T(8,128)(2,1)}), bf16[16,8,2048]{2,1,0:T(8,128)(2,1)}, u32[]{:S(2)}, u32[]{:S(2)}) async-start(bf16[16,8,2048]{2,1,0:T(8,128)(2,1)} %bitcast.13), calls=%async_computation.4 | async-start | bytes 1048576 | tf_op jit(solution)/shard_map/all_to_all | solution.py:539
  149.6 5.2 %collective-permute-start.10 = (bf16[8,512]{1,0:T(8,128)(2,1)}, bf16[8,512]{1,0:T(8,128)(2,1)}, u32[]{:S(2)}, u32[]{:S(2)}) collective-permute-start(bf16[8,512]{1,0:T(8,128)(2,1)} %get-tuple-element.48), channel_id=1, source_target_pairs={{0,16},{16,32},{32,48},{48,0},{64,80},{80,96},{96,112},{112,64},{1... | collective-permute-start | bytes 24584 | tf_op jit(solution)/shard_map/ppermute | solution.py:520
  149.8 5.6 %collective-permute-start.11 = (bf16[8,512]{1,0:T(8,128)(2,1)}, bf16[8,512]{1,0:T(8,128)(2,1)}, u32[]{:S(2)}, u32[]{:S(2)}) collective-permute-start(bf16[8,512]{1,0:T(8,128)(2,1)} %get-tuple-element.49), channel_id=1, source_target_pairs={{0,32},{16,48},{32,0},{48,16},{64,96},{80,112},{96,64},{112,80},{1... | collective-permute-start | bytes 24584 | tf_op jit(solution)/shard_map/ppermute | solution.py:520
  153.4 4.0 %collective-permute-start.12 = (bf16[8,512]{1,0:T(8,128)(2,1)}, bf16[8,512]{1,0:T(8,128)(2,1)}, u32[]{:S(2)}, u32[]{:S(2)}) collective-permute-start(bf16[8,512]{1,0:T(8,128)(2,1)} %get-tuple-element.50), channel_id=1, source_target_pairs={{0,48},{16,0},{32,16},{48,32},{64,112},{80,64},{96,80},{112,96},{1... | collective-permute-start | bytes 24584 | tf_op jit(solution)/shard_map/ppermute | solution.py:520
  160.7 11.7 %all-to-all-start.6 = ((bf16[8,8,2560]{2,1,0:T(8,128)(2,1)}), bf16[8,8,2560]{2,1,0:T(8,128)(2,1)}, u32[]{:S(2)}, u32[]{:S(2)}) async-start(bf16[8,8,2560]{2,1,0:T(8,128)(2,1)} %shard_map.149), calls=%async_computation.6 | async-start | bytes 655360 | tf_op jit(solution)/shard_map/all_to_all | solution.py:626

commit v10 on v9

--- a/solution.py
+++ b/solution.py
@@ -373,8 +373,6 @@
     ]
     for c in copies:
         c.start()
-    for c in copies:
-        c.wait()
     wide, heads_wide = d_out.shape[1], d_query.shape[1]
     gains = []
     for place in range(shared.shape[0]):
@@ -385,11 +383,14 @@
         d_query[rows, :] = query
         d_key[rows, :] = kv[:, :HS]
         d_value[rows, :] = kv[:, HS:]
-        row_sum = (
-            jnp.sum(w_query[rows, :].astype(jnp.float32) * query, axis=1, keepdims=True)
-            + jnp.sum(w_key[rows, :].astype(jnp.float32) * kv[:, :HS], axis=1, keepdims=True)
-            + jnp.sum(w_value[rows, :].astype(jnp.float32) * kv[:, HS:], axis=1, keepdims=True)
-        )
+    for c in copies:
+        c.wait()
+    for place in range(shared.shape[0]):
+        rows = slice(place * size, (place + 1) * size)
+        row_sum = 0.0
+        for weight, grad in ((w_query, d_query), (w_key, d_key), (w_value, d_value)):
+            terms = weight[rows, :].astype(jnp.float32) * grad[rows, :]
+            row_sum = row_sum + jnp.sum(terms, axis=1, keepdims=True)
         gains.append(jnp.broadcast_to(row_sum, (size, 128)))
     d_gain[...] = jnp.concatenate(gains, axis=0).T[0:1, :] / gain[pl.ds(info[0], 1), :]
 

time: 176 us -> 176 us (level)
  no operation moved by 1% of the time
where the time goes in v10:
time: 176 us; the launch traced here: 175 us
  Pallas kernels  62.5 us (36%)
  waiting for transfers between devices  58 us (33%)
  starting transfers between devices  50.6 us (29%)
  between operations  2.21 us (1%)
  local copies, waits for them, and re-layouts  2.01 us (1%)
    pallas_call x15, Pallas kernels, call(): pl.pallas_call(body, out_shape=outs, in_specs=specs, out_specs=out_specs,...  62.5 us
    all_to_all x4, waiting for transfers between devices, exchange_chips(): lax.all_to_all(value, 'blk', 0, 0, tiled=True, axis_index_groups=groups)  37.1 us
    all_to_all x4, starting transfers between devices, exchange_chips(): lax.all_to_all(value, 'blk', 0, 0, tiled=True, axis_index_groups=groups)  24.9 us
    ppermute x6, waiting for transfers between devices, send_along_x(): lax.ppermute(value, 'dp', [(i, i // X * X + (i + step) % X) for i in rang...  18.9 us
    all_to_all x2, starting transfers between devices, exchange_plane(): lax.all_to_all(value, ('dp', 'blk'), 0, 0, tiled=True, axis_index_groups=...  11.2 us
    ppermute x6, starting transfers between devices, send_along_x(): lax.ppermute(value, 'dp', [(i, i // X * X + (i + step) % X) for i in rang...  9.73 us
    all_to_all x1, starting transfers between devices, whole(): shared = lax.all_to_all(copies, 'dp', 0, 0, tiled=True)  4.08 us
  transfers between devices with their start and end apart: 20, of which 12 were waited for; matrix products, arithmetic and copies ran while one was open for 1% of the time, Pallas kernels for 25%

profile of v10, /device:TPU:0, one launch (start us, length us, event | category | flops | bytes accessed | tf_op | source)
XLA Modules:
  0.0 175.3 jit_solution(17465707016267590102)
XLA Ops:
  0.6 2.6 %shard_map.136 = (bf16[256,1024]{1,0:T(8,128)(2,1)}, bf16[8,256,256]{2,1,0:T(8,128)(2,1)}) custom-call(bf16[256,1024]{1,0:T(8,128)(2,1)} %bitcast.10, f32[1,1024]{1,0:T(1,128)} %bitcast.15, bf16[1024,256]{1,0:T(8,128)(2,1)} %wk_in.1), custom_call_target="tpu_custom_call" | custom-call | flops 268435456 | bytes 1048576 | tf_op jit(solution)/shard_map/pallas_call | solution.py:427
  3.2 7.9 %all-to-all-start = ((bf16[8,256,256]{2,1,0:T(8,128)(2,1)}), bf16[8,256,256]{2,1,0:T(8,128)(2,1)}, u32[]{:S(2)}, u32[]{:S(2)}) async-start(bf16[8,256,256]{2,1,0:T(8,128)(2,1)} %get-tuple-element.33), calls=%async_computation | async-start | bytes 2097152 | tf_op jit(solution)/shard_map/all_to_all | solution.py:529
  12.4 0.7 stack.16.info
  13.1 6.2 %shard_map.137 = (bf16[2,256,1024]{2,1,0:T(8,128)(2,1)}, bf16[8,256,256]{2,1,0:T(8,128)(2,1)}, bf16[4,2,8,8,256]{4,3,2,1,0:T(8,128)(2,1)}, bf16[4,2,8,8,256]{4,3,2,1,0:T(8,128)(2,1)}) custom-call(s32[5]{0:T(128)} %stack.16.info, bf16[256,1024]{1,0:T(8,128)(2,1)} %get-tuple-element.31.hidden, bf16[256,1024]{1,0:T(8,128)(2,1)} %bitcast.1.grad_out.go_own, ...), custom_call_target="tpu_custom_call" | custom-call | flops 1073741824 | bytes 1048576 | tf_op jit(solution)/shard_map/pallas_call | solution.py:427
  19.3 0.0 collective-permute-start
  19.3 7.8 %all-to-all-done.keys.keys_in = bf16[8,256,256]{2,1,0:T(8,128)(2,1)} async-done(((bf16[8,256,256]{2,1,0:T(8,128)(2,1)}), bf16[8,256,256]{2,1,0:T(8,128)(2,1)}, u32[]{:S(2)}, u32[]{:S(2)}) %all-to-all-start) | async-done | bytes 1048608 | tf_op jit(solution)/shard_map/all_to_all | solution.py:529
  27.2 4.2 %all-to-all-start.1 = ((bf16[8,256,256]{2,1,0:T(8,128)(2,1)}), bf16[8,256,256]{2,1,0:T(8,128)(2,1)}, u32[]{:S(2)}, u32[]{:S(2)}) async-start(bf16[8,256,256]{2,1,0:T(8,128)(2,1)} %get-tuple-element.34), calls=%async_computation.1 | async-start | bytes 2097152 | tf_op jit(solution)/shard_map/all_to_all | solution.py:529
  31.4 0.0 collective-permute-done.pair
  31.4 3.8 %shard_map.138.mine = f32[2,2,1024]{2,1,0:T(2,128)} custom-call(s32[5]{0:T(128)} %stack.16.info, bf16[2,256,1024]{2,1,0:T(8,128)(2,1)} %get-tuple-element.32.own, bf16[2,256,1024]{2,1,0:T(8,128)(2,1)} %collective-permute-done.pair, bf16[8,256,256]{2,1,0:T(8,128)(2,1)} %all-to-all-done.keys.keys_in), custom_call_target="tpu_custom_call" | custom-call | flops 2147483648 | bytes 1048576 | tf_op jit(solution)/shard_map/pallas_call | solution.py:427
  35.3 0.0 collective-permute-start.1
  35.3 11.7 %all-to-all-done.1.values_in.values = bf16[8,256,256]{2,1,0:T(8,128)(2,1)} async-done(((bf16[8,256,256]{2,1,0:T(8,128)(2,1)}), bf16[8,256,256]{2,1,0:T(8,128)(2,1)}, u32[]{:S(2)}, u32[]{:S(2)}) %all-to-all-start.1) | async-done | bytes 1048608 | tf_op jit(solution)/shard_map/all_to_all | solution.py:529
  46.9 0.0 collective-permute-done.1.other
  46.9 10.7 %shard_map.139 = (bf16[2,1024,256]{2,1,0:T(8,128)(2,1)}, bf16[8,256,256]{2,1,0:T(8,128)(2,1)}, bf16[2048,2048]{1,0:T(8,128)(2,1)}) custom-call(s32[5]{0:T(128)} %stack.16.info, bf16[2,256,1024]{2,1,0:T(8,128)(2,1)} %get-tuple-element.32.own, bf16[2,256,1024]{2,1,0:T(8,128)(2,1)} %collective-permute-done.pair, f32[2,2,1024]{2,1,0:T(2,128)} %shard_map.138.mine, ...), custom_call_target="tpu_custom_call" | custom-call | flops 6442450944 | bytes 1048576 | tf_op jit(solution)/shard_map/pallas_call | solution.py:427
  57.6 0.1 collective-permute-start.2
  57.7 7.3 %all-to-all-start.3 = ((bf16[8,256,256]{2,1,0:T(8,128)(2,1)}), bf16[8,256,256]{2,1,0:T(8,128)(2,1)}, u32[]{:S(2)}, u32[]{:S(2)}) async-start(bf16[8,256,256]{2,1,0:T(8,128)(2,1)} %get-tuple-element.42), calls=%async_computation.3 | async-start | bytes 2097152 | tf_op jit(solution)/shard_map/all_to_all | solution.py:529
  65.0 0.0 collective-permute-done.2.other.attn_other
  65.0 12.6 %shard_map.140 = (bf16[8,256,256]{2,1,0:T(8,128)(2,1)}, bf16[2,256,1024]{2,1,0:T(8,128)(2,1)}) custom-call(s32[5]{0:T(128)} %stack.16.info, bf16[2,256,1024]{2,1,0:T(8,128)(2,1)} %get-tuple-element.32.own, bf16[2,256,1024]{2,1,0:T(8,128)(2,1)} %collective-permute-done.pair, bf16[2,1024,256]{2,1,0:T(8,128)(2,1)} %get-tuple-element.35.mine.attn, ...), custom_call_target="tpu_custom_call" | custom-call | flops 6442450944 | bytes 1048576 | tf_op jit(solution)/shard_map/pallas_call | solution.py:427
  77.6 4.8 %all-to-all-done.3.parts = bf16[8,256,256]{2,1,0:T(8,128)(2,1)} async-done(((bf16[8,256,256]{2,1,0:T(8,128)(2,1)}), bf16[8,256,256]{2,1,0:T(8,128)(2,1)}, u32[]{:S(2)}, u32[]{:S(2)}) %all-to-all-start.3) | async-done | bytes 1048608 | tf_op jit(solution)/shard_map/all_to_all | solution.py:529
  82.4 5.4 %all-to-all-start.2 = ((bf16[8,256,256]{2,1,0:T(8,128)(2,1)}), bf16[8,256,256]{2,1,0:T(8,128)(2,1)}, u32[]{:S(2)}, u32[]{:S(2)}) async-start(bf16[8,256,256]{2,1,0:T(8,128)(2,1)} %get-tuple-element.41), calls=%async_computation.2 | async-start | bytes 2097152 | tf_op jit(solution)/shard_map/all_to_all | solution.py:529
  87.8 0.0 collective-permute-start.5
  87.8 0.5 collective-permute-start.3
  88.3 0.1 collective-permute-start.4
  88.4 2.0 %shard_map.142.dv_rows = bf16[256,256]{1,0:T(8,128)(2,1)} custom-call(bf16[8,256,256]{2,1,0:T(8,128)(2,1)} %all-to-all-done.3.parts), custom_call_target="tpu_custom_call" | custom-call | flops 1073741824 | bytes 1048576 | tf_op jit(solution)/shard_map/pallas_call | solution.py:427
  90.4 12.8 %all-to-all-done.2.dk_parts = bf16[8,256,256]{2,1,0:T(8,128)(2,1)} async-done(((bf16[8,256,256]{2,1,0:T(8,128)(2,1)}), bf16[8,256,256]{2,1,0:T(8,128)(2,1)}, u32[]{:S(2)}, u32[]{:S(2)}) %all-to-all-start.2) | async-done | bytes 1048608 | tf_op jit(solution)/shard_map/all_to_all | solution.py:529
  103.2 2.1 %shard_map.143.dkv = bf16[256,512]{1,0:T(8,128)(2,1)} custom-call(bf16[8,256,256]{2,1,0:T(8,128)(2,1)} %all-to-all-done.2.dk_parts, bf16[256,256]{1,0:T(8,128)(2,1)} %shard_map.142.dv_rows), custom_call_target="tpu_custom_call" | custom-call | flops 1073741824 | bytes 1048576 | tf_op jit(solution)/shard_map/pallas_call | solution.py:427
  105.3 0.0 collective-permute-start.9
  105.3 0.0 collective-permute-done.4.ht_pair
  105.3 0.0 collective-permute-done.3.go_pair
  105.3 0.0 collective-permute-done.5.dq_other
  105.3 5.3 %shard_map.141 = (bf16[256,1024]{1,0:T(8,128)(2,1)}, f32[128,2048]{1,0:T(8,128)}, bf16[128,2048]{1,0:T(8,128)(2,1)}, bf16[128,2048]{1,0:T(8,128)(2,1)}, bf16[128,2048]{1,0:T(8,128)(2,1)}) custom-call(s32[5]{0:T(128)} %stack.16.info, bf16[2,1024,256]{2,1,0:T(8,128)(2,1)} %get-tuple-element.35.mine.attn, ...), custom_call_target="tpu_custom_call" | custom-call | flops 1073741824 | bytes 1048576 | tf_op jit(solution)/shard_map/pallas_call | solution.py:427
  110.6 1.4 collective-permute-start.6
  112.0 1.9 %collective-permute-start.7 = (bf16[128,2048]{1,0:T(8,128)(2,1)}, bf16[128,2048]{1,0:T(8,128)(2,1)}, u32[]{:S(2)}, u32[]{:S(2)}) collective-permute-start(bf16[128,2048]{1,0:T(8,128)(2,1)} %get-tuple-element.45), channel_id=1, source_target_pairs={{0,32},{16,48},{32,0},{48,16},{64,96},{80,112},{96,64},{112,80},{1... | collective-permute-start | bytes 1572872 | tf_op jit(solution)/shard_map/ppermute | solution.py:521
  113.9 2.6 %collective-permute-start.8 = (bf16[128,2048]{1,0:T(8,128)(2,1)}, bf16[128,2048]{1,0:T(8,128)(2,1)}, u32[]{:S(2)}, u32[]{:S(2)}) collective-permute-start(bf16[128,2048]{1,0:T(8,128)(2,1)} %get-tuple-element.46), channel_id=1, source_target_pairs={{0,48},{16,0},{32,16},{48,32},{64,112},{80,64},{96,80},{112,96},{1... | collective-permute-start | bytes 1572872 | tf_op jit(solution)/shard_map/ppermute | solution.py:521
  116.5 0.0 collective-permute-done.9.dkv_pair
  116.5 2.5 %shard_map.146 = bf16[128,2048]{1,0:T(8,128)(2,1)} custom-call(s32[5]{0:T(128)} %stack.16.info, bf16[4,2,8,8,256]{4,3,2,1,0:T(8,128)(2,1)} %get-tuple-element.36.ht_own, bf16[4,2,8,8,256]{4,3,2,1,0:T(8,128)(2,1)} %collective-permute-done.4.ht_pair, bf16[256,512]{1,0:T(8,128)(2,1)} %shard_map.143.dkv, bf16[256,512]{1,0:T(8,128)(2,1)} %collective-permute-done.9.dkv_pair), custom_call_target="tpu_custom_call" | custom-call | flops 1073741824 | bytes 1048576 | tf_op jit(solution)/shard_map/pallas_call | solution.py:427
  119.0 4.3 %all-to-all-start.5 = ((bf16[16,8,2048]{2,1,0:T(8,128)(2,1)}), bf16[16,8,2048]{2,1,0:T(8,128)(2,1)}, u32[]{:S(2)}, u32[]{:S(2)}) async-start(bf16[16,8,2048]{2,1,0:T(8,128)(2,1)} %bitcast.14), calls=%async_computation.5 | async-start | bytes 1048576 | tf_op jit(solution)/shard_map/all_to_all | solution.py:540
  123.3 3.1 %collective-permute-done.6.one = bf16[128,2048]{1,0:T(8,128)(2,1)} collective-permute-done((bf16[128,2048]{1,0:T(8,128)(2,1)}, bf16[128,2048]{1,0:T(8,128)(2,1)}, u32[]{:S(2)}, u32[]{:S(2)}) %collective-permute-start.6) | collective-permute-done | bytes 524320 | tf_op jit(solution)/shard_map/ppermute | solution.py:521
  126.4 11.6 %collective-permute-done.7.two = bf16[128,2048]{1,0:T(8,128)(2,1)} collective-permute-done((bf16[128,2048]{1,0:T(8,128)(2,1)}, bf16[128,2048]{1,0:T(8,128)(2,1)}, u32[]{:S(2)}, u32[]{:S(2)}) %collective-permute-start.7) | collective-permute-done | bytes 524320 | tf_op jit(solution)/shard_map/ppermute | solution.py:521
  138.0 0.3 collective-permute-done.8.three
  138.3 2.7 %shard_map.145 = bf16[128,2048]{1,0:T(8,128)(2,1)} custom-call(f32[128,2048]{1,0:T(8,128)} %get-tuple-element.43.base, bf16[128,2048]{1,0:T(8,128)(2,1)} %collective-permute-done.6.one, bf16[128,2048]{1,0:T(8,128)(2,1)} %collective-permute-done.7.two, bf16[128,2048]{1,0:T(8,128)(2,1)} %collective-permute-done.8.three), custom_call_target="tpu_custom_call" | custom-call | flops 1073741824 | bytes 1048576 | tf_op jit(solution)/shard_map/pallas_call | solution.py:427
  141.0 0.0 all-to-all-done.5.parts
  141.0 6.9 %all-to-all-start.4 = ((bf16[16,8,2048]{2,1,0:T(8,128)(2,1)}), bf16[16,8,2048]{2,1,0:T(8,128)(2,1)}, u32[]{:S(2)}, u32[]{:S(2)}) async-start(bf16[16,8,2048]{2,1,0:T(8,128)(2,1)} %bitcast.13), calls=%async_computation.4 | async-start | bytes 1048576 | tf_op jit(solution)/shard_map/all_to_all | solution.py:540
  147.8 1.7 shard_map.147
  149.6 0.2 collective-permute-start.10
  149.8 3.6 %collective-permute-start.11 = (bf16[8,512]{1,0:T(8,128)(2,1)}, bf16[8,512]{1,0:T(8,128)(2,1)}, u32[]{:S(2)}, u32[]{:S(2)}) collective-permute-start(bf16[8,512]{1,0:T(8,128)(2,1)} %get-tuple-element.49), channel_id=1, source_target_pairs={{0,32},{16,48},{32,0},{48,16},{64,96},{80,112},{96,64},{112,80},{1... | collective-permute-start | bytes 24584 | tf_op jit(solution)/shard_map/ppermute | solution.py:521
  153.4 0.0 collective-permute-start.12
  153.4 1.4 collective-permute-done.10.one
  154.8 0.7 collective-permute-done.11.two
  155.4 1.9 %collective-permute-done.12.three = bf16[8,512]{1,0:T(8,128)(2,1)} collective-permute-done((bf16[8,512]{1,0:T(8,128)(2,1)}, bf16[8,512]{1,0:T(8,128)(2,1)}, u32[]{:S(2)}, u32[]{:S(2)}) %collective-permute-start.12) | collective-permute-done | bytes 8224 | tf_op jit(solution)/shard_map/ppermute | solution.py:521
  157.3 1.4 shard_map.148.kv
  158.7 0.1 all-to-all-done.4.parts
  158.8 1.8 %shard_map.149 = bf16[8,8,2560]{2,1,0:T(8,128)(2,1)} custom-call(bf16[16,8,2048]{2,1,0:T(8,128)(2,1)} %all-to-all-done.4.parts, bf16[8,512]{1,0:T(8,128)(2,1)} %shard_map.148.kv), custom_call_target="tpu_custom_call" | custom-call | flops 1073741824 | bytes 1048576 | tf_op jit(solution)/shard_map/pallas_call | solution.py:427
  160.7 4.1 %all-to-all-start.6 = ((bf16[8,8,2560]{2,1,0:T(8,128)(2,1)}), bf16[8,8,2560]{2,1,0:T(8,128)(2,1)}, u32[]{:S(2)}, u32[]{:S(2)}) async-start(bf16[8,8,2560]{2,1,0:T(8,128)(2,1)} %shard_map.149), calls=%async_computation.6 | async-start | bytes 655360 | tf_op jit(solution)/shard_map/all_to_all | solution.py:627
  164.8 1.3 reshape.33.gain
  166.1 4.4 %shard_map.144 = bf16[256,1024]{1,0:T(8,128)(2,1)} custom-call(bf16[256,1024]{1,0:T(8,128)(2,1)} %bitcast.11, bf16[256,1024]{1,0:T(8,128)(2,1)} %bitcast.1.grad_out.go_own, f32[1,1024]{1,0:T(1,128)} %bitcast.16, bf16[256,1024]{1,0:T(8,128)(2,1)} %get-tuple-element.40.dq, bf16[256,512]{1,0:T(8,128)(2,1)} %shard_map.143.dkv, bf16[1024,1024]{1,0:T(8,128)(2,1)} %wq_in.1, ...), custom_call_target="tpu_custom_call" | custom-call | flops 805306368 | bytes 1048576 | tf_op jit(solution)/shard_map/pallas_call | solution.py:427
  170.6 1.9 %all-to-all-done.6.shared = bf16[8,8,2560]{2,1,0:T(8,128)(2,1)} async-done(((bf16[8,8,2560]{2,1,0:T(8,128)(2,1)}), bf16[8,8,2560]{2,1,0:T(8,128)(2,1)}, u32[]{:S(2)}, u32[]{:S(2)}) %all-to-all-start.6) | async-done | bytes 327712 | tf_op jit(solution)/shard_map/all_to_all | solution.py:627
  172.4 2.7 %shard_map.150 = (f32[64,1024]{1,0:T(8,128)}, f32[64,256]{1,0:T(8,128)}, f32[64,256]{1,0:T(8,128)}, f32[64,1024]{1,0:T(8,128)}, f32[1,64]{1,0:T(1,128)}) custom-call(s32[5]{0:T(128)} %stack.16.info, bf16[8,8,2560]{2,1,0:T(8,128)(2,1)} %all-to-all-done.6.shared, f32[16,64]{1,0:T(8,128)} %reshape.33.gain, bf16[1024,1024]{1,0:T(8,128)(2,1)} %wq_in.1, ...), custom_call_target="tpu_custom_call" | custom-call | flops 1073741824 | bytes 1048576 | tf_op jit(solution)/shard_map/pallas_call | solution.py:427
Async XLA Ops:
  3.2 23.9 %all-to-all-start = ((bf16[8,256,256]{2,1,0:T(8,128)(2,1)}), bf16[8,256,256]{2,1,0:T(8,128)(2,1)}, u32[]{:S(2)}, u32[]{:S(2)}) async-start(bf16[8,256,256]{2,1,0:T(8,128)(2,1)} %get-tuple-element.33), calls=%async_computation | async-start | bytes 2097152 | tf_op jit(solution)/shard_map/all_to_all | solution.py:529
  19.3 12.1 %collective-permute-start = (bf16[2,256,1024]{2,1,0:T(8,128)(2,1)}, bf16[2,256,1024]{2,1,0:T(8,128)(2,1)}, u32[]{:S(2)}, u32[]{:S(2)}) collective-permute-start(bf16[2,256,1024]{2,1,0:T(8,128)(2,1)} %get-tuple-element.32.own), channel_id=1, source_target_pairs={{0,1},{1,0},{2,3},{3,2},{4,5},{5,4},{6,7},{7,6},{8,9},{9,8},{10,11... | collective-permute-start | bytes 3145736 | tf_op jit(solution)/shard_map/ppermute | solution.py:516
  27.2 19.8 %all-to-all-start.1 = ((bf16[8,256,256]{2,1,0:T(8,128)(2,1)}), bf16[8,256,256]{2,1,0:T(8,128)(2,1)}, u32[]{:S(2)}, u32[]{:S(2)}) async-start(bf16[8,256,256]{2,1,0:T(8,128)(2,1)} %get-tuple-element.34), calls=%async_computation.1 | async-start | bytes 2097152 | tf_op jit(solution)/shard_map/all_to_all | solution.py:529
  35.3 11.7 %collective-permute-start.1 = (f32[2,2,1024]{2,1,0:T(2,128)}, f32[2,2,1024]{2,1,0:T(2,128)}, u32[]{:S(2)}, u32[]{:S(2)}) collective-permute-start(f32[2,2,1024]{2,1,0:T(2,128)} %shard_map.138.mine), channel_id=1, source_target_pairs={{0,1},{1,0},{2,3},{3,2},{4,5},{5,4},{6,7},{7,6},{8,9},{9,8},{10,11... | collective-permute-start | bytes 49160 | tf_op jit(solution)/shard_map/ppermute | solution.py:516
  57.6 7.4 %collective-permute-start.2 = (bf16[2,1024,256]{2,1,0:T(8,128)(2,1)}, bf16[2,1024,256]{2,1,0:T(8,128)(2,1)}, u32[]{:S(2)}, u32[]{:S(2)}) collective-permute-start(bf16[2,1024,256]{2,1,0:T(8,128)(2,1)} %get-tuple-element.35.mine.attn), channel_id=1, source_target_pairs={{0,1},{1,0},{2,3},{3,2},{4,5},{5,4},{6,7},{7,6},{8,9},{9,8},{10,11... | collective-permute-start | bytes 3145736 | tf_op jit(solution)/shard_map/ppermute | solution.py:516
  57.7 24.7 %all-to-all-start.3 = ((bf16[8,256,256]{2,1,0:T(8,128)(2,1)}), bf16[8,256,256]{2,1,0:T(8,128)(2,1)}, u32[]{:S(2)}, u32[]{:S(2)}) async-start(bf16[8,256,256]{2,1,0:T(8,128)(2,1)} %get-tuple-element.42), calls=%async_computation.3 | async-start | bytes 2097152 | tf_op jit(solution)/shard_map/all_to_all | solution.py:529
  82.4 20.8 %all-to-all-start.2 = ((bf16[8,256,256]{2,1,0:T(8,128)(2,1)}), bf16[8,256,256]{2,1,0:T(8,128)(2,1)}, u32[]{:S(2)}, u32[]{:S(2)}) async-start(bf16[8,256,256]{2,1,0:T(8,128)(2,1)} %get-tuple-element.41), calls=%async_computation.2 | async-start | bytes 2097152 | tf_op jit(solution)/shard_map/all_to_all | solution.py:529
  87.8 17.5 %collective-permute-start.5 = (bf16[2,256,1024]{2,1,0:T(8,128)(2,1)}, bf16[2,256,1024]{2,1,0:T(8,128)(2,1)}, u32[]{:S(2)}, u32[]{:S(2)}) collective-permute-start(bf16[2,256,1024]{2,1,0:T(8,128)(2,1)} %get-tuple-element.39.dq_mine), channel_id=1, source_target_pairs={{0,1},{1,0},{2,3},{3,2},{4,5},{5,4},{6,7},{7,6},{8,9},{9,8},{10,11... | collective-permute-start | bytes 3145736 | tf_op jit(solution)/shard_map/ppermute | solution.py:516
  87.8 17.5 %collective-permute-start.3 = (bf16[256,1024]{1,0:T(8,128)(2,1)}, bf16[256,1024]{1,0:T(8,128)(2,1)}, u32[]{:S(2)}, u32[]{:S(2)}) collective-permute-start(bf16[256,1024]{1,0:T(8,128)(2,1)} %bitcast.1.grad_out.go_own), channel_id=1, source_target_pairs={{0,1},{1,0},{2,3},{3,2},{4,5},{5,4},{6,7},{7,6},{8,9},{9,8},{10,11... | collective-permute-start | bytes 1572872 | tf_op jit(solution)/shard_map/ppermute | solution.py:516
  88.3 17.0 %collective-permute-start.4 = (bf16[4,2,8,8,256]{4,3,2,1,0:T(8,128)(2,1)}, bf16[4,2,8,8,256]{4,3,2,1,0:T(8,128)(2,1)}, u32[]{:S(2)}, u32[]{:S(2)}) collective-permute-start(bf16[4,2,8,8,256]{4,3,2,1,0:T(8,128)(2,1)} %get-tuple-element.37), channel_id=1, source_target_pairs={{0,1},{1,0},{2,3},{3,2},{4,5},{5,4},{6,7},{7,6},{8,9},{9,8},{10,11... | collective-permute-start | bytes 786440 | tf_op jit(solution)/shard_map/ppermute | solution.py:516
  105.3 11.2 %collective-permute-start.9 = (bf16[256,512]{1,0:T(8,128)(2,1)}, bf16[256,512]{1,0:T(8,128)(2,1)}, u32[]{:S(2)}, u32[]{:S(2)}) collective-permute-start(bf16[256,512]{1,0:T(8,128)(2,1)} %shard_map.143.dkv), channel_id=1, source_target_pairs={{0,1},{1,0},{2,3},{3,2},{4,5},{5,4},{6,7},{7,6},{8,9},{9,8},{10,11... | collective-permute-start | bytes 786440 | tf_op jit(solution)/shard_map/ppermute | solution.py:516
  110.6 15.8 %collective-permute-start.6 = (bf16[128,2048]{1,0:T(8,128)(2,1)}, bf16[128,2048]{1,0:T(8,128)(2,1)}, u32[]{:S(2)}, u32[]{:S(2)}) collective-permute-start(bf16[128,2048]{1,0:T(8,128)(2,1)} %get-tuple-element.44), channel_id=1, source_target_pairs={{0,16},{16,32},{32,48},{48,0},{64,80},{80,96},{96,112},{112,64},{1... | collective-permute-start | bytes 1572872 | tf_op jit(solution)/shard_map/ppermute | solution.py:521
  112.0 26.0 %collective-permute-start.7 = (bf16[128,2048]{1,0:T(8,128)(2,1)}, bf16[128,2048]{1,0:T(8,128)(2,1)}, u32[]{:S(2)}, u32[]{:S(2)}) collective-permute-start(bf16[128,2048]{1,0:T(8,128)(2,1)} %get-tuple-element.45), channel_id=1, source_target_pairs={{0,32},{16,48},{32,0},{48,16},{64,96},{80,112},{96,64},{112,80},{1... | collective-permute-start | bytes 1572872 | tf_op jit(solution)/shard_map/ppermute | solution.py:521
  113.9 24.4 %collective-permute-start.8 = (bf16[128,2048]{1,0:T(8,128)(2,1)}, bf16[128,2048]{1,0:T(8,128)(2,1)}, u32[]{:S(2)}, u32[]{:S(2)}) collective-permute-start(bf16[128,2048]{1,0:T(8,128)(2,1)} %get-tuple-element.46), channel_id=1, source_target_pairs={{0,48},{16,0},{32,16},{48,32},{64,112},{80,64},{96,80},{112,96},{1... | collective-permute-start | bytes 1572872 | tf_op jit(solution)/shard_map/ppermute | solution.py:521
  119.0 22.0 %all-to-all-start.5 = ((bf16[16,8,2048]{2,1,0:T(8,128)(2,1)}), bf16[16,8,2048]{2,1,0:T(8,128)(2,1)}, u32[]{:S(2)}, u32[]{:S(2)}) async-start(bf16[16,8,2048]{2,1,0:T(8,128)(2,1)} %bitcast.14), calls=%async_computation.5 | async-start | bytes 1048576 | tf_op jit(solution)/shard_map/all_to_all | solution.py:540
  141.0 17.9 %all-to-all-start.4 = ((bf16[16,8,2048]{2,1,0:T(8,128)(2,1)}), bf16[16,8,2048]{2,1,0:T(8,128)(2,1)}, u32[]{:S(2)}, u32[]{:S(2)}) async-start(bf16[16,8,2048]{2,1,0:T(8,128)(2,1)} %bitcast.13), calls=%async_computation.4 | async-start | bytes 1048576 | tf_op jit(solution)/shard_map/all_to_all | solution.py:540
  149.6 5.2 %collective-permute-start.10 = (bf16[8,512]{1,0:T(8,128)(2,1)}, bf16[8,512]{1,0:T(8,128)(2,1)}, u32[]{:S(2)}, u32[]{:S(2)}) collective-permute-start(bf16[8,512]{1,0:T(8,128)(2,1)} %get-tuple-element.48), channel_id=1, source_target_pairs={{0,16},{16,32},{32,48},{48,0},{64,80},{80,96},{96,112},{112,64},{1... | collective-permute-start | bytes 24584 | tf_op jit(solution)/shard_map/ppermute | solution.py:521
  149.8 5.6 %collective-permute-start.11 = (bf16[8,512]{1,0:T(8,128)(2,1)}, bf16[8,512]{1,0:T(8,128)(2,1)}, u32[]{:S(2)}, u32[]{:S(2)}) collective-permute-start(bf16[8,512]{1,0:T(8,128)(2,1)} %get-tuple-element.49), channel_id=1, source_target_pairs={{0,32},{16,48},{32,0},{48,16},{64,96},{80,112},{96,64},{112,80},{1... | collective-permute-start | bytes 24584 | tf_op jit(solution)/shard_map/ppermute | solution.py:521
  153.4 4.0 %collective-permute-start.12 = (bf16[8,512]{1,0:T(8,128)(2,1)}, bf16[8,512]{1,0:T(8,128)(2,1)}, u32[]{:S(2)}, u32[]{:S(2)}) collective-permute-start(bf16[8,512]{1,0:T(8,128)(2,1)} %get-tuple-element.50), channel_id=1, source_target_pairs={{0,48},{16,0},{32,16},{48,32},{64,112},{80,64},{96,80},{112,96},{1... | collective-permute-start | bytes 24584 | tf_op jit(solution)/shard_map/ppermute | solution.py:521
  160.7 11.7 %all-to-all-start.6 = ((bf16[8,8,2560]{2,1,0:T(8,128)(2,1)}), bf16[8,8,2560]{2,1,0:T(8,128)(2,1)}, u32[]{:S(2)}, u32[]{:S(2)}) async-start(bf16[8,8,2560]{2,1,0:T(8,128)(2,1)} %shard_map.149), calls=%async_computation.6 | async-start | bytes 655360 | tf_op jit(solution)/shard_map/all_to_all | solution.py:627
